TPU v7x, 128 devices: a whole 4x4x4 slice. The times are simulated.
128 devices in a mesh: dp: 4 (over z_lo, core), ulysses: 4 (over y), expert: 8 (over x, z_hi).
Axes of the slice: x: 4, y: 4, z: 4 (z_hi: 2, z_lo: 2; z = z_hi * 2 + z_lo), core: 2. Of those that a mesh axis runs over, the one named last changes fastest.
Arguments:
- residual: bfloat16 [16384, 4096], P(('dp', 'ulysses', 'expert')), may hold values from -24 to 24
- norm_gain: float32 [4096], replicated, may hold values from 0.1 to 1.9
- grad_out: bfloat16 [16384, 4096], P(('dp', 'ulysses', 'expert')), may hold values from -24 to 24
- expert_ids: int32 [16384, 2], P(('dp', 'ulysses', 'expert')), may hold values from 0 to 7, all different within a row; in each aligned block of 128 rows (0 to 127, 128 to 255, ...) at most 48 rows name the same one
- route_weights: bfloat16 [16384, 2], P(('dp', 'ulysses', 'expert')), may hold values from 0.099609375 to 1
- weight_in: bfloat16 [8, 4096, 1536], P('expert'), may hold values from -0.09375 to 0.09375
- weight_down: bfloat16 [8, 768, 4096], P('expert'), may hold values from -0.21875 to 0.21875
Outputs:
- grad_residual: bfloat16 [16384, 4096], P(('dp', 'ulysses', 'expert'))
- route_grad: bfloat16 [16384, 2], P(('dp', 'ulysses', 'expert'))
- grad_in: float32 [8, 4096, 1536], P('expert', ('dp', 'ulysses'))
- grad_down: float32 [8, 4096, 768], P('expert', ('dp', 'ulysses'))
Inputs may be any that keep to these rules, and one draw needn't show every extreme that they name: `expert_ids`: each row names 2 different experts. Among the rows of one device no expert is named more than 48 times, and in some devices' rows one expert is named exactly 48 times.
All inputs are finite; a program needn't handle non-finite values.
Results may differ from a plain program's by a relative error of at most 0.017.
Values may be sent and summed in bfloat16 or wider, within the bound.
No kernel may reach another device: no remote copies, remote signals or barrier semaphores. Data moves between devices by JAX's collectives and lax.ppermute only.
A program may use at most 192 MiB of HBM per device.

v0:
```python
import jax
import jax.numpy as jnp
from jax import lax
from jax.sharding import Mesh
from jax.sharding import PartitionSpec as P

DP_ULYSSES = ("dp_0", "dp_1", "ulysses")
DP_ULYSSES_EXPERT = ("dp_0", "dp_1", "ulysses", "expert")


eps = 1e-06


def sum_in_order(blocks, axes, sequence):
    dims = [lax.axis_size(a) for a in axes]
    blocks = blocks.reshape(*dims, *blocks.shape[1:])
    blocks = blocks.transpose(*sequence, *range(len(axes), blocks.ndim))
    blocks = blocks.reshape(-1, *blocks.shape[len(axes) :])
    for k in sequence:
        blocks = lax.psum_scatter(blocks, axes[k], scatter_dimension=0, tiled=True)
    return blocks[0]


def split_up(value, dim, length):
    before, after = (value.shape[:dim], value.shape[dim + 1 :])
    return jnp.moveaxis(value.reshape(*before, length, -1, *after), dim, 0)


def sum_by_axis(value, axes, sequence, dim):
    length = lax.axis_size(axes)
    return sum_in_order(split_up(value, dim, length), axes, sequence)


def contract_rows(left, right):
    return lax.dot_general(
        left, right, (((0,), (0,)), ((), ())), preferred_element_type=jnp.float32
    )


def contract_cols(left, right):
    return lax.dot_general(
        left, right, (((1,), (1,)), ((), ())), preferred_element_type=jnp.float32
    )


def per_device(residual, norm_gain, grad_out, expert_ids, route_weights, weight_in, weight_down):
    tok_rows, width = residual.shape
    topk = expert_ids.shape[1]
    hidden_width = weight_down.shape[1]
    experts = lax.axis_size("expert")
    capacity = min(tok_rows, 3 * tok_rows * topk // (2 * experts))
    slot_total = experts * capacity
    resid = residual.astype(jnp.float32)
    inv_rms = lax.rsqrt(jnp.mean(resid * resid, axis=-1, keepdims=True) + eps)
    unit_rows = resid * inv_rms
    normed = (unit_rows * norm_gain).astype(jnp.bfloat16)
    flat_ids = expert_ids.reshape(-1)
    one_hot = (flat_ids[:, None] == jnp.arange(experts, dtype=jnp.int32)[None, :]).astype(jnp.int32)
    ranks = jnp.cumsum(one_hot, axis=0) - one_hot
    target = flat_ids * capacity + jnp.sum(ranks * one_hot, axis=1)
    select = (target[None, :] == jnp.arange(slot_total, dtype=jnp.int32)[:, None]).astype(
        jnp.bfloat16
    )
    per_token = jnp.sum(select.reshape(slot_total, tok_rows, topk), axis=2)
    send_normed = jnp.dot(per_token, normed, preferred_element_type=jnp.float32).astype(
        jnp.bfloat16
    )
    send_grad = jnp.dot(per_token, grad_out, preferred_element_type=jnp.float32).astype(
        jnp.bfloat16
    )
    send_weight = jnp.dot(
        select, route_weights.reshape(-1), preferred_element_type=jnp.float32
    ).astype(jnp.bfloat16)
    send_normed = send_normed.reshape(experts, capacity, width)
    send_grad = send_grad.reshape(experts, capacity, width)
    send_weight = send_weight.reshape(experts, capacity)
    w_in = weight_in[0]
    w_down = weight_down[0]
    got_normed = lax.all_to_all(send_normed, "expert", split_axis=0, concat_axis=0, tiled=True)
    got_grad = lax.all_to_all(send_grad, "expert", split_axis=0, concat_axis=0, tiled=True)
    got_weight = lax.all_to_all(send_weight, "expert", split_axis=0, concat_axis=0, tiled=True)
    count = got_normed.shape[1]
    expert_rows_normed = got_normed.reshape(-1, width)
    rows_grad = got_grad.reshape(-1, width)
    weight_col = got_weight.reshape(-1, 1).astype(jnp.float32)
    proj = jnp.dot(expert_rows_normed, w_in, preferred_element_type=jnp.float32)
    gate_proj = proj[:, :hidden_width]
    up_proj = proj[:, hidden_width:]
    sigmoid_gate = jax.nn.sigmoid(gate_proj)
    silu_gate = gate_proj * sigmoid_gate
    hidden = (silu_gate * up_proj).astype(jnp.bfloat16)
    back_proj = contract_cols(rows_grad, w_down)
    slot_grad = jnp.sum(back_proj * hidden.astype(jnp.float32), axis=1).astype(jnp.bfloat16)
    grad_hidden = weight_col * back_proj
    d_gate = grad_hidden * up_proj * sigmoid_gate * (1.0 + gate_proj * (1.0 - sigmoid_gate))
    d_up = grad_hidden * silu_gate
    d_proj = jnp.concatenate([d_gate, d_up], axis=1).astype(jnp.bfloat16)
    slot_normed = contract_cols(d_proj, w_in).astype(jnp.bfloat16)
    scaled = (weight_col * rows_grad.astype(jnp.float32)).astype(jnp.bfloat16)
    back_normed = lax.all_to_all(
        slot_normed.reshape(experts, count, width),
        "expert",
        split_axis=0,
        concat_axis=0,
        tiled=True,
    )
    back_route = lax.all_to_all(
        slot_grad.reshape(experts, count), "expert", split_axis=0, concat_axis=0, tiled=True
    )
    results = (
        back_normed,
        back_route,
        got_normed,
        scaled.reshape(experts, count, width),
        hidden.reshape(experts, count, hidden_width),
        d_proj.reshape(experts, count, 2 * hidden_width),
    )
    back_normed, back_route, kept_normed, kept_scaled, kept_hidden, kept_proj = results
    grad_normed = contract_rows(per_token, back_normed.reshape(slot_total, width))
    route_grad = (
        contract_rows(select, back_route.reshape(slot_total))
        .astype(jnp.bfloat16)
        .reshape(tok_rows, topk)
    )
    scaled_normed = grad_normed * norm_gain
    branch = inv_rms * (
        scaled_normed - unit_rows * jnp.mean(scaled_normed * unit_rows, axis=-1, keepdims=True)
    )
    grad_residual = (grad_out.astype(jnp.float32) + branch).astype(jnp.bfloat16)
    rows_normed = kept_normed.reshape(slot_total, width)
    rows_scaled = kept_scaled.reshape(slot_total, width)
    rows_hidden = kept_hidden.reshape(slot_total, hidden_width)
    rows_proj = kept_proj.reshape(slot_total, 2 * hidden_width)
    part_in = contract_rows(rows_normed, rows_proj)
    part_down = contract_rows(rows_scaled, rows_hidden)
    summed = sum_by_axis(
        jnp.concatenate([part_in, part_down], axis=1).astype(jnp.bfloat16), DP_ULYSSES, (1, 2, 0), 0
    ).astype(jnp.float32)
    grad_in = summed[:, : 2 * hidden_width][None]
    grad_down = summed[:, 2 * hidden_width :][None]
    return (grad_residual, route_grad, grad_in, grad_down)


def solution(mesh):
    finer = Mesh(
        mesh.devices.reshape(2, 2, mesh.shape["ulysses"], mesh.shape["expert"]),
        ("dp_0", "dp_1", "ulysses", "expert"),
    )
    return jax.shard_map(
        per_device,
        mesh=finer,
        in_specs=(
            P(DP_ULYSSES_EXPERT, None),
            P(),
            P(DP_ULYSSES_EXPERT, None),
            P(DP_ULYSSES_EXPERT, None),
            P(DP_ULYSSES_EXPERT, None),
            P("expert", None, None),
            P("expert", None, None),
        ),
        out_specs=(
            P(DP_ULYSSES_EXPERT, None),
            P(DP_ULYSSES_EXPERT, None),
            P("expert", DP_ULYSSES, None),
            P("expert", DP_ULYSSES, None),
        ),
        check_vma=False,
    )
```

profile of v0, /device:TPU:0, one launch (start us, length us, event | category | flops | bytes accessed | tf_op | source)
XLA Modules:
  0.0 374.1 jit_solution(11919955308758647606)
XLA Ops:
  7.2 0.9 copy.46
  8.1 0.1 eq.45
  8.2 0.1 eq.49
  8.3 0.8 copy.49
  9.1 0.1 reshape.138
  9.3 0.6 reduce-window.6
  9.9 0.2 slice_reduce_fusion
  10.1 0.1 fusion.31
  10.2 0.2 convolution_reduce_fusion
  10.4 0.7 all_to_all.25
  11.1 7.7 %all-to-all-start = ((bf16[8,1,48]{2,1,0:T(2,128)(2,1)}), bf16[8,1,48]{2,1,0:T(2,128)(2,1)S(1)}, u32[]{:S(2)}, u32[]{:S(2)}) async-start(bf16[8,1,48]{2,1,0:T(2,128)(2,1)} %all_to_all.25), calls=%async_computation | async-start | bytes 8192 | tf_op jit(solution)/shard_map/all_to_all | solution.py:81
  18.9 0.1 reduce_sum.52
  19.0 1.5 fusion.18
  20.6 0.7 multiply_add_fusion.1
  21.4 3.5 convolution_convert_fusion.1
  24.8 1.6 all-to-all-done
  26.5 5.7 %all-to-all-start.2 = ((bf16[8,48,4096]{2,1,0:T(8,128)(2,1)}), bf16[8,48,4096]{2,1,0:T(8,128)(2,1)}, u32[]{:S(2)}, u32[]{:S(2)}) async-start(bf16[8,48,4096]{2,1,0:T(8,128)(2,1)} %bitcast.65), calls=%async_computation.2 | async-start | bytes 6291456 | tf_op jit(solution)/shard_map/all_to_all | solution.py:79
  32.2 2.6 convolution_convert_fusion.2
  34.8 42.4 %all-to-all-done.2 = bf16[8,48,4096]{2,1,0:T(8,128)(2,1)} async-done(((bf16[8,48,4096]{2,1,0:T(8,128)(2,1)}), bf16[8,48,4096]{2,1,0:T(8,128)(2,1)}, u32[]{:S(2)}, u32[]{:S(2)}) %all-to-all-start.2) | async-done | bytes 3145760 | tf_op jit(solution)/shard_map/all_to_all | solution.py:79
  77.2 4.4 %all-to-all-start.1 = ((bf16[8,48,4096]{2,1,0:T(8,128)(2,1)}), bf16[8,48,4096]{2,1,0:T(8,128)(2,1)}, u32[]{:S(2)}, u32[]{:S(2)}) async-start(bf16[8,48,4096]{2,1,0:T(8,128)(2,1)} %bitcast.2), calls=%async_computation.1 | async-start | bytes 6291456 | tf_op jit(solution)/shard_map/all_to_all | solution.py:80
  81.6 0.2 reduce-scatter.4.cloned.1.call-start
  81.9 4.7 %copy.52 = bf16[384,4096]{0,1:T(8,128)(2,1)} copy(bf16[384,4096]{1,0:T(8,128)(2,1)} %bitcast.6) | data formatting | bytes 6291456 | tf_op jit(solution)/shard_map/reshape | solution.py:83
  86.6 11.3 %fusion.2 = f32[384,1536]{1,0:T(8,128)} fusion(bf16[384,4096]{1,0:T(8,128)(2,1)} %bitcast.6, bf16[1,4096,1536]{2,1,0:T(8,128)(2,1)} %param.12), kind=kOutput, calls=%fused_computation.3 | convolution fusion | flops 4831838208 | bytes 18087936 | tf_op jit(solution)/shard_map/dot_general | solution.py:86
  97.9 28.3 %all-to-all-done.1 = bf16[8,48,4096]{2,1,0:T(8,128)(2,1)} async-done(((bf16[8,48,4096]{2,1,0:T(8,128)(2,1)}), bf16[8,48,4096]{2,1,0:T(8,128)(2,1)}, u32[]{:S(2)}, u32[]{:S(2)}) %all-to-all-start.1) | async-done | bytes 3145760 | tf_op jit(solution)/shard_map/all_to_all | solution.py:80
  126.2 4.7 %copy.53 = bf16[384,4096]{0,1:T(8,128)(2,1)} copy(bf16[384,4096]{1,0:T(8,128)(2,1)} %bitcast.3) | data formatting | bytes 6291456 | tf_op jit(solution)/shard_map/reshape | solution.py:84
  130.9 2.7 multiply_convert_fusion
  133.6 7.7 %multiply_reduce_fusion = (bf16[384]{0:T(512)(128)(2,1)S(1)}, bf16[384,768]{1,0:T(8,128)(2,1)S(1)}, bf16[384,768]{1,0:T(8,128)(2,1)S(1)}, bf16[384,768]{1,0:T(8,128)(2,1)}) fusion(f32[384,1536]{1,0:T(8,128)S(1)} %copy-done.4, f32[384]{0:T(512)S(1)} %reshape.136, bf16[384,4096]{1,0:T(8,128)(2,1)} %bitcast.3, bf16[1,768,4096]{2,1,0:T(8,128)(2,1)} %param.13), kind=kOutput, calls=%fused_computation.30 | convolution fusion | flops 2421521920 | bytes 13568256 | tf_op jit(solution)/shard_map/dot_general | solution.py:41
  141.3 3.6 convolution_convert_fusion.3
  145.0 8.0 %convolution_convert_fusion = bf16[2,2,4,256,1536]{4,3,2,1,0:T(8,128)(2,1)S(1)} fusion(bf16[2,2,4,256,384]{4,3,2,1,0:T(8,128)(2,1)S(1)} %bitcast.67, bf16[384,768]{1,0:T(8,128)(2,1)S(1)} %get-tuple-element.24, bf16[384,768]{1,0:T(8,128)(2,1)} %get-tuple-element.25), kind=kOutput, calls=%fused_computation.5 | convolution fusion | flops 4840488960 | bytes 16908288 | tf_op jit(solution)/shard_map/dot_general | solution.py:35
  153.0 7.7 %maximum_bitcast_fusion = bf16[2,4,2,256,2304]{4,3,1,0,2:T(8,128)(2,1)S(1)} fusion(bf16[2,2,4,256,768]{4,3,2,1,0:T(8,128)(2,1)S(1)} %convolution_convert_fusion.3, bf16[2,2,4,256,1536]{4,3,2,1,0:T(8,128)(2,1)S(1)} %convolution_convert_fusion), kind=kLoop, calls=%fused_computation | loop fusion | flops 37748736 | bytes 37748736 | tf_op jit(solution)/shard_map/transpose | solution.py:17
  160.6 6.7 %copy.54 = bf16[2,4,2,256,2304]{4,3,2,1,0:T(8,128)(2,1)} copy(bf16[2,4,2,256,2304]{4,3,1,0,2:T(8,128)(2,1)S(1)} %maximum_bitcast_fusion) | data formatting | bytes 37748736 | tf_op jit(solution)/shard_map/transpose | solution.py:17
  167.4 26.8 %reduce-scatter.4.cloned.1.call-done = bf16[8,256,2304]{2,1,0:T(8,128)(2,1)} async-done(((bf16[16,256,2304]{2,1,0:T(8,128)(2,1)}), bf16[8,256,2304]{2,1,0:T(8,128)(2,1)}) %reduce-scatter.4.cloned.1.call-update) | async-done | bytes 9437200 | tf_op jit(solution)/shard_map/reduce_scatter | solution.py:20
  194.3 0.7 convert_element_type.110
  195.0 6.9 %all-to-all-start.4 = ((bf16[8,1,48]{2,1,0:T(2,128)(2,1)}), bf16[8,1,48]{2,1,0:T(2,128)(2,1)S(1)}, u32[]{:S(2)}, u32[]{:S(2)}) async-start(bf16[8,1,48]{2,1,0:T(2,128)(2,1)} %convert_element_type.110), calls=%async_computation.4 | async-start | bytes 8192 | tf_op jit(solution)/shard_map/all_to_all | solution.py:107
  201.9 0.3 reduce-scatter.8.cloned.1.call-start
  202.2 85.0 %reduce-scatter.6.cloned.1.call-done = bf16[2,256,2304]{2,1,0:T(8,128)(2,1)} async-done(((bf16[8,256,2304]{2,1,0:T(8,128)(2,1)}), bf16[2,256,2304]{2,1,0:T(8,128)(2,1)}) %reduce-scatter.6.cloned.1.call-update) | async-done | bytes 2359312 | tf_op jit(solution)/shard_map/reduce_scatter | solution.py:20
  287.2 18.1 %fusion.6 = bf16[384,4096]{1,0:T(8,128)(2,1)} fusion(bf16[1,4096,1536]{2,1,0:T(8,128)(2,1)} %param.12, bf16[384,768]{1,0:T(8,128)(2,1)S(1)} %copy-done.6, bf16[384,768]{1,0:T(8,128)(2,1)S(1)} %copy-done.7), kind=kOutput, calls=%fused_computation.9 | convolution fusion | flops 4835770368 | bytes 16908288 | tf_op jit(solution)/shard_map/dot_general | solution.py:41
  305.3 7.0 %all-to-all-start.3 = ((bf16[8,48,4096]{2,1,0:T(8,128)(2,1)}), bf16[8,48,4096]{2,1,0:T(8,128)(2,1)}, u32[]{:S(2)}, u32[]{:S(2)}) async-start(bf16[8,48,4096]{2,1,0:T(8,128)(2,1)} %bitcast.66), calls=%async_computation.3 | async-start | bytes 6291456 | tf_op jit(solution)/shard_map/all_to_all | solution.py:100
  312.3 0.1 reshape.140
  312.4 0.2 fusion.25
  312.6 0.2 reshape.134
  312.7 0.6 copy.55
  313.3 46.0 %all-to-all-done.3 = bf16[8,48,4096]{2,1,0:T(8,128)(2,1)} async-done(((bf16[8,48,4096]{2,1,0:T(8,128)(2,1)}), bf16[8,48,4096]{2,1,0:T(8,128)(2,1)}, u32[]{:S(2)}, u32[]{:S(2)}) %all-to-all-start.3) | async-done | bytes 3145760 | tf_op jit(solution)/shard_map/all_to_all | solution.py:100
  359.3 2.9 fusion.13
  362.2 1.7 fusion.17
  363.9 1.4 bitcast_convert_fusion
  365.3 0.9 slice_bitcast_fusion.1
  366.2 1.3 slice_bitcast_fusion
  (34 shorter events, 0.4 us)
Async XLA Ops:
  7.2 14.2 %copy-start = (bf16[128,4096]{1,0:T(8,128)(2,1)S(1)}, bf16[128,4096]{1,0:T(8,128)(2,1)}, u32[]{:S(2)}) copy-start(bf16[128,4096]{1,0:T(8,128)(2,1)} %param.7) | copy-start | bytes 3145732
  11.1 15.3 %all-to-all-start = ((bf16[8,1,48]{2,1,0:T(2,128)(2,1)}), bf16[8,1,48]{2,1,0:T(2,128)(2,1)S(1)}, u32[]{:S(2)}, u32[]{:S(2)}) async-start(bf16[8,1,48]{2,1,0:T(2,128)(2,1)} %all_to_all.25), calls=%async_computation | async-start | bytes 8192 | tf_op jit(solution)/shard_map/all_to_all | solution.py:81
  26.5 5.7 %copy-start.1 = (bf16[128,4096]{1,0:T(8,128)(2,1)S(1)}, bf16[128,4096]{1,0:T(8,128)(2,1)}, u32[]{:S(2)}) copy-start(bf16[128,4096]{1,0:T(8,128)(2,1)} %param.9) | copy-start | bytes 3145732
  26.5 50.7 %all-to-all-start.2 = ((bf16[8,48,4096]{2,1,0:T(8,128)(2,1)}), bf16[8,48,4096]{2,1,0:T(8,128)(2,1)}, u32[]{:S(2)}, u32[]{:S(2)}) async-start(bf16[8,48,4096]{2,1,0:T(8,128)(2,1)} %bitcast.65), calls=%async_computation.2 | async-start | bytes 6291456 | tf_op jit(solution)/shard_map/all_to_all | solution.py:79
  77.2 49.0 %all-to-all-start.1 = ((bf16[8,48,4096]{2,1,0:T(8,128)(2,1)}), bf16[8,48,4096]{2,1,0:T(8,128)(2,1)}, u32[]{:S(2)}, u32[]{:S(2)}) async-start(bf16[8,48,4096]{2,1,0:T(8,128)(2,1)} %bitcast.2), calls=%async_computation.1 | async-start | bytes 6291456 | tf_op jit(solution)/shard_map/all_to_all | solution.py:80
  81.6 112.6 %reduce-scatter.4.cloned.1.call-start = ((), (), s32[]{:S(2)}) async-start(), calls=%async_computation.8 | async-start | bytes 28311552 | tf_op jit(solution)/shard_map/reduce_scatter | solution.py:20
  130.9 2.7 copy-start.4
  141.3 3.6 copy-start.5
  141.3 3.6 copy-start.2
  167.4 119.7 %reduce-scatter.6.cloned.1.call-start = ((), (), s32[]{:S(2)}) async-start(), calls=%async_computation.9 | async-start | bytes 11796480 | tf_op jit(solution)/shard_map/reduce_scatter | solution.py:20
  194.3 92.9 %copy-start.6 = (bf16[384,768]{1,0:T(8,128)(2,1)S(1)}, bf16[384,768]{1,0:T(8,128)(2,1)}, u32[]{:S(2)}) copy-start(bf16[384,768]{1,0:T(8,128)(2,1)} %copy-done.5) | copy-start | bytes 1769476
  194.3 92.9 %copy-start.7 = (bf16[384,768]{1,0:T(8,128)(2,1)S(1)}, bf16[384,768]{1,0:T(8,128)(2,1)}, u32[]{:S(2)}) copy-start(bf16[384,768]{1,0:T(8,128)(2,1)} %get-tuple-element.25) | copy-start | bytes 1769476
  195.0 110.3 %all-to-all-start.4 = ((bf16[8,1,48]{2,1,0:T(2,128)(2,1)}), bf16[8,1,48]{2,1,0:T(2,128)(2,1)S(1)}, u32[]{:S(2)}, u32[]{:S(2)}) async-start(bf16[8,1,48]{2,1,0:T(2,128)(2,1)} %convert_element_type.110), calls=%async_computation.4 | async-start | bytes 8192 | tf_op jit(solution)/shard_map/all_to_all | solution.py:107
  201.9 162.0 %reduce-scatter.8.cloned.1.call-start = ((), (), s32[]{:S(2)}) async-start(), calls=%async_computation.10 | async-start | bytes 3538944 | tf_op jit(solution)/shard_map/reduce_scatter | solution.py:20
  305.3 54.0 %copy-start.3 = (f32[4096]{0:T(1024)S(1)}, f32[4096]{0:T(1024)}, u32[]{:S(2)}) copy-start(f32[4096]{0:T(1024)} %param.8) | copy-start | bytes 49156
  305.3 54.0 %all-to-all-start.3 = ((bf16[8,48,4096]{2,1,0:T(8,128)(2,1)}), bf16[8,48,4096]{2,1,0:T(8,128)(2,1)}, u32[]{:S(2)}, u32[]{:S(2)}) async-start(bf16[8,48,4096]{2,1,0:T(8,128)(2,1)} %bitcast.66), calls=%async_computation.3 | async-start | bytes 6291456 | tf_op jit(solution)/shard_map/all_to_all | solution.py:100
Sparse Core Ops, SparseCore 0:
  167.5 26.6 reduce-scatter.3
  196.7 90.3 reduce-scatter.5
  289.5 70.7 reduce-scatter.7
where the time goes:
time: 375 us; the launch traced here: 374 us
  waiting for transfers between devices  230 us (61%)
  matrix products  58.1 us (15%)
  starting transfers between devices  32.3 us (9%)
  local copies, waits for them, and re-layouts  23.3 us (6%)
  other arithmetic  16.4 us (4%)
  between operations  13.9 us (4%)
    reduce_scatter x3, waiting for transfers between devices, sum_in_order(): blocks = lax.psum_scatter(blocks, axes[k], scatter_dimension=0, tiled=True)  112 us
    all_to_all x1, waiting for transfers between devices, per_device(): lax.all_to_all(slot_normed.reshape(experts, count, width), 'expert', spli...  46 us
    all_to_all x1, waiting for transfers between devices, per_device(): lax.all_to_all(send_normed, 'expert', split_axis=0, concat_axis=0, tiled=...  42.4 us
    all_to_all x1, waiting for transfers between devices, per_device(): lax.all_to_all(send_grad, 'expert', split_axis=0, concat_axis=0, tiled=True)  28.3 us
    dot_general x2, matrix products, contract_cols(): lax.dot_general(left, right, (((1,), (1,)), ((), ())), preferred_element_...  25.8 us
    dot_general x4, matrix products, contract_rows(): lax.dot_general(left, right, (((0,), (0,)), ((), ())), preferred_element_...  14.7 us
    dot_general x1, matrix products, per_device(): proj = jnp.dot(expert_rows_normed, w_in, preferred_element_type=jnp.float32)  11.3 us
    all_to_all x1, starting transfers between devices, per_device(): lax.all_to_all(send_weight, 'expert', split_axis=0, concat_axis=0, tiled=...  7.72 us
  transfers between devices with their start and end apart: 8, of which 6 were waited for; matrix products, arithmetic and copies ran while one was open for 13% of the time, Pallas kernels for 0%

commit v1 on v0

v1 whole, which is shorter than its diff:
```python
import jax
import jax.numpy as jnp
from jax import lax
from jax.sharding import Mesh
from jax.sharding import PartitionSpec as P

DP_ULYSSES = ("dp_0", "dp_1", "ulysses")
DP_ULYSSES_EXPERT = ("dp_0", "dp_1", "ulysses", "expert")

SWAP = [(0, 1), (1, 0)]

eps = 1e-06


def contract_rows(left, right):
    return lax.dot_general(
        left, right, (((0,), (0,)), ((), ())), preferred_element_type=jnp.float32
    )


def contract_cols(left, right):
    return lax.dot_general(
        left, right, (((1,), (1,)), ((), ())), preferred_element_type=jnp.float32
    )


def slot_tables(ids_t, weights_t, experts, capacity):
    tok_rows = ids_t.shape[1]
    lanes = (experts, tok_rows)
    chosen = ids_t[:, None, :] == lax.broadcasted_iota(jnp.int32, (1, experts, tok_rows), 1)
    hit = jnp.any(chosen, axis=0)
    weight = jnp.sum(jnp.where(chosen, weights_t[:, None, :].astype(jnp.float32), 0.0), axis=0)
    square = (tok_rows, tok_rows)
    before = lax.broadcasted_iota(jnp.int32, square, 0) < lax.broadcasted_iota(jnp.int32, square, 1)
    rank = jnp.dot(
        hit.astype(jnp.bfloat16), before.astype(jnp.bfloat16), preferred_element_type=jnp.float32
    )
    rank = jnp.where(hit, rank.astype(jnp.int32), capacity)
    slot = lax.broadcasted_iota(jnp.int32, (1, capacity, 1), 1)
    held = rank[:, None, :] == slot
    select = jnp.where(held, 1.0, 0.0).astype(jnp.bfloat16).reshape(-1, tok_rows)
    scale = jnp.where(held, weight[:, None, :], 0.0).astype(jnp.bfloat16).reshape(-1, tok_rows)
    return chosen, select, scale


def per_device(residual, norm_gain, grad_out, expert_ids, route_weights, weight_in, weight_down):
    tok_rows, width = residual.shape
    topk = expert_ids.shape[1]
    hidden_width = weight_down.shape[1]
    experts = lax.axis_size("expert")
    capacity = min(tok_rows, 3 * tok_rows * topk // (2 * experts))
    slot_total = experts * capacity
    rings = lax.axis_size("ulysses")
    stretch = width // (lax.axis_size("dp_0") * lax.axis_size("dp_1"))
    resid = residual.astype(jnp.float32)
    inv_rms = lax.rsqrt(jnp.mean(resid * resid, axis=-1, keepdims=True) + eps)
    unit_rows = resid * inv_rms
    normed = (unit_rows * norm_gain).astype(jnp.bfloat16)
    weights_t = route_weights.T
    chosen, select, scale = slot_tables(expert_ids.T, weights_t, experts, capacity)
    send_normed = jnp.dot(select, normed, preferred_element_type=jnp.float32).astype(jnp.bfloat16)
    send_scaled = jnp.dot(scale, grad_out, preferred_element_type=jnp.float32).astype(jnp.bfloat16)
    send = jnp.concatenate([send_normed, send_scaled], axis=1)
    got = lax.all_to_all(
        send.reshape(experts, capacity, 2 * width), "expert", split_axis=0, concat_axis=0, tiled=True
    ).reshape(slot_total, 2 * width)
    rows_normed = got[:, :width]
    rows_scaled = got[:, width:]
    w_in = weight_in[0]
    w_down = weight_down[0]
    proj = jnp.dot(rows_normed, w_in, preferred_element_type=jnp.float32)
    gate_proj = proj[:, :hidden_width]
    up_proj = proj[:, hidden_width:]
    sigmoid_gate = jax.nn.sigmoid(gate_proj)
    silu_gate = gate_proj * sigmoid_gate
    hidden = (silu_gate * up_proj).astype(jnp.bfloat16)
    grad_hidden = contract_cols(rows_scaled, w_down)
    slot_grad = jnp.sum(grad_hidden * hidden.astype(jnp.float32), axis=1).astype(jnp.bfloat16)
    d_gate = grad_hidden * up_proj * sigmoid_gate * (1.0 + gate_proj * (1.0 - sigmoid_gate))
    d_up = grad_hidden * silu_gate
    d_proj = jnp.concatenate([d_gate, d_up], axis=1).astype(jnp.bfloat16)

    side = lax.axis_index("dp_0")
    core = lax.axis_index("dp_1")

    def columns(rows, half, quarter):
        return lax.dynamic_slice_in_dim(rows, (half * 2 + quarter) * stretch, stretch, axis=1)

    def core_sum(rows, right, half):
        give = contract_rows(columns(rows, half, 1 - core), right).astype(jnp.bfloat16)
        came = lax.ppermute(give, "dp_1", SWAP)
        keep = contract_rows(columns(rows, half, core), right)
        return (keep + came.astype(jnp.float32)).astype(jnp.bfloat16)

    def ring_sum(rows, right, half):
        part = core_sum(rows, right, half)
        return lax.psum_scatter(part, "ulysses", scatter_dimension=0, tiled=True)

    far_down = ring_sum(rows_scaled, hidden, 1 - side)
    far_in = ring_sum(rows_normed, d_proj, 1 - side)
    near_down = ring_sum(rows_scaled, hidden, side)
    near_in = ring_sum(rows_normed, d_proj, side)
    came_down = lax.ppermute(far_down, "dp_0", SWAP)
    came_in = lax.ppermute(far_in, "dp_0", SWAP)
    grad_down = (near_down.astype(jnp.float32) + came_down.astype(jnp.float32))[None]
    grad_in = (near_in.astype(jnp.float32) + came_in.astype(jnp.float32))[None]

    slot_normed = contract_cols(d_proj, w_in).astype(jnp.bfloat16)
    back_normed = lax.all_to_all(
        slot_normed.reshape(experts, capacity, width),
        "expert",
        split_axis=0,
        concat_axis=0,
        tiled=True,
    )
    back_route = lax.all_to_all(
        slot_grad.reshape(experts, capacity), "expert", split_axis=0, concat_axis=0, tiled=True
    )
    grad_normed = contract_rows(select, back_normed.reshape(slot_total, width))
    token_route = jnp.sum(
        select.reshape(experts, capacity, tok_rows).astype(jnp.float32)
        * back_route.astype(jnp.float32)[:, :, None],
        axis=1,
    )
    route_t = jnp.sum(jnp.where(chosen, token_route[None], 0.0), axis=1)
    route_grad = (route_t / weights_t.astype(jnp.float32)).astype(jnp.bfloat16).T
    scaled_normed = grad_normed * norm_gain
    branch = inv_rms * (
        scaled_normed - unit_rows * jnp.mean(scaled_normed * unit_rows, axis=-1, keepdims=True)
    )
    grad_residual = (grad_out.astype(jnp.float32) + branch).astype(jnp.bfloat16)
    return (grad_residual, route_grad, grad_in, grad_down)


def solution(mesh):
    finer = Mesh(
        mesh.devices.reshape(2, 2, mesh.shape["ulysses"], mesh.shape["expert"]),
        ("dp_0", "dp_1", "ulysses", "expert"),
    )
    return jax.shard_map(
        per_device,
        mesh=finer,
        in_specs=(
            P(DP_ULYSSES_EXPERT, None),
            P(),
            P(DP_ULYSSES_EXPERT, None),
            P(DP_ULYSSES_EXPERT, None),
            P(DP_ULYSSES_EXPERT, None),
            P("expert", None, None),
            P("expert", None, None),
        ),
        out_specs=(
            P(DP_ULYSSES_EXPERT, None),
            P(DP_ULYSSES_EXPERT, None),
            P("expert", DP_ULYSSES, None),
            P("expert", DP_ULYSSES, None),
        ),
        check_vma=False,
    )
```

time: 375 us -> 287 us (0.77)
  waiting for transfers between devices: 230 us -> 155 us
  local copies, waits for them, and re-layouts: 23.3 us -> 4.26 us
  matrix products: 58.1 us -> 73.1 us
  starting transfers between devices: 32.3 us -> 23.5 us
    reduce_scatter x3 -> x4, waiting for transfers between devices: 112 us -> 13.4 us  [ring_sum(): return lax.psum_scatter(part, 'ulysses', scatter_dimension=0, tiled=True)]
    dot_general x4 -> x9, matrix products: 14.7 us -> 35.8 us  [contract_rows(): lax.dot_general(left, right, (((0,), (0,)), ((), ())), preferred_element_...]
    all_to_all x5 -> x3, waiting for transfers between devices: 118 us -> 132 us  [the longest x1 87.6 us: per_device(): lax.all_to_all(send.reshape(experts, capacity, 2 * width), 'expert', spli...]
    all_to_all x5 -> x3, starting transfers between devices: 31.8 us -> 20.1 us  [the longest x1 7.73 us: per_device(): lax.all_to_all(send.reshape(experts, capacity, 2 * width), 'expert', spli...]
    reshape x5 -> x0, local copies, waits for them, and re-layouts: 9.82 us -> none  [the longest x1 4.73 us: per_device(): rows_grad = got_grad.reshape(-1, width)]
    ppermute x0 -> x6, waiting for transfers between devices: none -> 9.82 us  [the longest x1 6.41 us: per_device(): came_down = lax.ppermute(far_down, 'dp_0', SWAP)]
    transpose x1 -> x0, other arithmetic: 7.65 us -> none  [sum_in_order(): blocks = blocks.transpose(*sequence, *range(len(axes), blocks.ndim))]
    transpose x1 -> x0, local copies, waits for them, and re-layouts: 6.75 us -> none  [sum_in_order(): blocks = blocks.transpose(*sequence, *range(len(axes), blocks.ndim))]
  transfers between devices with their start and end apart: 8 -> 13, of which waited for: 6 -> 6; matrix products, arithmetic and copies ran while one was open for 13% -> 21% of each run, Pallas kernels for 0% -> 0%
where the time goes in v1:
time: 287 us; the launch traced here: 286 us
  waiting for transfers between devices  155 us (54%)
  matrix products  73.1 us (25%)
  starting transfers between devices  23.5 us (8%)
  other arithmetic  16.1 us (6%)
  between operations  14 us (5%)
  local copies, waits for them, and re-layouts  4.26 us (1%)
    all_to_all x1, waiting for transfers between devices, per_device(): lax.all_to_all(send.reshape(experts, capacity, 2 * width), 'expert', spli...  87.6 us
    all_to_all x1, waiting for transfers between devices, per_device(): lax.all_to_all(slot_normed.reshape(experts, capacity, width), 'expert', s...  44.1 us
    dot_general x9, matrix products, contract_rows(): lax.dot_general(left, right, (((0,), (0,)), ((), ())), preferred_element_...  35.8 us
    dot_general x2, matrix products, contract_cols(): lax.dot_general(left, right, (((1,), (1,)), ((), ())), preferred_element_...  23.6 us
    reduce_scatter x4, waiting for transfers between devices, ring_sum(): return lax.psum_scatter(part, 'ulysses', scatter_dimension=0, tiled=True)  13.4 us
    dot_general x1, matrix products, per_device(): proj = jnp.dot(rows_normed, w_in, preferred_element_type=jnp.float32)  10.1 us
    all_to_all x1, starting transfers between devices, per_device(): lax.all_to_all(send.reshape(experts, capacity, 2 * width), 'expert', spli...  7.73 us
    all_to_all x1, starting transfers between devices, per_device(): lax.all_to_all(slot_normed.reshape(experts, capacity, width), 'expert', s...  7.46 us
  transfers between devices with their start and end apart: 13, of which 6 were waited for; matrix products, arithmetic and copies ran while one was open for 21% of the time, Pallas kernels for 0%

profile of v1, /device:TPU:0, one launch (start us, length us, event | category | flops | bytes accessed | tf_op | source)
XLA Modules:
  0.0 285.9 jit_solution(9064485428101454125)
XLA Ops:
  7.2 0.7 fusion.51
  7.9 0.1 fusion.21
  8.0 0.7 convert_bitcast_fusion
  8.6 0.7 select_reduce_fusion.1
  9.3 0.1 eq.40
  9.4 0.1 fusion.47
  9.5 0.1 fusion.45
  9.7 1.5 fusion.19
  11.2 2.3 convolution_convert_fusion
  13.5 1.1 convolution_convert_fusion.1
  14.6 3.4 %pad_maximum_fusion = bf16[384,8192]{1,0:T(8,128)(2,1)} fusion(bf16[384,4096]{1,0:T(8,128)(2,1)S(1)} %convolution_convert_fusion, bf16[384,4096]{1,0:T(8,128)(2,1)S(1)} %convolution_convert_fusion.1), kind=kLoop, calls=%fused_computation.4 | loop fusion | flops 12582912 | bytes 12582912 | tf_op jit(solution)/shard_map/concatenate | solution.py:63
  18.0 7.7 %all-to-all-start = ((bf16[8,48,8192]{2,1,0:T(8,128)(2,1)}), bf16[8,48,8192]{2,1,0:T(8,128)(2,1)}, u32[]{:S(2)}, u32[]{:S(2)}) async-start(bf16[8,48,8192]{2,1,0:T(8,128)(2,1)} %bitcast.52), calls=%async_computation | async-start | bytes 12582912 | tf_op jit(solution)/shard_map/all_to_all | solution.py:64
  25.7 0.0 reduce-scatter.11.cloned.1.call-start
  25.8 87.6 %all-to-all-done = bf16[8,48,8192]{2,1,0:T(8,128)(2,1)} async-done(((bf16[8,48,8192]{2,1,0:T(8,128)(2,1)}), bf16[8,48,8192]{2,1,0:T(8,128)(2,1)}, u32[]{:S(2)}, u32[]{:S(2)}) %all-to-all-start) | async-done | bytes 6291488 | tf_op jit(solution)/shard_map/all_to_all | solution.py:64
  113.4 3.4 %fusion.65 = (bf16[384,4096]{1,0:T(8,128)(2,1)S(1)}, bf16[384,4096]{1,0:T(8,128)(2,1)S(1)}) fusion(bf16[384,8192]{1,0:T(8,128)(2,1)} %bitcast.5), kind=kLoop, calls=%fused_computation.90 | loop fusion | bytes 12582912 | tf_op jit(solution)/shard_map/slice | solution.py:68
  116.8 10.1 %fusion.2 = f32[384,1536]{1,0:T(8,128)S(1)} fusion(bf16[1,4096,1536]{2,1,0:T(8,128)(2,1)} %param.12, bf16[384,8192]{1,0:T(8,128)(2,1)} %bitcast.5), kind=kOutput, calls=%fused_computation.2 | convolution fusion | flops 4831838208 | bytes 18087936 | tf_op jit(solution)/shard_map/dot_general | solution.py:71
  127.0 5.0 %multiply_reduce_fusion = (bf16[384]{0:T(512)(128)(2,1)S(1)}, bf16[384,768]{1,0:T(8,128)(2,1)S(1)}, bf16[384,768]{1,0:T(8,128)(2,1)S(1)}, bf16[384,768]{1,0:T(8,128)(2,1)S(1)}) fusion(f32[384,1536]{1,0:T(8,128)S(1)} %fusion.2, bf16[1,768,4096]{2,1,0:T(8,128)(2,1)S(1)} %bitcast.59, bf16[384,8192]{1,0:T(8,128)(2,1)} %bitcast.5), kind=kOutput, calls=%fused_computation.34 | convolution fusion | flops 2421227008 | bytes 13566720 | tf_op jit(solution)/shard_map/dot_general | solution.py:22
  132.1 2.2 convolution_convert_fusion.4
  134.2 3.5 %convolution_convert_fusion.2 = bf16[1024,1536]{1,0:T(8,128)(2,1)} fusion(bf16[384,4096]{1,0:T(8,128)(2,1)S(1)} %get-tuple-element.7, s32[]{:T(128)S(6)} %select_n.49, bf16[384,768]{1,0:T(8,128)(2,1)S(1)} %get-tuple-element.8, bf16[384,768]{1,0:T(8,128)(2,1)S(1)} %get-tuple-element.9), kind=kOutput, calls=%fused_computation.14 | convolution fusion | flops 1211891712 | bytes 5111812 | tf_op jit(solution)/shard_map/dot_general | solution.py:16
  137.7 0.8 collective-permute-start.1
  138.5 4.0 %add_convert_fusion.2 = bf16[1024,768]{1,0:T(8,128)(2,1)} fusion(bf16[1024,768]{1,0:T(8,128)(2,1)} %collective-permute-done.4, bf16[384,768]{1,0:T(8,128)(2,1)} %copy-done.5, bf16[384,4096]{1,0:T(8,128)(2,1)} %copy-done.1, s32[]{:T(128)S(6)} %select_n.48), kind=kOutput, calls=%fused_computation.16 | convolution fusion | flops 606339072 | bytes 4521988 | tf_op jit(solution)/shard_map/dot_general | solution.py:16
  142.5 0.0 reduce-scatter.7.cloned.1.call-start
  142.6 1.6 collective-permute-done.1
  144.1 5.7 %add_convert_fusion = bf16[1024,1536]{1,0:T(8,128)(2,1)} fusion(bf16[1024,1536]{1,0:T(8,128)(2,1)} %collective-permute-done.1, bf16[384,4096]{1,0:T(8,128)(2,1)S(1)} %get-tuple-element.7, s32[]{:T(128)S(6)} %select_n.48, bf16[384,768]{1,0:T(8,128)(2,1)} %copy-done.6, bf16[384,768]{1,0:T(8,128)(2,1)} %copy-done.9), kind=kOutput, calls=%fused_computation.7 | convolution fusion | flops 1215037440 | bytes 8257540 | tf_op jit(solution)/shard_map/dot_general | solution.py:16
  149.9 0.0 reduce-scatter.9.cloned.1.call-start
  149.9 3.7 %convolution_convert_fusion.5 = bf16[1024,768]{1,0:T(8,128)(2,1)} fusion(bf16[384,768]{1,0:T(8,128)(2,1)} %copy-done.5, bf16[384,4096]{1,0:T(8,128)(2,1)} %copy-done.1, s32[]{:T(128)S(6)} %select_n.47), kind=kOutput, calls=%fused_computation.31 | convolution fusion | flops 604766208 | bytes 2949124 | tf_op jit(solution)/shard_map/dot_general | solution.py:16
  153.6 0.5 collective-permute-start.3
  154.1 3.5 %convolution_convert_fusion.3 = bf16[1024,1536]{1,0:T(8,128)(2,1)} fusion(bf16[384,4096]{1,0:T(8,128)(2,1)S(1)} %get-tuple-element.7, s32[]{:T(128)S(6)} %select_n.47, bf16[384,768]{1,0:T(8,128)(2,1)S(1)} %copy-done.7, bf16[384,768]{1,0:T(8,128)(2,1)S(1)} %copy-done.10), kind=kOutput, calls=%fused_computation.15 | convolution fusion | flops 1211891712 | bytes 5111812 | tf_op jit(solution)/shard_map/dot_general | solution.py:16
  157.7 4.1 %add_convert_fusion.3 = bf16[1024,768]{1,0:T(8,128)(2,1)} fusion(bf16[1024,768]{1,0:T(8,128)(2,1)} %collective-permute-done.3, bf16[384,768]{1,0:T(8,128)(2,1)} %copy-done.5, bf16[384,4096]{1,0:T(8,128)(2,1)} %copy-done.1, s32[]{:T(128)S(6)} %select_n.46), kind=kOutput, calls=%fused_computation.17 | convolution fusion | flops 606339072 | bytes 4521988 | tf_op jit(solution)/shard_map/dot_general | solution.py:16
  161.7 0.0 reduce-scatter.9.cloned.1.call-update
  161.8 0.0 reduce-scatter.5.cloned.1.call-start
  161.8 1.9 collective-permute-done
  163.7 5.8 %add_convert_fusion.1 = bf16[1024,1536]{1,0:T(8,128)(2,1)} fusion(bf16[1024,1536]{1,0:T(8,128)(2,1)} %collective-permute-done, bf16[384,4096]{1,0:T(8,128)(2,1)S(1)} %get-tuple-element.7, s32[]{:T(128)S(6)} %select_n.46, bf16[384,768]{1,0:T(8,128)(2,1)} %copy-done.6, bf16[384,768]{1,0:T(8,128)(2,1)} %copy-done.9), kind=kOutput, calls=%fused_computation.8 | convolution fusion | flops 1215037440 | bytes 8257540 | tf_op jit(solution)/shard_map/dot_general | solution.py:16
  169.5 0.7 convert_element_type.173
  170.2 4.9 %all-to-all-start.2 = ((bf16[8,1,48]{2,1,0:T(2,128)(2,1)}), bf16[8,1,48]{2,1,0:T(2,128)(2,1)S(1)}, u32[]{:S(2)}, u32[]{:S(2)}) async-start(bf16[8,1,48]{2,1,0:T(2,128)(2,1)} %convert_element_type.173), calls=%async_computation.2 | async-start | bytes 8192 | tf_op jit(solution)/shard_map/all_to_all | solution.py:116
  175.1 18.6 %fusion.6 = bf16[384,4096]{1,0:T(8,128)(2,1)} fusion(bf16[1,4096,1536]{2,1,0:T(8,128)(2,1)} %param.12, bf16[384,768]{1,0:T(8,128)(2,1)S(1)} %copy-done.8, bf16[384,768]{1,0:T(8,128)(2,1)S(1)} %copy-done.11), kind=kOutput, calls=%fused_computation.9 | convolution fusion | flops 4835770368 | bytes 16908288 | tf_op jit(solution)/shard_map/dot_general | solution.py:22
  193.7 7.5 %all-to-all-start.1 = ((bf16[8,48,4096]{2,1,0:T(8,128)(2,1)}), bf16[8,48,4096]{2,1,0:T(8,128)(2,1)S(1)}, u32[]{:S(2)}, u32[]{:S(2)}) async-start(bf16[8,48,4096]{2,1,0:T(8,128)(2,1)} %bitcast.53), calls=%async_computation.1 | async-start | bytes 6291456 | tf_op jit(solution)/shard_map/all_to_all | solution.py:109
  201.1 0.1 multiply_reduce_fusion.1
  201.3 0.5 fusion.60
  201.8 44.1 %all-to-all-done.1 = bf16[8,48,4096]{2,1,0:T(8,128)(2,1)S(1)} async-done(((bf16[8,48,4096]{2,1,0:T(8,128)(2,1)}), bf16[8,48,4096]{2,1,0:T(8,128)(2,1)S(1)}, u32[]{:S(2)}, u32[]{:S(2)}) %all-to-all-start.1) | async-done | bytes 3145760 | tf_op jit(solution)/shard_map/all_to_all | solution.py:109
  245.9 3.4 %fusion.14 = (f32[128]{0:T(128)S(1)}, f32[128,4096]{1,0:T(8,128)}) fusion(bf16[128,4096]{1,0:T(8,128)(2,1)} %param.7, f32[128]{0:T(128)S(1)} %add_rsqrt_fusion, f32[4096]{0:T(1024)S(1)} %copy-done.2, bf16[8,48,4096]{2,1,0:T(8,128)(2,1)S(1)} %all-to-all-done.1, s32[8,128]{1,0:T(8,128)S(1)} %fusion.21), kind=kOutput, calls=%fused_computation.24 | convolution fusion | flops 405421952 | bytes 6312960 | tf_op jit(solution)/shard_map/dot_general | solution.py:16
  249.3 1.4 collective-permute-start.5
  250.7 0.7 collective-permute-start.2
  251.4 3.8 %fusion.18 = bf16[128,4096]{1,0:T(8,128)(2,1)} fusion(f32[128,4096]{1,0:T(8,128)} %get-tuple-element.11, bf16[128,4096]{1,0:T(8,128)(2,1)} %param.7, bf16[128,4096]{1,0:T(8,128)(2,1)} %param.9, f32[128]{0:T(128)S(1)} %broadcast_multiply_fusion, f32[128]{0:T(128)S(1)} %add_rsqrt_fusion), kind=kLoop, calls=%fused_computation.28 | loop fusion | flops 4194304 | bytes 5243904 | tf_op jit(solution)/shard_map/convert_element_type | solution.py:131
  255.1 6.4 %collective-permute-done.5 = bf16[256,768]{1,0:T(8,128)(2,1)S(1)} collective-permute-done((bf16[256,768]{1,0:T(8,128)(2,1)}, bf16[256,768]{1,0:T(8,128)(2,1)S(1)}, u32[]{:S(2)}, u32[]{:S(2)}) %collective-permute-start.5) | collective-permute-done | bytes 393248 | tf_op jit(solution)/shard_map/ppermute | solution.py:103
  261.5 2.0 add_bitcast_fusion.1
  263.5 13.4 %reduce-scatter.5.cloned.1.call-done = bf16[256,1536]{1,0:T(8,128)(2,1)} async-done(((bf16[1024,1536]{1,0:T(8,128)(2,1)}), bf16[256,1536]{1,0:T(8,128)(2,1)}) %reduce-scatter.5.cloned.1.call-update) | async-done | bytes 786448 | tf_op jit(solution)/shard_map/reduce_scatter | solution.py:97
  276.9 2.5 add_bitcast_fusion
  (46 shorter events, 0.2 us)
Async XLA Ops:
  11.2 2.3 copy-start
  11.2 2.3 copy-start.2
  18.0 95.4 %all-to-all-start = ((bf16[8,48,8192]{2,1,0:T(8,128)(2,1)}), bf16[8,48,8192]{2,1,0:T(8,128)(2,1)}, u32[]{:S(2)}, u32[]{:S(2)}) async-start(bf16[8,48,8192]{2,1,0:T(8,128)(2,1)} %bitcast.52), calls=%async_computation | async-start | bytes 12582912 | tf_op jit(solution)/shard_map/all_to_all | solution.py:64
  25.7 223.6 %reduce-scatter.11.cloned.1.call-start = ((), (), s32[]{:S(2)}) async-start(), calls=%async_computation.10 | async-start | bytes 1966080 | tf_op jit(solution)/shard_map/reduce_scatter | solution.py:97
  113.4 13.6 %slice-start = ((s8[6291456]{0:T(1024)(128)(4,1)}), s8[4194304]{0:T(1024)(128)(4,1)S(1)}, s32[]{:S(2)}) async-start(s8[6291456]{0:T(1024)(128)(4,1)} %bitcast.58), calls=%async_computation.11 | async-start | bytes 8388608
  116.8 15.2 %copy-start.1 = (bf16[384,4096]{1,0:T(8,128)(2,1)}, bf16[384,4096]{1,0:T(8,128)(2,1)S(1)}, u32[]{:S(2)}) copy-start(bf16[384,4096]{1,0:T(8,128)(2,1)S(1)} %get-tuple-element.6) | copy-start | bytes 9437188
  116.8 10.1 %slice-start.1 = ((s8[6291456]{0:T(1024)(128)(4,1)}), s8[2097152]{0:T(1024)(128)(4,1)S(1)}, s32[]{:S(2)}) async-start(s8[6291456]{0:T(1024)(128)(4,1)} %bitcast.58), calls=%async_computation.12 | async-start | bytes 4194304
  132.0 5.7 %copy-start.5 = (bf16[384,768]{1,0:T(8,128)(2,1)}, bf16[384,768]{1,0:T(8,128)(2,1)S(1)}, u32[]{:S(2)}) copy-start(bf16[384,768]{1,0:T(8,128)(2,1)S(1)} %get-tuple-element.5) | copy-start | bytes 1769476
  132.0 5.7 %copy-start.6 = (bf16[384,768]{1,0:T(8,128)(2,1)}, bf16[384,768]{1,0:T(8,128)(2,1)S(1)}, u32[]{:S(2)}) copy-start(bf16[384,768]{1,0:T(8,128)(2,1)S(1)} %get-tuple-element.8) | copy-start | bytes 1769476
  132.1 5.7 %copy-start.9 = (bf16[384,768]{1,0:T(8,128)(2,1)}, bf16[384,768]{1,0:T(8,128)(2,1)S(1)}, u32[]{:S(2)}) copy-start(bf16[384,768]{1,0:T(8,128)(2,1)S(1)} %get-tuple-element.9) | copy-start | bytes 1769476
  134.2 4.2 %collective-permute-start.4 = (bf16[1024,768]{1,0:T(8,128)(2,1)}, bf16[1024,768]{1,0:T(8,128)(2,1)}, u32[]{:S(2)}, u32[]{:S(2)}) collective-permute-start(bf16[1024,768]{1,0:T(8,128)(2,1)} %convolution_convert_fusion.4), channel_id=1, source_target_pairs={{0,32},{32,0},{1,33},{33,1},{2,34},{34,2},{3,35},{35,3},{4,36},{36... | collective-permute-start | bytes 4718600 | tf_op jit(solution)/shard_map/ppermute | solution.py:91
  137.7 6.4 %collective-permute-start.1 = (bf16[1024,1536]{1,0:T(8,128)(2,1)}, bf16[1024,1536]{1,0:T(8,128)(2,1)}, u32[]{:S(2)}, u32[]{:S(2)}) collective-permute-start(bf16[1024,1536]{1,0:T(8,128)(2,1)} %convolution_convert_fusion.2), channel_id=1, source_target_pairs={{0,32},{32,0},{1,33},{33,1},{2,34},{34,2},{3,35},{35,3},{4,36},{36... | collective-permute-start | bytes 9437192 | tf_op jit(solution)/shard_map/ppermute | solution.py:91
  142.5 108.2 %reduce-scatter.7.cloned.1.call-start = ((), (), s32[]{:S(2)}) async-start(), calls=%async_computation.8 | async-start | bytes 3932160 | tf_op jit(solution)/shard_map/reduce_scatter | solution.py:97
  149.9 105.3 %reduce-scatter.9.cloned.1.call-start = ((), (), s32[]{:S(2)}) async-start(), calls=%async_computation.9 | async-start | bytes 1966080 | tf_op jit(solution)/shard_map/reduce_scatter | solution.py:97
  149.9 4.2 %copy-start.7 = (bf16[384,768]{1,0:T(8,128)(2,1)S(1)}, bf16[384,768]{1,0:T(8,128)(2,1)}, u32[]{:S(2)}) copy-start(bf16[384,768]{1,0:T(8,128)(2,1)} %copy-done.6) | copy-start | bytes 1769476
  149.9 4.2 %copy-start.10 = (bf16[384,768]{1,0:T(8,128)(2,1)S(1)}, bf16[384,768]{1,0:T(8,128)(2,1)}, u32[]{:S(2)}) copy-start(bf16[384,768]{1,0:T(8,128)(2,1)} %copy-done.9) | copy-start | bytes 1769476
  153.6 4.1 %collective-permute-start.3 = (bf16[1024,768]{1,0:T(8,128)(2,1)}, bf16[1024,768]{1,0:T(8,128)(2,1)}, u32[]{:S(2)}, u32[]{:S(2)}) collective-permute-start(bf16[1024,768]{1,0:T(8,128)(2,1)} %convolution_convert_fusion.5), channel_id=1, source_target_pairs={{0,32},{32,0},{1,33},{33,1},{2,34},{34,2},{3,35},{35,3},{4,36},{36... | collective-permute-start | bytes 4718600 | tf_op jit(solution)/shard_map/ppermute | solution.py:91
  157.7 6.0 %collective-permute-start = (bf16[1024,1536]{1,0:T(8,128)(2,1)}, bf16[1024,1536]{1,0:T(8,128)(2,1)}, u32[]{:S(2)}, u32[]{:S(2)}) collective-permute-start(bf16[1024,1536]{1,0:T(8,128)(2,1)} %convolution_convert_fusion.3), channel_id=1, source_target_pairs={{0,32},{32,0},{1,33},{33,1},{2,34},{34,2},{3,35},{35,3},{4,36},{36... | collective-permute-start | bytes 9437192 | tf_op jit(solution)/shard_map/ppermute | solution.py:91
  161.8 115.1 %reduce-scatter.5.cloned.1.call-start = ((), (), s32[]{:S(2)}) async-start(), calls=%async_computation.7 | async-start | bytes 3932160 | tf_op jit(solution)/shard_map/reduce_scatter | solution.py:97
  169.4 5.6 %copy-start.8 = (bf16[384,768]{1,0:T(8,128)(2,1)S(1)}, bf16[384,768]{1,0:T(8,128)(2,1)}, u32[]{:S(2)}) copy-start(bf16[384,768]{1,0:T(8,128)(2,1)} %copy-done.6) | copy-start | bytes 1769476
  169.4 5.6 %copy-start.11 = (bf16[384,768]{1,0:T(8,128)(2,1)S(1)}, bf16[384,768]{1,0:T(8,128)(2,1)}, u32[]{:S(2)}) copy-start(bf16[384,768]{1,0:T(8,128)(2,1)} %copy-done.9) | copy-start | bytes 1769476
  170.2 23.5 %all-to-all-start.2 = ((bf16[8,1,48]{2,1,0:T(2,128)(2,1)}), bf16[8,1,48]{2,1,0:T(2,128)(2,1)S(1)}, u32[]{:S(2)}, u32[]{:S(2)}) async-start(bf16[8,1,48]{2,1,0:T(2,128)(2,1)} %convert_element_type.173), calls=%async_computation.2 | async-start | bytes 8192 | tf_op jit(solution)/shard_map/all_to_all | solution.py:116
  193.7 7.6 %copy-start.3 = (s32[128,2]{0,1:T(2,128)S(1)}, s32[128,2]{0,1:T(2,128)}, u32[]{:S(2)}) copy-start(s32[128,2]{0,1:T(2,128)} %param.10) | copy-start | bytes 3076
  193.7 7.6 %copy-start.4 = (bf16[128,2]{0,1:T(2,128)(2,1)S(1)}, bf16[128,2]{0,1:T(2,128)(2,1)}, u32[]{:S(2)}) copy-start(bf16[128,2]{0,1:T(2,128)(2,1)} %param.11) | copy-start | bytes 1540
  193.7 52.2 %all-to-all-start.1 = ((bf16[8,48,4096]{2,1,0:T(8,128)(2,1)}), bf16[8,48,4096]{2,1,0:T(8,128)(2,1)S(1)}, u32[]{:S(2)}, u32[]{:S(2)}) async-start(bf16[8,48,4096]{2,1,0:T(8,128)(2,1)} %bitcast.53), calls=%async_computation.1 | async-start | bytes 6291456 | tf_op jit(solution)/shard_map/all_to_all | solution.py:109
  249.3 12.2 %collective-permute-start.5 = (bf16[256,768]{1,0:T(8,128)(2,1)}, bf16[256,768]{1,0:T(8,128)(2,1)S(1)}, u32[]{:S(2)}, u32[]{:S(2)}) collective-permute-start(bf16[256,768]{1,0:T(8,128)(2,1)} %reduce-scatter.11.cloned.1.call-done), channel_id=1, source_target_pairs={{0,64},{64,0},{1,65},{65,1},{2,66},{66,2},{3,67},{67,3},{4,68},{68... | collective-permute-start | bytes 1179656 | tf_op jit(solution)/shard_map/ppermute | solution.py:103
  250.7 26.2 %collective-permute-start.2 = (bf16[256,1536]{1,0:T(8,128)(2,1)}, bf16[256,1536]{1,0:T(8,128)(2,1)S(1)}, u32[]{:S(2)}, u32[]{:S(2)}) collective-permute-start(bf16[256,1536]{1,0:T(8,128)(2,1)} %reduce-scatter.7.cloned.1.call-done), channel_id=1, source_target_pairs={{0,64},{64,0},{1,65},{65,1},{2,66},{66,2},{3,67},{67,3},{4,68},{68... | collective-permute-start | bytes 2359304 | tf_op jit(solution)/shard_map/ppermute | solution.py:104
Sparse Core Ops, SparseCore 0:
  142.6 25.5 reduce-scatter.10
  170.6 38.0 reduce-scatter.6
  211.1 25.3 reduce-scatter.8
  238.7 38.0 reduce-scatter.4

commit v2 on v1

v2 whole, which is shorter than its diff:
```python
import jax
import jax.numpy as jnp
from jax import lax
from jax.experimental import pallas as pl
from jax.experimental.pallas import tpu as pltpu
from jax.sharding import Mesh
from jax.sharding import PartitionSpec as P

DP_ULYSSES = ("dp_0", "dp_1", "ulysses")
DP_ULYSSES_EXPERT = ("dp_0", "dp_1", "ulysses", "expert")

SWAP = [(0, 1), (1, 0)]

eps = 1e-06


def contract(left, right, over_left, over_right):
    return lax.dot_general(
        left, right, (((over_left,), (over_right,)), ((), ())), preferred_element_type=jnp.float32
    )


def slot_matrices(ids, weights, experts, capacity):
    tok_rows = ids.shape[1]
    expert = lax.broadcasted_iota(jnp.int32, (experts, tok_rows), 0)
    first, second = ids[0:1] == expert, ids[1:2] == expert
    hit = first | second
    weight = jnp.where(first, weights[0:1], jnp.where(second, weights[1:2], 0.0))
    square = (tok_rows, tok_rows)
    before = lax.broadcasted_iota(jnp.int32, square, 0) < lax.broadcasted_iota(jnp.int32, square, 1)
    rank = contract(
        jnp.where(hit, 1.0, 0.0).astype(jnp.bfloat16),
        jnp.where(before, 1.0, 0.0).astype(jnp.bfloat16),
        1,
        0,
    ).astype(jnp.int32)
    rank = jnp.where(hit, rank, capacity)
    slot = lax.broadcasted_iota(jnp.int32, (capacity, tok_rows), 0)
    select, scale = [], []
    for e in range(experts):
        held = rank[e : e + 1] == slot
        select.append(jnp.where(held, 1.0, 0.0))
        scale.append(jnp.where(held, weight[e : e + 1], 0.0))
    return (
        jnp.concatenate(select, axis=0).astype(jnp.bfloat16),
        jnp.concatenate(scale, axis=0).astype(jnp.bfloat16),
    )


def pack_kernel(ids_ref, w_ref, gain_ref, resid_ref, grad_ref, out_ref, sel_ref, inv_ref, scale_ref):
    experts, _, capacity, block = out_ref.shape

    @pl.when(pl.program_id(0) == 0)
    def _():
        full = resid_ref[...].astype(jnp.float32)
        mean = jnp.mean(full * full, axis=-1, keepdims=True)
        inv_ref[...] = lax.rsqrt(mean + eps)
        select, scale = slot_matrices(ids_ref[...], w_ref[...].astype(jnp.float32), experts, capacity)
        sel_ref[...] = select
        scale_ref[...] = scale

    at = pl.ds(pl.multiple_of(pl.program_id(0) * block, block), block)
    unit = resid_ref[:, at].astype(jnp.float32) * inv_ref[...]
    normed = (unit * gain_ref[:, at]).astype(jnp.bfloat16)
    sent = contract(sel_ref[...], normed, 1, 0).astype(jnp.bfloat16)
    out_ref[:, 0] = sent.reshape(experts, capacity, block)
    sent = contract(scale_ref[...], grad_ref[:, at], 1, 0).astype(jnp.bfloat16)
    out_ref[:, 1] = sent.reshape(experts, capacity, block)


def pack(ids_t, w_t, gain, resid, grad, experts, capacity, block=512):
    rows, width = resid.shape
    whole = lambda a: pl.BlockSpec(a.shape, lambda j: (0,) * a.ndim)
    args = (ids_t, w_t, gain, resid, grad)
    slots = experts * capacity
    return pl.pallas_call(
        pack_kernel,
        grid=(width // block,),
        in_specs=[whole(a) for a in args],
        out_specs=[
            pl.BlockSpec((experts, 2, capacity, block), lambda j: (0, 0, 0, j)),
            pl.BlockSpec((slots, rows), lambda j: (0, 0)),
        ],
        out_shape=[
            jax.ShapeDtypeStruct((experts, 2, capacity, width), jnp.bfloat16),
            jax.ShapeDtypeStruct((slots, rows), jnp.bfloat16),
        ],
        scratch_shapes=[
            pltpu.VMEM((rows, 1), jnp.float32),
            pltpu.VMEM((slots, rows), jnp.bfloat16),
        ],
        compiler_params=pltpu.CompilerParams(vmem_limit_bytes=40 * 2**20),
        cost_estimate=pl.CostEstimate(
            flops=4 * slots * rows * width, bytes_accessed=4 * slots * width, transcendentals=0
        ),
        name="pack",
    )(*args)


def expert_kernel(got_ref, gate_w_ref, up_w_ref, down_w_ref, out_ref, route_ref, acc_ref):
    parts, _, capacity, width = got_ref.shape
    slots = parts * capacity
    normed = got_ref[:, 0].reshape(slots, width)
    gate = contract(normed, gate_w_ref[...], 1, 0)
    up = contract(normed, up_w_ref[...], 1, 0)
    grad_hidden = contract(got_ref[:, 1].reshape(slots, width), down_w_ref[...], 1, 1)
    sigmoid = jax.nn.sigmoid(gate)
    silu = gate * sigmoid
    hidden = (silu * up).astype(jnp.bfloat16)
    out_ref[0] = hidden
    out_ref[1] = (grad_hidden * up * sigmoid * (1.0 + gate * (1.0 - sigmoid))).astype(jnp.bfloat16)
    out_ref[2] = (grad_hidden * silu).astype(jnp.bfloat16)
    part = jnp.sum(grad_hidden * hidden.astype(jnp.float32), axis=1, keepdims=True)

    @pl.when(pl.program_id(0) == 0)
    def _():
        acc_ref[...] = part

    @pl.when(pl.program_id(0) > 0)
    def _():
        acc_ref[...] += part

    @pl.when(pl.program_id(0) == pl.num_programs(0) - 1)
    def _():
        route_ref[...] = jnp.broadcast_to(acc_ref[...], route_ref.shape).astype(jnp.bfloat16)


def expert(got, w_in, w_down, block=256):
    parts, _, capacity, width = got.shape
    slots = parts * capacity
    hidden_width = w_down.shape[0]
    steps = hidden_width // block
    return pl.pallas_call(
        expert_kernel,
        grid=(steps,),
        in_specs=[
            pl.BlockSpec(got.shape, lambda j: (0, 0, 0, 0)),
            pl.BlockSpec((width, block), lambda j: (0, j)),
            pl.BlockSpec((width, block), lambda j: (0, steps + j)),
            pl.BlockSpec((block, width), lambda j: (j, 0)),
        ],
        out_specs=[
            pl.BlockSpec((3, slots, block), lambda j: (0, 0, j)),
            pl.BlockSpec((slots, 128), lambda j: (0, 0)),
        ],
        out_shape=[
            jax.ShapeDtypeStruct((3, slots, hidden_width), jnp.bfloat16),
            jax.ShapeDtypeStruct((slots, 128), jnp.bfloat16),
        ],
        scratch_shapes=[pltpu.VMEM((slots, 1), jnp.float32)],
        compiler_params=pltpu.CompilerParams(vmem_limit_bytes=58 * 2**20),
        cost_estimate=pl.CostEstimate(
            flops=6 * slots * hidden_width * width,
            bytes_accessed=6 * hidden_width * width + 4 * slots * width,
            transcendentals=slots * hidden_width,
        ),
        name="expert",
    )(got, w_in, w_in, w_down)


def weight_block(own_ref, far_ref, near_ref, mine_ref, theirs_ref, units):
    slots = mine_ref.shape[1]
    own = own_ref[:, 0].reshape(slots, -1)
    came = jnp.where(pl.program_id(0) == 0, far_ref[:, 0], near_ref[:, 0]).reshape(slots, -1)
    return [
        contract(own, mine_ref[u], 0, 0) + contract(came, theirs_ref[u], 0, 0) for u in units
    ]


def grad_in_kernel(_, own_ref, far_ref, near_ref, mine_ref, theirs_ref, out_ref):
    gate, up = weight_block(own_ref, far_ref, near_ref, mine_ref, theirs_ref, (1, 2))
    width = gate.shape[1]
    out_ref[0, 0, :, :width] = gate.astype(jnp.bfloat16)
    out_ref[0, 0, :, width:] = up.astype(jnp.bfloat16)


def grad_down_kernel(_, own_ref, far_ref, near_ref, mine_ref, theirs_ref, far_out, near_out):
    (down,) = weight_block(own_ref, far_ref, near_ref, mine_ref, theirs_ref, (0,))
    down = down.astype(jnp.bfloat16)

    @pl.when(pl.program_id(0) == 0)
    def _():
        far_out[0] = down

    @pl.when(pl.program_id(0) == 1)
    def _():
        near_out[0] = down


def weight_grads(kernel, kind, units, place, got, far, near, mine, theirs, rings, out_specs, out_shape):
    parts, _, capacity, width = got.shape
    block = width // (4 * rings)
    slots, hidden_width = mine.shape[1:]
    stretch = (parts, 1, capacity, block)

    def own_at(half, ring, place_ref):
        side = jnp.where(half == 0, 1 - place_ref[0], place_ref[0])
        return (0, kind, 0, (side * 2 + place_ref[1]) * rings + ring)

    def far_at(half, ring, place_ref):
        return (0, kind, 0, jnp.where(half == 0, ring, rings - 1))

    def near_at(half, ring, place_ref):
        return (0, kind, 0, jnp.where(half == 0, 0, ring))

    whole = pl.BlockSpec(mine.shape, lambda half, ring, place_ref: (0, 0, 0))
    return pl.pallas_call(
        kernel,
        grid_spec=pltpu.PrefetchScalarGridSpec(
            num_scalar_prefetch=1,
            grid=(2, rings),
            in_specs=[
                pl.BlockSpec(stretch, own_at),
                pl.BlockSpec(stretch, far_at),
                pl.BlockSpec(stretch, near_at),
                whole,
                whole,
            ],
            out_specs=out_specs,
        ),
        out_shape=out_shape,
        compiler_params=pltpu.CompilerParams(vmem_limit_bytes=58 * 2**20),
        cost_estimate=pl.CostEstimate(
            flops=2 * slots * width * hidden_width * units,
            bytes_accessed=width * hidden_width * units + 2 * slots * width,
            transcendentals=0,
        ),
    )(place, got, far, near, mine, theirs)


def slot_kernel(grads_ref, w_ref, out_ref):
    width = grads_ref.shape[2]
    rows = contract(grads_ref[1], w_ref[:, :width], 1, 1) + contract(
        grads_ref[2], w_ref[:, width:], 1, 1
    )
    out_ref[...] = rows.astype(jnp.bfloat16).reshape(out_ref.shape)


def slot_rows(grads, w_in, parts, block=512):
    _, slots, hidden_width = grads.shape
    width = w_in.shape[0]
    return pl.pallas_call(
        slot_kernel,
        grid=(width // block,),
        in_specs=[
            pl.BlockSpec(grads.shape, lambda j: (0, 0, 0)),
            pl.BlockSpec((block, 2 * hidden_width), lambda j: (j, 0)),
        ],
        out_specs=pl.BlockSpec((parts, slots // parts, block), lambda j: (0, 0, j)),
        out_shape=jax.ShapeDtypeStruct((parts, slots // parts, width), jnp.bfloat16),
        compiler_params=pltpu.CompilerParams(vmem_limit_bytes=60 * 2**20),
        cost_estimate=pl.CostEstimate(
            flops=4 * slots * hidden_width * width,
            bytes_accessed=4 * hidden_width * width + 2 * slots * width,
            transcendentals=0,
        ),
        name="slot_rows",
    )(grads, w_in)


def per_device(residual, norm_gain, grad_out, expert_ids, route_weights, weight_in, weight_down):
    tok_rows, width = residual.shape
    topk = expert_ids.shape[1]
    hidden_width = weight_down.shape[1]
    experts = lax.axis_size("expert")
    capacity = min(tok_rows, 3 * tok_rows * topk // (2 * experts))
    slot_total = experts * capacity
    rings = lax.axis_size("ulysses")
    quarter = width // 4
    block = quarter // rings
    side = lax.axis_index("dp_0")
    core = lax.axis_index("dp_1")
    ids_t = expert_ids.T
    weights_t = route_weights.T
    place, residual = lax.optimization_barrier(
        (jnp.stack([side, core]).astype(jnp.int32), residual)
    )
    side, core = place[0], place[1]

    send, select = pack(ids_t, weights_t, norm_gain[None], residual, grad_out, experts, capacity)
    got = lax.all_to_all(
        send.reshape(experts, 2 * capacity, width),
        "expert",
        split_axis=0,
        concat_axis=0,
        tiled=True,
    )
    (got, place, ids_t, weights_t, residual, grad_out, norm_gain, weight_in, weight_down, select) = (
        lax.optimization_barrier(
            (got, place, ids_t, weights_t, residual, grad_out, norm_gain, weight_in, weight_down, select)
        )
    )
    side, core = place[0], place[1]
    got = got.reshape(experts, 2, capacity, width)
    w_in = weight_in[0]
    w_down = weight_down[0]

    def swap_cores(half):
        start = (half * 2 + 1 - core) * quarter
        return lax.ppermute(lax.dynamic_slice_in_dim(got, start, quarter, axis=3), "dp_1", SWAP)

    far = swap_cores(1 - side)
    near = swap_cores(side)
    mine, route = expert(got, w_in, w_down)
    theirs = lax.ppermute(mine, "dp_1", SWAP)
    shared = (place, got, far, near, mine, theirs, rings)
    part_in = weight_grads(
        grad_in_kernel,
        0,
        2,
        *shared,
        pl.BlockSpec((1, 1, block, 2 * hidden_width), lambda half, ring, _: (ring, half, 0, 0)),
        jax.ShapeDtypeStruct((rings, 2, block, 2 * hidden_width), jnp.bfloat16),
    )
    far_down, near_down = weight_grads(
        grad_down_kernel,
        1,
        1,
        *shared,
        [
            pl.BlockSpec(
                (1, block, hidden_width),
                lambda half, ring, _: (jnp.where(half == 0, ring, rings - 1), 0, 0),
            ),
            pl.BlockSpec(
                (1, block, hidden_width), lambda half, ring, _: (jnp.where(half == 0, 0, ring), 0, 0)
            ),
        ],
        [jax.ShapeDtypeStruct((rings, block, hidden_width), jnp.bfloat16)] * 2,
    )
    came_down = lax.ppermute(far_down, "dp_0", SWAP)
    summed_in = lax.psum_scatter(
        part_in.reshape(rings, 2 * block, 2 * hidden_width),
        "ulysses",
        scatter_dimension=0,
        tiled=True,
    )[0]
    came_in = lax.ppermute(summed_in[:block], "dp_0", SWAP)
    grad_in = (summed_in[block:].astype(jnp.float32) + came_in.astype(jnp.float32))[None]
    part_down = (near_down.astype(jnp.float32) + came_down.astype(jnp.float32)).astype(jnp.bfloat16)
    summed_down = lax.psum_scatter(part_down, "ulysses", scatter_dimension=0, tiled=True)
    grad_down = summed_down.astype(jnp.float32)

    back_normed = lax.all_to_all(
        slot_rows(mine, w_in, experts), "expert", split_axis=0, concat_axis=0, tiled=True
    )
    back_route = lax.all_to_all(
        route[:, 0].reshape(experts, capacity), "expert", split_axis=0, concat_axis=0, tiled=True
    )
    resid = residual.astype(jnp.float32)
    inv_rms = lax.rsqrt(jnp.mean(resid * resid, axis=-1, keepdims=True) + eps)
    unit_rows = resid * inv_rms
    grad_normed = contract(select, back_normed.reshape(slot_total, width), 0, 0)
    token_route = jnp.sum(
        select.reshape(experts, capacity, tok_rows).astype(jnp.float32)
        * back_route.astype(jnp.float32)[:, :, None],
        axis=1,
    )
    chosen = ids_t[:, None, :] == lax.broadcasted_iota(jnp.int32, (1, experts, tok_rows), 1)
    route_t = jnp.sum(jnp.where(chosen, token_route[None], 0.0), axis=1)
    route_grad = (route_t / weights_t.astype(jnp.float32)).astype(jnp.bfloat16).T
    scaled_normed = grad_normed * norm_gain
    branch = inv_rms * (
        scaled_normed - unit_rows * jnp.mean(scaled_normed * unit_rows, axis=-1, keepdims=True)
    )
    grad_residual = (grad_out.astype(jnp.float32) + branch).astype(jnp.bfloat16)
    return (grad_residual, route_grad, grad_in, grad_down)


def solution(mesh):
    finer = Mesh(
        mesh.devices.reshape(2, 2, mesh.shape["ulysses"], mesh.shape["expert"]),
        ("dp_0", "dp_1", "ulysses", "expert"),
    )
    return jax.shard_map(
        per_device,
        mesh=finer,
        in_specs=(
            P(DP_ULYSSES_EXPERT, None),
            P(),
            P(DP_ULYSSES_EXPERT, None),
            P(DP_ULYSSES_EXPERT, None),
            P(DP_ULYSSES_EXPERT, None),
            P("expert", None, None),
            P("expert", None, None),
        ),
        out_specs=(
            P(DP_ULYSSES_EXPERT, None),
            P(DP_ULYSSES_EXPERT, None),
            P("expert", DP_ULYSSES, None),
            P("expert", DP_ULYSSES, None),
        ),
        check_vma=False,
    )
```

time: 287 us -> 264 us (0.920)
  waiting for transfers between devices: 155 us -> 67 us
  blocking collectives: 0 us -> 81.2 us
  matrix products: 73.1 us -> 4.04 us
  Pallas kernels: 0 us -> 56.1 us
  starting transfers between devices: 23.5 us -> 13.2 us
  local copies, waits for them, and re-layouts: 4.26 us -> 13 us
  other arithmetic: 16.1 us -> 11.9 us
    all_to_all x3 -> x2, waiting for transfers between devices: 132 us -> 6.22 us  [the longest x1 6.22 us: per_device(): lax.all_to_all(slot_rows(mine, w_in, experts), 'expert', split_axis=0, co...]
    all_to_all x0 -> x1, blocking collectives: none -> 81.2 us  [per_device(): lax.all_to_all(send.reshape(experts, 2 * capacity, width), 'expert', spli...]
    dot_general x15 -> x1, matrix products: 73.1 us -> 4.04 us  [contract(): lax.dot_general(left, right, (((over_left,), (over_right,)), ((), ())), p...]
    pallas_call x0 -> x5, Pallas kernels: none -> 56.1 us  [the longest x2 25.1 us: weight_grads(): pl.pallas_call(kernel, grid_spec=pltpu.PrefetchScalarGridSpec(num_scalar_...]
    ppermute x1, waiting for transfers between devices: 6.41 us -> 42.1 us  [per_device(): came_down = lax.ppermute(far_down, 'dp_0', SWAP)]
    all_to_all x3 -> x2, starting transfers between devices: 20.1 us -> 12 us  [the longest x1 8.47 us: per_device(): lax.all_to_all(slot_rows(mine, w_in, experts), 'expert', split_axis=0, co...]
    unnamed x28 -> x32, local copies, waits for them, and re-layouts: 0.07 us -> 8.06 us
    ppermute x5 -> x4, waiting for transfers between devices: 3.41 us -> 7.21 us  [the longest x2 5.19 us: swap_cores(): lax.ppermute(lax.dynamic_slice_in_dim(got, start, quarter, axis=3), 'dp_1...]
  transfers between devices with their start and end apart: 13 -> 9, of which waited for: 6 -> 6; matrix products, arithmetic and copies ran while one was open for 21% -> 7% of each run, Pallas kernels for 0% -> 9%
where the time goes in v2:
time: 264 us; the launch traced here: 263 us
  blocking collectives  81.2 us (31%)
  waiting for transfers between devices  67 us (25%)
  Pallas kernels  56.1 us (21%)
  between operations  16.7 us (6%)
  starting transfers between devices  13.2 us (5%)
  local copies, waits for them, and re-layouts  13 us (5%)
  other arithmetic  11.9 us (5%)
  matrix products  4.04 us (2%)
    all_to_all x1, blocking collectives, per_device(): lax.all_to_all(send.reshape(experts, 2 * capacity, width), 'expert', spli...  81.2 us
    ppermute x1, waiting for transfers between devices, per_device(): came_down = lax.ppermute(far_down, 'dp_0', SWAP)  42.1 us
    pallas_call x2, Pallas kernels, weight_grads(): pl.pallas_call(kernel, grid_spec=pltpu.PrefetchScalarGridSpec(num_scalar_...  25.1 us
    pallas_call x1, Pallas kernels, expert(): pl.pallas_call(expert_kernel, grid=(steps,), in_specs=[pl.BlockSpec(got.s...  14.9 us
    pallas_call x1, Pallas kernels, slot_rows(): pl.pallas_call(slot_kernel, grid=(width // block,), in_specs=[pl.BlockSpe...  11.9 us
    reduce_scatter x1, waiting for transfers between devices, per_device(): lax.psum_scatter(part_down, 'ulysses', scatter_dimension=0, tiled=True)  11.5 us
    all_to_all x1, starting transfers between devices, per_device(): lax.all_to_all(slot_rows(mine, w_in, experts), 'expert', split_axis=0, co...  8.47 us
    unnamed x32, local copies, waits for them, and re-layouts  8.06 us
  transfers between devices with their start and end apart: 9, of which 6 were waited for; matrix products, arithmetic and copies ran while one was open for 7% of the time, Pallas kernels for 9%

profile of v2, /device:TPU:0, one launch (start us, length us, event | category | flops | bytes accessed | tf_op | source)
XLA Modules:
  0.0 263.2 jit_solution(9917489823528568609)
XLA Ops:
  7.2 0.0 reduce-scatter.3.cloned.1.call-start
  7.2 0.1 pad_add_fusion._
  7.3 1.2 copy-done
  8.5 1.2 copy-done.2
  9.7 0.7 copy-done.4
  10.5 0.7 copy-done.6
  11.1 0.7 copy-done.8
  11.8 4.2 %pack.1 = (bf16[8,2,48,4096]{3,2,1,0:T(8,128)(2,1)S(1)}, bf16[384,128]{1,0:T(8,128)(2,1)S(1)}) custom-call(s32[2,128]{1,0:T(2,128)S(1)} %bitcast.32, bf16[2,128]{1,0:T(2,128)(2,1)S(1)} %bitcast.34, f32[1,4096]{1,0:T(1,128)S(1)} %bitcast.31, bf16[128,4096]{1,0:T(8,128)(2,1)S(1)} %copy-done, bf16[128,4096]{1,0:T(8,128)(2,1)S(1)} %copy-done.2), custom_call_target="tpu_custom_call" | custom-call | flops 805306368 | bytes 6291456 | tf_op jit(solution)/shard_map/pack/pallas_call | solution.py:76
  16.0 81.2 %all_to_all.20 = bf16[8,96,4096]{2,1,0:T(8,128)(2,1)} all-to-all(bf16[8,96,4096]{2,1,0:T(8,128)(2,1)S(1)} %bitcast.29), channel_id=1, replica_groups=mesh['dp_0'=2,'dp_1'=2,'ulysses'=4,'expert'=8] {'expert'}, dimensions={0} | all-to-all | bytes 12582912 | tf_op jit(solution)/shard_map/all_to_all | solution.py:281
  97.3 14.9 %expert.1 = (bf16[3,384,768]{2,1,0:T(8,128)(2,1)}, bf16[384,128]{1,0:T(8,128)(2,1)}) custom-call(bf16[8,2,48,4096]{3,2,1,0:T(8,128)(2,1)} %bitcast.36, bf16[4096,1536]{1,0:T(8,128)(2,1)} %bitcast.40, bf16[4096,1536]{1,0:T(8,128)(2,1)} %bitcast.41, bf16[768,4096]{1,0:T(8,128)(2,1)} %bitcast.44), custom_call_target="tpu_custom_call" | custom-call | flops 7247757312 | bytes 25165824 | tf_op jit(solution)/shard_map/expert/pallas_call | solution.py:133
  112.2 0.0 collective-permute-start.2
  112.2 0.6 fusion.12
  115.4 2.3 constant_dynamic-slice_fusion
  117.6 0.6 collective-permute-start
  118.2 0.1 collective-permute-start.1
  118.3 2.9 %collective-permute-done.far_ref = bf16[8,2,48,1024]{3,2,1,0:T(8,128)(2,1)S(1)} collective-permute-done((bf16[8,2,48,1024]{3,2,1,0:T(8,128)(2,1)S(1)}, bf16[8,2,48,1024]{3,2,1,0:T(8,128)(2,1)S(1)}, u32[]{:S(2)}, u32[]{:S(2)}) %collective-permute-start) | collective-permute-done | bytes 1572896 | tf_op jit(solution)/shard_map/ppermute | solution.py:300
  121.3 2.2 collective-permute-done.1.near_ref
  123.5 0.0 collective-permute-done.2.theirs_ref
  123.5 1.2 copy-done.12
  124.7 1.2 copy-done.10
  125.9 13.2 %shard_map.102 = bf16[4,2,256,1536]{3,2,1,0:T(8,128)(2,1)} custom-call(s32[2]{0:T(128)} %copy-done.15, bf16[8,2,48,4096]{3,2,1,0:T(8,128)(2,1)} %bitcast.38, bf16[8,2,48,1024]{3,2,1,0:T(8,128)(2,1)} %copy-done.11, bf16[8,2,48,1024]{3,2,1,0:T(8,128)(2,1)} %copy-done.12, bf16[3,384,768]{2,1,0:T(8,128)(2,1)} %get-tuple-element.32.grads_ref.mine_ref, ...), custom_call_target="tpu_custom_call" | custom-call | flops 4831838208 | bytes 9437184 | tf_op jit(solution)/shard_map/pallas_call | solution.py:207
  139.1 0.0 reduce-scatter.3.cloned.1.call-update
  139.1 0.9 copy-done.14
  139.9 0.1 slice_reduce_fusion
  140.1 0.7 all_to_all.16
  140.7 3.5 %all-to-all-start.2 = ((bf16[8,1,48]{2,1,0:T(2,128)(2,1)}), bf16[8,1,48]{2,1,0:T(2,128)(2,1)S(1)}, u32[]{:S(2)}, u32[]{:S(2)}) async-start(bf16[8,1,48]{2,1,0:T(2,128)(2,1)} %all_to_all.16), calls=%async_computation.2 | async-start | bytes 8192 | tf_op jit(solution)/shard_map/all_to_all | solution.py:347
  144.2 11.9 %shard_map.103 = (bf16[4,256,768]{2,1,0:T(8,128)(2,1)}, bf16[4,256,768]{2,1,0:T(8,128)(2,1)}) custom-call(s32[2]{0:T(128)} %copy-done.15, bf16[8,2,48,4096]{3,2,1,0:T(8,128)(2,1)} %bitcast.39, bf16[8,2,48,1024]{3,2,1,0:T(8,128)(2,1)} %copy-done.11, bf16[8,2,48,1024]{3,2,1,0:T(8,128)(2,1)} %copy-done.12, ...), custom_call_target="tpu_custom_call" | custom-call | flops 2415919104 | bytes 6291456 | tf_op jit(solution)/shard_map/pallas_call | solution.py:207
  156.2 0.4 collective-permute-start.4
  156.6 11.9 %slot_rows.1 = bf16[8,48,4096]{2,1,0:T(8,128)(2,1)} custom-call(bf16[3,384,768]{2,1,0:T(8,128)(2,1)} %get-tuple-element.32.grads_ref.mine_ref, bf16[4096,1536]{1,0:T(8,128)(2,1)} %bitcast.42), custom_call_target="tpu_custom_call" | custom-call | flops 4831838208 | bytes 15728640 | tf_op jit(solution)/shard_map/slot_rows/pallas_call | solution.py:242
  168.4 8.5 %all-to-all-start.1 = ((bf16[8,48,4096]{2,1,0:T(8,128)(2,1)}), bf16[8,48,4096]{2,1,0:T(8,128)(2,1)}, u32[]{:S(2)}, u32[]{:S(2)}) async-start(bf16[8,48,4096]{2,1,0:T(8,128)(2,1)} %slot_rows.1), calls=%async_computation.1 | async-start | bytes 6291456 | tf_op jit(solution)/shard_map/all_to_all | solution.py:344
  176.9 0.0 reduce-scatter.5.cloned.1.call-start
  177.0 42.1 %collective-permute-done.4 = bf16[4,256,768]{2,1,0:T(8,128)(2,1)} collective-permute-done((bf16[4,256,768]{2,1,0:T(8,128)(2,1)}, bf16[4,256,768]{2,1,0:T(8,128)(2,1)}, u32[]{:S(2)}, u32[]{:S(2)}) %collective-permute-start.4) | collective-permute-done | bytes 1572896 | tf_op jit(solution)/shard_map/ppermute | solution.py:331
  219.1 3.0 %add_convert_fusion = bf16[4,256,768]{2,1,0:T(8,128)(2,1)} fusion(bf16[4,256,768]{2,1,0:T(8,128)(2,1)} %collective-permute-done.4, bf16[4,256,768]{2,1,0:T(8,128)(2,1)S(1)} %copy-done.13), kind=kLoop, calls=%fused_computation.1 | loop fusion | flops 3145728 | bytes 4718592 | tf_op jit(solution)/shard_map/convert_element_type | solution.py:340
  222.1 0.0 reduce-scatter.5.cloned.1.call-update
  222.1 0.3 fusion.7
  222.4 0.1 fusion.9
  222.5 0.2 copy-done.7
  222.8 0.5 fusion.11
  223.3 6.2 %all-to-all-done.1 = bf16[8,48,4096]{2,1,0:T(8,128)(2,1)} async-done(((bf16[8,48,4096]{2,1,0:T(8,128)(2,1)}), bf16[8,48,4096]{2,1,0:T(8,128)(2,1)}, u32[]{:S(2)}, u32[]{:S(2)}) %all-to-all-start.1) | async-done | bytes 3145760 | tf_op jit(solution)/shard_map/all_to_all | solution.py:344
  229.5 4.0 %fusion.2 = (f32[128]{0:T(128)S(1)}, f32[128,4096]{1,0:T(8,128)}) fusion(bf16[128,4096]{1,0:T(8,128)(2,1)S(1)} %copy-done.1, f32[128]{0:T(128)S(1)} %add_rsqrt_fusion, f32[4096]{0:T(1024)S(1)} %copy-done.5, bf16[384,128]{1,0:T(8,128)(2,1)S(1)} %get-tuple-element.28, bf16[384,4096]{1,0:T(8,128)(2,1)} %bitcast.9), kind=kOutput, calls=%fused_computation.6 | convolution fusion | flops 405274496 | bytes 6407168 | tf_op jit(solution)/shard_map/dot_general | solution.py:18
  233.6 1.3 slice_bitcast_fusion
  234.8 0.1 collective-permute-start.3
  234.9 0.1 copy-done.3
  235.0 3.2 %fusion.6 = bf16[128,4096]{1,0:T(8,128)(2,1)} fusion(f32[128,4096]{1,0:T(8,128)} %get-tuple-element.45, bf16[128,4096]{1,0:T(8,128)(2,1)S(1)} %copy-done.1, bf16[128,4096]{1,0:T(8,128)(2,1)S(1)} %copy-done.3, f32[128]{0:T(128)S(1)} %broadcast_multiply_fusion, f32[128]{0:T(128)S(1)} %add_rsqrt_fusion), kind=kLoop, calls=%fused_computation.10 | loop fusion | flops 4194304 | bytes 5243904 | tf_op jit(solution)/shard_map/convert_element_type | solution.py:366
  238.2 11.5 %reduce-scatter.5.cloned.1.call-done = bf16[1,256,768]{2,1,0:T(8,128)(2,1)} async-done(((bf16[4,256,768]{2,1,0:T(8,128)(2,1)}), bf16[1,256,768]{2,1,0:T(8,128)(2,1)}) %reduce-scatter.5.cloned.1.call-update) | async-done | bytes 393232 | tf_op jit(solution)/shard_map/reduce_scatter | solution.py:341
  249.7 1.9 convert_element_type.67
  251.6 2.0 collective-permute-done.3
  253.6 2.7 %fusion.8 = f32[1,256,1536]{2,1,0:T(8,128)} fusion(bf16[256,1536]{1,0:T(8,128)(2,1)} %collective-permute-done.3, bf16[1,512,1536]{2,1,0:T(8,128)(2,1)} %reduce-scatter.3.cloned.1.call-done), kind=kLoop, calls=%fused_computation.13 | loop fusion | flops 1179648 | bytes 3145728 | tf_op jit(solution)/shard_map/broadcast_in_dim | solution.py:339
  (28 shorter events, 0.1 us)
Async XLA Ops:
  7.2 226.4 %reduce-scatter.3.cloned.1.call-start = ((), (), s32[]{:S(2)}) async-start(), calls=%async_computation.5 | async-start | bytes 7864320 | tf_op jit(solution)/shard_map/reduce_scatter | solution.py:332
  7.3 104.9 %copy-start.15 = (s32[2]{0:T(128)}, s32[2]{0:T(128)S(1)}, u32[]{:S(2)}) copy-start(s32[2]{0:T(128)S(1)} %pad_add_fusion._) | copy-start | bytes 28
  7.3 1.2 copy-start
  8.5 1.2 copy-start.2
  9.7 0.7 copy-start.4
  10.5 0.7 copy-start.6
  11.1 0.7 copy-start.8
  112.2 11.3 %collective-permute-start.2 = (bf16[3,384,768]{2,1,0:T(8,128)(2,1)}, bf16[3,384,768]{2,1,0:T(8,128)(2,1)S(1)}, u32[]{:S(2)}, u32[]{:S(2)}) collective-permute-start(bf16[3,384,768]{2,1,0:T(8,128)(2,1)} %get-tuple-element.32.grads_ref.mine_ref), channel_id=1, source_target_pairs={{0,32},{32,0},{1,33},{33,1},{2,34},{34,2},{3,35},{35,3},{4,36},{36... | collective-permute-start | bytes 5308424 | tf_op jit(solution)/shard_map/ppermute | solution.py:305
  117.6 3.6 %collective-permute-start = (bf16[8,2,48,1024]{3,2,1,0:T(8,128)(2,1)S(1)}, bf16[8,2,48,1024]{3,2,1,0:T(8,128)(2,1)S(1)}, u32[]{:S(2)}, u32[]{:S(2)}) collective-permute-start(bf16[8,2,48,1024]{3,2,1,0:T(8,128)(2,1)S(1)} %get-tuple-element.41), channel_id=1, source_target_pairs={{0,32},{32,0},{1,33},{33,1},{2,34},{34,2},{3,35},{35,3},{4,36},{36... | collective-permute-start | bytes 4718600 | tf_op jit(solution)/shard_map/ppermute | solution.py:300
  118.2 5.3 %collective-permute-start.1 = (bf16[8,2,48,1024]{3,2,1,0:T(8,128)(2,1)S(1)}, bf16[8,2,48,1024]{3,2,1,0:T(8,128)(2,1)S(1)}, u32[]{:S(2)}, u32[]{:S(2)}) collective-permute-start(bf16[8,2,48,1024]{3,2,1,0:T(8,128)(2,1)S(1)} %get-tuple-element.40), channel_id=1, source_target_pairs={{0,32},{32,0},{1,33},{33,1},{2,34},{34,2},{3,35},{35,3},{4,36},{36... | collective-permute-start | bytes 4718600 | tf_op jit(solution)/shard_map/ppermute | solution.py:300
  121.3 2.3 copy-start.11
  123.5 1.2 copy-start.12
  124.7 1.2 copy-start.10
  139.1 0.9 copy-start.14
  140.7 27.7 %all-to-all-start.2 = ((bf16[8,1,48]{2,1,0:T(2,128)(2,1)}), bf16[8,1,48]{2,1,0:T(2,128)(2,1)S(1)}, u32[]{:S(2)}, u32[]{:S(2)}) async-start(bf16[8,1,48]{2,1,0:T(2,128)(2,1)} %all_to_all.16), calls=%async_computation.2 | async-start | bytes 8192 | tf_op jit(solution)/shard_map/all_to_all | solution.py:347
  156.2 62.9 %collective-permute-start.4 = (bf16[4,256,768]{2,1,0:T(8,128)(2,1)}, bf16[4,256,768]{2,1,0:T(8,128)(2,1)}, u32[]{:S(2)}, u32[]{:S(2)}) collective-permute-start(bf16[4,256,768]{2,1,0:T(8,128)(2,1)} %get-tuple-element.39), channel_id=1, source_target_pairs={{0,64},{64,0},{1,65},{65,1},{2,66},{66,2},{3,67},{67,3},{4,68},{68... | collective-permute-start | bytes 4718600 | tf_op jit(solution)/shard_map/ppermute | solution.py:331
  168.4 50.6 %copy-start.13 = (bf16[4,256,768]{2,1,0:T(8,128)(2,1)S(1)}, bf16[4,256,768]{2,1,0:T(8,128)(2,1)}, u32[]{:S(2)}) copy-start(bf16[4,256,768]{2,1,0:T(8,128)(2,1)} %get-tuple-element.38) | copy-start | bytes 4718596
  168.4 61.1 %all-to-all-start.1 = ((bf16[8,48,4096]{2,1,0:T(8,128)(2,1)}), bf16[8,48,4096]{2,1,0:T(8,128)(2,1)}, u32[]{:S(2)}, u32[]{:S(2)}) async-start(bf16[8,48,4096]{2,1,0:T(8,128)(2,1)} %slot_rows.1), calls=%async_computation.1 | async-start | bytes 6291456 | tf_op jit(solution)/shard_map/all_to_all | solution.py:344
  176.9 72.8 %reduce-scatter.5.cloned.1.call-start = ((), (), s32[]{:S(2)}) async-start(), calls=%async_computation.6 | async-start | bytes 1966080 | tf_op jit(solution)/shard_map/reduce_scatter | solution.py:341
  219.1 3.0 %copy-start.1 = (bf16[128,4096]{1,0:T(8,128)(2,1)S(1)}, bf16[128,4096]{1,0:T(8,128)(2,1)}, u32[]{:S(2)}) copy-start(bf16[128,4096]{1,0:T(8,128)(2,1)} %resid_ref) | copy-start | bytes 3145732
  222.1 0.7 copy-start.7
  222.1 0.7 copy-start.9
  222.1 7.4 %copy-start.5 = (f32[4096]{0:T(1024)S(1)}, f32[4096]{0:T(1024)}, u32[]{:S(2)}) copy-start(f32[4096]{0:T(1024)} %param.8) | copy-start | bytes 49156
  233.5 1.5 copy-start.3
  234.8 18.8 %collective-permute-start.3 = (bf16[256,1536]{1,0:T(8,128)(2,1)S(1)}, bf16[256,1536]{1,0:T(8,128)(2,1)}, u32[]{:S(2)}, u32[]{:S(2)}) collective-permute-start(bf16[256,1536]{1,0:T(8,128)(2,1)S(1)} %slice_bitcast_fusion), channel_id=1, source_target_pairs={{0,64},{64,0},{1,65},{65,1},{2,66},{66,2},{3,67},{67,3},{4,68},{68... | collective-permute-start | bytes 2359304 | tf_op jit(solution)/shard_map/ppermute | solution.py:338
Sparse Core Ops, SparseCore 0:
  139.2 62.2 reduce-scatter.2
  222.2 27.4 reduce-scatter.4

commit v3 on v2

v3 whole, which is shorter than its diff:
```python
import jax
import jax.numpy as jnp
from jax import lax
from jax.experimental import pallas as pl
from jax.experimental.pallas import tpu as pltpu
from jax.sharding import Mesh
from jax.sharding import PartitionSpec as P

DP_ULYSSES = ("dp_0", "dp_1", "ulysses")
DP_ULYSSES_EXPERT = ("dp_0", "dp_1", "ulysses", "expert")

SWAP = [(0, 1), (1, 0)]

eps = 1e-06

VMEM = 62 * 2**20


def contract(left, right, over_left, over_right):
    return lax.dot_general(
        left, right, (((over_left,), (over_right,)), ((), ())), preferred_element_type=jnp.float32
    )


def slot_matrices(ids, weights, experts, capacity):
    tok_rows = ids.shape[1]
    expert = lax.broadcasted_iota(jnp.int32, (experts, tok_rows), 0)
    first, second = ids[0:1] == expert, ids[1:2] == expert
    hit = first | second
    weight = jnp.where(first, weights[0:1], jnp.where(second, weights[1:2], 0.0))
    square = (tok_rows, tok_rows)
    before = lax.broadcasted_iota(jnp.int32, square, 0) < lax.broadcasted_iota(jnp.int32, square, 1)
    rank = contract(
        jnp.where(hit, 1.0, 0.0).astype(jnp.bfloat16),
        jnp.where(before, 1.0, 0.0).astype(jnp.bfloat16),
        1,
        0,
    ).astype(jnp.int32)
    rank = jnp.where(hit, rank, capacity)
    slot = lax.broadcasted_iota(jnp.int32, (capacity, tok_rows), 0)
    select, scale = [], []
    for e in range(experts):
        held = rank[e : e + 1] == slot
        select.append(jnp.where(held, 1.0, 0.0))
        scale.append(jnp.where(held, weight[e : e + 1], 0.0))
    return (
        jnp.concatenate(select, axis=0).astype(jnp.bfloat16),
        jnp.concatenate(scale, axis=0).astype(jnp.bfloat16),
    )


def pack_kernel(
    ids_ref, w_ref, gain_ref, resid_ref, grad_ref, normed_ref, scaled_ref, sel_ref, inv_ref, scale_ref
):
    experts, capacity, block = normed_ref.shape

    @pl.when(pl.program_id(0) == 0)
    def _():
        full = resid_ref[...].astype(jnp.float32)
        mean = jnp.mean(full * full, axis=-1, keepdims=True)
        inv_ref[...] = lax.rsqrt(mean + eps)
        select, scale = slot_matrices(ids_ref[...], w_ref[...].astype(jnp.float32), experts, capacity)
        sel_ref[...] = select
        scale_ref[...] = scale

    at = pl.ds(pl.multiple_of(pl.program_id(0) * block, block), block)
    unit = resid_ref[:, at].astype(jnp.float32) * inv_ref[...]
    normed = (unit * gain_ref[:, at]).astype(jnp.bfloat16)
    sent = contract(sel_ref[...], normed, 1, 0).astype(jnp.bfloat16)
    normed_ref[...] = sent.reshape(experts, capacity, block)
    sent = contract(scale_ref[...], grad_ref[:, at], 1, 0).astype(jnp.bfloat16)
    scaled_ref[...] = sent.reshape(experts, capacity, block)


def pack(ids_t, w_t, gain, resid, grad, experts, capacity, block=512):
    rows, width = resid.shape
    whole = lambda a: pl.BlockSpec(a.shape, lambda j: (0,) * a.ndim)
    args = (ids_t, w_t, gain, resid, grad)
    slots = experts * capacity
    return pl.pallas_call(
        pack_kernel,
        grid=(width // block,),
        in_specs=[whole(a) for a in args],
        out_specs=[
            pl.BlockSpec((experts, capacity, block), lambda j: (0, 0, j)),
            pl.BlockSpec((experts, capacity, block), lambda j: (0, 0, j)),
            pl.BlockSpec((slots, rows), lambda j: (0, 0)),
        ],
        out_shape=[
            jax.ShapeDtypeStruct((experts, capacity, width), jnp.bfloat16),
            jax.ShapeDtypeStruct((experts, capacity, width), jnp.bfloat16),
            jax.ShapeDtypeStruct((slots, rows), jnp.bfloat16),
        ],
        scratch_shapes=[
            pltpu.VMEM((rows, 1), jnp.float32),
            pltpu.VMEM((slots, rows), jnp.bfloat16),
        ],
        compiler_params=pltpu.CompilerParams(vmem_limit_bytes=VMEM),
        cost_estimate=pl.CostEstimate(
            flops=4 * slots * rows * width, bytes_accessed=4 * slots * width, transcendentals=0
        ),
        name="pack",
    )(*args)


def forward_kernel(got_ref, gate_w_ref, up_w_ref, hidden_ref, gate_ref, up_ref):
    parts, capacity, width = got_ref.shape
    normed = got_ref[...].reshape(parts * capacity, width)
    gate = contract(normed, gate_w_ref[...], 1, 0)
    up = contract(normed, up_w_ref[...], 1, 0)
    sigmoid = jax.nn.sigmoid(gate)
    silu = gate * sigmoid
    hidden_ref[...] = (silu * up).astype(jnp.bfloat16)
    gate_ref[...] = up * sigmoid * (1.0 + gate * (1.0 - sigmoid))
    up_ref[...] = silu


def forward(got, w_in, block=256):
    parts, capacity, width = got.shape
    slots = parts * capacity
    hidden_width = w_in.shape[1] // 2
    steps = hidden_width // block
    out = pl.BlockSpec((slots, block), lambda j: (0, j))
    return pl.pallas_call(
        forward_kernel,
        grid=(steps,),
        in_specs=[
            pl.BlockSpec(got.shape, lambda j: (0, 0, 0)),
            pl.BlockSpec((width, block), lambda j: (0, j)),
            pl.BlockSpec((width, block), lambda j: (0, steps + j)),
        ],
        out_specs=[out] * 3,
        out_shape=[
            jax.ShapeDtypeStruct((slots, hidden_width), t)
            for t in (jnp.bfloat16, jnp.float32, jnp.float32)
        ],
        compiler_params=pltpu.CompilerParams(vmem_limit_bytes=VMEM),
        cost_estimate=pl.CostEstimate(
            flops=4 * slots * hidden_width * width,
            bytes_accessed=4 * hidden_width * width + 2 * slots * width,
            transcendentals=slots * hidden_width,
        ),
        name="forward",
    )(got, w_in, w_in)


def back_kernel(got_ref, w_ref, hidden_ref, gate_ref, up_ref, out_ref, route_ref, acc_ref):
    parts, capacity, width = got_ref.shape
    grad_hidden = contract(got_ref[...].reshape(parts * capacity, width), w_ref[...], 1, 1)
    out_ref[0] = (grad_hidden * gate_ref[...]).astype(jnp.bfloat16)
    out_ref[1] = (grad_hidden * up_ref[...]).astype(jnp.bfloat16)
    part = jnp.sum(grad_hidden * hidden_ref[...].astype(jnp.float32), axis=1, keepdims=True)

    @pl.when(pl.program_id(0) == 0)
    def _():
        acc_ref[...] = part

    @pl.when(pl.program_id(0) > 0)
    def _():
        acc_ref[...] += part

    @pl.when(pl.program_id(0) == pl.num_programs(0) - 1)
    def _():
        route_ref[...] = jnp.broadcast_to(acc_ref[...], route_ref.shape).astype(jnp.bfloat16)


def back(got, w_down, hidden, gate, up, block=256):
    parts, capacity, width = got.shape
    slots = parts * capacity
    hidden_width = w_down.shape[0]
    column = pl.BlockSpec((slots, block), lambda j: (0, j))
    return pl.pallas_call(
        back_kernel,
        grid=(hidden_width // block,),
        in_specs=[
            pl.BlockSpec(got.shape, lambda j: (0, 0, 0)),
            pl.BlockSpec((block, width), lambda j: (j, 0)),
            column,
            column,
            column,
        ],
        out_specs=[
            pl.BlockSpec((2, slots, block), lambda j: (0, 0, j)),
            pl.BlockSpec((slots, 128), lambda j: (0, 0)),
        ],
        out_shape=[
            jax.ShapeDtypeStruct((2, slots, hidden_width), jnp.bfloat16),
            jax.ShapeDtypeStruct((slots, 128), jnp.bfloat16),
        ],
        scratch_shapes=[pltpu.VMEM((slots, 1), jnp.float32)],
        compiler_params=pltpu.CompilerParams(vmem_limit_bytes=VMEM),
        cost_estimate=pl.CostEstimate(
            flops=2 * slots * hidden_width * width,
            bytes_accessed=2 * hidden_width * width + 2 * slots * width + 10 * slots * hidden_width,
            transcendentals=0,
        ),
        name="back",
    )(got, w_down, hidden, gate, up)


def turn_kernel(_, keep_ref, give_ref, keep_out, give_out):
    parts, capacity, block = keep_ref.shape
    keep_out[0, 0] = keep_ref[...].reshape(parts * capacity, block).T
    give_out[0, 0] = give_ref[...].reshape(parts * capacity, block).T


def turn(place, got, rings):
    parts, capacity, width = got.shape
    slots = parts * capacity
    block = width // (4 * rings)

    def column(half, ring, place_ref, core):
        side = jnp.where(half == 0, 1 - place_ref[0], place_ref[0])
        return (0, 0, (side * 2 + core) * rings + ring)

    out = pl.BlockSpec((1, 1, block, slots), lambda half, ring, _: (half, ring, 0, 0))
    return pl.pallas_call(
        turn_kernel,
        grid_spec=pltpu.PrefetchScalarGridSpec(
            num_scalar_prefetch=1,
            grid=(2, rings),
            in_specs=[
                pl.BlockSpec(
                    (parts, capacity, block), lambda half, ring, at: column(half, ring, at, at[1])
                ),
                pl.BlockSpec(
                    (parts, capacity, block), lambda half, ring, at: column(half, ring, at, 1 - at[1])
                ),
            ],
            out_specs=[out, out],
        ),
        out_shape=[jax.ShapeDtypeStruct((2, rings, block, slots), jnp.bfloat16)] * 2,
        compiler_params=pltpu.CompilerParams(vmem_limit_bytes=VMEM),
        cost_estimate=pl.CostEstimate(
            flops=slots * width * 1024, bytes_accessed=4 * slots * width, transcendentals=0
        ),
        name="turn",
    )(place, got, got)


def grad_in_kernel(keep_ref, came_ref, mine_ref, theirs_ref, out_ref):
    keep, came = keep_ref[0, 0], came_ref[0, 0]
    width = mine_ref.shape[2]
    for u in range(2):
        rows = contract(keep, mine_ref[u], 1, 0) + contract(came, theirs_ref[u], 1, 0)
        out_ref[0, 0, :, u * width : (u + 1) * width] = rows.astype(jnp.bfloat16)


def grad_down_kernel(keep_ref, came_ref, mine_ref, theirs_ref, far_out, near_out):
    rows = contract(keep_ref[0, 0], mine_ref[...], 1, 0) + contract(
        came_ref[0, 0], theirs_ref[...], 1, 0
    )
    rows = rows.astype(jnp.bfloat16)

    @pl.when(pl.program_id(0) == 0)
    def _():
        far_out[0] = rows

    @pl.when(pl.program_id(0) == 1)
    def _():
        near_out[0] = rows


def weight_grads(kernel, keep, came, mine, theirs, out_specs, out_shape):
    _, rings, block, slots = keep.shape
    left = pl.BlockSpec((1, 1, block, slots), lambda half, ring: (half, ring, 0, 0))
    whole = pl.BlockSpec(mine.shape, lambda half, ring: (0,) * mine.ndim)
    return pl.pallas_call(
        kernel,
        grid=(2, rings),
        in_specs=[left, left, whole, whole],
        out_specs=out_specs,
        out_shape=out_shape,
        compiler_params=pltpu.CompilerParams(vmem_limit_bytes=58 * 2**20),
        cost_estimate=pl.CostEstimate(
            flops=8 * rings * block * mine.size,
            bytes_accessed=8 * keep.size + 4 * mine.size + 4 * rings * block * mine.size // slots,
            transcendentals=0,
        ),
    )(keep, came, mine, theirs)


def slot_kernel(grads_ref, w_ref, out_ref):
    width = grads_ref.shape[2]
    rows = contract(grads_ref[0], w_ref[:, :width], 1, 1) + contract(
        grads_ref[1], w_ref[:, width:], 1, 1
    )
    out_ref[...] = rows.astype(jnp.bfloat16).reshape(out_ref.shape)


def slot_rows(grads, w_in, parts, block=512):
    _, slots, hidden_width = grads.shape
    width = w_in.shape[0]
    return pl.pallas_call(
        slot_kernel,
        grid=(width // block,),
        in_specs=[
            pl.BlockSpec(grads.shape, lambda j: (0, 0, 0)),
            pl.BlockSpec((block, 2 * hidden_width), lambda j: (j, 0)),
        ],
        out_specs=pl.BlockSpec((parts, slots // parts, block), lambda j: (0, 0, j)),
        out_shape=jax.ShapeDtypeStruct((parts, slots // parts, width), jnp.bfloat16),
        compiler_params=pltpu.CompilerParams(vmem_limit_bytes=VMEM),
        cost_estimate=pl.CostEstimate(
            flops=4 * slots * hidden_width * width,
            bytes_accessed=4 * hidden_width * width + 2 * slots * width,
            transcendentals=0,
        ),
        name="slot_rows",
    )(grads, w_in)


def exchange(rows):
    experts = lax.axis_size("expert")
    groups = [[(g ^ (e & 1)) * experts + e for e in range(experts)] for g in range(2)]
    return lax.all_to_all(
        rows,
        ("dp_0", "expert"),
        split_axis=0,
        concat_axis=0,
        axis_index_groups=groups,
        tiled=True,
    )


def per_device(residual, norm_gain, grad_out, expert_ids, route_weights, weight_in, weight_down):
    tok_rows, width = residual.shape
    topk = expert_ids.shape[1]
    hidden_width = weight_down.shape[1]
    experts = lax.axis_size("expert")
    capacity = min(tok_rows, 3 * tok_rows * topk // (2 * experts))
    slot_total = experts * capacity
    rings = lax.axis_size("ulysses")
    block = width // (4 * rings)
    side = lax.axis_index("dp_0")
    core = lax.axis_index("dp_1")
    ids_t = expert_ids.T
    weights_t = route_weights.T
    place, residual = lax.optimization_barrier(
        (jnp.stack([side, core]).astype(jnp.int32), residual)
    )

    send_normed, send_scaled, select = pack(
        ids_t, weights_t, norm_gain[None], residual, grad_out, experts, capacity
    )
    got_normed = exchange(send_normed)
    (got_normed, place, ids_t, weights_t, residual, grad_out, norm_gain, weight_in, weight_down) = (
        lax.optimization_barrier(
            (got_normed, place, ids_t, weights_t, residual, grad_out, norm_gain, weight_in, weight_down)
        )
    )
    got_scaled = exchange(send_scaled)
    w_in = weight_in[0]
    w_down = weight_down[0]
    keep_normed, give_normed = turn(place, got_normed, rings)
    came_normed = lax.ppermute(give_normed, "dp_1", SWAP)
    hidden, gate, up = forward(got_normed, w_in)
    their_hidden = lax.ppermute(hidden, "dp_1", SWAP)
    mine, route = back(got_scaled, w_down, hidden, gate, up)
    theirs = lax.ppermute(mine, "dp_1", SWAP)
    part_in = weight_grads(
        grad_in_kernel,
        keep_normed,
        came_normed,
        mine,
        theirs,
        pl.BlockSpec((1, 1, block, 2 * hidden_width), lambda half, ring: (ring, half, 0, 0)),
        jax.ShapeDtypeStruct((rings, 2, block, 2 * hidden_width), jnp.bfloat16),
    )
    keep_scaled, give_scaled = turn(place, got_scaled, rings)
    came_scaled = lax.ppermute(give_scaled, "dp_1", SWAP)
    far_down, near_down = weight_grads(
        grad_down_kernel,
        keep_scaled,
        came_scaled,
        hidden,
        their_hidden,
        [
            pl.BlockSpec(
                (1, block, hidden_width),
                lambda half, ring: (jnp.where(half == 0, ring, rings - 1), 0, 0),
            ),
            pl.BlockSpec(
                (1, block, hidden_width), lambda half, ring: (jnp.where(half == 0, 0, ring), 0, 0)
            ),
        ],
        [jax.ShapeDtypeStruct((rings, block, hidden_width), jnp.bfloat16)] * 2,
    )
    came_down = lax.ppermute(far_down, "dp_0", SWAP)
    summed_in = lax.psum_scatter(
        part_in.reshape(rings, 2 * block, 2 * hidden_width),
        "ulysses",
        scatter_dimension=0,
        tiled=True,
    )[0]
    came_in = lax.ppermute(summed_in[:block], "dp_0", SWAP)
    grad_in = (summed_in[block:].astype(jnp.float32) + came_in.astype(jnp.float32))[None]
    part_down = (near_down.astype(jnp.float32) + came_down.astype(jnp.float32)).astype(jnp.bfloat16)
    summed_down = lax.psum_scatter(part_down, "ulysses", scatter_dimension=0, tiled=True)
    summed_down, grad_in = lax.optimization_barrier((summed_down, grad_in))
    grad_down = summed_down.astype(jnp.float32)

    back_normed = exchange(slot_rows(mine, w_in, experts))
    back_route = exchange(route[:, 0].reshape(experts, capacity))
    resid = residual.astype(jnp.float32)
    inv_rms = lax.rsqrt(jnp.mean(resid * resid, axis=-1, keepdims=True) + eps)
    unit_rows = resid * inv_rms
    grad_normed = contract(select, back_normed.reshape(slot_total, width), 0, 0)
    token_route = jnp.sum(
        select.reshape(experts, capacity, tok_rows).astype(jnp.float32)
        * back_route.astype(jnp.float32)[:, :, None],
        axis=1,
    )
    chosen = ids_t[:, None, :] == lax.broadcasted_iota(jnp.int32, (1, experts, tok_rows), 1)
    route_t = jnp.sum(jnp.where(chosen, token_route[None], 0.0), axis=1)
    route_grad = (route_t / weights_t.astype(jnp.float32)).astype(jnp.bfloat16).T
    scaled_normed = grad_normed * norm_gain
    branch = inv_rms * (
        scaled_normed - unit_rows * jnp.mean(scaled_normed * unit_rows, axis=-1, keepdims=True)
    )
    grad_residual = (grad_out.astype(jnp.float32) + branch).astype(jnp.bfloat16)
    return (grad_residual, route_grad, grad_in, grad_down)


def solution(mesh):
    finer = Mesh(
        mesh.devices.reshape(2, 2, mesh.shape["ulysses"], mesh.shape["expert"]),
        ("dp_0", "dp_1", "ulysses", "expert"),
    )
    return jax.shard_map(
        per_device,
        mesh=finer,
        in_specs=(
            P(DP_ULYSSES_EXPERT, None),
            P(),
            P(DP_ULYSSES_EXPERT, None),
            P(DP_ULYSSES_EXPERT, None),
            P(DP_ULYSSES_EXPERT, None),
            P("expert", None, None),
            P("expert", None, None),
        ),
        out_specs=(
            P(DP_ULYSSES_EXPERT, None),
            P(DP_ULYSSES_EXPERT, None),
            P("expert", DP_ULYSSES, None),
            P("expert", DP_ULYSSES, None),
        ),
        check_vma=False,
    )
```

time: 264 us -> 252 us (0.955)
  blocking collectives: 81.2 us -> 47 us
  Pallas kernels: 56.1 us -> 74.2 us
  waiting for transfers between devices: 67 us -> 81.2 us
  local copies, waits for them, and re-layouts: 13 us -> 3.6 us
    all_to_all x1, blocking collectives: 81.2 us -> 47 us  [exchange(): lax.all_to_all(rows, ('dp_0', 'expert'), split_axis=0, concat_axis=0, axi...]
    all_to_all x2 -> x3, waiting for transfers between devices: 6.22 us -> 26 us  [exchange(): lax.all_to_all(rows, ('dp_0', 'expert'), split_axis=0, concat_axis=0, axi...]
    pallas_call x3 -> x6, Pallas kernels: 40 us -> 55 us  [the longest x2 21 us: weight_grads(): pl.pallas_call(kernel, grid=(2, rings), in_specs=[left, left, whole, whol...]
    ppermute x1, waiting for transfers between devices: 2.01 us -> 14.3 us  [per_device(): came_in = lax.ppermute(summed_in[:block], 'dp_0', SWAP)]
    reduce_scatter x1, waiting for transfers between devices: 11.5 us -> 2.08 us  [per_device(): lax.psum_scatter(part_down, 'ulysses', scatter_dimension=0, tiled=True)]
    unnamed x32 -> x20, local copies, waits for them, and re-layouts: 8.06 us -> 1.53 us
    ppermute x1, waiting for transfers between devices: 42.1 us -> 35.7 us  [per_device(): came_down = lax.ppermute(far_down, 'dp_0', SWAP)]
    ppermute x2 -> x3, waiting for transfers between devices: 5.19 us -> 0.01 us  [the longest x1 0.01 us: per_device(): came_normed = lax.ppermute(give_normed, 'dp_1', SWAP)]
  transfers between devices with their start and end apart: 9 -> 11, of which waited for: 6 -> 5; matrix products, arithmetic and copies ran while one was open for 7% -> 5% of each run, Pallas kernels for 9% -> 22%
where the time goes in v3:
time: 252 us; the launch traced here: 250 us
  waiting for transfers between devices  81.2 us (32%)
  Pallas kernels  74.2 us (29%)
  blocking collectives  47 us (19%)
  starting transfers between devices  15.5 us (6%)
  between operations  14.2 us (6%)
  other arithmetic  11.4 us (5%)
  local copies, waits for them, and re-layouts  3.6 us (1%)
  matrix products  3.41 us (1%)
    all_to_all x1, blocking collectives, exchange(): lax.all_to_all(rows, ('dp_0', 'expert'), split_axis=0, concat_axis=0, axi...  47 us
    ppermute x1, waiting for transfers between devices, per_device(): came_down = lax.ppermute(far_down, 'dp_0', SWAP)  35.7 us
    all_to_all x3, waiting for transfers between devices, exchange(): lax.all_to_all(rows, ('dp_0', 'expert'), split_axis=0, concat_axis=0, axi...  26 us
    pallas_call x2, Pallas kernels, weight_grads(): pl.pallas_call(kernel, grid=(2, rings), in_specs=[left, left, whole, whol...  21 us
    pallas_call x2, Pallas kernels, turn(): pl.pallas_call(turn_kernel, grid_spec=pltpu.PrefetchScalarGridSpec(num_sc...  14.8 us
    all_to_all x3, starting transfers between devices, exchange(): lax.all_to_all(rows, ('dp_0', 'expert'), split_axis=0, concat_axis=0, axi...  14.5 us
    ppermute x1, waiting for transfers between devices, per_device(): came_in = lax.ppermute(summed_in[:block], 'dp_0', SWAP)  14.3 us
    pallas_call x1, Pallas kernels, slot_rows(): pl.pallas_call(slot_kernel, grid=(width // block,), in_specs=[pl.BlockSpe...  11.7 us
  transfers between devices with their start and end apart: 11, of which 5 were waited for; matrix products, arithmetic and copies ran while one was open for 5% of the time, Pallas kernels for 22%

profile of v3, /device:TPU:0, one launch (start us, length us, event | category | flops | bytes accessed | tf_op | source)
XLA Modules:
  0.0 250.5 jit_solution(17252497575807518808)
XLA Ops:
  7.2 0.6 pad_add_fusion._
  7.8 7.5 %pack.1 = (bf16[8,48,4096]{2,1,0:T(8,128)(2,1)}, bf16[8,48,4096]{2,1,0:T(8,128)(2,1)}, bf16[384,128]{1,0:T(8,128)(2,1)}) custom-call(s32[2,128]{1,0:T(2,128)} %bitcast.34, bf16[2,128]{1,0:T(2,128)(2,1)} %bitcast.36, f32[1,4096]{1,0:T(1,128)} %bitcast.32, bf16[128,4096]{1,0:T(8,128)(2,1)} %resid_ref, bf16[128,4096]{1,0:T(8,128)(2,1)} %grad_ref.1), custom_call_target="tpu_custom_call" | custom-call | flops 805306368 | bytes 6291456 | tf_op jit(solution)/shard_map/pack/pallas_call | solution.py:80
  15.2 47.0 %all_to_all.25.got_ref.keep_ref.give_ref = bf16[8,48,4096]{2,1,0:T(8,128)(2,1)} all-to-all(bf16[8,48,4096]{2,1,0:T(8,128)(2,1)} %get-tuple-element.32), channel_id=1, replica_groups={{0,65,2,67,4,69,6,71},{64,1,66,3,68,5,70,7},{8,73,10,75,12,77,14,79},{7..., dimensions={0} | all-to-all | bytes 6291456 | tf_op jit(solution)/shard_map/all_to_all | solution.py:316
  62.3 4.5 %all-to-all-start.1 = ((bf16[8,48,4096]{2,1,0:T(8,128)(2,1)}), bf16[8,48,4096]{2,1,0:T(8,128)(2,1)}, u32[]{:S(2)}, u32[]{:S(2)}) async-start(bf16[8,48,4096]{2,1,0:T(8,128)(2,1)} %get-tuple-element.37), calls=%async_computation.1 | async-start | bytes 6291456 | tf_op jit(solution)/shard_map/all_to_all | solution.py:316
  66.8 0.0 reduce-scatter.5.cloned.1.call-start
  66.8 7.3 %turn.3 = (bf16[2,4,256,384]{3,2,1,0:T(8,128)(2,1)}, bf16[2,4,256,384]{3,2,1,0:T(8,128)(2,1)}) custom-call(s32[2]{0:T(128)} %pad_add_fusion._, bf16[8,48,4096]{2,1,0:T(8,128)(2,1)} %all_to_all.25.got_ref.keep_ref.give_ref, bf16[8,48,4096]{2,1,0:T(8,128)(2,1)} %all_to_all.25.got_ref.keep_ref.give_ref), custom_call_target="tpu_custom_call" | custom-call | flops 1610612736 | bytes 6291456 | tf_op jit(solution)/shard_map/turn/pallas_call | solution.py:217
  74.1 0.0 collective-permute-start.3
  74.1 10.5 %forward.1 = (bf16[384,768]{1,0:T(8,128)(2,1)}, f32[384,768]{1,0:T(8,128)}, f32[384,768]{1,0:T(8,128)}) custom-call(bf16[8,48,4096]{2,1,0:T(8,128)(2,1)} %all_to_all.25.got_ref.keep_ref.give_ref, bf16[4096,1536]{1,0:T(8,128)(2,1)} %bitcast.25, bf16[4096,1536]{1,0:T(8,128)(2,1)} %bitcast.26), custom_call_target="tpu_custom_call" | custom-call | flops 4831838208 | bytes 15728640 | tf_op jit(solution)/shard_map/forward/pallas_call | solution.py:124
  84.6 26.0 %all-to-all-done.1.got_ref.keep_ref.give_ref = bf16[8,48,4096]{2,1,0:T(8,128)(2,1)} async-done(((bf16[8,48,4096]{2,1,0:T(8,128)(2,1)}), bf16[8,48,4096]{2,1,0:T(8,128)(2,1)}, u32[]{:S(2)}, u32[]{:S(2)}) %all-to-all-start.1) | async-done | bytes 3145760 | tf_op jit(solution)/shard_map/all_to_all | solution.py:316
  110.6 8.7 %back.1 = (bf16[2,384,768]{2,1,0:T(8,128)(2,1)}, bf16[384,128]{1,0:T(8,128)(2,1)}) custom-call(bf16[8,48,4096]{2,1,0:T(8,128)(2,1)} %all-to-all-done.1.got_ref.keep_ref.give_ref, bf16[768,4096]{1,0:T(8,128)(2,1)} %bitcast.29, bf16[384,768]{1,0:T(8,128)(2,1)} %get-tuple-element.41.hidden_ref.mine_ref, f32[384,768]{1,0:T(8,128)} %get-tuple-element.42.gate_ref, ...), custom_call_target="tpu_custom_call" | custom-call | flops 2415919104 | bytes 12386304 | tf_op jit(solution)/shard_map/back/pallas_call | solution.py:172
  119.3 0.0 collective-permute-start.4
  119.3 3.0 %collective-permute-done.4.theirs_ref = bf16[2,384,768]{2,1,0:T(8,128)(2,1)S(1)} collective-permute-done((bf16[2,384,768]{2,1,0:T(8,128)(2,1)}, bf16[2,384,768]{2,1,0:T(8,128)(2,1)S(1)}, u32[]{:S(2)}, u32[]{:S(2)}) %collective-permute-start.4) | collective-permute-done | bytes 1179680 | tf_op jit(solution)/shard_map/ppermute | solution.py:360
  122.3 0.0 collective-permute-done.3.came_ref
  122.3 1.0 copy-done.9
  123.3 0.5 copy-done.8
  123.8 11.8 %shard_map.103 = bf16[4,2,256,1536]{3,2,1,0:T(8,128)(2,1)} custom-call(bf16[2,4,256,384]{3,2,1,0:T(8,128)(2,1)} %get-tuple-element.54.keep_ref, bf16[2,4,256,384]{3,2,1,0:T(8,128)(2,1)} %copy-done.8, bf16[2,384,768]{2,1,0:T(8,128)(2,1)} %get-tuple-element.44.grads_ref.mine_ref, bf16[2,384,768]{2,1,0:T(8,128)(2,1)} %copy-done.9), custom_call_target="tpu_custom_call" | custom-call | flops 4831838208 | bytes 14942208 | tf_op jit(solution)/shard_map/pallas_call | solution.py:268
  135.6 0.0 reduce-scatter.5.cloned.1.call-update
  135.6 7.6 %turn.2 = (bf16[2,4,256,384]{3,2,1,0:T(8,128)(2,1)}, bf16[2,4,256,384]{3,2,1,0:T(8,128)(2,1)}) custom-call(s32[2]{0:T(128)} %pad_add_fusion._, bf16[8,48,4096]{2,1,0:T(8,128)(2,1)} %all-to-all-done.1.got_ref.keep_ref.give_ref, bf16[8,48,4096]{2,1,0:T(8,128)(2,1)} %all-to-all-done.1.got_ref.keep_ref.give_ref), custom_call_target="tpu_custom_call" | custom-call | flops 1610612736 | bytes 6291456 | tf_op jit(solution)/shard_map/turn/pallas_call | solution.py:217
  143.2 0.1 collective-permute-start
  143.3 0.4 collective-permute-start.1
  143.7 0.1 slice_reduce_fusion
  143.8 0.7 all_to_all.20
  144.5 3.3 %all-to-all-start.3 = ((bf16[8,1,48]{2,1,0:T(2,128)(2,1)}), bf16[8,1,48]{2,1,0:T(2,128)(2,1)S(1)}, u32[]{:S(2)}, u32[]{:S(2)}) async-start(bf16[8,1,48]{2,1,0:T(2,128)(2,1)} %all_to_all.20), calls=%async_computation.3 | async-start | bytes 8192 | tf_op jit(solution)/shard_map/all_to_all | solution.py:316
  147.8 11.7 %slot_rows.1 = bf16[8,48,4096]{2,1,0:T(8,128)(2,1)} custom-call(bf16[2,384,768]{2,1,0:T(8,128)(2,1)} %get-tuple-element.44.grads_ref.mine_ref, bf16[4096,1536]{1,0:T(8,128)(2,1)} %bitcast.27), custom_call_target="tpu_custom_call" | custom-call | flops 4831838208 | bytes 15728640 | tf_op jit(solution)/shard_map/slot_rows/pallas_call | solution.py:294
  159.5 0.0 all-to-all-done.3
  159.5 6.8 %all-to-all-start.2 = ((bf16[8,48,4096]{2,1,0:T(8,128)(2,1)}), bf16[8,48,4096]{2,1,0:T(8,128)(2,1)S(1)}, u32[]{:S(2)}, u32[]{:S(2)}) async-start(bf16[8,48,4096]{2,1,0:T(8,128)(2,1)} %slot_rows.1), calls=%async_computation.2 | async-start | bytes 6291456 | tf_op jit(solution)/shard_map/all_to_all | solution.py:316
  166.3 0.0 reduce-scatter.3.cloned.1.call-start
  166.3 0.0 collective-permute-done.1.theirs_ref
  166.4 0.0 collective-permute-done.came_ref
  166.4 0.0 copy-start
  166.4 9.2 %shard_map.102 = (bf16[4,256,768]{2,1,0:T(8,128)(2,1)}, bf16[4,256,768]{2,1,0:T(8,128)(2,1)}) custom-call(bf16[2,4,256,384]{3,2,1,0:T(8,128)(2,1)} %get-tuple-element.50.keep_ref, bf16[2,4,256,384]{3,2,1,0:T(8,128)(2,1)} %collective-permute-done.came_ref, bf16[384,768]{1,0:T(8,128)(2,1)} %get-tuple-element.41.hidden_ref.mine_ref, ...), custom_call_target="tpu_custom_call" | custom-call | flops 2415919104 | bytes 10616832 | tf_op jit(solution)/shard_map/pallas_call | solution.py:268
  175.6 0.0 collective-permute-start.2
  175.6 0.3 fusion.7
  175.9 35.7 %collective-permute-done.2 = bf16[4,256,768]{2,1,0:T(8,128)(2,1)S(1)} collective-permute-done((bf16[4,256,768]{2,1,0:T(8,128)(2,1)}, bf16[4,256,768]{2,1,0:T(8,128)(2,1)S(1)}, u32[]{:S(2)}, u32[]{:S(2)}) %collective-permute-start.2) | collective-permute-done | bytes 1572896 | tf_op jit(solution)/shard_map/ppermute | solution.py:389
  211.7 3.0 %add_convert_fusion = bf16[4,256,768]{2,1,0:T(8,128)(2,1)} fusion(bf16[4,256,768]{2,1,0:T(8,128)(2,1)S(1)} %collective-permute-done.2, bf16[4,256,768]{2,1,0:T(8,128)(2,1)} %get-tuple-element.52), kind=kLoop, calls=%fused_computation.1 | loop fusion | flops 3145728 | bytes 4718592 | tf_op jit(solution)/shard_map/convert_element_type | solution.py:398
  214.6 0.0 reduce-scatter.3.cloned.1.call-update
  214.7 0.1 fusion.9
  214.8 0.0 copy-done.7
  214.8 0.5 fusion.11
  215.4 0.0 all-to-all-done.2
  215.4 3.4 %fusion.2 = (f32[128]{0:T(128)S(1)}, f32[128,4096]{1,0:T(8,128)}) fusion(bf16[128,4096]{1,0:T(8,128)(2,1)} %resid_ref, f32[128]{0:T(128)S(1)} %add_rsqrt_fusion, f32[4096]{0:T(1024)S(1)} %copy-done.5, bf16[384,128]{1,0:T(8,128)(2,1)S(1)} %copy-done.3, bf16[384,4096]{1,0:T(8,128)(2,1)S(1)} %bitcast.28), kind=kOutput, calls=%fused_computation.6 | convolution fusion | flops 405274496 | bytes 6407168 | tf_op jit(solution)/shard_map/dot_general | solution.py:20
  218.8 1.3 slice_bitcast_fusion
  220.1 0.4 collective-permute-start.5
  220.4 3.6 %fusion.6 = bf16[128,4096]{1,0:T(8,128)(2,1)} fusion(f32[128,4096]{1,0:T(8,128)} %get-tuple-element.59, bf16[128,4096]{1,0:T(8,128)(2,1)S(1)} %copy-done.1, bf16[128,4096]{1,0:T(8,128)(2,1)} %grad_ref.1, f32[128]{0:T(128)S(1)} %broadcast_multiply_fusion, f32[128]{0:T(128)S(1)} %add_rsqrt_fusion), kind=kLoop, calls=%fused_computation.10 | loop fusion | flops 4194304 | bytes 5243904 | tf_op jit(solution)/shard_map/convert_element_type | solution.py:421
  224.0 14.3 %collective-permute-done.5 = bf16[256,1536]{1,0:T(8,128)(2,1)S(1)} collective-permute-done((bf16[256,1536]{1,0:T(8,128)(2,1)S(1)}, bf16[256,1536]{1,0:T(8,128)(2,1)S(1)}, u32[]{:S(2)}, u32[]{:S(2)}) %collective-permute-start.5) | collective-permute-done | bytes 786464 | tf_op jit(solution)/shard_map/ppermute | solution.py:396
  238.3 1.4 fusion.8
  239.6 2.1 reduce-scatter.3.cloned.1.call-done
  241.7 1.9 convert_element_type.67
  (21 shorter events, 0.1 us)
Async XLA Ops:
  62.3 48.3 %all-to-all-start.1 = ((bf16[8,48,4096]{2,1,0:T(8,128)(2,1)}), bf16[8,48,4096]{2,1,0:T(8,128)(2,1)}, u32[]{:S(2)}, u32[]{:S(2)}) async-start(bf16[8,48,4096]{2,1,0:T(8,128)(2,1)} %get-tuple-element.37), calls=%async_computation.1 | async-start | bytes 6291456 | tf_op jit(solution)/shard_map/all_to_all | solution.py:316
  66.8 152.0 %reduce-scatter.5.cloned.1.call-start = ((), (), s32[]{:S(2)}) async-start(), calls=%async_computation.7 | async-start | bytes 7864320 | tf_op jit(solution)/shard_map/reduce_scatter | solution.py:390
  74.1 48.2 %collective-permute-start.3 = (bf16[2,4,256,384]{3,2,1,0:T(8,128)(2,1)}, bf16[2,4,256,384]{3,2,1,0:T(8,128)(2,1)S(1)}, u32[]{:S(2)}, u32[]{:S(2)}) collective-permute-start(bf16[2,4,256,384]{3,2,1,0:T(8,128)(2,1)} %get-tuple-element.55), channel_id=1, source_target_pairs={{0,32},{32,0},{1,33},{33,1},{2,34},{34,2},{3,35},{35,3},{4,36},{36... | collective-permute-start | bytes 4718600 | tf_op jit(solution)/shard_map/ppermute | solution.py:356
  119.3 3.1 %collective-permute-start.4 = (bf16[2,384,768]{2,1,0:T(8,128)(2,1)}, bf16[2,384,768]{2,1,0:T(8,128)(2,1)S(1)}, u32[]{:S(2)}, u32[]{:S(2)}) collective-permute-start(bf16[2,384,768]{2,1,0:T(8,128)(2,1)} %get-tuple-element.44.grads_ref.mine_ref), channel_id=1, source_target_pairs={{0,32},{32,0},{1,33},{33,1},{2,34},{34,2},{3,35},{35,3},{4,36},{36... | collective-permute-start | bytes 3538952 | tf_op jit(solution)/shard_map/ppermute | solution.py:360
  122.3 1.0 copy-start.9
  122.3 1.5 copy-start.8
  135.6 8.1 %copy-start.4 = (bf16[384,128]{1,0:T(8,128)(2,1)S(1)}, bf16[384,128]{1,0:T(8,128)(2,1)}, u32[]{:S(2)}) copy-start(bf16[384,128]{1,0:T(8,128)(2,1)} %get-tuple-element.47) | copy-start | bytes 294916
  143.2 23.2 %collective-permute-start = (bf16[2,4,256,384]{3,2,1,0:T(8,128)(2,1)}, bf16[2,4,256,384]{3,2,1,0:T(8,128)(2,1)}, u32[]{:S(2)}, u32[]{:S(2)}) collective-permute-start(bf16[2,4,256,384]{3,2,1,0:T(8,128)(2,1)} %get-tuple-element.51), channel_id=1, source_target_pairs={{0,32},{32,0},{1,33},{33,1},{2,34},{34,2},{3,35},{35,3},{4,36},{36... | collective-permute-start | bytes 4718600 | tf_op jit(solution)/shard_map/ppermute | solution.py:371
  143.3 23.0 %collective-permute-start.1 = (bf16[384,768]{1,0:T(8,128)(2,1)}, bf16[384,768]{1,0:T(8,128)(2,1)}, u32[]{:S(2)}, u32[]{:S(2)}) collective-permute-start(bf16[384,768]{1,0:T(8,128)(2,1)} %get-tuple-element.41.hidden_ref.mine_ref), channel_id=1, source_target_pairs={{0,32},{32,0},{1,33},{33,1},{2,34},{34,2},{3,35},{35,3},{4,36},{36... | collective-permute-start | bytes 1769480 | tf_op jit(solution)/shard_map/ppermute | solution.py:358
  144.5 15.0 %all-to-all-start.3 = ((bf16[8,1,48]{2,1,0:T(2,128)(2,1)}), bf16[8,1,48]{2,1,0:T(2,128)(2,1)S(1)}, u32[]{:S(2)}, u32[]{:S(2)}) async-start(bf16[8,1,48]{2,1,0:T(2,128)(2,1)} %all_to_all.20), calls=%async_computation.3 | async-start | bytes 8192 | tf_op jit(solution)/shard_map/all_to_all | solution.py:316
  159.5 55.9 %all-to-all-start.2 = ((bf16[8,48,4096]{2,1,0:T(8,128)(2,1)}), bf16[8,48,4096]{2,1,0:T(8,128)(2,1)S(1)}, u32[]{:S(2)}, u32[]{:S(2)}) async-start(bf16[8,48,4096]{2,1,0:T(8,128)(2,1)} %slot_rows.1), calls=%async_computation.2 | async-start | bytes 6291456 | tf_op jit(solution)/shard_map/all_to_all | solution.py:316
  166.3 75.4 %reduce-scatter.3.cloned.1.call-start = ((), (), s32[]{:S(2)}) async-start(), calls=%async_computation.6 | async-start | bytes 1966080 | tf_op jit(solution)/shard_map/reduce_scatter | solution.py:399
  166.4 9.2 %copy-start = (bf16[128,4096]{1,0:T(8,128)(2,1)S(1)}, bf16[128,4096]{1,0:T(8,128)(2,1)}, u32[]{:S(2)}) copy-start(bf16[128,4096]{1,0:T(8,128)(2,1)} %resid_ref) | copy-start | bytes 3145732
  175.6 36.0 %collective-permute-start.2 = (bf16[4,256,768]{2,1,0:T(8,128)(2,1)}, bf16[4,256,768]{2,1,0:T(8,128)(2,1)S(1)}, u32[]{:S(2)}, u32[]{:S(2)}) collective-permute-start(bf16[4,256,768]{2,1,0:T(8,128)(2,1)} %get-tuple-element.53), channel_id=1, source_target_pairs={{0,64},{64,0},{1,65},{65,1},{2,66},{66,2},{3,67},{67,3},{4,68},{68... | collective-permute-start | bytes 4718600 | tf_op jit(solution)/shard_map/ppermute | solution.py:389
  211.7 3.0 %copy-start.3 = (bf16[384,128]{1,0:T(8,128)(2,1)S(1)}, bf16[384,128]{1,0:T(8,128)(2,1)}, u32[]{:S(2)}) copy-start(bf16[384,128]{1,0:T(8,128)(2,1)} %get-tuple-element.36) | copy-start | bytes 294916
  211.7 3.1 %copy-start.6 = (s32[128,2]{0,1:T(2,128)S(1)}, s32[128,2]{0,1:T(2,128)}, u32[]{:S(2)}) copy-start(s32[128,2]{0,1:T(2,128)} %param.10) | copy-start | bytes 3076
  211.7 3.2 %copy-start.7 = (bf16[128,2]{0,1:T(2,128)(2,1)S(1)}, bf16[128,2]{0,1:T(2,128)(2,1)}, u32[]{:S(2)}) copy-start(bf16[128,2]{0,1:T(2,128)(2,1)} %param.11) | copy-start | bytes 1540
  211.7 3.7 %copy-start.5 = (f32[4096]{0:T(1024)S(1)}, f32[4096]{0:T(1024)}, u32[]{:S(2)}) copy-start(f32[4096]{0:T(1024)} %param.8) | copy-start | bytes 49156
  218.8 1.6 copy-start.1
  220.1 18.2 %collective-permute-start.5 = (bf16[256,1536]{1,0:T(8,128)(2,1)S(1)}, bf16[256,1536]{1,0:T(8,128)(2,1)S(1)}, u32[]{:S(2)}, u32[]{:S(2)}) collective-permute-start(bf16[256,1536]{1,0:T(8,128)(2,1)S(1)} %slice_bitcast_fusion), channel_id=1, source_target_pairs={{0,64},{64,0},{1,65},{65,1},{2,66},{66,2},{3,67},{67,3},{4,68},{68... | collective-permute-start | bytes 2359304 | tf_op jit(solution)/shard_map/ppermute | solution.py:396
  220.4 17.8 %copy-start.2 = (bf16[1,512,1536]{2,1,0:T(8,128)(2,1)S(1)}, bf16[1,512,1536]{2,1,0:T(8,128)(2,1)}, u32[]{:S(2)}) copy-start(bf16[1,512,1536]{2,1,0:T(8,128)(2,1)} %reduce-scatter.5.cloned.1.call-done) | copy-start | bytes 4718596
Sparse Core Ops, SparseCore 0:
  135.7 60.4 reduce-scatter.4
  214.8 26.8 reduce-scatter.2

commit v4 on v3

--- a/solution.py
+++ b/solution.py
@@ -72,7 +72,7 @@
     scaled_ref[...] = sent.reshape(experts, capacity, block)
 
 
-def pack(ids_t, w_t, gain, resid, grad, experts, capacity, block=512):
+def pack(ids_t, w_t, gain, resid, grad, experts, capacity, block=1024):
     rows, width = resid.shape
     whole = lambda a: pl.BlockSpec(a.shape, lambda j: (0,) * a.ndim)
     args = (ids_t, w_t, gain, resid, grad)
@@ -200,31 +200,34 @@
 
 def turn_kernel(_, keep_ref, give_ref, keep_out, give_out):
     parts, capacity, block = keep_ref.shape
-    keep_out[0, 0] = keep_ref[...].reshape(parts * capacity, block).T
-    give_out[0, 0] = give_ref[...].reshape(parts * capacity, block).T
-
-
-def turn(place, got, rings):
+    keep_out[0] = keep_ref[...].reshape(parts * capacity, block).T.reshape(keep_out.shape[1:])
+    give_out[0] = give_ref[...].reshape(parts * capacity, block).T.reshape(give_out.shape[1:])
+
+
+def turn(place, got, rings, span):
     parts, capacity, width = got.shape
     slots = parts * capacity
     block = width // (4 * rings)
+    steps = rings // span
 
     def column(half, ring, place_ref, core):
         side = jnp.where(half == 0, 1 - place_ref[0], place_ref[0])
-        return (0, 0, (side * 2 + core) * rings + ring)
-
-    out = pl.BlockSpec((1, 1, block, slots), lambda half, ring, _: (half, ring, 0, 0))
+        return (0, 0, (side * 2 + core) * steps + ring)
+
+    out = pl.BlockSpec((1, span, block, slots), lambda half, ring, _: (half, ring, 0, 0))
     return pl.pallas_call(
         turn_kernel,
         grid_spec=pltpu.PrefetchScalarGridSpec(
             num_scalar_prefetch=1,
-            grid=(2, rings),
+            grid=(2, steps),
             in_specs=[
                 pl.BlockSpec(
-                    (parts, capacity, block), lambda half, ring, at: column(half, ring, at, at[1])
+                    (parts, capacity, span * block),
+                    lambda half, ring, at: column(half, ring, at, at[1]),
                 ),
                 pl.BlockSpec(
-                    (parts, capacity, block), lambda half, ring, at: column(half, ring, at, 1 - at[1])
+                    (parts, capacity, span * block),
+                    lambda half, ring, at: column(half, ring, at, 1 - at[1]),
                 ),
             ],
             out_specs=[out, out],
@@ -238,39 +241,56 @@
     )(place, got, got)
 
 
-def grad_in_kernel(keep_ref, came_ref, mine_ref, theirs_ref, out_ref):
-    keep, came = keep_ref[0, 0], came_ref[0, 0]
-    width = mine_ref.shape[2]
-    for u in range(2):
-        rows = contract(keep, mine_ref[u], 1, 0) + contract(came, theirs_ref[u], 1, 0)
-        out_ref[0, 0, :, u * width : (u + 1) * width] = rows.astype(jnp.bfloat16)
-
-
-def grad_down_kernel(keep_ref, came_ref, mine_ref, theirs_ref, far_out, near_out):
-    rows = contract(keep_ref[0, 0], mine_ref[...], 1, 0) + contract(
-        came_ref[0, 0], theirs_ref[...], 1, 0
-    )
-    rows = rows.astype(jnp.bfloat16)
+def both_cores(keep_ref, came_ref):
+    span, block, slots = keep_ref.shape[1:]
+    both = (keep_ref[0].reshape(span * block, slots), came_ref[0].reshape(span * block, slots))
+    return jnp.concatenate(both, axis=1)
+
+
+def grad_in_kernel(keep_ref, came_ref, mine_ref, theirs_ref, out_ref, right_ref):
+    span, _, block, _ = out_ref.shape
+    _, slots, width = mine_ref.shape
+
+    @pl.when((pl.program_id(0) == 0) & (pl.program_id(1) == 0))
+    def _():
+        for u in range(2):
+            right_ref[:slots, u * width : (u + 1) * width] = mine_ref[u]
+            right_ref[slots:, u * width : (u + 1) * width] = theirs_ref[u]
+
+    rows = contract(both_cores(keep_ref, came_ref), right_ref[...], 1, 0).astype(jnp.bfloat16)
+    out_ref[:, 0] = rows.reshape(span, block, 2 * width)
+
+
+def grad_down_kernel(keep_ref, came_ref, mine_ref, theirs_ref, far_out, near_out, right_ref):
+    slots = mine_ref.shape[0]
+
+    @pl.when((pl.program_id(0) == 0) & (pl.program_id(1) == 0))
+    def _():
+        right_ref[:slots] = mine_ref[...]
+        right_ref[slots:] = theirs_ref[...]
+
+    rows = contract(both_cores(keep_ref, came_ref), right_ref[...], 1, 0).astype(jnp.bfloat16)
 
     @pl.when(pl.program_id(0) == 0)
     def _():
-        far_out[0] = rows
+        far_out[...] = rows.reshape(far_out.shape)
 
     @pl.when(pl.program_id(0) == 1)
     def _():
-        near_out[0] = rows
-
-
-def weight_grads(kernel, keep, came, mine, theirs, out_specs, out_shape):
+        near_out[...] = rows.reshape(near_out.shape)
+
+
+def weight_grads(kernel, keep, came, mine, theirs, span, out_specs, out_shape):
     _, rings, block, slots = keep.shape
-    left = pl.BlockSpec((1, 1, block, slots), lambda half, ring: (half, ring, 0, 0))
+    left = pl.BlockSpec((1, span, block, slots), lambda half, ring: (half, ring, 0, 0))
     whole = pl.BlockSpec(mine.shape, lambda half, ring: (0,) * mine.ndim)
     return pl.pallas_call(
         kernel,
-        grid=(2, rings),
+        grid=(2, rings // span),
         in_specs=[left, left, whole, whole],
         out_specs=out_specs,
         out_shape=out_shape,
+        scratch_shapes=[pltpu.VMEM((2 * slots, mine.size // slots), jnp.bfloat16)],
         compiler_params=pltpu.CompilerParams(vmem_limit_bytes=58 * 2**20),
         cost_estimate=pl.CostEstimate(
             flops=8 * rings * block * mine.size,
@@ -288,7 +308,7 @@
     out_ref[...] = rows.astype(jnp.bfloat16).reshape(out_ref.shape)
 
 
-def slot_rows(grads, w_in, parts, block=512):
+def slot_rows(grads, w_in, parts, block=1024):
     _, slots, hidden_width = grads.shape
     width = w_in.shape[0]
     return pl.pallas_call(
@@ -332,6 +352,7 @@
     slot_total = experts * capacity
     rings = lax.axis_size("ulysses")
     block = width // (4 * rings)
+    span = 2 if rings % 2 == 0 else 1
     side = lax.axis_index("dp_0")
     core = lax.axis_index("dp_1")
     ids_t = expert_ids.T
@@ -352,7 +373,7 @@
     got_scaled = exchange(send_scaled)
     w_in = weight_in[0]
     w_down = weight_down[0]
-    keep_normed, give_normed = turn(place, got_normed, rings)
+    keep_normed, give_normed = turn(place, got_normed, rings, span)
     came_normed = lax.ppermute(give_normed, "dp_1", SWAP)
     hidden, gate, up = forward(got_normed, w_in)
     their_hidden = lax.ppermute(hidden, "dp_1", SWAP)
@@ -364,10 +385,11 @@
         came_normed,
         mine,
         theirs,
-        pl.BlockSpec((1, 1, block, 2 * hidden_width), lambda half, ring: (ring, half, 0, 0)),
+        span,
+        pl.BlockSpec((span, 1, block, 2 * hidden_width), lambda half, ring: (ring, half, 0, 0)),
         jax.ShapeDtypeStruct((rings, 2, block, 2 * hidden_width), jnp.bfloat16),
     )
-    keep_scaled, give_scaled = turn(place, got_scaled, rings)
+    keep_scaled, give_scaled = turn(place, got_scaled, rings, span)
     came_scaled = lax.ppermute(give_scaled, "dp_1", SWAP)
     far_down, near_down = weight_grads(
         grad_down_kernel,
@@ -375,13 +397,15 @@
         came_scaled,
         hidden,
         their_hidden,
+        span,
         [
             pl.BlockSpec(
-                (1, block, hidden_width),
-                lambda half, ring: (jnp.where(half == 0, ring, rings - 1), 0, 0),
+                (span, block, hidden_width),
+                lambda half, ring: (jnp.where(half == 0, ring, rings // span - 1), 0, 0),
             ),
             pl.BlockSpec(
-                (1, block, hidden_width), lambda half, ring: (jnp.where(half == 0, 0, ring), 0, 0)
+                (span, block, hidden_width),
+                lambda half, ring: (jnp.where(half == 0, 0, ring), 0, 0),
             ),
         ],
         [jax.ShapeDtypeStruct((rings, block, hidden_width), jnp.bfloat16)] * 2,
@@ -400,7 +424,9 @@
     summed_down, grad_in = lax.optimization_barrier((summed_down, grad_in))
     grad_down = summed_down.astype(jnp.float32)
 
-    back_normed = exchange(slot_rows(mine, w_in, experts))
+    mine, route, far_down = lax.optimization_barrier((mine, route, far_down))
+    slot_normed = slot_rows(mine, w_in, experts)
+    back_normed = exchange(slot_normed)
     back_route = exchange(route[:, 0].reshape(experts, capacity))
     resid = residual.astype(jnp.float32)
     inv_rms = lax.rsqrt(jnp.mean(resid * resid, axis=-1, keepdims=True) + eps)

time: 252 us -> 250 us (level)
  Pallas kernels: 74.2 us -> 61.3 us
  waiting for transfers between devices: 81.2 us -> 89.8 us
    all_to_all x3, waiting for transfers between devices: 26 us -> 33.7 us  [exchange(): lax.all_to_all(rows, ('dp_0', 'expert'), split_axis=0, concat_axis=0, axi...]
    pallas_call x2, Pallas kernels: 21 us -> 15.9 us  [weight_grads(): pl.pallas_call(kernel, grid=(2, rings // span), in_specs=[left, left, who...]
    pallas_call x2, Pallas kernels: 14.8 us -> 10.2 us  [turn(): pl.pallas_call(turn_kernel, grid_spec=pltpu.PrefetchScalarGridSpec(num_sc...]
    ppermute x1, waiting for transfers between devices: 0.01 us -> 3.95 us  [per_device(): their_hidden = lax.ppermute(hidden, 'dp_1', SWAP)]
  transfers between devices with their start and end apart: 11 -> 11, of which waited for: 5 -> 6; matrix products, arithmetic and copies ran while one was open for 5% -> 6% of each run, Pallas kernels for 22% -> 19%
where the time goes in v4:
time: 250 us; the launch traced here: 249 us
  waiting for transfers between devices  89.8 us (36%)
  Pallas kernels  61.3 us (25%)
  blocking collectives  47 us (19%)
  starting transfers between devices  15.4 us (6%)
  between operations  14.2 us (6%)
  other arithmetic  12.7 us (5%)
  local copies, waits for them, and re-layouts  5.09 us (2%)
  matrix products  3.42 us (1%)
    all_to_all x1, blocking collectives, exchange(): lax.all_to_all(rows, ('dp_0', 'expert'), split_axis=0, concat_axis=0, axi...  47 us
    ppermute x1, waiting for transfers between devices, per_device(): came_down = lax.ppermute(far_down, 'dp_0', SWAP)  34.4 us
    all_to_all x3, waiting for transfers between devices, exchange(): lax.all_to_all(rows, ('dp_0', 'expert'), split_axis=0, concat_axis=0, axi...  33.7 us
    pallas_call x2, Pallas kernels, weight_grads(): pl.pallas_call(kernel, grid=(2, rings // span), in_specs=[left, left, who...  15.9 us
    ppermute x1, waiting for transfers between devices, per_device(): came_in = lax.ppermute(summed_in[:block], 'dp_0', SWAP)  14.6 us
    all_to_all x3, starting transfers between devices, exchange(): lax.all_to_all(rows, ('dp_0', 'expert'), split_axis=0, concat_axis=0, axi...  14.6 us
    pallas_call x1, Pallas kernels, forward(): pl.pallas_call(forward_kernel, grid=(steps,), in_specs=[pl.BlockSpec(got....  10.5 us
    pallas_call x2, Pallas kernels, turn(): pl.pallas_call(turn_kernel, grid_spec=pltpu.PrefetchScalarGridSpec(num_sc...  10.2 us
  transfers between devices with their start and end apart: 11, of which 6 were waited for; matrix products, arithmetic and copies ran while one was open for 6% of the time, Pallas kernels for 19%

profile of v4, /device:TPU:0, one launch (start us, length us, event | category | flops | bytes accessed | tf_op | source)
XLA Modules:
  0.0 248.9 jit_solution(17028798689366215985)
XLA Ops:
  7.2 0.6 pad_add_fusion._
  7.8 6.0 %pack.1 = (bf16[8,48,4096]{2,1,0:T(8,128)(2,1)}, bf16[8,48,4096]{2,1,0:T(8,128)(2,1)}, bf16[384,128]{1,0:T(8,128)(2,1)}) custom-call(s32[2,128]{1,0:T(2,128)} %bitcast.34, bf16[2,128]{1,0:T(2,128)(2,1)} %bitcast.36, f32[1,4096]{1,0:T(1,128)} %bitcast.32, bf16[128,4096]{1,0:T(8,128)(2,1)} %resid_ref, bf16[128,4096]{1,0:T(8,128)(2,1)} %grad_ref.1), custom_call_target="tpu_custom_call" | custom-call | flops 805306368 | bytes 6291456 | tf_op jit(solution)/shard_map/pack/pallas_call | solution.py:80
  13.7 47.0 %all_to_all.25.got_ref.keep_ref.give_ref = bf16[8,48,4096]{2,1,0:T(8,128)(2,1)} all-to-all(bf16[8,48,4096]{2,1,0:T(8,128)(2,1)} %get-tuple-element.34), channel_id=1, replica_groups={{0,65,2,67,4,69,6,71},{64,1,66,3,68,5,70,7},{8,73,10,75,12,77,14,79},{7..., dimensions={0} | all-to-all | bytes 6291456 | tf_op jit(solution)/shard_map/all_to_all | solution.py:336
  60.8 4.5 %all-to-all-start.1 = ((bf16[8,48,4096]{2,1,0:T(8,128)(2,1)}), bf16[8,48,4096]{2,1,0:T(8,128)(2,1)}, u32[]{:S(2)}, u32[]{:S(2)}) async-start(bf16[8,48,4096]{2,1,0:T(8,128)(2,1)} %get-tuple-element.39), calls=%async_computation.1 | async-start | bytes 6291456 | tf_op jit(solution)/shard_map/all_to_all | solution.py:336
  65.2 0.0 reduce-scatter.5.cloned.1.call-start
  65.3 5.1 %turn.3 = (bf16[2,4,256,384]{3,2,1,0:T(8,128)(2,1)}, bf16[2,4,256,384]{3,2,1,0:T(8,128)(2,1)}) custom-call(s32[2]{0:T(128)} %pad_add_fusion._, bf16[8,48,4096]{2,1,0:T(8,128)(2,1)} %all_to_all.25.got_ref.keep_ref.give_ref, bf16[8,48,4096]{2,1,0:T(8,128)(2,1)} %all_to_all.25.got_ref.keep_ref.give_ref), custom_call_target="tpu_custom_call" | custom-call | flops 1610612736 | bytes 6291456 | tf_op jit(solution)/shard_map/turn/pallas_call | solution.py:218
  70.3 0.0 collective-permute-start.3
  70.3 10.5 %forward.1 = (bf16[384,768]{1,0:T(8,128)(2,1)}, f32[384,768]{1,0:T(8,128)}, f32[384,768]{1,0:T(8,128)}) custom-call(bf16[8,48,4096]{2,1,0:T(8,128)(2,1)} %all_to_all.25.got_ref.keep_ref.give_ref, bf16[4096,1536]{1,0:T(8,128)(2,1)} %bitcast.25, bf16[4096,1536]{1,0:T(8,128)(2,1)} %bitcast.26), custom_call_target="tpu_custom_call" | custom-call | flops 4831838208 | bytes 15728640 | tf_op jit(solution)/shard_map/forward/pallas_call | solution.py:124
  80.8 28.2 %all-to-all-done.1.got_ref.keep_ref.give_ref = bf16[8,48,4096]{2,1,0:T(8,128)(2,1)} async-done(((bf16[8,48,4096]{2,1,0:T(8,128)(2,1)}), bf16[8,48,4096]{2,1,0:T(8,128)(2,1)}, u32[]{:S(2)}, u32[]{:S(2)}) %all-to-all-start.1) | async-done | bytes 3145760 | tf_op jit(solution)/shard_map/all_to_all | solution.py:336
  109.0 8.7 %back.1 = (bf16[2,384,768]{2,1,0:T(8,128)(2,1)}, bf16[384,128]{1,0:T(8,128)(2,1)}) custom-call(bf16[8,48,4096]{2,1,0:T(8,128)(2,1)} %all-to-all-done.1.got_ref.keep_ref.give_ref, bf16[768,4096]{1,0:T(8,128)(2,1)} %bitcast.29, bf16[384,768]{1,0:T(8,128)(2,1)} %get-tuple-element.43.hidden_ref.mine_ref, f32[384,768]{1,0:T(8,128)} %get-tuple-element.44.gate_ref, ...), custom_call_target="tpu_custom_call" | custom-call | flops 2415919104 | bytes 12386304 | tf_op jit(solution)/shard_map/back/pallas_call | solution.py:172
  117.7 0.0 collective-permute-start.4
  117.7 3.0 %collective-permute-done.4.theirs_ref = bf16[2,384,768]{2,1,0:T(8,128)(2,1)S(1)} collective-permute-done((bf16[2,384,768]{2,1,0:T(8,128)(2,1)}, bf16[2,384,768]{2,1,0:T(8,128)(2,1)S(1)}, u32[]{:S(2)}, u32[]{:S(2)}) %collective-permute-start.4) | collective-permute-done | bytes 1179680 | tf_op jit(solution)/shard_map/ppermute | solution.py:381
  120.8 0.0 collective-permute-done.3.came_ref
  120.8 1.0 copy-done.10
  121.8 0.5 copy-done.8
  122.3 9.1 %shard_map.103 = bf16[4,2,256,1536]{3,2,1,0:T(8,128)(2,1)} custom-call(bf16[2,4,256,384]{3,2,1,0:T(8,128)(2,1)} %get-tuple-element.58.keep_ref, bf16[2,4,256,384]{3,2,1,0:T(8,128)(2,1)} %copy-done.8, bf16[2,384,768]{2,1,0:T(8,128)(2,1)} %get-tuple-element.52.grads_ref.mine_ref, bf16[2,384,768]{2,1,0:T(8,128)(2,1)} %copy-done.10), custom_call_target="tpu_custom_call" | custom-call | flops 4831838208 | bytes 14942208 | tf_op jit(solution)/shard_map/pallas_call | solution.py:287
  131.4 0.0 reduce-scatter.5.cloned.1.call-update
  131.4 0.0 copy-start.2
  131.4 5.2 %turn.2 = (bf16[2,4,256,384]{3,2,1,0:T(8,128)(2,1)}, bf16[2,4,256,384]{3,2,1,0:T(8,128)(2,1)}) custom-call(s32[2]{0:T(128)} %pad_add_fusion._, bf16[8,48,4096]{2,1,0:T(8,128)(2,1)} %all-to-all-done.1.got_ref.keep_ref.give_ref, bf16[8,48,4096]{2,1,0:T(8,128)(2,1)} %all-to-all-done.1.got_ref.keep_ref.give_ref), custom_call_target="tpu_custom_call" | custom-call | flops 1610612736 | bytes 6291456 | tf_op jit(solution)/shard_map/turn/pallas_call | solution.py:218
  136.6 0.1 collective-permute-start
  136.7 0.4 collective-permute-start.1
  137.1 4.0 %collective-permute-done.1.theirs_ref = bf16[384,768]{1,0:T(8,128)(2,1)S(1)} collective-permute-done((bf16[384,768]{1,0:T(8,128)(2,1)S(1)}, bf16[384,768]{1,0:T(8,128)(2,1)S(1)}, u32[]{:S(2)}, u32[]{:S(2)}) %collective-permute-start.1) | collective-permute-done | bytes 589856 | tf_op jit(solution)/shard_map/ppermute | solution.py:379
  141.1 0.0 collective-permute-done.came_ref
  141.1 0.8 copy-done.11
  141.9 0.5 copy-done.9
  142.4 6.8 %shard_map.102 = (bf16[4,256,768]{2,1,0:T(8,128)(2,1)}, bf16[4,256,768]{2,1,0:T(8,128)(2,1)}) custom-call(bf16[2,4,256,384]{3,2,1,0:T(8,128)(2,1)} %get-tuple-element.49.keep_ref, bf16[2,4,256,384]{3,2,1,0:T(8,128)(2,1)} %copy-done.9, bf16[384,768]{1,0:T(8,128)(2,1)} %get-tuple-element.43.hidden_ref.mine_ref, bf16[384,768]{1,0:T(8,128)(2,1)} %copy-done.11), custom_call_target="tpu_custom_call" | custom-call | flops 2415919104 | bytes 10616832 | tf_op jit(solution)/shard_map/pallas_call | solution.py:287
  149.2 0.1 slice_reduce_fusion
  149.3 0.7 all_to_all.20
  150.0 3.3 %all-to-all-start.3 = ((bf16[8,1,48]{2,1,0:T(2,128)(2,1)}), bf16[8,1,48]{2,1,0:T(2,128)(2,1)S(1)}, u32[]{:S(2)}, u32[]{:S(2)}) async-start(bf16[8,1,48]{2,1,0:T(2,128)(2,1)} %all_to_all.20), calls=%async_computation.3 | async-start | bytes 8192 | tf_op jit(solution)/shard_map/all_to_all | solution.py:336
  153.3 10.0 %slot_rows.1 = bf16[8,48,4096]{2,1,0:T(8,128)(2,1)} custom-call(bf16[2,384,768]{2,1,0:T(8,128)(2,1)} %get-tuple-element.52.grads_ref.mine_ref, bf16[4096,1536]{1,0:T(8,128)(2,1)} %bitcast.27), custom_call_target="tpu_custom_call" | custom-call | flops 4831838208 | bytes 15728640 | tf_op jit(solution)/shard_map/slot_rows/pallas_call | solution.py:314
  163.3 6.8 %all-to-all-start.2 = ((bf16[8,48,4096]{2,1,0:T(8,128)(2,1)}), bf16[8,48,4096]{2,1,0:T(8,128)(2,1)S(1)}, u32[]{:S(2)}, u32[]{:S(2)}) async-start(bf16[8,48,4096]{2,1,0:T(8,128)(2,1)} %slot_rows.1), calls=%async_computation.2 | async-start | bytes 6291456 | tf_op jit(solution)/shard_map/all_to_all | solution.py:336
  170.2 0.0 reduce-scatter.3.cloned.1.call-start
  170.2 0.1 collective-permute-start.2
  170.3 1.5 fusion.7
  171.9 34.4 %collective-permute-done.2 = bf16[4,256,768]{2,1,0:T(8,128)(2,1)S(1)} collective-permute-done((bf16[4,256,768]{2,1,0:T(8,128)(2,1)}, bf16[4,256,768]{2,1,0:T(8,128)(2,1)S(1)}, u32[]{:S(2)}, u32[]{:S(2)}) %collective-permute-start.2) | collective-permute-done | bytes 1572896 | tf_op jit(solution)/shard_map/ppermute | solution.py:413
  206.3 3.0 %add_convert_fusion = bf16[4,256,768]{2,1,0:T(8,128)(2,1)} fusion(bf16[4,256,768]{2,1,0:T(8,128)(2,1)S(1)} %collective-permute-done.2, bf16[4,256,768]{2,1,0:T(8,128)(2,1)} %get-tuple-element.57), kind=kLoop, calls=%fused_computation.1 | loop fusion | flops 3145728 | bytes 4718592 | tf_op jit(solution)/shard_map/convert_element_type | solution.py:422
  209.4 0.0 reduce-scatter.3.cloned.1.call-update
  209.4 0.1 fusion.9
  209.6 0.5 fusion.11
  210.1 5.5 %all-to-all-done.2 = bf16[8,48,4096]{2,1,0:T(8,128)(2,1)S(1)} async-done(((bf16[8,48,4096]{2,1,0:T(8,128)(2,1)}), bf16[8,48,4096]{2,1,0:T(8,128)(2,1)S(1)}, u32[]{:S(2)}, u32[]{:S(2)}) %all-to-all-start.2) | async-done | bytes 3145760 | tf_op jit(solution)/shard_map/all_to_all | solution.py:336
  215.6 3.4 %fusion.2 = (f32[128]{0:T(128)S(1)}, f32[128,4096]{1,0:T(8,128)}) fusion(bf16[128,4096]{1,0:T(8,128)(2,1)} %resid_ref, f32[128]{0:T(128)S(1)} %add_rsqrt_fusion, f32[4096]{0:T(1024)S(1)} %copy-done.5, bf16[384,128]{1,0:T(8,128)(2,1)S(1)} %copy-done.3, bf16[384,4096]{1,0:T(8,128)(2,1)S(1)} %bitcast.28), kind=kOutput, calls=%fused_computation.6 | convolution fusion | flops 405274496 | bytes 6407168 | tf_op jit(solution)/shard_map/dot_general | solution.py:20
  219.0 1.3 slice_bitcast_fusion
  220.3 0.1 collective-permute-start.5
  220.4 0.1 copy-done
  220.5 3.6 %fusion.6 = bf16[128,4096]{1,0:T(8,128)(2,1)} fusion(f32[128,4096]{1,0:T(8,128)} %get-tuple-element.63, bf16[128,4096]{1,0:T(8,128)(2,1)S(1)} %copy-done, bf16[128,4096]{1,0:T(8,128)(2,1)} %grad_ref.1, f32[128]{0:T(128)S(1)} %broadcast_multiply_fusion, f32[128]{0:T(128)S(1)} %add_rsqrt_fusion), kind=kLoop, calls=%fused_computation.10 | loop fusion | flops 4194304 | bytes 5243904 | tf_op jit(solution)/shard_map/convert_element_type | solution.py:447
  224.1 14.6 %collective-permute-done.5 = bf16[256,1536]{1,0:T(8,128)(2,1)S(1)} collective-permute-done((bf16[256,1536]{1,0:T(8,128)(2,1)S(1)}, bf16[256,1536]{1,0:T(8,128)(2,1)S(1)}, u32[]{:S(2)}, u32[]{:S(2)}) %collective-permute-start.5) | collective-permute-done | bytes 786464 | tf_op jit(solution)/shard_map/ppermute | solution.py:420
  238.7 1.4 fusion.8
  240.1 1.9 convert_element_type.67
  (25 shorter events, 0.1 us)
Async XLA Ops:
  60.8 48.3 %all-to-all-start.1 = ((bf16[8,48,4096]{2,1,0:T(8,128)(2,1)}), bf16[8,48,4096]{2,1,0:T(8,128)(2,1)}, u32[]{:S(2)}, u32[]{:S(2)}) async-start(bf16[8,48,4096]{2,1,0:T(8,128)(2,1)} %get-tuple-element.39), calls=%async_computation.1 | async-start | bytes 6291456 | tf_op jit(solution)/shard_map/all_to_all | solution.py:336
  65.2 153.8 %reduce-scatter.5.cloned.1.call-start = ((), (), s32[]{:S(2)}) async-start(), calls=%async_computation.7 | async-start | bytes 7864320 | tf_op jit(solution)/shard_map/reduce_scatter | solution.py:414
  70.3 50.4 %collective-permute-start.3 = (bf16[2,4,256,384]{3,2,1,0:T(8,128)(2,1)}, bf16[2,4,256,384]{3,2,1,0:T(8,128)(2,1)S(1)}, u32[]{:S(2)}, u32[]{:S(2)}) collective-permute-start(bf16[2,4,256,384]{3,2,1,0:T(8,128)(2,1)} %get-tuple-element.59), channel_id=1, source_target_pairs={{0,32},{32,0},{1,33},{33,1},{2,34},{34,2},{3,35},{35,3},{4,36},{36... | collective-permute-start | bytes 4718600 | tf_op jit(solution)/shard_map/ppermute | solution.py:377
  117.7 3.1 %collective-permute-start.4 = (bf16[2,384,768]{2,1,0:T(8,128)(2,1)}, bf16[2,384,768]{2,1,0:T(8,128)(2,1)S(1)}, u32[]{:S(2)}, u32[]{:S(2)}) collective-permute-start(bf16[2,384,768]{2,1,0:T(8,128)(2,1)} %get-tuple-element.52.grads_ref.mine_ref), channel_id=1, source_target_pairs={{0,32},{32,0},{1,33},{33,1},{2,34},{34,2},{3,35},{35,3},{4,36},{36... | collective-permute-start | bytes 3538952 | tf_op jit(solution)/shard_map/ppermute | solution.py:381
  120.8 1.0 copy-start.10
  120.8 1.5 copy-start.8
  131.4 5.3 %copy-start.2 = (bf16[384,768]{1,0:T(8,128)(2,1)S(1)}, bf16[384,768]{1,0:T(8,128)(2,1)}, u32[]{:S(2)}) copy-start(bf16[384,768]{1,0:T(8,128)(2,1)} %get-tuple-element.43.hidden_ref.mine_ref) | copy-start | bytes 1769476
  136.6 4.5 %collective-permute-start = (bf16[2,4,256,384]{3,2,1,0:T(8,128)(2,1)}, bf16[2,4,256,384]{3,2,1,0:T(8,128)(2,1)S(1)}, u32[]{:S(2)}, u32[]{:S(2)}) collective-permute-start(bf16[2,4,256,384]{3,2,1,0:T(8,128)(2,1)} %get-tuple-element.50), channel_id=1, source_target_pairs={{0,32},{32,0},{1,33},{33,1},{2,34},{34,2},{3,35},{35,3},{4,36},{36... | collective-permute-start | bytes 4718600 | tf_op jit(solution)/shard_map/ppermute | solution.py:393
  136.7 4.3 %collective-permute-start.1 = (bf16[384,768]{1,0:T(8,128)(2,1)S(1)}, bf16[384,768]{1,0:T(8,128)(2,1)S(1)}, u32[]{:S(2)}, u32[]{:S(2)}) collective-permute-start(bf16[384,768]{1,0:T(8,128)(2,1)S(1)} %copy-done.2), channel_id=1, source_target_pairs={{0,32},{32,0},{1,33},{33,1},{2,34},{34,2},{3,35},{35,3},{4,36},{36... | collective-permute-start | bytes 1769480 | tf_op jit(solution)/shard_map/ppermute | solution.py:379
  141.1 0.8 copy-start.11
  141.1 1.3 copy-start.9
  142.4 6.8 %copy-start.4 = (bf16[384,128]{1,0:T(8,128)(2,1)S(1)}, bf16[384,128]{1,0:T(8,128)(2,1)}, u32[]{:S(2)}) copy-start(bf16[384,128]{1,0:T(8,128)(2,1)} %get-tuple-element.55) | copy-start | bytes 294916
  150.0 13.3 %all-to-all-start.3 = ((bf16[8,1,48]{2,1,0:T(2,128)(2,1)}), bf16[8,1,48]{2,1,0:T(2,128)(2,1)S(1)}, u32[]{:S(2)}, u32[]{:S(2)}) async-start(bf16[8,1,48]{2,1,0:T(2,128)(2,1)} %all_to_all.20), calls=%async_computation.3 | async-start | bytes 8192 | tf_op jit(solution)/shard_map/all_to_all | solution.py:336
  163.3 52.2 %all-to-all-start.2 = ((bf16[8,48,4096]{2,1,0:T(8,128)(2,1)}), bf16[8,48,4096]{2,1,0:T(8,128)(2,1)S(1)}, u32[]{:S(2)}, u32[]{:S(2)}) async-start(bf16[8,48,4096]{2,1,0:T(8,128)(2,1)} %slot_rows.1), calls=%async_computation.2 | async-start | bytes 6291456 | tf_op jit(solution)/shard_map/all_to_all | solution.py:336
  170.2 69.9 %reduce-scatter.3.cloned.1.call-start = ((), (), s32[]{:S(2)}) async-start(), calls=%async_computation.6 | async-start | bytes 1966080 | tf_op jit(solution)/shard_map/reduce_scatter | solution.py:423
  170.2 36.1 %collective-permute-start.2 = (bf16[4,256,768]{2,1,0:T(8,128)(2,1)}, bf16[4,256,768]{2,1,0:T(8,128)(2,1)S(1)}, u32[]{:S(2)}, u32[]{:S(2)}) collective-permute-start(bf16[4,256,768]{2,1,0:T(8,128)(2,1)} %get-tuple-element.51), channel_id=1, source_target_pairs={{0,64},{64,0},{1,65},{65,1},{2,66},{66,2},{3,67},{67,3},{4,68},{68... | collective-permute-start | bytes 4718600 | tf_op jit(solution)/shard_map/ppermute | solution.py:413
  206.3 3.1 %copy-start.3 = (bf16[384,128]{1,0:T(8,128)(2,1)S(1)}, bf16[384,128]{1,0:T(8,128)(2,1)}, u32[]{:S(2)}) copy-start(bf16[384,128]{1,0:T(8,128)(2,1)} %get-tuple-element.38) | copy-start | bytes 294916
  206.3 3.2 %copy-start.6 = (s32[128,2]{0,1:T(2,128)S(1)}, s32[128,2]{0,1:T(2,128)}, u32[]{:S(2)}) copy-start(s32[128,2]{0,1:T(2,128)} %param.10) | copy-start | bytes 3076
  206.3 3.2 %copy-start.7 = (bf16[128,2]{0,1:T(2,128)(2,1)S(1)}, bf16[128,2]{0,1:T(2,128)(2,1)}, u32[]{:S(2)}) copy-start(bf16[128,2]{0,1:T(2,128)(2,1)} %param.11) | copy-start | bytes 1540
  206.3 9.3 %copy-start.5 = (f32[4096]{0:T(1024)S(1)}, f32[4096]{0:T(1024)}, u32[]{:S(2)}) copy-start(f32[4096]{0:T(1024)} %param.8) | copy-start | bytes 49156
  219.0 1.5 copy-start
  220.3 18.4 %collective-permute-start.5 = (bf16[256,1536]{1,0:T(8,128)(2,1)S(1)}, bf16[256,1536]{1,0:T(8,128)(2,1)S(1)}, u32[]{:S(2)}, u32[]{:S(2)}) collective-permute-start(bf16[256,1536]{1,0:T(8,128)(2,1)S(1)} %slice_bitcast_fusion), channel_id=1, source_target_pairs={{0,64},{64,0},{1,65},{65,1},{2,66},{66,2},{3,67},{67,3},{4,68},{68... | collective-permute-start | bytes 2359304 | tf_op jit(solution)/shard_map/ppermute | solution.py:420
  220.5 18.2 %copy-start.1 = (bf16[1,512,1536]{2,1,0:T(8,128)(2,1)S(1)}, bf16[1,512,1536]{2,1,0:T(8,128)(2,1)}, u32[]{:S(2)}) copy-start(bf16[1,512,1536]{2,1,0:T(8,128)(2,1)} %reduce-scatter.5.cloned.1.call-done) | copy-start | bytes 4718596
Sparse Core Ops, SparseCore 0:
  131.5 60.4 reduce-scatter.4
  209.5 26.7 reduce-scatter.2

commit v5 on v4

--- a/solution.py
+++ b/solution.py
@@ -5,6 +5,7 @@
 from jax.experimental.pallas import tpu as pltpu
 from jax.sharding import Mesh
 from jax.sharding import PartitionSpec as P
+
 
 DP_ULYSSES = ("dp_0", "dp_1", "ulysses")
 DP_ULYSSES_EXPERT = ("dp_0", "dp_1", "ulysses", "expert")
@@ -241,63 +242,39 @@
     )(place, got, got)
 
 
-def both_cores(keep_ref, came_ref):
-    span, block, slots = keep_ref.shape[1:]
-    both = (keep_ref[0].reshape(span * block, slots), came_ref[0].reshape(span * block, slots))
-    return jnp.concatenate(both, axis=1)
-
-
-def grad_in_kernel(keep_ref, came_ref, mine_ref, theirs_ref, out_ref, right_ref):
-    span, _, block, _ = out_ref.shape
-    _, slots, width = mine_ref.shape
-
-    @pl.when((pl.program_id(0) == 0) & (pl.program_id(1) == 0))
-    def _():
-        for u in range(2):
-            right_ref[:slots, u * width : (u + 1) * width] = mine_ref[u]
-            right_ref[slots:, u * width : (u + 1) * width] = theirs_ref[u]
-
-    rows = contract(both_cores(keep_ref, came_ref), right_ref[...], 1, 0).astype(jnp.bfloat16)
-    out_ref[:, 0] = rows.reshape(span, block, 2 * width)
-
-
-def grad_down_kernel(keep_ref, came_ref, mine_ref, theirs_ref, far_out, near_out, right_ref):
-    slots = mine_ref.shape[0]
-
-    @pl.when((pl.program_id(0) == 0) & (pl.program_id(1) == 0))
-    def _():
-        right_ref[:slots] = mine_ref[...]
-        right_ref[slots:] = theirs_ref[...]
-
-    rows = contract(both_cores(keep_ref, came_ref), right_ref[...], 1, 0).astype(jnp.bfloat16)
-
-    @pl.when(pl.program_id(0) == 0)
-    def _():
-        far_out[...] = rows.reshape(far_out.shape)
-
-    @pl.when(pl.program_id(0) == 1)
-    def _():
-        near_out[...] = rows.reshape(near_out.shape)
-
-
-def weight_grads(kernel, keep, came, mine, theirs, span, out_specs, out_shape):
+def rows_kernel(_, keep_ref, came_ref, mine_ref, theirs_ref, far_ref, near_ref):
+    block, slots = keep_ref.shape[2:]
+    keep, came = keep_ref[...].reshape(2 * block, slots), came_ref[...].reshape(2 * block, slots)
+    rows = contract(keep, mine_ref[0], 1, 0) + contract(came, theirs_ref[0], 1, 0)
+    rows = rows.astype(jnp.bfloat16)
+    far_ref[0] = rows[:block]
+    near_ref[0] = rows[block:]
+
+
+def weight_rows(place, keep, came, mine, theirs, first, count):
     _, rings, block, slots = keep.shape
-    left = pl.BlockSpec((1, span, block, slots), lambda half, ring: (half, ring, 0, 0))
-    whole = pl.BlockSpec(mine.shape, lambda half, ring: (0,) * mine.ndim)
-    return pl.pallas_call(
-        kernel,
-        grid=(2, rings // span),
-        in_specs=[left, left, whole, whole],
-        out_specs=out_specs,
-        out_shape=out_shape,
-        scratch_shapes=[pltpu.VMEM((2 * slots, mine.size // slots), jnp.bfloat16)],
-        compiler_params=pltpu.CompilerParams(vmem_limit_bytes=58 * 2**20),
-        cost_estimate=pl.CostEstimate(
-            flops=8 * rings * block * mine.size,
-            bytes_accessed=8 * keep.size + 4 * mine.size + 4 * rings * block * mine.size // slots,
+    units, _, width = mine.shape
+    left = pl.BlockSpec(
+        (2, 1, block, slots), lambda i, u, at: (0, lax.rem(at[2] + (first + i), rings), 0, 0)
+    )
+    right = pl.BlockSpec((1, slots, width), lambda i, u, at: (u, 0, 0))
+    out = pl.BlockSpec((1, block, width), lambda i, u, at: (i, 0, u))
+    return pl.pallas_call(
+        rows_kernel,
+        grid_spec=pltpu.PrefetchScalarGridSpec(
+            num_scalar_prefetch=1,
+            grid=(count, units),
+            in_specs=[left, left, right, right],
+            out_specs=[out, out],
+        ),
+        out_shape=[jax.ShapeDtypeStruct((count, block, units * width), jnp.bfloat16)] * 2,
+        compiler_params=pltpu.CompilerParams(vmem_limit_bytes=VMEM),
+        cost_estimate=pl.CostEstimate(
+            flops=8 * count * block * mine.size,
+            bytes_accessed=4 * mine.size + 4 * count * block * (2 * slots + units * width),
             transcendentals=0,
         ),
-    )(keep, came, mine, theirs)
+    )(place, keep, came, mine, theirs)
 
 
 def slot_kernel(grads_ref, w_ref, out_ref):
@@ -328,6 +305,26 @@
         ),
         name="slot_rows",
     )(grads, w_in)
+
+
+def added(*terms):
+    return sum(t.astype(jnp.float32) for t in terms)
+
+
+def ring_sum(low, high):
+    size = lax.axis_size("ulysses")
+    ahead = [(i, (i + 1) % size) for i in range(size)]
+    behind = [(i, (i - 1) % size) for i in range(size)]
+    low_two = lax.ppermute(low[2], "ulysses", ahead)
+    high_two = lax.ppermute(high[2], "ulysses", behind)
+    high_side = lax.ppermute(high[1], "ulysses", ahead)
+    low_side = lax.ppermute(low[3], "ulysses", behind)
+    low_both = added(low[1], low_two).astype(jnp.bfloat16)
+    high_both = added(high[3], high_two).astype(jnp.bfloat16)
+    low_last = lax.ppermute(low_both, "ulysses", ahead)
+    high_last = lax.ppermute(high_both, "ulysses", behind)
+    sums = added(low[0], low_last, low_side), added(high[0], high_last, high_side)
+    return sums, low_both, high_both
 
 
 def exchange(rows):
@@ -346,7 +343,6 @@
 def per_device(residual, norm_gain, grad_out, expert_ids, route_weights, weight_in, weight_down):
     tok_rows, width = residual.shape
     topk = expert_ids.shape[1]
-    hidden_width = weight_down.shape[1]
     experts = lax.axis_size("expert")
     capacity = min(tok_rows, 3 * tok_rows * topk // (2 * experts))
     slot_total = experts * capacity
@@ -358,7 +354,7 @@
     ids_t = expert_ids.T
     weights_t = route_weights.T
     place, residual = lax.optimization_barrier(
-        (jnp.stack([side, core]).astype(jnp.int32), residual)
+        (jnp.stack([side, core, lax.axis_index("ulysses")]).astype(jnp.int32), residual)
     )
 
     send_normed, send_scaled, select = pack(
@@ -377,54 +373,38 @@
     came_normed = lax.ppermute(give_normed, "dp_1", SWAP)
     hidden, gate, up = forward(got_normed, w_in)
     their_hidden = lax.ppermute(hidden, "dp_1", SWAP)
+    keep_scaled, give_scaled = turn(place, got_scaled, rings, span)
+    came_scaled = lax.ppermute(give_scaled, "dp_1", SWAP)
+    got_scaled, keep_scaled = lax.optimization_barrier((got_scaled, keep_scaled))
     mine, route = back(got_scaled, w_down, hidden, gate, up)
     theirs = lax.ppermute(mine, "dp_1", SWAP)
-    part_in = weight_grads(
-        grad_in_kernel,
-        keep_normed,
-        came_normed,
-        mine,
-        theirs,
-        span,
-        pl.BlockSpec((span, 1, block, 2 * hidden_width), lambda half, ring: (ring, half, 0, 0)),
-        jax.ShapeDtypeStruct((rings, 2, block, 2 * hidden_width), jnp.bfloat16),
-    )
-    keep_scaled, give_scaled = turn(place, got_scaled, rings, span)
-    came_scaled = lax.ppermute(give_scaled, "dp_1", SWAP)
-    far_down, near_down = weight_grads(
-        grad_down_kernel,
-        keep_scaled,
-        came_scaled,
-        hidden,
-        their_hidden,
-        span,
-        [
-            pl.BlockSpec(
-                (span, block, hidden_width),
-                lambda half, ring: (jnp.where(half == 0, ring, rings // span - 1), 0, 0),
-            ),
-            pl.BlockSpec(
-                (span, block, hidden_width),
-                lambda half, ring: (jnp.where(half == 0, 0, ring), 0, 0),
-            ),
-        ],
-        [jax.ShapeDtypeStruct((rings, block, hidden_width), jnp.bfloat16)] * 2,
+    keep_scaled, mine, route = lax.optimization_barrier((keep_scaled, mine, route))
+    far_down, near_down = weight_rows(
+        place, keep_scaled, came_scaled, hidden[None], their_hidden[None], 0, rings
     )
     came_down = lax.ppermute(far_down, "dp_0", SWAP)
-    summed_in = lax.psum_scatter(
-        part_in.reshape(rings, 2 * block, 2 * hidden_width),
-        "ulysses",
-        scatter_dimension=0,
-        tiled=True,
-    )[0]
-    came_in = lax.ppermute(summed_in[:block], "dp_0", SWAP)
-    grad_in = (summed_in[block:].astype(jnp.float32) + came_in.astype(jnp.float32))[None]
-    part_down = (near_down.astype(jnp.float32) + came_down.astype(jnp.float32)).astype(jnp.bfloat16)
-    summed_down = lax.psum_scatter(part_down, "ulysses", scatter_dimension=0, tiled=True)
-    summed_down, grad_in = lax.optimization_barrier((summed_down, grad_in))
-    grad_down = summed_down.astype(jnp.float32)
-
-    mine, route, far_down = lax.optimization_barrier((mine, route, far_down))
+
+    far, near = {}, {}
+
+    def in_rows(ring, after):
+        nonlocal keep_normed
+        keep_normed, _ = lax.optimization_barrier((keep_normed, after))
+        far[ring], near[ring] = weight_rows(place, keep_normed, came_normed, mine, theirs, ring, 1)
+
+    in_rows(2, near_down)
+    in_rows(1, near[2])
+    in_rows(3, near[1])
+    in_rows(0, near[3])
+    (far_in, near_in), far_both, near_both = ring_sum(far, near)
+    came_in = lax.ppermute(far_in.astype(jnp.bfloat16), "dp_0", SWAP)
+    came_down, _, _ = lax.optimization_barrier((came_down, far_both, near_both))
+    part_down = added(near_down, came_down).astype(jnp.bfloat16)
+    upper = {r: part_down[r, : block // 2] for r in range(rings)}
+    lower = {r: part_down[r, block // 2 :] for r in range(rings)}
+    halves_down, _, _ = ring_sum(upper, lower)
+    grad_down = jnp.concatenate(halves_down, axis=0)[None]
+
+    mine, route, _ = lax.optimization_barrier((mine, route, near[3]))
     slot_normed = slot_rows(mine, w_in, experts)
     back_normed = exchange(slot_normed)
     back_route = exchange(route[:, 0].reshape(experts, capacity))
@@ -445,6 +425,8 @@
         scaled_normed - unit_rows * jnp.mean(scaled_normed * unit_rows, axis=-1, keepdims=True)
     )
     grad_residual = (grad_out.astype(jnp.float32) + branch).astype(jnp.bfloat16)
+    came_in, _ = lax.optimization_barrier((came_in, grad_residual))
+    grad_in = near_in + came_in.astype(jnp.float32)
     return (grad_residual, route_grad, grad_in, grad_down)
 
 

time: 250 us -> 257 us (1.028)
  starting transfers between devices: 15.4 us -> 33 us
  between operations: 14.2 us -> 0.89 us
  Pallas kernels: 61.3 us -> 72.9 us
  waiting for transfers between devices: 89.8 us -> 79.7 us
  other arithmetic: 12.7 us -> 16.8 us
    ppermute x1, waiting for transfers between devices: 34.4 us -> 0.01 us  [per_device(): came_down = lax.ppermute(far_down, 'dp_0', SWAP)]
    ppermute x1 -> x13, starting transfers between devices: 0.09 us -> 19.4 us  [the longest x2 6.99 us: ring_sum(): high_last = lax.ppermute(high_both, 'ulysses', behind)]
    ppermute x1 -> x13, waiting for transfers between devices: 14.6 us -> 31.8 us  [the longest x2 15.1 us: ring_sum(): low_last = lax.ppermute(low_both, 'ulysses', ahead)]
    all_to_all x3, waiting for transfers between devices: 33.7 us -> 45.9 us  [exchange(): lax.all_to_all(rows, ('dp_0', 'expert'), split_axis=0, concat_axis=0, axi...]
    pallas_call x2 -> x5, Pallas kernels: 15.9 us -> 27.9 us  [weight_rows(): pl.pallas_call(rows_kernel, grid_spec=pltpu.PrefetchScalarGridSpec(num_sc...]
    add x0 -> x3, other arithmetic: none -> 3.31 us  [the longest x1 3.12 us: per_device(): grad_in = near_in + came_in.astype(jnp.float32)]
    convert_element_type x2 -> x5, other arithmetic: 4.97 us -> 8.14 us  [the longest x1 2.52 us: ring_sum(): high_both = added(high[3], high_two).astype(jnp.bfloat16)]
    ppermute x1, waiting for transfers between devices: 3.05 us -> 0.01 us  [per_device(): theirs = lax.ppermute(mine, 'dp_1', SWAP)]
  transfers between devices with their start and end apart: 11 -> 21, of which waited for: 6 -> 7; matrix products, arithmetic and copies ran while one was open for 6% -> 6% of each run, Pallas kernels for 19% -> 22%
where the time goes in v5:
time: 257 us; the launch traced here: 256 us
  waiting for transfers between devices  79.7 us (31%)
  Pallas kernels  72.9 us (28%)
  blocking collectives  47 us (18%)
  starting transfers between devices  33 us (13%)
  other arithmetic  16.8 us (7%)
  local copies, waits for them, and re-layouts  3.01 us (1%)
    all_to_all x1, blocking collectives, exchange(): lax.all_to_all(rows, ('dp_0', 'expert'), split_axis=0, concat_axis=0, axi...  47 us
    all_to_all x3, waiting for transfers between devices, exchange(): lax.all_to_all(rows, ('dp_0', 'expert'), split_axis=0, concat_axis=0, axi...  45.9 us
    pallas_call x5, Pallas kernels, weight_rows(): pl.pallas_call(rows_kernel, grid_spec=pltpu.PrefetchScalarGridSpec(num_sc...  27.9 us
    ppermute x2, waiting for transfers between devices, ring_sum(): low_last = lax.ppermute(low_both, 'ulysses', ahead)  15.1 us
    all_to_all x3, starting transfers between devices, exchange(): lax.all_to_all(rows, ('dp_0', 'expert'), split_axis=0, concat_axis=0, axi...  12.5 us
    ppermute x2, waiting for transfers between devices, ring_sum(): high_side = lax.ppermute(high[1], 'ulysses', ahead)  12.3 us
    pallas_call x1, Pallas kernels, forward(): pl.pallas_call(forward_kernel, grid=(steps,), in_specs=[pl.BlockSpec(got....  10.4 us
    pallas_call x2, Pallas kernels, turn(): pl.pallas_call(turn_kernel, grid_spec=pltpu.PrefetchScalarGridSpec(num_sc...  10.2 us
  transfers between devices with their start and end apart: 21, of which 7 were waited for; matrix products, arithmetic and copies ran while one was open for 6% of the time, Pallas kernels for 22%

profile of v5, /device:TPU:0, one launch (start us, length us, event | category | flops | bytes accessed | tf_op | source)
XLA Modules:
  0.0 255.7 jit_solution(3866906533422201582)
XLA Ops:
  0.6 0.6 pad_add_fusion._
  1.2 6.0 %pack.1 = (bf16[8,48,4096]{2,1,0:T(8,128)(2,1)}, bf16[8,48,4096]{2,1,0:T(8,128)(2,1)}, bf16[384,128]{1,0:T(8,128)(2,1)}) custom-call(s32[2,128]{1,0:T(2,128)} %bitcast.57, bf16[2,128]{1,0:T(2,128)(2,1)} %bitcast.59, f32[1,4096]{1,0:T(1,128)} %bitcast.55, bf16[128,4096]{1,0:T(8,128)(2,1)} %resid_ref, bf16[128,4096]{1,0:T(8,128)(2,1)} %grad_ref.1), custom_call_target="tpu_custom_call" | custom-call | flops 805306368 | bytes 6291456 | tf_op jit(solution)/shard_map/pack/pallas_call | solution.py:81
  7.2 47.0 %all_to_all.25.got_ref.keep_ref.give_ref = bf16[8,48,4096]{2,1,0:T(8,128)(2,1)} all-to-all(bf16[8,48,4096]{2,1,0:T(8,128)(2,1)} %get-tuple-element.51), channel_id=1, replica_groups={{0,65,2,67,4,69,6,71},{64,1,66,3,68,5,70,7},{8,73,10,75,12,77,14,79},{7..., dimensions={0} | all-to-all | bytes 6291456 | tf_op jit(solution)/shard_map/all_to_all | solution.py:333
  54.3 4.4 %all-to-all-start.1 = ((bf16[8,48,4096]{2,1,0:T(8,128)(2,1)}), bf16[8,48,4096]{2,1,0:T(8,128)(2,1)}, u32[]{:S(2)}, u32[]{:S(2)}) async-start(bf16[8,48,4096]{2,1,0:T(8,128)(2,1)} %get-tuple-element.56), calls=%async_computation.1 | async-start | bytes 6291456 | tf_op jit(solution)/shard_map/all_to_all | solution.py:333
  58.7 43.8 %all-to-all-done.1.keep_ref.give_ref.got_ref = bf16[8,48,4096]{2,1,0:T(8,128)(2,1)} async-done(((bf16[8,48,4096]{2,1,0:T(8,128)(2,1)}), bf16[8,48,4096]{2,1,0:T(8,128)(2,1)}, u32[]{:S(2)}, u32[]{:S(2)}) %all-to-all-start.1) | async-done | bytes 3145760 | tf_op jit(solution)/shard_map/all_to_all | solution.py:333
  102.5 5.1 %turn.2 = (bf16[2,4,256,384]{3,2,1,0:T(8,128)(2,1)}, bf16[2,4,256,384]{3,2,1,0:T(8,128)(2,1)}) custom-call(s32[3]{0:T(128)} %pad_add_fusion._, bf16[8,48,4096]{2,1,0:T(8,128)(2,1)} %all-to-all-done.1.keep_ref.give_ref.got_ref, bf16[8,48,4096]{2,1,0:T(8,128)(2,1)} %all-to-all-done.1.keep_ref.give_ref.got_ref), custom_call_target="tpu_custom_call" | custom-call | flops 1610612736 | bytes 6291456 | tf_op jit(solution)/shard_map/turn/pallas_call | solution.py:219
  107.6 5.1 %turn.3 = (bf16[2,4,256,384]{3,2,1,0:T(8,128)(2,1)}, bf16[2,4,256,384]{3,2,1,0:T(8,128)(2,1)}) custom-call(s32[3]{0:T(128)} %pad_add_fusion._, bf16[8,48,4096]{2,1,0:T(8,128)(2,1)} %all_to_all.25.got_ref.keep_ref.give_ref, bf16[8,48,4096]{2,1,0:T(8,128)(2,1)} %all_to_all.25.got_ref.keep_ref.give_ref), custom_call_target="tpu_custom_call" | custom-call | flops 1610612736 | bytes 6291456 | tf_op jit(solution)/shard_map/turn/pallas_call | solution.py:219
  112.7 0.5 collective-permute-start.2
  113.2 10.4 %forward.1 = (bf16[384,768]{1,0:T(8,128)(2,1)}, f32[384,768]{1,0:T(8,128)}, f32[384,768]{1,0:T(8,128)}) custom-call(bf16[8,48,4096]{2,1,0:T(8,128)(2,1)} %all_to_all.25.got_ref.keep_ref.give_ref, bf16[4096,1536]{1,0:T(8,128)(2,1)} %bitcast.48, bf16[4096,1536]{1,0:T(8,128)(2,1)} %bitcast.49), custom_call_target="tpu_custom_call" | custom-call | flops 4831838208 | bytes 15728640 | tf_op jit(solution)/shard_map/forward/pallas_call | solution.py:125
  123.7 8.7 %back.1 = (bf16[2,384,768]{2,1,0:T(8,128)(2,1)}, bf16[384,128]{1,0:T(8,128)(2,1)}) custom-call(bf16[8,48,4096]{2,1,0:T(8,128)(2,1)} %all-to-all-done.1.keep_ref.give_ref.got_ref, bf16[768,4096]{1,0:T(8,128)(2,1)} %bitcast.52, bf16[384,768]{1,0:T(8,128)(2,1)} %get-tuple-element.64.hidden_ref, f32[384,768]{1,0:T(8,128)} %get-tuple-element.65.gate_ref, ...), custom_call_target="tpu_custom_call" | custom-call | flops 2415919104 | bytes 12386304 | tf_op jit(solution)/shard_map/back/pallas_call | solution.py:173
  132.4 0.5 collective-permute-start.1
  132.9 1.5 fusion.7
  134.4 2.0 collective-permute-done.1
  136.4 7.5 %shard_map.102 = (bf16[4,256,768]{2,1,0:T(8,128)(2,1)}, bf16[4,256,768]{2,1,0:T(8,128)(2,1)}) custom-call(s32[3]{0:T(128)} %pad_add_fusion._, bf16[2,4,256,384]{3,2,1,0:T(8,128)(2,1)} %get-tuple-element.72.keep_ref, bf16[2,4,256,384]{3,2,1,0:T(8,128)(2,1)} %collective-permute-done.came_ref, bf16[1,384,768]{2,1,0:T(8,128)(2,1)} %bitcast.53, ...), custom_call_target="tpu_custom_call" | custom-call | flops 2415919104 | bytes 7471104 | tf_op jit(solution)/shard_map/pallas_call | solution.py:262
  144.0 1.2 copy-done
  145.2 5.1 %shard_map.103 = (bf16[1,256,1536]{2,1,0:T(8,128)(2,1)}, bf16[1,256,1536]{2,1,0:T(8,128)(2,1)}) custom-call(s32[3]{0:T(128)} %pad_add_fusion._, bf16[2,4,256,384]{3,2,1,0:T(8,128)(2,1)} %get-tuple-element.87.keep_ref, bf16[2,4,256,384]{3,2,1,0:T(8,128)(2,1)} %copy-done, bf16[2,384,768]{2,1,0:T(8,128)(2,1)} %get-tuple-element.82.mine_ref.grads_ref, ...), custom_call_target="tpu_custom_call" | custom-call | flops 1207959552 | bytes 4718592 | tf_op jit(solution)/shard_map/pallas_call | solution.py:262
  150.3 3.0 %collective-permute-start.4 = (bf16[1,256,1536]{2,1,0:T(8,128)(2,1)}, bf16[1,256,1536]{2,1,0:T(8,128)(2,1)}, u32[]{:S(2)}, u32[]{:S(2)}) collective-permute-start(bf16[1,256,1536]{2,1,0:T(8,128)(2,1)} %get-tuple-element.77), channel_id=1, source_target_pairs={{0,24},{8,0},{16,8},{24,16},{1,25},{9,1},{17,9},{25,17},{2,26},{10... | collective-permute-start | bytes 2359304 | tf_op jit(solution)/shard_map/ppermute | solution.py:319
  153.3 5.1 %shard_map.104 = (bf16[1,256,1536]{2,1,0:T(8,128)(2,1)}, bf16[1,256,1536]{2,1,0:T(8,128)(2,1)}) custom-call(s32[3]{0:T(128)} %pad_add_fusion._, bf16[2,4,256,384]{3,2,1,0:T(8,128)(2,1)} %get-tuple-element.87.keep_ref, bf16[2,4,256,384]{3,2,1,0:T(8,128)(2,1)} %copy-done, bf16[2,384,768]{2,1,0:T(8,128)(2,1)} %get-tuple-element.82.mine_ref.grads_ref, ...), custom_call_target="tpu_custom_call" | custom-call | flops 1207959552 | bytes 4718592 | tf_op jit(solution)/shard_map/pallas_call | solution.py:262
  158.5 5.0 %shard_map.105 = (bf16[1,256,1536]{2,1,0:T(8,128)(2,1)}, bf16[1,256,1536]{2,1,0:T(8,128)(2,1)}) custom-call(s32[3]{0:T(128)} %pad_add_fusion._, bf16[2,4,256,384]{3,2,1,0:T(8,128)(2,1)} %get-tuple-element.87.keep_ref, bf16[2,4,256,384]{3,2,1,0:T(8,128)(2,1)} %copy-done, bf16[2,384,768]{2,1,0:T(8,128)(2,1)} %get-tuple-element.82.mine_ref.grads_ref, ...), custom_call_target="tpu_custom_call" | custom-call | flops 1207959552 | bytes 4718592 | tf_op jit(solution)/shard_map/pallas_call | solution.py:262
  163.5 9.8 %slot_rows.1 = bf16[8,48,4096]{2,1,0:T(8,128)(2,1)} custom-call(bf16[2,384,768]{2,1,0:T(8,128)(2,1)} %get-tuple-element.82.mine_ref.grads_ref, bf16[4096,1536]{1,0:T(8,128)(2,1)} %bitcast.50), custom_call_target="tpu_custom_call" | custom-call | flops 4831838208 | bytes 15728640 | tf_op jit(solution)/shard_map/slot_rows/pallas_call | solution.py:291
  173.3 3.1 %collective-permute-start.9 = (bf16[1,256,1536]{2,1,0:T(8,128)(2,1)}, bf16[1,256,1536]{2,1,0:T(8,128)(2,1)}, u32[]{:S(2)}, u32[]{:S(2)}) collective-permute-start(bf16[1,256,1536]{2,1,0:T(8,128)(2,1)} %get-tuple-element.92), channel_id=1, source_target_pairs={{0,24},{8,0},{16,8},{24,16},{1,25},{9,1},{17,9},{25,17},{2,26},{10... | collective-permute-start | bytes 2359304 | tf_op jit(solution)/shard_map/ppermute | solution.py:321
  176.6 0.7 all_to_all.20
  177.2 3.3 %all-to-all-start.3 = ((bf16[8,1,48]{2,1,0:T(2,128)(2,1)}), bf16[8,1,48]{2,1,0:T(2,128)(2,1)S(1)}, u32[]{:S(2)}, u32[]{:S(2)}) async-start(bf16[8,1,48]{2,1,0:T(2,128)(2,1)} %all_to_all.20), calls=%async_computation.3 | async-start | bytes 8192 | tf_op jit(solution)/shard_map/all_to_all | solution.py:333
  180.6 5.1 %shard_map.106 = (bf16[1,256,1536]{2,1,0:T(8,128)(2,1)}, bf16[1,256,1536]{2,1,0:T(8,128)(2,1)}) custom-call(s32[3]{0:T(128)} %pad_add_fusion._, bf16[2,4,256,384]{3,2,1,0:T(8,128)(2,1)} %get-tuple-element.87.keep_ref, bf16[2,4,256,384]{3,2,1,0:T(8,128)(2,1)} %copy-done, bf16[2,384,768]{2,1,0:T(8,128)(2,1)} %get-tuple-element.82.mine_ref.grads_ref, ...), custom_call_target="tpu_custom_call" | custom-call | flops 1207959552 | bytes 4718592 | tf_op jit(solution)/shard_map/pallas_call | solution.py:262
  185.7 2.1 all-to-all-done.3
  187.7 4.8 %all-to-all-start.2 = ((bf16[8,48,4096]{2,1,0:T(8,128)(2,1)}), bf16[8,48,4096]{2,1,0:T(8,128)(2,1)S(1)}, u32[]{:S(2)}, u32[]{:S(2)}) async-start(bf16[8,48,4096]{2,1,0:T(8,128)(2,1)} %slot_rows.1), calls=%async_computation.2 | async-start | bytes 6291456 | tf_op jit(solution)/shard_map/all_to_all | solution.py:333
  192.5 2.5 add_convert_fusion.3
  195.1 1.4 add_convert_fusion.2
  196.5 0.2 copy-done.2
  196.7 1.8 add_convert_fusion
  198.7 0.7 copy-done.7
  199.4 0.1 fusion.12
  199.7 3.3 %collective-permute-start.14 = (bf16[128,768]{1,0:T(8,128)(2,1)S(1)}, bf16[128,768]{1,0:T(8,128)(2,1)S(1)}, u32[]{:S(2)}, u32[]{:S(2)}) collective-permute-start(bf16[128,768]{1,0:T(8,128)(2,1)S(1)} %get-tuple-element.101), channel_id=1, source_target_pairs={{0,24},{8,0},{16,8},{24,16},{1,25},{9,1},{17,9},{25,17},{2,26},{10... | collective-permute-start | bytes 589832 | tf_op jit(solution)/shard_map/ppermute | solution.py:321
  202.9 1.3 collective-permute-start.15
  204.3 3.4 %collective-permute-done.12 = bf16[128,768]{1,0:T(8,128)(2,1)S(1)} collective-permute-done((bf16[128,768]{1,0:T(8,128)(2,1)S(1)}, bf16[128,768]{1,0:T(8,128)(2,1)S(1)}, u32[]{:S(2)}, u32[]{:S(2)}) %collective-permute-start.12) | collective-permute-done | bytes 196640 | tf_op jit(solution)/shard_map/ppermute | solution.py:318
  207.8 0.5 fusion.14
  208.4 0.6 collective-permute-start.6
  209.0 0.9 collective-permute-done.15
  209.9 3.7 %collective-permute-start.5 = (bf16[1,256,1536]{2,1,0:T(8,128)(2,1)}, bf16[1,256,1536]{2,1,0:T(8,128)(2,1)}, u32[]{:S(2)}, u32[]{:S(2)}) collective-permute-start(bf16[1,256,1536]{2,1,0:T(8,128)(2,1)} %add_convert_fusion.3), channel_id=1, source_target_pairs={{0,24},{8,0},{16,8},{24,16},{1,25},{9,1},{17,9},{25,17},{2,26},{10... | collective-permute-start | bytes 2359304 | tf_op jit(solution)/shard_map/ppermute | solution.py:325
  213.6 15.1 %collective-permute-done.13 = bf16[128,768]{1,0:T(8,128)(2,1)S(1)} collective-permute-done((bf16[128,768]{1,0:T(8,128)(2,1)S(1)}, bf16[128,768]{1,0:T(8,128)(2,1)S(1)}, u32[]{:S(2)}, u32[]{:S(2)}) %collective-permute-start.13) | collective-permute-done | bytes 196640 | tf_op jit(solution)/shard_map/ppermute | solution.py:324
  228.9 3.3 %collective-permute-start.16 = (bf16[128,768]{1,0:T(8,128)(2,1)S(1)}, bf16[128,768]{1,0:T(8,128)(2,1)S(1)}, u32[]{:S(2)}, u32[]{:S(2)}) collective-permute-start(bf16[128,768]{1,0:T(8,128)(2,1)S(1)} %get-tuple-element.97), channel_id=1, source_target_pairs={{0,24},{8,0},{16,8},{24,16},{1,25},{9,1},{17,9},{25,17},{2,26},{10... | collective-permute-start | bytes 589832 | tf_op jit(solution)/shard_map/ppermute | solution.py:325
  232.2 2.3 add_convert_fusion.1
  234.5 0.8 collective-permute-start.10
  235.3 12.3 %collective-permute-done.17 = bf16[128,768]{1,0:T(8,128)(2,1)S(1)} collective-permute-done((bf16[128,768]{1,0:T(8,128)(2,1)S(1)}, bf16[128,768]{1,0:T(8,128)(2,1)S(1)}, u32[]{:S(2)}, u32[]{:S(2)}) %collective-permute-start.17) | collective-permute-done | bytes 196640 | tf_op jit(solution)/shard_map/ppermute | solution.py:320
  247.7 0.9 maximum_bitcast_fusion
  248.6 2.3 fusion.2
  250.9 1.6 fusion.6
  252.6 3.1 %convert_add_fusion = f32[1,256,1536]{2,1,0:T(8,128)} fusion(bf16[1,256,1536]{2,1,0:T(8,128)(2,1)} %collective-permute-done.10, bf16[1,256,1536]{2,1,0:T(8,128)(2,1)} %collective-permute-done.6, bf16[1,256,1536]{2,1,0:T(8,128)(2,1)} %collective-permute-done.5, bf16[1,256,1536]{2,1,0:T(8,128)(2,1)S(1)} %copy-done.4), kind=kLoop, calls=%fused_computation.12 | loop fusion | flops 2752512 | bytes 4718592 | tf_op jit(solution)/shard_map/add | solution.py:429
  (52 shorter events, 0.9 us)
Async XLA Ops:
  54.3 48.3 %all-to-all-start.1 = ((bf16[8,48,4096]{2,1,0:T(8,128)(2,1)}), bf16[8,48,4096]{2,1,0:T(8,128)(2,1)}, u32[]{:S(2)}, u32[]{:S(2)}) async-start(bf16[8,48,4096]{2,1,0:T(8,128)(2,1)} %get-tuple-element.56), calls=%async_computation.1 | async-start | bytes 6291456 | tf_op jit(solution)/shard_map/all_to_all | solution.py:333
  107.6 28.8 %collective-permute-start = (bf16[2,4,256,384]{3,2,1,0:T(8,128)(2,1)}, bf16[2,4,256,384]{3,2,1,0:T(8,128)(2,1)}, u32[]{:S(2)}, u32[]{:S(2)}) collective-permute-start(bf16[2,4,256,384]{3,2,1,0:T(8,128)(2,1)} %get-tuple-element.73), channel_id=1, source_target_pairs={{0,32},{32,0},{1,33},{33,1},{2,34},{34,2},{3,35},{35,3},{4,36},{36... | collective-permute-start | bytes 4718600 | tf_op jit(solution)/shard_map/ppermute | solution.py:377
  112.7 31.2 %collective-permute-start.2 = (bf16[2,4,256,384]{3,2,1,0:T(8,128)(2,1)}, bf16[2,4,256,384]{3,2,1,0:T(8,128)(2,1)S(1)}, u32[]{:S(2)}, u32[]{:S(2)}) collective-permute-start(bf16[2,4,256,384]{3,2,1,0:T(8,128)(2,1)} %get-tuple-element.76), channel_id=1, source_target_pairs={{0,32},{32,0},{1,33},{33,1},{2,34},{34,2},{3,35},{35,3},{4,36},{36... | collective-permute-start | bytes 4718600 | tf_op jit(solution)/shard_map/ppermute | solution.py:373
  132.4 11.6 %collective-permute-start.3 = (bf16[2,384,768]{2,1,0:T(8,128)(2,1)}, bf16[2,384,768]{2,1,0:T(8,128)(2,1)}, u32[]{:S(2)}, u32[]{:S(2)}) collective-permute-start(bf16[2,384,768]{2,1,0:T(8,128)(2,1)} %get-tuple-element.82.mine_ref.grads_ref), channel_id=1, source_target_pairs={{0,32},{32,0},{1,33},{33,1},{2,34},{34,2},{3,35},{35,3},{4,36},{36... | collective-permute-start | bytes 3538952 | tf_op jit(solution)/shard_map/ppermute | solution.py:380
  132.4 4.0 %collective-permute-start.1 = (bf16[384,768]{1,0:T(8,128)(2,1)}, bf16[384,768]{1,0:T(8,128)(2,1)}, u32[]{:S(2)}, u32[]{:S(2)}) collective-permute-start(bf16[384,768]{1,0:T(8,128)(2,1)} %get-tuple-element.64.hidden_ref), channel_id=1, source_target_pairs={{0,32},{32,0},{1,33},{33,1},{2,34},{34,2},{3,35},{35,3},{4,36},{36... | collective-permute-start | bytes 1769480 | tf_op jit(solution)/shard_map/ppermute | solution.py:375
  144.0 1.2 copy-start
  150.3 42.3 %collective-permute-start.4 = (bf16[1,256,1536]{2,1,0:T(8,128)(2,1)}, bf16[1,256,1536]{2,1,0:T(8,128)(2,1)}, u32[]{:S(2)}, u32[]{:S(2)}) collective-permute-start(bf16[1,256,1536]{2,1,0:T(8,128)(2,1)} %get-tuple-element.77), channel_id=1, source_target_pairs={{0,24},{8,0},{16,8},{24,16},{1,25},{9,1},{17,9},{25,17},{2,26},{10... | collective-permute-start | bytes 2359304 | tf_op jit(solution)/shard_map/ppermute | solution.py:319
  158.4 36.7 %collective-permute-start.7 = (bf16[1,256,1536]{2,1,0:T(8,128)(2,1)}, bf16[1,256,1536]{2,1,0:T(8,128)(2,1)}, u32[]{:S(2)}, u32[]{:S(2)}) collective-permute-start(bf16[1,256,1536]{2,1,0:T(8,128)(2,1)} %get-tuple-element.91), channel_id=1, source_target_pairs={{0,8},{8,16},{16,24},{24,0},{1,9},{9,17},{17,25},{25,1},{2,10},{10... | collective-permute-start | bytes 2359304 | tf_op jit(solution)/shard_map/ppermute | solution.py:318
  158.4 38.1 %collective-permute-start.11 = (bf16[4,256,768]{2,1,0:T(8,128)(2,1)}, bf16[4,256,768]{2,1,0:T(8,128)(2,1)}, u32[]{:S(2)}, u32[]{:S(2)}) collective-permute-start(bf16[4,256,768]{2,1,0:T(8,128)(2,1)} %get-tuple-element.94), channel_id=1, source_target_pairs={{0,64},{64,0},{1,65},{65,1},{2,66},{66,2},{3,67},{67,3},{4,68},{68... | collective-permute-start | bytes 4718600 | tf_op jit(solution)/shard_map/ppermute | solution.py:385
  163.5 12.9 %copy-start.8 = (bf16[384,128]{1,0:T(8,128)(2,1)S(1)}, bf16[384,128]{1,0:T(8,128)(2,1)}, u32[]{:S(2)}) copy-start(bf16[384,128]{1,0:T(8,128)(2,1)} %get-tuple-element.85) | copy-start | bytes 294916
  173.3 55.6 %collective-permute-start.9 = (bf16[1,256,1536]{2,1,0:T(8,128)(2,1)}, bf16[1,256,1536]{2,1,0:T(8,128)(2,1)}, u32[]{:S(2)}, u32[]{:S(2)}) collective-permute-start(bf16[1,256,1536]{2,1,0:T(8,128)(2,1)} %get-tuple-element.92), channel_id=1, source_target_pairs={{0,24},{8,0},{16,8},{24,16},{1,25},{9,1},{17,9},{25,17},{2,26},{10... | collective-permute-start | bytes 2359304 | tf_op jit(solution)/shard_map/ppermute | solution.py:321
  177.2 10.5 %all-to-all-start.3 = ((bf16[8,1,48]{2,1,0:T(2,128)(2,1)}), bf16[8,1,48]{2,1,0:T(2,128)(2,1)S(1)}, u32[]{:S(2)}, u32[]{:S(2)}) async-start(bf16[8,1,48]{2,1,0:T(2,128)(2,1)} %all_to_all.20), calls=%async_computation.3 | async-start | bytes 8192 | tf_op jit(solution)/shard_map/all_to_all | solution.py:333
  187.7 60.9 %all-to-all-start.2 = ((bf16[8,48,4096]{2,1,0:T(8,128)(2,1)}), bf16[8,48,4096]{2,1,0:T(8,128)(2,1)S(1)}, u32[]{:S(2)}, u32[]{:S(2)}) async-start(bf16[8,48,4096]{2,1,0:T(8,128)(2,1)} %slot_rows.1), calls=%async_computation.2 | async-start | bytes 6291456 | tf_op jit(solution)/shard_map/all_to_all | solution.py:333
  192.5 2.6 copy-start.6
  195.1 1.6 copy-start.2
  198.5 0.9 copy-start.7
  198.5 1.1 copy-start.10
  198.6 9.3 %copy-start.11 = (bf16[128,2]{0,1:T(2,128)(2,1)S(1)}, bf16[128,2]{0,1:T(2,128)(2,1)}, u32[]{:S(2)}) copy-start(bf16[128,2]{0,1:T(2,128)(2,1)} %param.11) | copy-start | bytes 1540
  198.6 33.6 %copy-start.5 = (bf16[1,256,1536]{2,1,0:T(8,128)(2,1)S(1)}, bf16[1,256,1536]{2,1,0:T(8,128)(2,1)}, u32[]{:S(2)}) copy-start(bf16[1,256,1536]{2,1,0:T(8,128)(2,1)} %get-tuple-element.89) | copy-start | bytes 2359300
  198.6 9.1 %collective-permute-start.12 = (bf16[128,768]{1,0:T(8,128)(2,1)S(1)}, bf16[128,768]{1,0:T(8,128)(2,1)S(1)}, u32[]{:S(2)}, u32[]{:S(2)}) collective-permute-start(bf16[128,768]{1,0:T(8,128)(2,1)S(1)} %get-tuple-element.98), channel_id=1, source_target_pairs={{0,8},{8,16},{16,24},{24,0},{1,9},{9,17},{17,25},{25,1},{2,10},{10... | collective-permute-start | bytes 589832 | tf_op jit(solution)/shard_map/ppermute | solution.py:318
  199.6 32.6 %collective-permute-start.8 = (bf16[1,256,1536]{2,1,0:T(8,128)(2,1)S(1)}, bf16[1,256,1536]{2,1,0:T(8,128)(2,1)S(1)}, u32[]{:S(2)}, u32[]{:S(2)}) collective-permute-start(bf16[1,256,1536]{2,1,0:T(8,128)(2,1)S(1)} %add_convert_fusion.2), channel_id=1, source_target_pairs={{0,8},{8,16},{16,24},{24,0},{1,9},{9,17},{17,25},{25,1},{2,10},{10... | collective-permute-start | bytes 2359304 | tf_op jit(solution)/shard_map/ppermute | solution.py:324
  199.7 8.7 %collective-permute-start.14 = (bf16[128,768]{1,0:T(8,128)(2,1)S(1)}, bf16[128,768]{1,0:T(8,128)(2,1)S(1)}, u32[]{:S(2)}, u32[]{:S(2)}) collective-permute-start(bf16[128,768]{1,0:T(8,128)(2,1)S(1)} %get-tuple-element.101), channel_id=1, source_target_pairs={{0,24},{8,0},{16,8},{24,16},{1,25},{9,1},{17,9},{25,17},{2,26},{10... | collective-permute-start | bytes 589832 | tf_op jit(solution)/shard_map/ppermute | solution.py:321
  202.9 7.0 %collective-permute-start.15 = (bf16[128,768]{1,0:T(8,128)(2,1)S(1)}, bf16[128,768]{1,0:T(8,128)(2,1)S(1)}, u32[]{:S(2)}, u32[]{:S(2)}) collective-permute-start(bf16[128,768]{1,0:T(8,128)(2,1)S(1)} %get-tuple-element.100), channel_id=1, source_target_pairs={{0,24},{8,0},{16,8},{24,16},{1,25},{9,1},{17,9},{25,17},{2,26},{10... | collective-permute-start | bytes 589832 | tf_op jit(solution)/shard_map/ppermute | solution.py:319
  207.7 21.0 %collective-permute-start.13 = (bf16[128,768]{1,0:T(8,128)(2,1)S(1)}, bf16[128,768]{1,0:T(8,128)(2,1)S(1)}, u32[]{:S(2)}, u32[]{:S(2)}) collective-permute-start(bf16[128,768]{1,0:T(8,128)(2,1)S(1)} %fusion.10), channel_id=1, source_target_pairs={{0,8},{8,16},{16,24},{24,0},{1,9},{9,17},{17,25},{25,1},{2,10},{10... | collective-permute-start | bytes 589832 | tf_op jit(solution)/shard_map/ppermute | solution.py:324
  208.4 44.2 %collective-permute-start.6 = (bf16[1,256,1536]{2,1,0:T(8,128)(2,1)}, bf16[1,256,1536]{2,1,0:T(8,128)(2,1)}, u32[]{:S(2)}, u32[]{:S(2)}) collective-permute-start(bf16[1,256,1536]{2,1,0:T(8,128)(2,1)} %get-tuple-element.79), channel_id=1, source_target_pairs={{0,8},{8,16},{16,24},{24,0},{1,9},{9,17},{17,25},{25,1},{2,10},{10... | collective-permute-start | bytes 2359304 | tf_op jit(solution)/shard_map/ppermute | solution.py:320
  209.9 42.6 %collective-permute-start.5 = (bf16[1,256,1536]{2,1,0:T(8,128)(2,1)}, bf16[1,256,1536]{2,1,0:T(8,128)(2,1)}, u32[]{:S(2)}, u32[]{:S(2)}) collective-permute-start(bf16[1,256,1536]{2,1,0:T(8,128)(2,1)} %add_convert_fusion.3), channel_id=1, source_target_pairs={{0,24},{8,0},{16,8},{24,16},{1,25},{9,1},{17,9},{25,17},{2,26},{10... | collective-permute-start | bytes 2359304 | tf_op jit(solution)/shard_map/ppermute | solution.py:325
  228.8 18.8 %collective-permute-start.17 = (bf16[128,768]{1,0:T(8,128)(2,1)S(1)}, bf16[128,768]{1,0:T(8,128)(2,1)S(1)}, u32[]{:S(2)}, u32[]{:S(2)}) collective-permute-start(bf16[128,768]{1,0:T(8,128)(2,1)S(1)} %get-tuple-element.99), channel_id=1, source_target_pairs={{0,8},{8,16},{16,24},{24,0},{1,9},{9,17},{17,25},{25,1},{2,10},{10... | collective-permute-start | bytes 589832 | tf_op jit(solution)/shard_map/ppermute | solution.py:320
  228.9 18.7 %collective-permute-start.16 = (bf16[128,768]{1,0:T(8,128)(2,1)S(1)}, bf16[128,768]{1,0:T(8,128)(2,1)S(1)}, u32[]{:S(2)}, u32[]{:S(2)}) collective-permute-start(bf16[128,768]{1,0:T(8,128)(2,1)S(1)} %get-tuple-element.97), channel_id=1, source_target_pairs={{0,24},{8,0},{16,8},{24,16},{1,25},{9,1},{17,9},{25,17},{2,26},{10... | collective-permute-start | bytes 589832 | tf_op jit(solution)/shard_map/ppermute | solution.py:325
  234.5 14.1 %copy-start.9 = (f32[4096]{0:T(1024)S(1)}, f32[4096]{0:T(1024)}, u32[]{:S(2)}) copy-start(f32[4096]{0:T(1024)} %param.8) | copy-start | bytes 49156
  234.5 18.1 %collective-permute-start.10 = (bf16[1,256,1536]{2,1,0:T(8,128)(2,1)}, bf16[1,256,1536]{2,1,0:T(8,128)(2,1)}, u32[]{:S(2)}, u32[]{:S(2)}) collective-permute-start(bf16[1,256,1536]{2,1,0:T(8,128)(2,1)} %add_convert_fusion.1), channel_id=1, source_target_pairs={{0,64},{64,0},{1,65},{65,1},{2,66},{66,2},{3,67},{67,3},{4,68},{68... | collective-permute-start | bytes 2359304 | tf_op jit(solution)/shard_map/ppermute | solution.py:399
  248.6 2.3 copy-start.1
  248.6 2.3 copy-start.3
  250.9 1.6 copy-start.4

commit v6 on v5

--- a/solution.py
+++ b/solution.py
@@ -277,6 +277,66 @@
     )(place, keep, came, mine, theirs)
 
 
+SEND_ORDER = (2, 1, 3, 0)
+
+
+def ring_at(step):
+    ring = SEND_ORDER[-1]
+    for at, value in enumerate(SEND_ORDER[:-1]):
+        ring = jnp.where(step == at, value, ring)
+    return ring
+
+
+def messages_kernel(_, keep_ref, came_ref, mine_ref, theirs_ref, *out_refs):
+    block, slots = keep_ref.shape[2:]
+    unit = pl.program_id(1)
+    keep, came = keep_ref[...].reshape(2 * block, slots), came_ref[...].reshape(2 * block, slots)
+    rows = contract(keep, mine_ref[unit], 1, 0) + contract(came, theirs_ref[unit], 1, 0)
+    rows = rows.astype(jnp.bfloat16)
+    for at in range(len(SEND_ORDER)):
+
+        @pl.when(pl.program_id(0) == at)
+        def _():
+            out_refs[2 * at][0] = rows[:block]
+            out_refs[2 * at + 1][0] = rows[block:]
+
+
+def weight_messages(place, keep, came, mine, theirs):
+    _, rings, block, slots = keep.shape
+    units, _, width = mine.shape
+    left = pl.BlockSpec(
+        (2, 1, block, slots), lambda i, u, at: (0, lax.rem(at[2] + ring_at(i), rings), 0, 0)
+    )
+    right = pl.BlockSpec(mine.shape, lambda i, u, at: (0, 0, 0))
+
+    def out(k):
+        return pl.BlockSpec(
+            (1, block, width),
+            lambda i, u, at: (0, 0, jnp.where(i == k, u, jnp.where(i < k, 0, units - 1))),
+        )
+
+    outs = pl.pallas_call(
+        messages_kernel,
+        grid_spec=pltpu.PrefetchScalarGridSpec(
+            num_scalar_prefetch=1,
+            grid=(rings, units),
+            in_specs=[left, left, right, right],
+            out_specs=[out(k) for k in range(rings) for _ in range(2)],
+        ),
+        out_shape=[jax.ShapeDtypeStruct((1, block, units * width), jnp.bfloat16)] * (2 * rings),
+        compiler_params=pltpu.CompilerParams(vmem_limit_bytes=VMEM),
+        cost_estimate=pl.CostEstimate(
+            flops=8 * rings * block * mine.size,
+            bytes_accessed=4 * mine.size + 4 * rings * block * (2 * slots + units * width),
+            transcendentals=0,
+        ),
+        name="grad_in",
+    )(place, keep, came, mine, theirs)
+    far = {ring: outs[2 * k] for k, ring in enumerate(SEND_ORDER)}
+    near = {ring: outs[2 * k + 1] for k, ring in enumerate(SEND_ORDER)}
+    return far, near
+
+
 def slot_kernel(grads_ref, w_ref, out_ref):
     width = grads_ref.shape[2]
     rows = contract(grads_ref[0], w_ref[:, :width], 1, 1) + contract(
@@ -373,28 +433,18 @@
     came_normed = lax.ppermute(give_normed, "dp_1", SWAP)
     hidden, gate, up = forward(got_normed, w_in)
     their_hidden = lax.ppermute(hidden, "dp_1", SWAP)
+    mine, route = back(got_scaled, w_down, hidden, gate, up)
+    theirs = lax.ppermute(mine, "dp_1", SWAP)
+    got_scaled, mine, route = lax.optimization_barrier((got_scaled, mine, route))
     keep_scaled, give_scaled = turn(place, got_scaled, rings, span)
     came_scaled = lax.ppermute(give_scaled, "dp_1", SWAP)
-    got_scaled, keep_scaled = lax.optimization_barrier((got_scaled, keep_scaled))
-    mine, route = back(got_scaled, w_down, hidden, gate, up)
-    theirs = lax.ppermute(mine, "dp_1", SWAP)
-    keep_scaled, mine, route = lax.optimization_barrier((keep_scaled, mine, route))
+    keep_normed, keep_scaled = lax.optimization_barrier((keep_normed, keep_scaled))
+    far, near = weight_messages(place, keep_normed, came_normed, mine, theirs)
+    keep_scaled, _ = lax.optimization_barrier((keep_scaled, near[0]))
     far_down, near_down = weight_rows(
         place, keep_scaled, came_scaled, hidden[None], their_hidden[None], 0, rings
     )
     came_down = lax.ppermute(far_down, "dp_0", SWAP)
-
-    far, near = {}, {}
-
-    def in_rows(ring, after):
-        nonlocal keep_normed
-        keep_normed, _ = lax.optimization_barrier((keep_normed, after))
-        far[ring], near[ring] = weight_rows(place, keep_normed, came_normed, mine, theirs, ring, 1)
-
-    in_rows(2, near_down)
-    in_rows(1, near[2])
-    in_rows(3, near[1])
-    in_rows(0, near[3])
     (far_in, near_in), far_both, near_both = ring_sum(far, near)
     came_in = lax.ppermute(far_in.astype(jnp.bfloat16), "dp_0", SWAP)
     came_down, _, _ = lax.optimization_barrier((came_down, far_both, near_both))
@@ -404,7 +454,7 @@
     halves_down, _, _ = ring_sum(upper, lower)
     grad_down = jnp.concatenate(halves_down, axis=0)[None]
 
-    mine, route, _ = lax.optimization_barrier((mine, route, near[3]))
+    mine, route, _ = lax.optimization_barrier((mine, route, near_down))
     slot_normed = slot_rows(mine, w_in, experts)
     back_normed = exchange(slot_normed)
     back_route = exchange(route[:, 0].reshape(experts, capacity))

time: 257 us -> 240 us (0.934)
  waiting for transfers between devices: 79.7 us -> 68.7 us
  Pallas kernels: 72.9 us -> 67 us
  starting transfers between devices: 33 us -> 35.6 us
    pallas_call x5 -> x1, Pallas kernels: 27.9 us -> 7.64 us  [weight_rows(): pl.pallas_call(rows_kernel, grid_spec=pltpu.PrefetchScalarGridSpec(num_sc...]
    all_to_all x3, waiting for transfers between devices: 45.9 us -> 28.2 us  [exchange(): lax.all_to_all(rows, ('dp_0', 'expert'), split_axis=0, concat_axis=0, axi...]
    pallas_call x0 -> x1, Pallas kernels: none -> 14 us  [weight_messages(): pl.pallas_call(messages_kernel, grid_spec=pltpu.PrefetchScalarGridSpec(nu...]
    ppermute x1, waiting for transfers between devices: 0.01 us -> 8.77 us  [per_device(): came_down = lax.ppermute(far_down, 'dp_0', SWAP)]
  transfers between devices with their start and end apart: 21 -> 21, of which waited for: 7 -> 7; matrix products, arithmetic and copies ran while one was open for 6% -> 6% of each run, Pallas kernels for 22% -> 26%
where the time goes in v6:
time: 240 us; the launch traced here: 238 us
  waiting for transfers between devices  68.7 us (29%)
  Pallas kernels  67 us (28%)
  blocking collectives  47 us (20%)
  starting transfers between devices  35.6 us (15%)
  other arithmetic  15.6 us (6%)
    all_to_all x1, blocking collectives, exchange(): lax.all_to_all(rows, ('dp_0', 'expert'), split_axis=0, concat_axis=0, axi...  47 us
    all_to_all x3, waiting for transfers between devices, exchange(): lax.all_to_all(rows, ('dp_0', 'expert'), split_axis=0, concat_axis=0, axi...  28.2 us
    all_to_all x3, starting transfers between devices, exchange(): lax.all_to_all(rows, ('dp_0', 'expert'), split_axis=0, concat_axis=0, axi...  14.5 us
    ppermute x2, waiting for transfers between devices, ring_sum(): low_last = lax.ppermute(low_both, 'ulysses', ahead)  14.4 us
    pallas_call x1, Pallas kernels, weight_messages(): pl.pallas_call(messages_kernel, grid_spec=pltpu.PrefetchScalarGridSpec(nu...  14 us
    ppermute x2, waiting for transfers between devices, ring_sum(): high_side = lax.ppermute(high[1], 'ulysses', ahead)  13.4 us
    pallas_call x1, Pallas kernels, forward(): pl.pallas_call(forward_kernel, grid=(steps,), in_specs=[pl.BlockSpec(got....  10.6 us
    pallas_call x2, Pallas kernels, turn(): pl.pallas_call(turn_kernel, grid_spec=pltpu.PrefetchScalarGridSpec(num_sc...  10.3 us
  transfers between devices with their start and end apart: 21, of which 7 were waited for; matrix products, arithmetic and copies ran while one was open for 6% of the time, Pallas kernels for 26%

profile of v6, /device:TPU:0, one launch (start us, length us, event | category | flops | bytes accessed | tf_op | source)
XLA Modules:
  0.0 238.4 jit_solution(5513692194115610854)
XLA Ops:
  0.6 0.6 pad_add_fusion._
  1.2 6.0 %pack.1 = (bf16[8,48,4096]{2,1,0:T(8,128)(2,1)}, bf16[8,48,4096]{2,1,0:T(8,128)(2,1)}, bf16[384,128]{1,0:T(8,128)(2,1)}) custom-call(s32[2,128]{1,0:T(2,128)} %bitcast.57, bf16[2,128]{1,0:T(2,128)(2,1)} %bitcast.59, f32[1,4096]{1,0:T(1,128)} %bitcast.55, bf16[128,4096]{1,0:T(8,128)(2,1)} %resid_ref, bf16[128,4096]{1,0:T(8,128)(2,1)} %grad_ref.1), custom_call_target="tpu_custom_call" | custom-call | flops 805306368 | bytes 6291456 | tf_op jit(solution)/shard_map/pack/pallas_call | solution.py:81
  7.2 47.0 %all_to_all.25.got_ref.keep_ref.give_ref = bf16[8,48,4096]{2,1,0:T(8,128)(2,1)} all-to-all(bf16[8,48,4096]{2,1,0:T(8,128)(2,1)} %get-tuple-element.48), channel_id=1, replica_groups={{0,65,2,67,4,69,6,71},{64,1,66,3,68,5,70,7},{8,73,10,75,12,77,14,79},{7..., dimensions={0} | all-to-all | bytes 6291456 | tf_op jit(solution)/shard_map/all_to_all | solution.py:393
  54.2 4.5 %all-to-all-start.1 = ((bf16[8,48,4096]{2,1,0:T(8,128)(2,1)}), bf16[8,48,4096]{2,1,0:T(8,128)(2,1)}, u32[]{:S(2)}, u32[]{:S(2)}) async-start(bf16[8,48,4096]{2,1,0:T(8,128)(2,1)} %get-tuple-element.53), calls=%async_computation.1 | async-start | bytes 6291456 | tf_op jit(solution)/shard_map/all_to_all | solution.py:393
  58.7 5.1 %turn.2 = (bf16[2,4,256,384]{3,2,1,0:T(8,128)(2,1)}, bf16[2,4,256,384]{3,2,1,0:T(8,128)(2,1)}) custom-call(s32[3]{0:T(128)} %pad_add_fusion._, bf16[8,48,4096]{2,1,0:T(8,128)(2,1)} %all_to_all.25.got_ref.keep_ref.give_ref, bf16[8,48,4096]{2,1,0:T(8,128)(2,1)} %all_to_all.25.got_ref.keep_ref.give_ref), custom_call_target="tpu_custom_call" | custom-call | flops 1610612736 | bytes 6291456 | tf_op jit(solution)/shard_map/turn/pallas_call | solution.py:219
  63.8 10.6 %forward.1 = (bf16[384,768]{1,0:T(8,128)(2,1)}, f32[384,768]{1,0:T(8,128)}, f32[384,768]{1,0:T(8,128)}) custom-call(bf16[8,48,4096]{2,1,0:T(8,128)(2,1)} %all_to_all.25.got_ref.keep_ref.give_ref, bf16[4096,1536]{1,0:T(8,128)(2,1)} %bitcast.48, bf16[4096,1536]{1,0:T(8,128)(2,1)} %bitcast.49), custom_call_target="tpu_custom_call" | custom-call | flops 4831838208 | bytes 15728640 | tf_op jit(solution)/shard_map/forward/pallas_call | solution.py:125
  74.3 28.2 %all-to-all-done.1.got_ref.keep_ref.give_ref = bf16[8,48,4096]{2,1,0:T(8,128)(2,1)} async-done(((bf16[8,48,4096]{2,1,0:T(8,128)(2,1)}), bf16[8,48,4096]{2,1,0:T(8,128)(2,1)}, u32[]{:S(2)}, u32[]{:S(2)}) %all-to-all-start.1) | async-done | bytes 3145760 | tf_op jit(solution)/shard_map/all_to_all | solution.py:393
  102.5 8.7 %back.1 = (bf16[2,384,768]{2,1,0:T(8,128)(2,1)}, bf16[384,128]{1,0:T(8,128)(2,1)}) custom-call(bf16[8,48,4096]{2,1,0:T(8,128)(2,1)} %all-to-all-done.1.got_ref.keep_ref.give_ref, bf16[768,4096]{1,0:T(8,128)(2,1)} %bitcast.52, bf16[384,768]{1,0:T(8,128)(2,1)} %get-tuple-element.57.hidden_ref, f32[384,768]{1,0:T(8,128)} %get-tuple-element.58.gate_ref, ...), custom_call_target="tpu_custom_call" | custom-call | flops 2415919104 | bytes 12386304 | tf_op jit(solution)/shard_map/back/pallas_call | solution.py:173
  111.2 5.2 %turn.3 = (bf16[2,4,256,384]{3,2,1,0:T(8,128)(2,1)}, bf16[2,4,256,384]{3,2,1,0:T(8,128)(2,1)}) custom-call(s32[3]{0:T(128)} %pad_add_fusion._, bf16[8,48,4096]{2,1,0:T(8,128)(2,1)} %all-to-all-done.1.got_ref.keep_ref.give_ref, bf16[8,48,4096]{2,1,0:T(8,128)(2,1)} %all-to-all-done.1.got_ref.keep_ref.give_ref), custom_call_target="tpu_custom_call" | custom-call | flops 1610612736 | bytes 6291456 | tf_op jit(solution)/shard_map/turn/pallas_call | solution.py:219
  116.4 0.5 collective-permute-start.2
  116.9 0.1 collective-permute-start.3
  117.0 0.3 fusion.7
  117.3 14.0 %grad_in.1 = (bf16[1,256,1536]{2,1,0:T(8,128)(2,1)}, bf16[1,256,1536]{2,1,0:T(8,128)(2,1)}, bf16[1,256,1536]{2,1,0:T(8,128)(2,1)}, bf16[1,256,1536]{2,1,0:T(8,12...) custom-call(s32[3]{0:T(128)} %pad_add_fusion._, ...), custom_call_target="tpu_custom_call" | custom-call | flops 4831838208 | bytes 11796480 | tf_op jit(solution)/shard_map/grad_in/pallas_call | solution.py:318
  131.4 3.1 %collective-permute-start.4 = (bf16[1,256,1536]{2,1,0:T(8,128)(2,1)}, bf16[1,256,1536]{2,1,0:T(8,128)(2,1)}, u32[]{:S(2)}, u32[]{:S(2)}) collective-permute-start(bf16[1,256,1536]{2,1,0:T(8,128)(2,1)} %get-tuple-element.81), channel_id=1, source_target_pairs={{0,24},{8,0},{16,8},{24,16},{1,25},{9,1},{17,9},{25,17},{2,26},{10... | collective-permute-start | bytes 2359304 | tf_op jit(solution)/shard_map/ppermute | solution.py:379
  134.5 7.6 %shard_map.102 = (bf16[4,256,768]{2,1,0:T(8,128)(2,1)}, bf16[4,256,768]{2,1,0:T(8,128)(2,1)}) custom-call(s32[3]{0:T(128)} %pad_add_fusion._, bf16[2,4,256,384]{3,2,1,0:T(8,128)(2,1)} %get-tuple-element.72.keep_ref, bf16[2,4,256,384]{3,2,1,0:T(8,128)(2,1)} %collective-permute-done.2.came_ref, bf16[1,384,768]{2,1,0:T(8,128)(2,1)} %bitcast.53, ...), custom_call_target="tpu_custom_call" | custom-call | flops 2415919104 | bytes 7471104 | tf_op jit(solution)/shard_map/pallas_call | solution.py:262
  142.1 3.3 %collective-permute-start.9 = (bf16[1,256,1536]{2,1,0:T(8,128)(2,1)}, bf16[1,256,1536]{2,1,0:T(8,128)(2,1)}, u32[]{:S(2)}, u32[]{:S(2)}) collective-permute-start(bf16[1,256,1536]{2,1,0:T(8,128)(2,1)} %get-tuple-element.86), channel_id=1, source_target_pairs={{0,24},{8,0},{16,8},{24,16},{1,25},{9,1},{17,9},{25,17},{2,26},{10... | collective-permute-start | bytes 2359304 | tf_op jit(solution)/shard_map/ppermute | solution.py:381
  145.4 0.1 slice_reduce_fusion
  145.5 0.7 all_to_all.20
  146.2 3.2 %all-to-all-start.3 = ((bf16[8,1,48]{2,1,0:T(2,128)(2,1)}), bf16[8,1,48]{2,1,0:T(2,128)(2,1)S(1)}, u32[]{:S(2)}, u32[]{:S(2)}) async-start(bf16[8,1,48]{2,1,0:T(2,128)(2,1)} %all_to_all.20), calls=%async_computation.3 | async-start | bytes 8192 | tf_op jit(solution)/shard_map/all_to_all | solution.py:393
  149.5 9.8 %slot_rows.1 = bf16[8,48,4096]{2,1,0:T(8,128)(2,1)} custom-call(bf16[2,384,768]{2,1,0:T(8,128)(2,1)} %get-tuple-element.75.mine_ref.grads_ref, bf16[4096,1536]{1,0:T(8,128)(2,1)} %bitcast.50), custom_call_target="tpu_custom_call" | custom-call | flops 4831838208 | bytes 15728640 | tf_op jit(solution)/shard_map/slot_rows/pallas_call | solution.py:351
  159.3 6.8 %all-to-all-start.2 = ((bf16[8,48,4096]{2,1,0:T(8,128)(2,1)}), bf16[8,48,4096]{2,1,0:T(8,128)(2,1)S(1)}, u32[]{:S(2)}, u32[]{:S(2)}) async-start(bf16[8,48,4096]{2,1,0:T(8,128)(2,1)} %slot_rows.1), calls=%async_computation.2 | async-start | bytes 6291456 | tf_op jit(solution)/shard_map/all_to_all | solution.py:393
  166.1 2.5 %add_convert_fusion.3 = bf16[1,256,1536]{2,1,0:T(8,128)(2,1)} fusion(bf16[1,256,1536]{2,1,0:T(8,128)(2,1)} %collective-permute-done.4, bf16[1,256,1536]{2,1,0:T(8,128)(2,1)} %get-tuple-element.80), kind=kLoop, calls=%fused_computation.15 | loop fusion | flops 1572864 | bytes 2359296 | tf_op jit(solution)/shard_map/convert_element_type | solution.py:383
  168.7 1.4 add_convert_fusion.2
  170.1 8.8 %collective-permute-done.11 = bf16[4,256,768]{2,1,0:T(8,128)(2,1)} collective-permute-done((bf16[4,256,768]{2,1,0:T(8,128)(2,1)}, bf16[4,256,768]{2,1,0:T(8,128)(2,1)}, u32[]{:S(2)}, u32[]{:S(2)}) %collective-permute-start.11) | collective-permute-done | bytes 1572896 | tf_op jit(solution)/shard_map/ppermute | solution.py:447
  178.9 1.8 add_convert_fusion
  180.8 0.4 collective-permute-start.12
  181.2 0.4 copy-done.8
  181.6 0.1 fusion.12
  181.7 1.2 collective-permute-start.8
  183.0 2.3 collective-permute-start.14
  185.3 1.7 collective-permute-start.15
  187.0 2.8 %collective-permute-done.12 = bf16[128,768]{1,0:T(8,128)(2,1)S(1)} collective-permute-done((bf16[128,768]{1,0:T(8,128)(2,1)S(1)}, bf16[128,768]{1,0:T(8,128)(2,1)S(1)}, u32[]{:S(2)}, u32[]{:S(2)}) %collective-permute-start.12) | collective-permute-done | bytes 196640 | tf_op jit(solution)/shard_map/ppermute | solution.py:378
  189.9 0.1 collective-permute-start.13
  190.0 0.5 fusion.14
  190.6 0.8 collective-permute-done.14
  191.3 1.7 collective-permute-start.6
  193.1 0.4 collective-permute-done.15
  193.5 3.1 %collective-permute-start.5 = (bf16[1,256,1536]{2,1,0:T(8,128)(2,1)}, bf16[1,256,1536]{2,1,0:T(8,128)(2,1)}, u32[]{:S(2)}, u32[]{:S(2)}) collective-permute-start(bf16[1,256,1536]{2,1,0:T(8,128)(2,1)} %add_convert_fusion.3), channel_id=1, source_target_pairs={{0,24},{8,0},{16,8},{24,16},{1,25},{9,1},{17,9},{25,17},{2,26},{10... | collective-permute-start | bytes 2359304 | tf_op jit(solution)/shard_map/ppermute | solution.py:385
  196.6 14.4 %collective-permute-done.13 = bf16[128,768]{1,0:T(8,128)(2,1)S(1)} collective-permute-done((bf16[128,768]{1,0:T(8,128)(2,1)S(1)}, bf16[128,768]{1,0:T(8,128)(2,1)S(1)}, u32[]{:S(2)}, u32[]{:S(2)}) %collective-permute-start.13) | collective-permute-done | bytes 196640 | tf_op jit(solution)/shard_map/ppermute | solution.py:384
  210.9 0.1 fusion.11
  211.1 3.3 %collective-permute-start.16 = (bf16[128,768]{1,0:T(8,128)(2,1)S(1)}, bf16[128,768]{1,0:T(8,128)(2,1)S(1)}, u32[]{:S(2)}, u32[]{:S(2)}) collective-permute-start(bf16[128,768]{1,0:T(8,128)(2,1)S(1)} %get-tuple-element.91), channel_id=1, source_target_pairs={{0,24},{8,0},{16,8},{24,16},{1,25},{9,1},{17,9},{25,17},{2,26},{10... | collective-permute-start | bytes 589832 | tf_op jit(solution)/shard_map/ppermute | solution.py:385
  214.4 2.3 add_convert_fusion.1
  216.7 0.3 collective-permute-start.10
  217.0 13.4 %collective-permute-done.17 = bf16[128,768]{1,0:T(8,128)(2,1)S(1)} collective-permute-done((bf16[128,768]{1,0:T(8,128)(2,1)S(1)}, bf16[128,768]{1,0:T(8,128)(2,1)S(1)}, u32[]{:S(2)}, u32[]{:S(2)}) %collective-permute-start.17) | collective-permute-done | bytes 196640 | tf_op jit(solution)/shard_map/ppermute | solution.py:380
  230.4 0.9 maximum_bitcast_fusion
  231.4 2.3 fusion.2
  233.7 1.6 fusion.6
  235.3 3.1 %convert_add_fusion = f32[1,256,1536]{2,1,0:T(8,128)} fusion(bf16[1,256,1536]{2,1,0:T(8,128)(2,1)} %collective-permute-done.10, bf16[1,256,1536]{2,1,0:T(8,128)(2,1)} %collective-permute-done.6, bf16[1,256,1536]{2,1,0:T(8,128)(2,1)} %collective-permute-done.5, bf16[1,256,1536]{2,1,0:T(8,128)(2,1)S(1)} %copy-done.4), kind=kLoop, calls=%fused_computation.12 | loop fusion | flops 2752512 | bytes 4718592 | tf_op jit(solution)/shard_map/add | solution.py:479
  (51 shorter events, 0.3 us)
Async XLA Ops:
  54.2 48.3 %all-to-all-start.1 = ((bf16[8,48,4096]{2,1,0:T(8,128)(2,1)}), bf16[8,48,4096]{2,1,0:T(8,128)(2,1)}, u32[]{:S(2)}, u32[]{:S(2)}) async-start(bf16[8,48,4096]{2,1,0:T(8,128)(2,1)} %get-tuple-element.53), calls=%async_computation.1 | async-start | bytes 6291456 | tf_op jit(solution)/shard_map/all_to_all | solution.py:393
  63.8 53.6 %collective-permute-start = (bf16[2,4,256,384]{3,2,1,0:T(8,128)(2,1)}, bf16[2,4,256,384]{3,2,1,0:T(8,128)(2,1)}, u32[]{:S(2)}, u32[]{:S(2)}) collective-permute-start(bf16[2,4,256,384]{3,2,1,0:T(8,128)(2,1)} %get-tuple-element.70), channel_id=1, source_target_pairs={{0,32},{32,0},{1,33},{33,1},{2,34},{34,2},{3,35},{35,3},{4,36},{36... | collective-permute-start | bytes 4718600 | tf_op jit(solution)/shard_map/ppermute | solution.py:433
  111.2 6.1 %collective-permute-start.1 = (bf16[2,384,768]{2,1,0:T(8,128)(2,1)}, bf16[2,384,768]{2,1,0:T(8,128)(2,1)}, u32[]{:S(2)}, u32[]{:S(2)}) collective-permute-start(bf16[2,384,768]{2,1,0:T(8,128)(2,1)} %get-tuple-element.75.mine_ref.grads_ref), channel_id=1, source_target_pairs={{0,32},{32,0},{1,33},{33,1},{2,34},{34,2},{3,35},{35,3},{4,36},{36... | collective-permute-start | bytes 3538952 | tf_op jit(solution)/shard_map/ppermute | solution.py:437
  111.2 5.7 %copy-start.7 = (bf16[384,768]{1,0:T(8,128)(2,1)S(1)}, bf16[384,768]{1,0:T(8,128)(2,1)}, u32[]{:S(2)}) copy-start(bf16[384,768]{1,0:T(8,128)(2,1)} %get-tuple-element.57.hidden_ref) | copy-start | bytes 1769476
  111.2 5.8 %copy-start = (bf16[128,4096]{1,0:T(8,128)(2,1)S(1)}, bf16[128,4096]{1,0:T(8,128)(2,1)}, u32[]{:S(2)}) copy-start(bf16[128,4096]{1,0:T(8,128)(2,1)} %resid_ref) | copy-start | bytes 3145732
  116.4 18.0 %collective-permute-start.2 = (bf16[2,4,256,384]{3,2,1,0:T(8,128)(2,1)}, bf16[2,4,256,384]{3,2,1,0:T(8,128)(2,1)}, u32[]{:S(2)}, u32[]{:S(2)}) collective-permute-start(bf16[2,4,256,384]{3,2,1,0:T(8,128)(2,1)} %get-tuple-element.73), channel_id=1, source_target_pairs={{0,32},{32,0},{1,33},{33,1},{2,34},{34,2},{3,35},{35,3},{4,36},{36... | collective-permute-start | bytes 4718600 | tf_op jit(solution)/shard_map/ppermute | solution.py:440
  116.9 17.5 %collective-permute-start.3 = (bf16[384,768]{1,0:T(8,128)(2,1)S(1)}, bf16[384,768]{1,0:T(8,128)(2,1)}, u32[]{:S(2)}, u32[]{:S(2)}) collective-permute-start(bf16[384,768]{1,0:T(8,128)(2,1)S(1)} %copy-done.7), channel_id=1, source_target_pairs={{0,32},{32,0},{1,33},{33,1},{2,34},{34,2},{3,35},{35,3},{4,36},{36... | collective-permute-start | bytes 1769480 | tf_op jit(solution)/shard_map/ppermute | solution.py:435
  131.4 34.7 %collective-permute-start.4 = (bf16[1,256,1536]{2,1,0:T(8,128)(2,1)}, bf16[1,256,1536]{2,1,0:T(8,128)(2,1)}, u32[]{:S(2)}, u32[]{:S(2)}) collective-permute-start(bf16[1,256,1536]{2,1,0:T(8,128)(2,1)} %get-tuple-element.81), channel_id=1, source_target_pairs={{0,24},{8,0},{16,8},{24,16},{1,25},{9,1},{17,9},{25,17},{2,26},{10... | collective-permute-start | bytes 2359304 | tf_op jit(solution)/shard_map/ppermute | solution.py:379
  134.5 34.2 %collective-permute-start.7 = (bf16[1,256,1536]{2,1,0:T(8,128)(2,1)}, bf16[1,256,1536]{2,1,0:T(8,128)(2,1)}, u32[]{:S(2)}, u32[]{:S(2)}) collective-permute-start(bf16[1,256,1536]{2,1,0:T(8,128)(2,1)} %get-tuple-element.85), channel_id=1, source_target_pairs={{0,8},{8,16},{16,24},{24,0},{1,9},{9,17},{17,25},{25,1},{2,10},{10... | collective-permute-start | bytes 2359304 | tf_op jit(solution)/shard_map/ppermute | solution.py:378
  134.5 11.0 %copy-start.9 = (bf16[384,128]{1,0:T(8,128)(2,1)S(1)}, bf16[384,128]{1,0:T(8,128)(2,1)}, u32[]{:S(2)}) copy-start(bf16[384,128]{1,0:T(8,128)(2,1)} %get-tuple-element.78) | copy-start | bytes 294916
  142.1 36.8 %collective-permute-start.11 = (bf16[4,256,768]{2,1,0:T(8,128)(2,1)}, bf16[4,256,768]{2,1,0:T(8,128)(2,1)}, u32[]{:S(2)}, u32[]{:S(2)}) collective-permute-start(bf16[4,256,768]{2,1,0:T(8,128)(2,1)} %get-tuple-element.88), channel_id=1, source_target_pairs={{0,64},{64,0},{1,65},{65,1},{2,66},{66,2},{3,67},{67,3},{4,68},{68... | collective-permute-start | bytes 4718600 | tf_op jit(solution)/shard_map/ppermute | solution.py:447
  142.1 68.9 %collective-permute-start.9 = (bf16[1,256,1536]{2,1,0:T(8,128)(2,1)}, bf16[1,256,1536]{2,1,0:T(8,128)(2,1)}, u32[]{:S(2)}, u32[]{:S(2)}) collective-permute-start(bf16[1,256,1536]{2,1,0:T(8,128)(2,1)} %get-tuple-element.86), channel_id=1, source_target_pairs={{0,24},{8,0},{16,8},{24,16},{1,25},{9,1},{17,9},{25,17},{2,26},{10... | collective-permute-start | bytes 2359304 | tf_op jit(solution)/shard_map/ppermute | solution.py:381
  146.2 13.1 %all-to-all-start.3 = ((bf16[8,1,48]{2,1,0:T(2,128)(2,1)}), bf16[8,1,48]{2,1,0:T(2,128)(2,1)S(1)}, u32[]{:S(2)}, u32[]{:S(2)}) async-start(bf16[8,1,48]{2,1,0:T(2,128)(2,1)} %all_to_all.20), calls=%async_computation.3 | async-start | bytes 8192 | tf_op jit(solution)/shard_map/all_to_all | solution.py:393
  159.3 72.1 %all-to-all-start.2 = ((bf16[8,48,4096]{2,1,0:T(8,128)(2,1)}), bf16[8,48,4096]{2,1,0:T(8,128)(2,1)S(1)}, u32[]{:S(2)}, u32[]{:S(2)}) async-start(bf16[8,48,4096]{2,1,0:T(8,128)(2,1)} %slot_rows.1), calls=%async_computation.2 | async-start | bytes 6291456 | tf_op jit(solution)/shard_map/all_to_all | solution.py:393
  166.1 2.6 %copy-start.6 = (bf16[1,256,1536]{2,1,0:T(8,128)(2,1)S(1)}, bf16[1,256,1536]{2,1,0:T(8,128)(2,1)}, u32[]{:S(2)}) copy-start(bf16[1,256,1536]{2,1,0:T(8,128)(2,1)} %get-tuple-element.84) | copy-start | bytes 2359300
  168.7 10.2 %copy-start.2 = (bf16[4,256,768]{2,1,0:T(8,128)(2,1)S(1)}, bf16[4,256,768]{2,1,0:T(8,128)(2,1)}, u32[]{:S(2)}) copy-start(bf16[4,256,768]{2,1,0:T(8,128)(2,1)} %get-tuple-element.74) | copy-start | bytes 4718596
  180.7 0.9 copy-start.8
  180.7 2.2 copy-start.11
  180.7 9.3 %copy-start.12 = (bf16[128,2]{0,1:T(2,128)(2,1)S(1)}, bf16[128,2]{0,1:T(2,128)(2,1)}, u32[]{:S(2)}) copy-start(bf16[128,2]{0,1:T(2,128)(2,1)} %param.11) | copy-start | bytes 1540
  180.8 33.6 %copy-start.5 = (bf16[1,256,1536]{2,1,0:T(8,128)(2,1)S(1)}, bf16[1,256,1536]{2,1,0:T(8,128)(2,1)}, u32[]{:S(2)}) copy-start(bf16[1,256,1536]{2,1,0:T(8,128)(2,1)} %get-tuple-element.83) | copy-start | bytes 2359300
  180.8 9.1 %collective-permute-start.12 = (bf16[128,768]{1,0:T(8,128)(2,1)S(1)}, bf16[128,768]{1,0:T(8,128)(2,1)S(1)}, u32[]{:S(2)}, u32[]{:S(2)}) collective-permute-start(bf16[128,768]{1,0:T(8,128)(2,1)S(1)} %get-tuple-element.92), channel_id=1, source_target_pairs={{0,8},{8,16},{16,24},{24,0},{1,9},{9,17},{17,25},{25,1},{2,10},{10... | collective-permute-start | bytes 589832 | tf_op jit(solution)/shard_map/ppermute | solution.py:378
  181.7 32.6 %collective-permute-start.8 = (bf16[1,256,1536]{2,1,0:T(8,128)(2,1)S(1)}, bf16[1,256,1536]{2,1,0:T(8,128)(2,1)S(1)}, u32[]{:S(2)}, u32[]{:S(2)}) collective-permute-start(bf16[1,256,1536]{2,1,0:T(8,128)(2,1)S(1)} %add_convert_fusion.2), channel_id=1, source_target_pairs={{0,8},{8,16},{16,24},{24,0},{1,9},{9,17},{17,25},{25,1},{2,10},{10... | collective-permute-start | bytes 2359304 | tf_op jit(solution)/shard_map/ppermute | solution.py:384
  183.0 8.4 %collective-permute-start.14 = (bf16[128,768]{1,0:T(8,128)(2,1)S(1)}, bf16[128,768]{1,0:T(8,128)(2,1)S(1)}, u32[]{:S(2)}, u32[]{:S(2)}) collective-permute-start(bf16[128,768]{1,0:T(8,128)(2,1)S(1)} %get-tuple-element.95), channel_id=1, source_target_pairs={{0,24},{8,0},{16,8},{24,16},{1,25},{9,1},{17,9},{25,17},{2,26},{10... | collective-permute-start | bytes 589832 | tf_op jit(solution)/shard_map/ppermute | solution.py:381
  185.3 8.1 %collective-permute-start.15 = (bf16[128,768]{1,0:T(8,128)(2,1)S(1)}, bf16[128,768]{1,0:T(8,128)(2,1)S(1)}, u32[]{:S(2)}, u32[]{:S(2)}) collective-permute-start(bf16[128,768]{1,0:T(8,128)(2,1)S(1)} %get-tuple-element.94), channel_id=1, source_target_pairs={{0,24},{8,0},{16,8},{24,16},{1,25},{9,1},{17,9},{25,17},{2,26},{10... | collective-permute-start | bytes 589832 | tf_op jit(solution)/shard_map/ppermute | solution.py:379
  189.9 21.0 %collective-permute-start.13 = (bf16[128,768]{1,0:T(8,128)(2,1)S(1)}, bf16[128,768]{1,0:T(8,128)(2,1)S(1)}, u32[]{:S(2)}, u32[]{:S(2)}) collective-permute-start(bf16[128,768]{1,0:T(8,128)(2,1)S(1)} %fusion.10), channel_id=1, source_target_pairs={{0,8},{8,16},{16,24},{24,0},{1,9},{9,17},{17,25},{25,1},{2,10},{10... | collective-permute-start | bytes 589832 | tf_op jit(solution)/shard_map/ppermute | solution.py:384
  191.3 44.0 %collective-permute-start.6 = (bf16[1,256,1536]{2,1,0:T(8,128)(2,1)}, bf16[1,256,1536]{2,1,0:T(8,128)(2,1)}, u32[]{:S(2)}, u32[]{:S(2)}) collective-permute-start(bf16[1,256,1536]{2,1,0:T(8,128)(2,1)} %get-tuple-element.82), channel_id=1, source_target_pairs={{0,8},{8,16},{16,24},{24,0},{1,9},{9,17},{17,25},{25,1},{2,10},{10... | collective-permute-start | bytes 2359304 | tf_op jit(solution)/shard_map/ppermute | solution.py:380
  193.5 41.9 %collective-permute-start.5 = (bf16[1,256,1536]{2,1,0:T(8,128)(2,1)}, bf16[1,256,1536]{2,1,0:T(8,128)(2,1)}, u32[]{:S(2)}, u32[]{:S(2)}) collective-permute-start(bf16[1,256,1536]{2,1,0:T(8,128)(2,1)} %add_convert_fusion.3), channel_id=1, source_target_pairs={{0,24},{8,0},{16,8},{24,16},{1,25},{9,1},{17,9},{25,17},{2,26},{10... | collective-permute-start | bytes 2359304 | tf_op jit(solution)/shard_map/ppermute | solution.py:385
  210.9 19.4 %collective-permute-start.17 = (bf16[128,768]{1,0:T(8,128)(2,1)S(1)}, bf16[128,768]{1,0:T(8,128)(2,1)S(1)}, u32[]{:S(2)}, u32[]{:S(2)}) collective-permute-start(bf16[128,768]{1,0:T(8,128)(2,1)S(1)} %get-tuple-element.93), channel_id=1, source_target_pairs={{0,8},{8,16},{16,24},{24,0},{1,9},{9,17},{17,25},{25,1},{2,10},{10... | collective-permute-start | bytes 589832 | tf_op jit(solution)/shard_map/ppermute | solution.py:380
  211.1 19.3 %collective-permute-start.16 = (bf16[128,768]{1,0:T(8,128)(2,1)S(1)}, bf16[128,768]{1,0:T(8,128)(2,1)S(1)}, u32[]{:S(2)}, u32[]{:S(2)}) collective-permute-start(bf16[128,768]{1,0:T(8,128)(2,1)S(1)} %get-tuple-element.91), channel_id=1, source_target_pairs={{0,24},{8,0},{16,8},{24,16},{1,25},{9,1},{17,9},{25,17},{2,26},{10... | collective-permute-start | bytes 589832 | tf_op jit(solution)/shard_map/ppermute | solution.py:385
  216.7 14.7 %copy-start.10 = (f32[4096]{0:T(1024)S(1)}, f32[4096]{0:T(1024)}, u32[]{:S(2)}) copy-start(f32[4096]{0:T(1024)} %param.8) | copy-start | bytes 49156
  216.7 18.6 %collective-permute-start.10 = (bf16[1,256,1536]{2,1,0:T(8,128)(2,1)}, bf16[1,256,1536]{2,1,0:T(8,128)(2,1)}, u32[]{:S(2)}, u32[]{:S(2)}) collective-permute-start(bf16[1,256,1536]{2,1,0:T(8,128)(2,1)} %add_convert_fusion.1), channel_id=1, source_target_pairs={{0,64},{64,0},{1,65},{65,1},{2,66},{66,2},{3,67},{67,3},{4,68},{68... | collective-permute-start | bytes 2359304 | tf_op jit(solution)/shard_map/ppermute | solution.py:449
  231.3 2.3 copy-start.1
  231.3 2.3 copy-start.3
  233.7 1.6 copy-start.4

commit v7 on v6

--- a/solution.py
+++ b/solution.py
@@ -50,10 +50,13 @@
     )
 
 
-def pack_kernel(
-    ids_ref, w_ref, gain_ref, resid_ref, grad_ref, normed_ref, scaled_ref, sel_ref, inv_ref, scale_ref
-):
-    experts, capacity, block = normed_ref.shape
+def shifted(expert, step, sign):
+    return (expert // 2 + sign * (step // 2) + 4) % 4 * 2 + (expert + step) % 2
+
+
+def pack_kernel(place_ref, ids_ref, w_ref, gain_ref, resid_ref, grad_ref, *out_refs):
+    *normed_refs, scaled_ref, sel_ref, inv_ref, scale_ref, turned_ref = out_refs
+    experts, capacity, block = scaled_ref.shape
 
     @pl.when(pl.program_id(0) == 0)
     def _():
@@ -63,45 +66,80 @@
         select, scale = slot_matrices(ids_ref[...], w_ref[...].astype(jnp.float32), experts, capacity)
         sel_ref[...] = select
         scale_ref[...] = scale
+        for step in range(experts):
+            start = pl.multiple_of(shifted(place_ref[3], step, 1) * capacity, 16)
+            turned_ref[step * capacity : (step + 1) * capacity] = sel_ref[pl.ds(start, capacity)]
 
     at = pl.ds(pl.multiple_of(pl.program_id(0) * block, block), block)
     unit = resid_ref[:, at].astype(jnp.float32) * inv_ref[...]
     normed = (unit * gain_ref[:, at]).astype(jnp.bfloat16)
-    sent = contract(sel_ref[...], normed, 1, 0).astype(jnp.bfloat16)
-    normed_ref[...] = sent.reshape(experts, capacity, block)
+    sent = contract(turned_ref[...], normed, 1, 0).astype(jnp.bfloat16)
+    for step in range(experts):
+        normed_refs[step][...] = sent[step * capacity : (step + 1) * capacity]
     sent = contract(scale_ref[...], grad_ref[:, at], 1, 0).astype(jnp.bfloat16)
     scaled_ref[...] = sent.reshape(experts, capacity, block)
 
 
-def pack(ids_t, w_t, gain, resid, grad, experts, capacity, block=1024):
+def pack(place, ids_t, w_t, gain, resid, grad, experts, capacity, block=1024):
     rows, width = resid.shape
-    whole = lambda a: pl.BlockSpec(a.shape, lambda j: (0,) * a.ndim)
     args = (ids_t, w_t, gain, resid, grad)
     slots = experts * capacity
     return pl.pallas_call(
         pack_kernel,
-        grid=(width // block,),
-        in_specs=[whole(a) for a in args],
-        out_specs=[
-            pl.BlockSpec((experts, capacity, block), lambda j: (0, 0, j)),
-            pl.BlockSpec((experts, capacity, block), lambda j: (0, 0, j)),
-            pl.BlockSpec((slots, rows), lambda j: (0, 0)),
-        ],
-        out_shape=[
-            jax.ShapeDtypeStruct((experts, capacity, width), jnp.bfloat16),
+        grid_spec=pltpu.PrefetchScalarGridSpec(
+            num_scalar_prefetch=1,
+            grid=(width // block,),
+            in_specs=[pl.BlockSpec(a.shape, lambda j, _: (0, 0)) for a in args],
+            out_specs=[pl.BlockSpec((capacity, block), lambda j, _: (0, j))] * experts
+            + [
+                pl.BlockSpec((experts, capacity, block), lambda j, _: (0, 0, j)),
+                pl.BlockSpec((slots, rows), lambda j, _: (0, 0)),
+            ],
+            scratch_shapes=[
+                pltpu.VMEM((rows, 1), jnp.float32),
+                pltpu.VMEM((slots, rows), jnp.bfloat16),
+                pltpu.VMEM((slots, rows), jnp.bfloat16),
+            ],
+        ),
+        out_shape=[jax.ShapeDtypeStruct((capacity, width), jnp.bfloat16)] * experts
+        + [
             jax.ShapeDtypeStruct((experts, capacity, width), jnp.bfloat16),
             jax.ShapeDtypeStruct((slots, rows), jnp.bfloat16),
         ],
-        scratch_shapes=[
-            pltpu.VMEM((rows, 1), jnp.float32),
-            pltpu.VMEM((slots, rows), jnp.bfloat16),
-        ],
         compiler_params=pltpu.CompilerParams(vmem_limit_bytes=VMEM),
         cost_estimate=pl.CostEstimate(
             flops=4 * slots * rows * width, bytes_accessed=4 * slots * width, transcendentals=0
         ),
         name="pack",
-    )(*args)
+    )(place, *args)
+
+
+def gather_kernel(place_ref, *refs):
+    *block_refs, out_ref = refs
+    for step, block_ref in enumerate(block_refs):
+        out_ref[shifted(place_ref[3], step, -1)] = block_ref[...]
+
+
+def gather(place, blocks, block=1024):
+    capacity, width = blocks[0].shape
+    experts = len(blocks)
+    return pl.pallas_call(
+        gather_kernel,
+        grid_spec=pltpu.PrefetchScalarGridSpec(
+            num_scalar_prefetch=1,
+            grid=(width // block,),
+            in_specs=[pl.BlockSpec((capacity, block), lambda j, _: (0, j))] * experts,
+            out_specs=pl.BlockSpec((experts, capacity, block), lambda j, _: (0, 0, j)),
+        ),
+        out_shape=jax.ShapeDtypeStruct((experts, capacity, width), jnp.bfloat16),
+        compiler_params=pltpu.CompilerParams(vmem_limit_bytes=VMEM),
+        cost_estimate=pl.CostEstimate(
+            flops=experts * capacity * width * 256,
+            bytes_accessed=4 * experts * capacity * width,
+            transcendentals=0,
+        ),
+        name="gather",
+    )(place, *blocks)
 
 
 def forward_kernel(got_ref, gate_w_ref, up_w_ref, hidden_ref, gate_ref, up_ref):
@@ -289,39 +327,35 @@
 
 def messages_kernel(_, keep_ref, came_ref, mine_ref, theirs_ref, *out_refs):
     block, slots = keep_ref.shape[2:]
-    unit = pl.program_id(1)
+    units, _, width = mine_ref.shape
     keep, came = keep_ref[...].reshape(2 * block, slots), came_ref[...].reshape(2 * block, slots)
-    rows = contract(keep, mine_ref[unit], 1, 0) + contract(came, theirs_ref[unit], 1, 0)
-    rows = rows.astype(jnp.bfloat16)
-    for at in range(len(SEND_ORDER)):
-
-        @pl.when(pl.program_id(0) == at)
-        def _():
-            out_refs[2 * at][0] = rows[:block]
-            out_refs[2 * at + 1][0] = rows[block:]
+    for unit in range(units):
+        columns = slice(unit * width, (unit + 1) * width)
+        rows = contract(keep, mine_ref[unit], 1, 0) + contract(came, theirs_ref[unit], 1, 0)
+        rows = rows.astype(jnp.bfloat16)
+        for at in range(len(SEND_ORDER)):
+
+            @pl.when(pl.program_id(0) == at)
+            def _():
+                out_refs[2 * at][0, :, columns] = rows[:block]
+                out_refs[2 * at + 1][0, :, columns] = rows[block:]
 
 
 def weight_messages(place, keep, came, mine, theirs):
     _, rings, block, slots = keep.shape
     units, _, width = mine.shape
     left = pl.BlockSpec(
-        (2, 1, block, slots), lambda i, u, at: (0, lax.rem(at[2] + ring_at(i), rings), 0, 0)
-    )
-    right = pl.BlockSpec(mine.shape, lambda i, u, at: (0, 0, 0))
-
-    def out(k):
-        return pl.BlockSpec(
-            (1, block, width),
-            lambda i, u, at: (0, 0, jnp.where(i == k, u, jnp.where(i < k, 0, units - 1))),
-        )
-
+        (2, 1, block, slots), lambda i, at: (0, lax.rem(at[2] + ring_at(i), rings), 0, 0)
+    )
+    right = pl.BlockSpec(mine.shape, lambda i, at: (0, 0, 0))
     outs = pl.pallas_call(
         messages_kernel,
         grid_spec=pltpu.PrefetchScalarGridSpec(
             num_scalar_prefetch=1,
-            grid=(rings, units),
+            grid=(rings,),
             in_specs=[left, left, right, right],
-            out_specs=[out(k) for k in range(rings) for _ in range(2)],
+            out_specs=[pl.BlockSpec((1, block, units * width), lambda i, at: (0, 0, 0))]
+            * (2 * rings),
         ),
         out_shape=[jax.ShapeDtypeStruct((1, block, units * width), jnp.bfloat16)] * (2 * rings),
         compiler_params=pltpu.CompilerParams(vmem_limit_bytes=VMEM),
@@ -365,6 +399,16 @@
         ),
         name="slot_rows",
     )(grads, w_in)
+
+
+def displaced(rows, step):
+    experts = lax.axis_size("expert")
+    pairs = [
+        (side * experts + e, (side + step) % 2 * experts + shifted(e, step, 1))
+        for side in range(2)
+        for e in range(experts)
+    ]
+    return lax.ppermute(rows, ("dp_0", "expert"), pairs)
 
 
 def added(*terms):
@@ -414,19 +458,20 @@
     ids_t = expert_ids.T
     weights_t = route_weights.T
     place, residual = lax.optimization_barrier(
-        (jnp.stack([side, core, lax.axis_index("ulysses")]).astype(jnp.int32), residual)
-    )
-
-    send_normed, send_scaled, select = pack(
-        ids_t, weights_t, norm_gain[None], residual, grad_out, experts, capacity
-    )
-    got_normed = exchange(send_normed)
-    (got_normed, place, ids_t, weights_t, residual, grad_out, norm_gain, weight_in, weight_down) = (
-        lax.optimization_barrier(
-            (got_normed, place, ids_t, weights_t, residual, grad_out, norm_gain, weight_in, weight_down)
+        (
+            jnp.stack([side, core, lax.axis_index("ulysses"), lax.axis_index("expert")]).astype(
+                jnp.int32
+            ),
+            residual,
         )
     )
+
+    *send_normed, send_scaled, select = pack(
+        place, ids_t, weights_t, norm_gain[None], residual, grad_out, experts, capacity
+    )
+    blocks = send_normed[:1] + [displaced(send_normed[k], k) for k in range(1, experts)]
     got_scaled = exchange(send_scaled)
+    got_normed = gather(place, blocks)
     w_in = weight_in[0]
     w_down = weight_down[0]
     keep_normed, give_normed = turn(place, got_normed, rings, span)

time: 240 us -> 268 us (1.12)
  blocking collectives: 47 us -> 0 us
  waiting for transfers between devices: 68.7 us -> 112 us
  starting transfers between devices: 35.6 us -> 58.9 us
  Pallas kernels: 67 us -> 74.6 us
    ppermute x0 -> x7, waiting for transfers between devices: none -> 68.3 us  [displaced(): return lax.ppermute(rows, ('dp_0', 'expert'), pairs)]
    all_to_all x1 -> x0, blocking collectives: 47 us -> none  [exchange(): lax.all_to_all(rows, ('dp_0', 'expert'), split_axis=0, concat_axis=0, axi...]
    all_to_all x3, waiting for transfers between devices: 28.2 us -> 0.01 us  [exchange(): lax.all_to_all(rows, ('dp_0', 'expert'), split_axis=0, concat_axis=0, axi...]
    ppermute x0 -> x7, starting transfers between devices: none -> 21.2 us  [displaced(): return lax.ppermute(rows, ('dp_0', 'expert'), pairs)]
    pallas_call x1 -> x2, Pallas kernels: 5.97 us -> 11.6 us  [the longest x1 6.47 us: pack(): pl.pallas_call(pack_kernel, grid_spec=pltpu.PrefetchScalarGridSpec(num_sc...]
    all_to_all x3, starting transfers between devices: 14.5 us -> 18.1 us  [exchange(): lax.all_to_all(rows, ('dp_0', 'expert'), split_axis=0, concat_axis=0, axi...]
  transfers between devices with their start and end apart: 21 -> 28, of which waited for: 7 -> 10; matrix products, arithmetic and copies ran while one was open for 6% -> 5% of each run, Pallas kernels for 26% -> 25%
where the time goes in v7:
time: 268 us; the launch traced here: 267 us
  waiting for transfers between devices  112 us (42%)
  Pallas kernels  74.6 us (28%)
  starting transfers between devices  58.9 us (22%)
  other arithmetic  15.6 us (6%)
  local copies, waits for them, and re-layouts  3.16 us (1%)
    ppermute x7, waiting for transfers between devices, displaced(): return lax.ppermute(rows, ('dp_0', 'expert'), pairs)  68.3 us
    ppermute x7, starting transfers between devices, displaced(): return lax.ppermute(rows, ('dp_0', 'expert'), pairs)  21.2 us
    all_to_all x3, starting transfers between devices, exchange(): lax.all_to_all(rows, ('dp_0', 'expert'), split_axis=0, concat_axis=0, axi...  18.1 us
    pallas_call x1, Pallas kernels, weight_messages(): pl.pallas_call(messages_kernel, grid_spec=pltpu.PrefetchScalarGridSpec(nu...  16 us
    ppermute x2, waiting for transfers between devices, ring_sum(): low_last = lax.ppermute(low_both, 'ulysses', ahead)  15.5 us
    ppermute x2, waiting for transfers between devices, ring_sum(): high_side = lax.ppermute(high[1], 'ulysses', ahead)  12.4 us
    ppermute x1, waiting for transfers between devices, per_device(): came_down = lax.ppermute(far_down, 'dp_0', SWAP)  11.1 us
    pallas_call x1, Pallas kernels, forward(): pl.pallas_call(forward_kernel, grid=(steps,), in_specs=[pl.BlockSpec(got....  10.5 us
  transfers between devices with their start and end apart: 28, of which 10 were waited for; matrix products, arithmetic and copies ran while one was open for 5% of the time, Pallas kernels for 25%

profile of v7, /device:TPU:0, one launch (start us, length us, event | category | flops | bytes accessed | tf_op | source)
XLA Modules:
  0.0 267.2 jit_solution(10933334268668023453)
XLA Ops:
  0.6 0.6 pad_add_fusion.place_ref._
  1.2 6.5 %pack.1 = (bf16[48,4096]{1,0:T(8,128)(2,1)}, bf16[48,4096]{1,0:T(8,128)(2,1)}, bf16[48,4096]{1,0:T(8,128)(2,1)}, bf16[48,4096]{1,0:T(8,128)(2,1)}, bf16[48,4096]...) custom-call(s32[4]{0:T(128)} %pad_add_fusion.place_ref._, ...), custom_call_target="tpu_custom_call" | custom-call | flops 805306368 | bytes 6291456 | tf_op jit(solution)/shard_map/pack/pallas_call | solution.py:87
  7.7 8.0 %all-to-all-start = ((bf16[8,48,4096]{2,1,0:T(8,128)(2,1)}), bf16[8,48,4096]{2,1,0:T(8,128)(2,1)}, u32[]{:S(2)}, u32[]{:S(2)}) async-start(bf16[8,48,4096]{2,1,0:T(8,128)(2,1)} %get-tuple-element.48), calls=%async_computation | async-start | bytes 6291456 | tf_op jit(solution)/shard_map/all_to_all | solution.py:437
  15.8 3.2 %collective-permute-start = (bf16[48,4096]{1,0:T(8,128)(2,1)}, bf16[48,4096]{1,0:T(8,128)(2,1)S(1)}, u32[]{:S(2)}, u32[]{:S(2)}) collective-permute-start(bf16[48,4096]{1,0:T(8,128)(2,1)} %get-tuple-element.50), channel_id=1, source_target_pairs={{0,65},{1,64},{2,67},{3,66},{4,69},{5,68},{6,71},{7,70},{64,1},{65... | collective-permute-start | bytes 1179656 | tf_op jit(solution)/shard_map/ppermute | solution.py:411
  19.0 1.5 collective-permute-start.1
  20.5 1.5 collective-permute-start.2
  21.9 1.2 collective-permute-start.3
  23.2 4.4 %collective-permute-start.4 = (bf16[48,4096]{1,0:T(8,128)(2,1)S(1)}, bf16[48,4096]{1,0:T(8,128)(2,1)S(1)}, u32[]{:S(2)}, u32[]{:S(2)}) collective-permute-start(bf16[48,4096]{1,0:T(8,128)(2,1)S(1)} %copy-done.21), channel_id=1, source_target_pairs={{0,69},{1,68},{2,71},{3,70},{4,65},{5,64},{6,67},{7,66},{64,5},{65... | collective-permute-start | bytes 1179656 | tf_op jit(solution)/shard_map/ppermute | solution.py:411
  27.6 33.9 %collective-permute-done.refs_1_ = bf16[48,4096]{1,0:T(8,128)(2,1)S(1)} collective-permute-done((bf16[48,4096]{1,0:T(8,128)(2,1)}, bf16[48,4096]{1,0:T(8,128)(2,1)S(1)}, u32[]{:S(2)}, u32[]{:S(2)}) %collective-permute-start) | collective-permute-done | bytes 393248 | tf_op jit(solution)/shard_map/ppermute | solution.py:411
  61.5 2.7 %collective-permute-start.5 = (bf16[48,4096]{1,0:T(8,128)(2,1)S(1)}, bf16[48,4096]{1,0:T(8,128)(2,1)}, u32[]{:S(2)}, u32[]{:S(2)}) collective-permute-start(bf16[48,4096]{1,0:T(8,128)(2,1)S(1)} %copy-done.20), channel_id=1, source_target_pairs={{0,6},{1,7},{2,0},{3,1},{4,2},{5,3},{6,4},{7,5},{64,70},{65,71},{6... | collective-permute-start | bytes 1179656 | tf_op jit(solution)/shard_map/ppermute | solution.py:411
  64.1 2.2 collective-permute-done.1.refs_2_
  66.3 6.7 %collective-permute-start.6 = (bf16[48,4096]{1,0:T(8,128)(2,1)S(1)}, bf16[48,4096]{1,0:T(8,128)(2,1)}, u32[]{:S(2)}, u32[]{:S(2)}) collective-permute-start(bf16[48,4096]{1,0:T(8,128)(2,1)S(1)} %copy-done.19), channel_id=1, source_target_pairs={{0,71},{1,70},{2,65},{3,64},{4,67},{5,66},{6,69},{7,68},{64,7},{65... | collective-permute-start | bytes 1179656 | tf_op jit(solution)/shard_map/ppermute | solution.py:411
  73.0 4.7 %collective-permute-done.2.refs_3_ = bf16[48,4096]{1,0:T(8,128)(2,1)S(1)} collective-permute-done((bf16[48,4096]{1,0:T(8,128)(2,1)}, bf16[48,4096]{1,0:T(8,128)(2,1)S(1)}, u32[]{:S(2)}, u32[]{:S(2)}) %collective-permute-start.2) | collective-permute-done | bytes 393248 | tf_op jit(solution)/shard_map/ppermute | solution.py:411
  77.7 17.2 %collective-permute-done.3.refs_4_ = bf16[48,4096]{1,0:T(8,128)(2,1)S(1)} collective-permute-done((bf16[48,4096]{1,0:T(8,128)(2,1)}, bf16[48,4096]{1,0:T(8,128)(2,1)S(1)}, u32[]{:S(2)}, u32[]{:S(2)}) %collective-permute-start.3) | collective-permute-done | bytes 393248 | tf_op jit(solution)/shard_map/ppermute | solution.py:411
  94.9 10.4 %collective-permute-done.4.refs_5_ = bf16[48,4096]{1,0:T(8,128)(2,1)S(1)} collective-permute-done((bf16[48,4096]{1,0:T(8,128)(2,1)S(1)}, bf16[48,4096]{1,0:T(8,128)(2,1)S(1)}, u32[]{:S(2)}, u32[]{:S(2)}) %collective-permute-start.4) | collective-permute-done | bytes 393248 | tf_op jit(solution)/shard_map/ppermute | solution.py:411
  105.3 0.7 copy-done.12
  106.0 5.1 %gather.1.got_ref.keep_ref.give_ref = bf16[8,48,4096]{2,1,0:T(8,128)(2,1)} custom-call(s32[4]{0:T(128)} %pad_add_fusion.place_ref._, bf16[48,4096]{1,0:T(8,128)(2,1)} %get-tuple-element.49.refs_0_, bf16[48,4096]{1,0:T(8,128)(2,1)} %copy-done.8, bf16[48,4096]{1,0:T(8,128)(2,1)} %copy-done.9, bf16[48,4096]{1,0:T(8,128)(2,1)} %copy-done.10, ...), custom_call_target="tpu_custom_call" | custom-call | flops 402653184 | bytes 6291456 | tf_op jit(solution)/shard_map/gather/pallas_call | solution.py:126
  111.2 5.1 %turn.2 = (bf16[2,4,256,384]{3,2,1,0:T(8,128)(2,1)}, bf16[2,4,256,384]{3,2,1,0:T(8,128)(2,1)}) custom-call(s32[4]{0:T(128)} %pad_add_fusion.place_ref._, bf16[8,48,4096]{2,1,0:T(8,128)(2,1)} %gather.1.got_ref.keep_ref.give_ref, bf16[8,48,4096]{2,1,0:T(8,128)(2,1)} %gather.1.got_ref.keep_ref.give_ref), custom_call_target="tpu_custom_call" | custom-call | flops 1610612736 | bytes 6291456 | tf_op jit(solution)/shard_map/turn/pallas_call | solution.py:257
  116.2 10.5 %forward.1 = (bf16[384,768]{1,0:T(8,128)(2,1)}, f32[384,768]{1,0:T(8,128)}, f32[384,768]{1,0:T(8,128)}) custom-call(bf16[8,48,4096]{2,1,0:T(8,128)(2,1)} %gather.1.got_ref.keep_ref.give_ref, bf16[4096,1536]{1,0:T(8,128)(2,1)} %bitcast.51, bf16[4096,1536]{1,0:T(8,128)(2,1)} %bitcast.52), custom_call_target="tpu_custom_call" | custom-call | flops 4831838208 | bytes 15728640 | tf_op jit(solution)/shard_map/forward/pallas_call | solution.py:163
  126.7 8.7 %back.1 = (bf16[2,384,768]{2,1,0:T(8,128)(2,1)}, bf16[384,128]{1,0:T(8,128)(2,1)}) custom-call(bf16[8,48,4096]{2,1,0:T(8,128)(2,1)} %all-to-all-done.got_ref.keep_ref.give_ref, bf16[768,4096]{1,0:T(8,128)(2,1)} %bitcast.55, bf16[384,768]{1,0:T(8,128)(2,1)} %get-tuple-element.57.hidden_ref, f32[384,768]{1,0:T(8,128)} %get-tuple-element.58.gate_ref, ...), custom_call_target="tpu_custom_call" | custom-call | flops 2415919104 | bytes 12386304 | tf_op jit(solution)/shard_map/back/pallas_call | solution.py:211
  135.9 5.3 %turn.3 = (bf16[2,4,256,384]{3,2,1,0:T(8,128)(2,1)}, bf16[2,4,256,384]{3,2,1,0:T(8,128)(2,1)}) custom-call(s32[4]{0:T(128)} %pad_add_fusion.place_ref._, bf16[8,48,4096]{2,1,0:T(8,128)(2,1)} %all-to-all-done.got_ref.keep_ref.give_ref, bf16[8,48,4096]{2,1,0:T(8,128)(2,1)} %all-to-all-done.got_ref.keep_ref.give_ref), custom_call_target="tpu_custom_call" | custom-call | flops 1610612736 | bytes 6291456 | tf_op jit(solution)/shard_map/turn/pallas_call | solution.py:257
  142.1 16.0 %grad_in.1 = (bf16[1,256,1536]{2,1,0:T(8,128)(2,1)}, bf16[1,256,1536]{2,1,0:T(8,128)(2,1)}, bf16[1,256,1536]{2,1,0:T(8,128)(2,1)}, bf16[1,256,1536]{2,1,0:T(8,12...) custom-call(s32[4]{0:T(128)} %pad_add_fusion.place_ref._, ...), custom_call_target="tpu_custom_call" | custom-call | flops 4831838208 | bytes 11796480 | tf_op jit(solution)/shard_map/grad_in/pallas_call | solution.py:351
  158.1 3.0 %collective-permute-start.11 = (bf16[1,256,1536]{2,1,0:T(8,128)(2,1)}, bf16[1,256,1536]{2,1,0:T(8,128)(2,1)}, u32[]{:S(2)}, u32[]{:S(2)}) collective-permute-start(bf16[1,256,1536]{2,1,0:T(8,128)(2,1)} %get-tuple-element.77), channel_id=1, source_target_pairs={{0,24},{8,0},{16,8},{24,16},{1,25},{9,1},{17,9},{25,17},{2,26},{10... | collective-permute-start | bytes 2359304 | tf_op jit(solution)/shard_map/ppermute | solution.py:423
  161.1 3.2 %collective-permute-start.16 = (bf16[1,256,1536]{2,1,0:T(8,128)(2,1)}, bf16[1,256,1536]{2,1,0:T(8,128)(2,1)}, u32[]{:S(2)}, u32[]{:S(2)}) collective-permute-start(bf16[1,256,1536]{2,1,0:T(8,128)(2,1)} %get-tuple-element.82), channel_id=1, source_target_pairs={{0,24},{8,0},{16,8},{24,16},{1,25},{9,1},{17,9},{25,17},{2,26},{10... | collective-permute-start | bytes 2359304 | tf_op jit(solution)/shard_map/ppermute | solution.py:425
  164.3 0.8 copy-done.18
  165.1 7.7 %shard_map.102 = (bf16[4,256,768]{2,1,0:T(8,128)(2,1)}, bf16[4,256,768]{2,1,0:T(8,128)(2,1)}) custom-call(s32[4]{0:T(128)} %pad_add_fusion.place_ref._, bf16[2,4,256,384]{3,2,1,0:T(8,128)(2,1)} %get-tuple-element.71.keep_ref, bf16[2,4,256,384]{3,2,1,0:T(8,128)(2,1)} %collective-permute-done.9.came_ref, bf16[1,384,768]{2,1,0:T(8,128)(2,1)} %bitcast.56, ...), custom_call_target="tpu_custom_call" | custom-call | flops 2415919104 | bytes 7471104 | tf_op jit(solution)/shard_map/pallas_call | solution.py:300
  172.9 0.7 all_to_all.16
  173.6 3.2 %all-to-all-start.2 = ((bf16[8,1,48]{2,1,0:T(2,128)(2,1)}), bf16[8,1,48]{2,1,0:T(2,128)(2,1)S(1)}, u32[]{:S(2)}, u32[]{:S(2)}) async-start(bf16[8,1,48]{2,1,0:T(2,128)(2,1)} %all_to_all.16), calls=%async_computation.2 | async-start | bytes 8192 | tf_op jit(solution)/shard_map/all_to_all | solution.py:437
  176.9 9.8 %slot_rows.1 = bf16[8,48,4096]{2,1,0:T(8,128)(2,1)} custom-call(bf16[2,384,768]{2,1,0:T(8,128)(2,1)} %get-tuple-element.74.mine_ref.grads_ref, bf16[4096,1536]{1,0:T(8,128)(2,1)} %bitcast.53), custom_call_target="tpu_custom_call" | custom-call | flops 4831838208 | bytes 15728640 | tf_op jit(solution)/shard_map/slot_rows/pallas_call | solution.py:385
  186.7 6.8 %all-to-all-start.1 = ((bf16[8,48,4096]{2,1,0:T(8,128)(2,1)}), bf16[8,48,4096]{2,1,0:T(8,128)(2,1)S(1)}, u32[]{:S(2)}, u32[]{:S(2)}) async-start(bf16[8,48,4096]{2,1,0:T(8,128)(2,1)} %slot_rows.1), calls=%async_computation.1 | async-start | bytes 6291456 | tf_op jit(solution)/shard_map/all_to_all | solution.py:437
  193.6 2.5 add_convert_fusion.3
  196.1 1.4 add_convert_fusion.2
  197.5 11.1 %collective-permute-done.18 = bf16[4,256,768]{2,1,0:T(8,128)(2,1)} collective-permute-done((bf16[4,256,768]{2,1,0:T(8,128)(2,1)}, bf16[4,256,768]{2,1,0:T(8,128)(2,1)}, u32[]{:S(2)}, u32[]{:S(2)}) %collective-permute-start.18) | collective-permute-done | bytes 1572896 | tf_op jit(solution)/shard_map/ppermute | solution.py:492
  208.6 1.8 add_convert_fusion
  210.6 0.7 copy-done.13
  211.6 3.3 %collective-permute-start.21 = (bf16[128,768]{1,0:T(8,128)(2,1)S(1)}, bf16[128,768]{1,0:T(8,128)(2,1)S(1)}, u32[]{:S(2)}, u32[]{:S(2)}) collective-permute-start(bf16[128,768]{1,0:T(8,128)(2,1)S(1)} %get-tuple-element.91), channel_id=1, source_target_pairs={{0,24},{8,0},{16,8},{24,16},{1,25},{9,1},{17,9},{25,17},{2,26},{10... | collective-permute-start | bytes 589832 | tf_op jit(solution)/shard_map/ppermute | solution.py:425
  214.9 1.3 collective-permute-start.22
  216.2 3.4 %collective-permute-done.19 = bf16[128,768]{1,0:T(8,128)(2,1)S(1)} collective-permute-done((bf16[128,768]{1,0:T(8,128)(2,1)S(1)}, bf16[128,768]{1,0:T(8,128)(2,1)S(1)}, u32[]{:S(2)}, u32[]{:S(2)}) %collective-permute-start.19) | collective-permute-done | bytes 196640 | tf_op jit(solution)/shard_map/ppermute | solution.py:422
  220.5 1.0 collective-permute-done.22
  221.5 3.6 %collective-permute-start.12 = (bf16[1,256,1536]{2,1,0:T(8,128)(2,1)}, bf16[1,256,1536]{2,1,0:T(8,128)(2,1)}, u32[]{:S(2)}, u32[]{:S(2)}) collective-permute-start(bf16[1,256,1536]{2,1,0:T(8,128)(2,1)} %add_convert_fusion.3), channel_id=1, source_target_pairs={{0,24},{8,0},{16,8},{24,16},{1,25},{9,1},{17,9},{25,17},{2,26},{10... | collective-permute-start | bytes 2359304 | tf_op jit(solution)/shard_map/ppermute | solution.py:429
  225.2 15.5 %collective-permute-done.20 = bf16[128,768]{1,0:T(8,128)(2,1)S(1)} collective-permute-done((bf16[128,768]{1,0:T(8,128)(2,1)S(1)}, bf16[128,768]{1,0:T(8,128)(2,1)S(1)}, u32[]{:S(2)}, u32[]{:S(2)}) %collective-permute-start.20) | collective-permute-done | bytes 196640 | tf_op jit(solution)/shard_map/ppermute | solution.py:428
  240.8 3.3 %collective-permute-start.23 = (bf16[128,768]{1,0:T(8,128)(2,1)S(1)}, bf16[128,768]{1,0:T(8,128)(2,1)S(1)}, u32[]{:S(2)}, u32[]{:S(2)}) collective-permute-start(bf16[128,768]{1,0:T(8,128)(2,1)S(1)} %get-tuple-element.87), channel_id=1, source_target_pairs={{0,24},{8,0},{16,8},{24,16},{1,25},{9,1},{17,9},{25,17},{2,26},{10... | collective-permute-start | bytes 589832 | tf_op jit(solution)/shard_map/ppermute | solution.py:429
  244.1 2.3 add_convert_fusion.1
  246.7 12.4 %collective-permute-done.24 = bf16[128,768]{1,0:T(8,128)(2,1)S(1)} collective-permute-done((bf16[128,768]{1,0:T(8,128)(2,1)S(1)}, bf16[128,768]{1,0:T(8,128)(2,1)S(1)}, u32[]{:S(2)}, u32[]{:S(2)}) %collective-permute-start.24) | collective-permute-done | bytes 196640 | tf_op jit(solution)/shard_map/ppermute | solution.py:424
  259.2 0.9 maximum_bitcast_fusion
  260.1 2.3 fusion.2
  262.5 1.6 fusion.6
  264.1 3.1 %convert_add_fusion = f32[1,256,1536]{2,1,0:T(8,128)} fusion(bf16[1,256,1536]{2,1,0:T(8,128)(2,1)} %collective-permute-done.17, bf16[1,256,1536]{2,1,0:T(8,128)(2,1)} %collective-permute-done.13, bf16[1,256,1536]{2,1,0:T(8,128)(2,1)} %collective-permute-done.12, bf16[1,256,1536]{2,1,0:T(8,128)(2,1)S(1)} %copy-done.4), kind=kLoop, calls=%fused_computation.12 | loop fusion | flops 2752512 | bytes 4718592 | tf_op jit(solution)/shard_map/add | solution.py:524
  (83 shorter events, 3.3 us)
Async XLA Ops:
  7.7 15.4 %copy-start.21 = (bf16[48,4096]{1,0:T(8,128)(2,1)S(1)}, bf16[48,4096]{1,0:T(8,128)(2,1)}, u32[]{:S(2)}) copy-start(bf16[48,4096]{1,0:T(8,128)(2,1)} %get-tuple-element.54) | copy-start | bytes 1179652
  7.7 53.7 %copy-start.20 = (bf16[48,4096]{1,0:T(8,128)(2,1)S(1)}, bf16[48,4096]{1,0:T(8,128)(2,1)}, u32[]{:S(2)}) copy-start(bf16[48,4096]{1,0:T(8,128)(2,1)} %get-tuple-element.55) | copy-start | bytes 1179652
  7.7 58.6 %copy-start.19 = (bf16[48,4096]{1,0:T(8,128)(2,1)S(1)}, bf16[48,4096]{1,0:T(8,128)(2,1)}, u32[]{:S(2)}) copy-start(bf16[48,4096]{1,0:T(8,128)(2,1)} %get-tuple-element.56) | copy-start | bytes 1179652
  7.7 119.0 %all-to-all-start = ((bf16[8,48,4096]{2,1,0:T(8,128)(2,1)}), bf16[8,48,4096]{2,1,0:T(8,128)(2,1)}, u32[]{:S(2)}, u32[]{:S(2)}) async-start(bf16[8,48,4096]{2,1,0:T(8,128)(2,1)} %get-tuple-element.48), calls=%async_computation | async-start | bytes 6291456 | tf_op jit(solution)/shard_map/all_to_all | solution.py:437
  15.8 45.7 %collective-permute-start = (bf16[48,4096]{1,0:T(8,128)(2,1)}, bf16[48,4096]{1,0:T(8,128)(2,1)S(1)}, u32[]{:S(2)}, u32[]{:S(2)}) collective-permute-start(bf16[48,4096]{1,0:T(8,128)(2,1)} %get-tuple-element.50), channel_id=1, source_target_pairs={{0,65},{1,64},{2,67},{3,66},{4,69},{5,68},{6,71},{7,70},{64,1},{65... | collective-permute-start | bytes 1179656 | tf_op jit(solution)/shard_map/ppermute | solution.py:411
  19.0 47.3 %collective-permute-start.1 = (bf16[48,4096]{1,0:T(8,128)(2,1)}, bf16[48,4096]{1,0:T(8,128)(2,1)S(1)}, u32[]{:S(2)}, u32[]{:S(2)}) collective-permute-start(bf16[48,4096]{1,0:T(8,128)(2,1)} %get-tuple-element.51), channel_id=1, source_target_pairs={{0,2},{1,3},{2,4},{3,5},{4,6},{5,7},{6,0},{7,1},{64,66},{65,67},{6... | collective-permute-start | bytes 1179656 | tf_op jit(solution)/shard_map/ppermute | solution.py:411
  20.5 57.3 %collective-permute-start.2 = (bf16[48,4096]{1,0:T(8,128)(2,1)}, bf16[48,4096]{1,0:T(8,128)(2,1)S(1)}, u32[]{:S(2)}, u32[]{:S(2)}) collective-permute-start(bf16[48,4096]{1,0:T(8,128)(2,1)} %get-tuple-element.52), channel_id=1, source_target_pairs={{0,67},{1,66},{2,69},{3,68},{4,71},{5,70},{6,65},{7,64},{64,3},{65... | collective-permute-start | bytes 1179656 | tf_op jit(solution)/shard_map/ppermute | solution.py:411
  21.9 73.0 %collective-permute-start.3 = (bf16[48,4096]{1,0:T(8,128)(2,1)}, bf16[48,4096]{1,0:T(8,128)(2,1)S(1)}, u32[]{:S(2)}, u32[]{:S(2)}) collective-permute-start(bf16[48,4096]{1,0:T(8,128)(2,1)} %get-tuple-element.53), channel_id=1, source_target_pairs={{0,4},{1,5},{2,6},{3,7},{4,0},{5,1},{6,2},{7,3},{64,68},{65,69},{6... | collective-permute-start | bytes 1179656 | tf_op jit(solution)/shard_map/ppermute | solution.py:411
  23.2 82.1 %collective-permute-start.4 = (bf16[48,4096]{1,0:T(8,128)(2,1)S(1)}, bf16[48,4096]{1,0:T(8,128)(2,1)S(1)}, u32[]{:S(2)}, u32[]{:S(2)}) collective-permute-start(bf16[48,4096]{1,0:T(8,128)(2,1)S(1)} %copy-done.21), channel_id=1, source_target_pairs={{0,69},{1,68},{2,71},{3,70},{4,65},{5,64},{6,67},{7,66},{64,5},{65... | collective-permute-start | bytes 1179656 | tf_op jit(solution)/shard_map/ppermute | solution.py:411
  61.5 43.9 %copy-start.8 = (bf16[48,4096]{1,0:T(8,128)(2,1)}, bf16[48,4096]{1,0:T(8,128)(2,1)S(1)}, u32[]{:S(2)}) copy-start(bf16[48,4096]{1,0:T(8,128)(2,1)S(1)} %collective-permute-done.refs_1_) | copy-start | bytes 1179652
  61.5 43.8 %collective-permute-start.5 = (bf16[48,4096]{1,0:T(8,128)(2,1)S(1)}, bf16[48,4096]{1,0:T(8,128)(2,1)}, u32[]{:S(2)}, u32[]{:S(2)}) collective-permute-start(bf16[48,4096]{1,0:T(8,128)(2,1)S(1)} %copy-done.20), channel_id=1, source_target_pairs={{0,6},{1,7},{2,0},{3,1},{4,2},{5,3},{6,4},{7,5},{64,70},{65,71},{6... | collective-permute-start | bytes 1179656 | tf_op jit(solution)/shard_map/ppermute | solution.py:411
  66.3 39.0 %copy-start.9 = (bf16[48,4096]{1,0:T(8,128)(2,1)}, bf16[48,4096]{1,0:T(8,128)(2,1)S(1)}, u32[]{:S(2)}) copy-start(bf16[48,4096]{1,0:T(8,128)(2,1)S(1)} %collective-permute-done.1.refs_2_) | copy-start | bytes 1179652
  66.3 39.0 %collective-permute-start.6 = (bf16[48,4096]{1,0:T(8,128)(2,1)S(1)}, bf16[48,4096]{1,0:T(8,128)(2,1)}, u32[]{:S(2)}, u32[]{:S(2)}) collective-permute-start(bf16[48,4096]{1,0:T(8,128)(2,1)S(1)} %copy-done.19), channel_id=1, source_target_pairs={{0,71},{1,70},{2,65},{3,64},{4,67},{5,66},{6,69},{7,68},{64,7},{65... | collective-permute-start | bytes 1179656 | tf_op jit(solution)/shard_map/ppermute | solution.py:411
  77.7 27.6 %copy-start.10 = (bf16[48,4096]{1,0:T(8,128)(2,1)}, bf16[48,4096]{1,0:T(8,128)(2,1)S(1)}, u32[]{:S(2)}) copy-start(bf16[48,4096]{1,0:T(8,128)(2,1)S(1)} %collective-permute-done.2.refs_3_) | copy-start | bytes 1179652
  94.9 10.4 %copy-start.11 = (bf16[48,4096]{1,0:T(8,128)(2,1)}, bf16[48,4096]{1,0:T(8,128)(2,1)S(1)}, u32[]{:S(2)}) copy-start(bf16[48,4096]{1,0:T(8,128)(2,1)S(1)} %collective-permute-done.3.refs_4_) | copy-start | bytes 1179652
  116.2 25.8 %collective-permute-start.7 = (bf16[2,4,256,384]{3,2,1,0:T(8,128)(2,1)}, bf16[2,4,256,384]{3,2,1,0:T(8,128)(2,1)}, u32[]{:S(2)}, u32[]{:S(2)}) collective-permute-start(bf16[2,4,256,384]{3,2,1,0:T(8,128)(2,1)} %get-tuple-element.69), channel_id=1, source_target_pairs={{0,32},{32,0},{1,33},{33,1},{2,34},{34,2},{3,35},{35,3},{4,36},{36... | collective-permute-start | bytes 4718600 | tf_op jit(solution)/shard_map/ppermute | solution.py:478
  135.4 6.7 %collective-permute-start.8 = (bf16[2,384,768]{2,1,0:T(8,128)(2,1)}, bf16[2,384,768]{2,1,0:T(8,128)(2,1)}, u32[]{:S(2)}, u32[]{:S(2)}) collective-permute-start(bf16[2,384,768]{2,1,0:T(8,128)(2,1)} %get-tuple-element.74.mine_ref.grads_ref), channel_id=1, source_target_pairs={{0,32},{32,0},{1,33},{33,1},{2,34},{34,2},{3,35},{35,3},{4,36},{36... | collective-permute-start | bytes 3538952 | tf_op jit(solution)/shard_map/ppermute | solution.py:482
  135.9 5.3 %copy-start = (bf16[128,4096]{1,0:T(8,128)(2,1)S(1)}, bf16[128,4096]{1,0:T(8,128)(2,1)}, u32[]{:S(2)}) copy-start(bf16[128,4096]{1,0:T(8,128)(2,1)} %resid_ref) | copy-start | bytes 3145732
  135.9 5.6 %copy-start.7 = (bf16[384,768]{1,0:T(8,128)(2,1)S(1)}, bf16[384,768]{1,0:T(8,128)(2,1)}, u32[]{:S(2)}) copy-start(bf16[384,768]{1,0:T(8,128)(2,1)} %get-tuple-element.57.hidden_ref) | copy-start | bytes 1769476
  141.2 23.2 %collective-permute-start.9 = (bf16[2,4,256,384]{3,2,1,0:T(8,128)(2,1)}, bf16[2,4,256,384]{3,2,1,0:T(8,128)(2,1)}, u32[]{:S(2)}, u32[]{:S(2)}) collective-permute-start(bf16[2,4,256,384]{3,2,1,0:T(8,128)(2,1)} %get-tuple-element.72), channel_id=1, source_target_pairs={{0,32},{32,0},{1,33},{33,1},{2,34},{34,2},{3,35},{35,3},{4,36},{36... | collective-permute-start | bytes 4718600 | tf_op jit(solution)/shard_map/ppermute | solution.py:485
  141.5 22.8 %collective-permute-start.10 = (bf16[384,768]{1,0:T(8,128)(2,1)S(1)}, bf16[384,768]{1,0:T(8,128)(2,1)S(1)}, u32[]{:S(2)}, u32[]{:S(2)}) collective-permute-start(bf16[384,768]{1,0:T(8,128)(2,1)S(1)} %copy-done.7), channel_id=1, source_target_pairs={{0,32},{32,0},{1,33},{33,1},{2,34},{34,2},{3,35},{35,3},{4,36},{36... | collective-permute-start | bytes 1769480 | tf_op jit(solution)/shard_map/ppermute | solution.py:480
  158.1 35.5 %collective-permute-start.11 = (bf16[1,256,1536]{2,1,0:T(8,128)(2,1)}, bf16[1,256,1536]{2,1,0:T(8,128)(2,1)}, u32[]{:S(2)}, u32[]{:S(2)}) collective-permute-start(bf16[1,256,1536]{2,1,0:T(8,128)(2,1)} %get-tuple-element.77), channel_id=1, source_target_pairs={{0,24},{8,0},{16,8},{24,16},{1,25},{9,1},{17,9},{25,17},{2,26},{10... | collective-permute-start | bytes 2359304 | tf_op jit(solution)/shard_map/ppermute | solution.py:423
  161.1 35.0 %collective-permute-start.14 = (bf16[1,256,1536]{2,1,0:T(8,128)(2,1)}, bf16[1,256,1536]{2,1,0:T(8,128)(2,1)}, u32[]{:S(2)}, u32[]{:S(2)}) collective-permute-start(bf16[1,256,1536]{2,1,0:T(8,128)(2,1)} %get-tuple-element.81), channel_id=1, source_target_pairs={{0,8},{8,16},{16,24},{24,0},{1,9},{9,17},{17,25},{25,1},{2,10},{10... | collective-permute-start | bytes 2359304 | tf_op jit(solution)/shard_map/ppermute | solution.py:422
  161.1 79.7 %collective-permute-start.16 = (bf16[1,256,1536]{2,1,0:T(8,128)(2,1)}, bf16[1,256,1536]{2,1,0:T(8,128)(2,1)}, u32[]{:S(2)}, u32[]{:S(2)}) collective-permute-start(bf16[1,256,1536]{2,1,0:T(8,128)(2,1)} %get-tuple-element.82), channel_id=1, source_target_pairs={{0,24},{8,0},{16,8},{24,16},{1,25},{9,1},{17,9},{25,17},{2,26},{10... | collective-permute-start | bytes 2359304 | tf_op jit(solution)/shard_map/ppermute | solution.py:425
  165.1 7.7 %copy-start.14 = (bf16[384,128]{1,0:T(8,128)(2,1)S(1)}, bf16[384,128]{1,0:T(8,128)(2,1)}, u32[]{:S(2)}) copy-start(bf16[384,128]{1,0:T(8,128)(2,1)} %get-tuple-element.75) | copy-start | bytes 294916
  172.8 35.8 %collective-permute-start.18 = (bf16[4,256,768]{2,1,0:T(8,128)(2,1)}, bf16[4,256,768]{2,1,0:T(8,128)(2,1)}, u32[]{:S(2)}, u32[]{:S(2)}) collective-permute-start(bf16[4,256,768]{2,1,0:T(8,128)(2,1)} %get-tuple-element.84), channel_id=1, source_target_pairs={{0,64},{64,0},{1,65},{65,1},{2,66},{66,2},{3,67},{67,3},{4,68},{68... | collective-permute-start | bytes 4718600 | tf_op jit(solution)/shard_map/ppermute | solution.py:492
  173.6 13.1 %all-to-all-start.2 = ((bf16[8,1,48]{2,1,0:T(2,128)(2,1)}), bf16[8,1,48]{2,1,0:T(2,128)(2,1)S(1)}, u32[]{:S(2)}, u32[]{:S(2)}) async-start(bf16[8,1,48]{2,1,0:T(2,128)(2,1)} %all_to_all.16), calls=%async_computation.2 | async-start | bytes 8192 | tf_op jit(solution)/shard_map/all_to_all | solution.py:437
  186.7 73.4 %all-to-all-start.1 = ((bf16[8,48,4096]{2,1,0:T(8,128)(2,1)}), bf16[8,48,4096]{2,1,0:T(8,128)(2,1)S(1)}, u32[]{:S(2)}, u32[]{:S(2)}) async-start(bf16[8,48,4096]{2,1,0:T(8,128)(2,1)} %slot_rows.1), calls=%async_computation.1 | async-start | bytes 6291456 | tf_op jit(solution)/shard_map/all_to_all | solution.py:437
  193.5 2.5 copy-start.6
  196.1 12.6 %copy-start.2 = (bf16[4,256,768]{2,1,0:T(8,128)(2,1)S(1)}, bf16[4,256,768]{2,1,0:T(8,128)(2,1)}, u32[]{:S(2)}) copy-start(bf16[4,256,768]{2,1,0:T(8,128)(2,1)} %get-tuple-element.73) | copy-start | bytes 4718596
  210.5 0.9 copy-start.13
  210.5 1.1 copy-start.16
  210.5 9.3 %copy-start.17 = (bf16[128,2]{0,1:T(2,128)(2,1)S(1)}, bf16[128,2]{0,1:T(2,128)(2,1)}, u32[]{:S(2)}) copy-start(bf16[128,2]{0,1:T(2,128)(2,1)} %param.11) | copy-start | bytes 1540
  210.5 33.6 %copy-start.5 = (bf16[1,256,1536]{2,1,0:T(8,128)(2,1)S(1)}, bf16[1,256,1536]{2,1,0:T(8,128)(2,1)}, u32[]{:S(2)}) copy-start(bf16[1,256,1536]{2,1,0:T(8,128)(2,1)} %get-tuple-element.79) | copy-start | bytes 2359300
  210.6 9.1 %collective-permute-start.19 = (bf16[128,768]{1,0:T(8,128)(2,1)S(1)}, bf16[128,768]{1,0:T(8,128)(2,1)S(1)}, u32[]{:S(2)}, u32[]{:S(2)}) collective-permute-start(bf16[128,768]{1,0:T(8,128)(2,1)S(1)} %get-tuple-element.88), channel_id=1, source_target_pairs={{0,8},{8,16},{16,24},{24,0},{1,9},{9,17},{17,25},{25,1},{2,10},{10... | collective-permute-start | bytes 589832 | tf_op jit(solution)/shard_map/ppermute | solution.py:422
  211.5 32.6 %collective-permute-start.15 = (bf16[1,256,1536]{2,1,0:T(8,128)(2,1)S(1)}, bf16[1,256,1536]{2,1,0:T(8,128)(2,1)S(1)}, u32[]{:S(2)}, u32[]{:S(2)}) collective-permute-start(bf16[1,256,1536]{2,1,0:T(8,128)(2,1)S(1)} %add_convert_fusion.2), channel_id=1, source_target_pairs={{0,8},{8,16},{16,24},{24,0},{1,9},{9,17},{17,25},{25,1},{2,10},{10... | collective-permute-start | bytes 2359304 | tf_op jit(solution)/shard_map/ppermute | solution.py:428
  211.6 8.7 %collective-permute-start.21 = (bf16[128,768]{1,0:T(8,128)(2,1)S(1)}, bf16[128,768]{1,0:T(8,128)(2,1)S(1)}, u32[]{:S(2)}, u32[]{:S(2)}) collective-permute-start(bf16[128,768]{1,0:T(8,128)(2,1)S(1)} %get-tuple-element.91), channel_id=1, source_target_pairs={{0,24},{8,0},{16,8},{24,16},{1,25},{9,1},{17,9},{25,17},{2,26},{10... | collective-permute-start | bytes 589832 | tf_op jit(solution)/shard_map/ppermute | solution.py:425
  214.9 6.7 %collective-permute-start.22 = (bf16[128,768]{1,0:T(8,128)(2,1)S(1)}, bf16[128,768]{1,0:T(8,128)(2,1)S(1)}, u32[]{:S(2)}, u32[]{:S(2)}) collective-permute-start(bf16[128,768]{1,0:T(8,128)(2,1)S(1)} %get-tuple-element.90), channel_id=1, source_target_pairs={{0,24},{8,0},{16,8},{24,16},{1,25},{9,1},{17,9},{25,17},{2,26},{10... | collective-permute-start | bytes 589832 | tf_op jit(solution)/shard_map/ppermute | solution.py:423
  219.7 21.0 %collective-permute-start.20 = (bf16[128,768]{1,0:T(8,128)(2,1)S(1)}, bf16[128,768]{1,0:T(8,128)(2,1)S(1)}, u32[]{:S(2)}, u32[]{:S(2)}) collective-permute-start(bf16[128,768]{1,0:T(8,128)(2,1)S(1)} %fusion.10), channel_id=1, source_target_pairs={{0,8},{8,16},{16,24},{24,0},{1,9},{9,17},{17,25},{25,1},{2,10},{10... | collective-permute-start | bytes 589832 | tf_op jit(solution)/shard_map/ppermute | solution.py:428
  220.3 43.8 %collective-permute-start.13 = (bf16[1,256,1536]{2,1,0:T(8,128)(2,1)}, bf16[1,256,1536]{2,1,0:T(8,128)(2,1)}, u32[]{:S(2)}, u32[]{:S(2)}) collective-permute-start(bf16[1,256,1536]{2,1,0:T(8,128)(2,1)} %get-tuple-element.78), channel_id=1, source_target_pairs={{0,8},{8,16},{16,24},{24,0},{1,9},{9,17},{17,25},{25,1},{2,10},{10... | collective-permute-start | bytes 2359304 | tf_op jit(solution)/shard_map/ppermute | solution.py:424
  221.5 42.6 %collective-permute-start.12 = (bf16[1,256,1536]{2,1,0:T(8,128)(2,1)}, bf16[1,256,1536]{2,1,0:T(8,128)(2,1)}, u32[]{:S(2)}, u32[]{:S(2)}) collective-permute-start(bf16[1,256,1536]{2,1,0:T(8,128)(2,1)} %add_convert_fusion.3), channel_id=1, source_target_pairs={{0,24},{8,0},{16,8},{24,16},{1,25},{9,1},{17,9},{25,17},{2,26},{10... | collective-permute-start | bytes 2359304 | tf_op jit(solution)/shard_map/ppermute | solution.py:429
  240.7 18.4 %collective-permute-start.24 = (bf16[128,768]{1,0:T(8,128)(2,1)S(1)}, bf16[128,768]{1,0:T(8,128)(2,1)S(1)}, u32[]{:S(2)}, u32[]{:S(2)}) collective-permute-start(bf16[128,768]{1,0:T(8,128)(2,1)S(1)} %get-tuple-element.89), channel_id=1, source_target_pairs={{0,8},{8,16},{16,24},{24,0},{1,9},{9,17},{17,25},{25,1},{2,10},{10... | collective-permute-start | bytes 589832 | tf_op jit(solution)/shard_map/ppermute | solution.py:424
  240.8 18.3 %collective-permute-start.23 = (bf16[128,768]{1,0:T(8,128)(2,1)S(1)}, bf16[128,768]{1,0:T(8,128)(2,1)S(1)}, u32[]{:S(2)}, u32[]{:S(2)}) collective-permute-start(bf16[128,768]{1,0:T(8,128)(2,1)S(1)} %get-tuple-element.87), channel_id=1, source_target_pairs={{0,24},{8,0},{16,8},{24,16},{1,25},{9,1},{17,9},{25,17},{2,26},{10... | collective-permute-start | bytes 589832 | tf_op jit(solution)/shard_map/ppermute | solution.py:429
  246.4 13.7 %copy-start.15 = (f32[4096]{0:T(1024)S(1)}, f32[4096]{0:T(1024)}, u32[]{:S(2)}) copy-start(f32[4096]{0:T(1024)} %param.8) | copy-start | bytes 49156
  246.4 17.7 %collective-permute-start.17 = (bf16[1,256,1536]{2,1,0:T(8,128)(2,1)}, bf16[1,256,1536]{2,1,0:T(8,128)(2,1)}, u32[]{:S(2)}, u32[]{:S(2)}) collective-permute-start(bf16[1,256,1536]{2,1,0:T(8,128)(2,1)} %add_convert_fusion.1), channel_id=1, source_target_pairs={{0,64},{64,0},{1,65},{65,1},{2,66},{66,2},{3,67},{67,3},{4,68},{68... | collective-permute-start | bytes 2359304 | tf_op jit(solution)/shard_map/ppermute | solution.py:494
  260.1 2.3 copy-start.1
  260.1 2.3 copy-start.3
  262.5 1.6 copy-start.4
  (2 other events, 1.6 us)

commit v8 on v7

--- a/solution.py
+++ b/solution.py
@@ -39,15 +39,15 @@
     ).astype(jnp.int32)
     rank = jnp.where(hit, rank, capacity)
     slot = lax.broadcasted_iota(jnp.int32, (capacity, tok_rows), 0)
-    select, scale = [], []
+    select, scale, choice = [], [], []
+    first, second = (jnp.where(f, 1.0, 0.0) for f in (first, second))
     for e in range(experts):
         held = rank[e : e + 1] == slot
         select.append(jnp.where(held, 1.0, 0.0))
         scale.append(jnp.where(held, weight[e : e + 1], 0.0))
-    return (
-        jnp.concatenate(select, axis=0).astype(jnp.bfloat16),
-        jnp.concatenate(scale, axis=0).astype(jnp.bfloat16),
-    )
+        both = [jnp.where(held, f[e : e + 1], 0.0) for f in (first, second)]
+        choice.append(jnp.concatenate(both, axis=1))
+    return [jnp.concatenate(m, axis=0).astype(jnp.bfloat16) for m in (select, scale, choice)]
 
 
 def shifted(expert, step, sign):
@@ -55,7 +55,7 @@
 
 
 def pack_kernel(place_ref, ids_ref, w_ref, gain_ref, resid_ref, grad_ref, *out_refs):
-    *normed_refs, scaled_ref, sel_ref, inv_ref, scale_ref, turned_ref = out_refs
+    *normed_refs, scaled_ref, sel_ref, choice_ref, inv_ref, scale_ref, turned_ref = out_refs
     experts, capacity, block = scaled_ref.shape
 
     @pl.when(pl.program_id(0) == 0)
@@ -63,8 +63,11 @@
         full = resid_ref[...].astype(jnp.float32)
         mean = jnp.mean(full * full, axis=-1, keepdims=True)
         inv_ref[...] = lax.rsqrt(mean + eps)
-        select, scale = slot_matrices(ids_ref[...], w_ref[...].astype(jnp.float32), experts, capacity)
+        select, scale, choice = slot_matrices(
+            ids_ref[...], w_ref[...].astype(jnp.float32), experts, capacity
+        )
         sel_ref[...] = select
+        choice_ref[...] = choice
         scale_ref[...] = scale
         for step in range(experts):
             start = pl.multiple_of(shifted(place_ref[3], step, 1) * capacity, 16)
@@ -94,6 +97,7 @@
             + [
                 pl.BlockSpec((experts, capacity, block), lambda j, _: (0, 0, j)),
                 pl.BlockSpec((slots, rows), lambda j, _: (0, 0)),
+                pl.BlockSpec((slots, 2 * rows), lambda j, _: (0, 0)),
             ],
             scratch_shapes=[
                 pltpu.VMEM((rows, 1), jnp.float32),
@@ -105,6 +109,7 @@
         + [
             jax.ShapeDtypeStruct((experts, capacity, width), jnp.bfloat16),
             jax.ShapeDtypeStruct((slots, rows), jnp.bfloat16),
+            jax.ShapeDtypeStruct((slots, 2 * rows), jnp.bfloat16),
         ],
         compiler_params=pltpu.CompilerParams(vmem_limit_bytes=VMEM),
         cost_estimate=pl.CostEstimate(
@@ -280,36 +285,49 @@
     )(place, got, got)
 
 
-def rows_kernel(_, keep_ref, came_ref, mine_ref, theirs_ref, far_ref, near_ref):
+def both_rows(keep_ref, came_ref):
     block, slots = keep_ref.shape[2:]
-    keep, came = keep_ref[...].reshape(2 * block, slots), came_ref[...].reshape(2 * block, slots)
-    rows = contract(keep, mine_ref[0], 1, 0) + contract(came, theirs_ref[0], 1, 0)
-    rows = rows.astype(jnp.bfloat16)
-    far_ref[0] = rows[:block]
-    near_ref[0] = rows[block:]
-
-
-def weight_rows(place, keep, came, mine, theirs, first, count):
+    both = [r[...].reshape(2 * block, slots) for r in (keep_ref, came_ref)]
+    return jnp.concatenate(both, axis=1)
+
+
+def fill_right(mine_ref, theirs_ref, right_ref):
+    units, slots, width = mine_ref.shape
+
+    @pl.when(pl.program_id(0) == 0)
+    def _():
+        for u in range(units):
+            right_ref[:slots, u * width : (u + 1) * width] = mine_ref[u]
+            right_ref[slots:, u * width : (u + 1) * width] = theirs_ref[u]
+
+
+def rows_kernel(_, keep_ref, came_ref, mine_ref, theirs_ref, far_ref, near_ref, right_ref):
+    fill_right(mine_ref, theirs_ref, right_ref)
+    rows = contract(both_rows(keep_ref, came_ref), right_ref[...], 1, 0).astype(jnp.bfloat16)
+    far_ref[0] = rows[: far_ref.shape[1]]
+    near_ref[0] = rows[far_ref.shape[1] :]
+
+
+def weight_rows(place, keep, came, mine, theirs):
     _, rings, block, slots = keep.shape
     units, _, width = mine.shape
-    left = pl.BlockSpec(
-        (2, 1, block, slots), lambda i, u, at: (0, lax.rem(at[2] + (first + i), rings), 0, 0)
-    )
-    right = pl.BlockSpec((1, slots, width), lambda i, u, at: (u, 0, 0))
-    out = pl.BlockSpec((1, block, width), lambda i, u, at: (i, 0, u))
+    left = pl.BlockSpec((2, 1, block, slots), lambda i, at: (0, lax.rem(at[2] + i, rings), 0, 0))
+    right = pl.BlockSpec(mine.shape, lambda i, at: (0, 0, 0))
+    out = pl.BlockSpec((1, block, units * width), lambda i, at: (i, 0, 0))
     return pl.pallas_call(
         rows_kernel,
         grid_spec=pltpu.PrefetchScalarGridSpec(
             num_scalar_prefetch=1,
-            grid=(count, units),
+            grid=(rings,),
             in_specs=[left, left, right, right],
             out_specs=[out, out],
-        ),
-        out_shape=[jax.ShapeDtypeStruct((count, block, units * width), jnp.bfloat16)] * 2,
-        compiler_params=pltpu.CompilerParams(vmem_limit_bytes=VMEM),
-        cost_estimate=pl.CostEstimate(
-            flops=8 * count * block * mine.size,
-            bytes_accessed=4 * mine.size + 4 * count * block * (2 * slots + units * width),
+            scratch_shapes=[pltpu.VMEM((2 * slots, units * width), jnp.bfloat16)],
+        ),
+        out_shape=[jax.ShapeDtypeStruct((rings, block, units * width), jnp.bfloat16)] * 2,
+        compiler_params=pltpu.CompilerParams(vmem_limit_bytes=VMEM),
+        cost_estimate=pl.CostEstimate(
+            flops=8 * rings * block * mine.size,
+            bytes_accessed=4 * mine.size + 4 * rings * block * (2 * slots + units * width),
             transcendentals=0,
         ),
     )(place, keep, came, mine, theirs)
@@ -326,19 +344,17 @@
 
 
 def messages_kernel(_, keep_ref, came_ref, mine_ref, theirs_ref, *out_refs):
-    block, slots = keep_ref.shape[2:]
-    units, _, width = mine_ref.shape
-    keep, came = keep_ref[...].reshape(2 * block, slots), came_ref[...].reshape(2 * block, slots)
-    for unit in range(units):
-        columns = slice(unit * width, (unit + 1) * width)
-        rows = contract(keep, mine_ref[unit], 1, 0) + contract(came, theirs_ref[unit], 1, 0)
-        rows = rows.astype(jnp.bfloat16)
-        for at in range(len(SEND_ORDER)):
-
-            @pl.when(pl.program_id(0) == at)
-            def _():
-                out_refs[2 * at][0, :, columns] = rows[:block]
-                out_refs[2 * at + 1][0, :, columns] = rows[block:]
+    *out_refs, right_ref = out_refs
+    block = keep_ref.shape[2]
+    fill_right(mine_ref, theirs_ref, right_ref)
+    for at in range(len(SEND_ORDER)):
+
+        @pl.when(pl.program_id(0) == at)
+        def _():
+            rows = contract(both_rows(keep_ref, came_ref), right_ref[...], 1, 0)
+            rows = rows.astype(jnp.bfloat16)
+            out_refs[2 * at][0] = rows[:block]
+            out_refs[2 * at + 1][0] = rows[block:]
 
 
 def weight_messages(place, keep, came, mine, theirs):
@@ -356,6 +372,7 @@
             in_specs=[left, left, right, right],
             out_specs=[pl.BlockSpec((1, block, units * width), lambda i, at: (0, 0, 0))]
             * (2 * rings),
+            scratch_shapes=[pltpu.VMEM((2 * slots, units * width), jnp.bfloat16)],
         ),
         out_shape=[jax.ShapeDtypeStruct((1, block, units * width), jnp.bfloat16)] * (2 * rings),
         compiler_params=pltpu.CompilerParams(vmem_limit_bytes=VMEM),
@@ -371,26 +388,37 @@
     return far, near
 
 
-def slot_kernel(grads_ref, w_ref, out_ref):
+def slot_kernel(grads_ref, w_ref, route_ref, out_ref):
     width = grads_ref.shape[2]
+    block = w_ref.shape[0]
     rows = contract(grads_ref[0], w_ref[:, :width], 1, 1) + contract(
         grads_ref[1], w_ref[:, width:], 1, 1
     )
-    out_ref[...] = rows.astype(jnp.bfloat16).reshape(out_ref.shape)
-
-
-def slot_rows(grads, w_in, parts, block=1024):
+    at = pl.ds(pl.multiple_of(pl.program_id(0) * block, block), block)
+    out_ref[:, :, at] = rows.astype(jnp.bfloat16).reshape(out_ref.shape[:2] + (block,))
+
+    @pl.when(pl.program_id(0) == 0)
+    def _():
+        lanes = route_ref.shape[1]
+        out_ref[:, :, out_ref.shape[2] - lanes :] = route_ref[...].reshape(
+            out_ref.shape[:2] + (lanes,)
+        )
+
+
+def slot_rows(grads, w_in, route, parts, block=1024):
     _, slots, hidden_width = grads.shape
     width = w_in.shape[0]
+    shape = (parts, slots // parts, width + route.shape[1])
     return pl.pallas_call(
         slot_kernel,
         grid=(width // block,),
         in_specs=[
             pl.BlockSpec(grads.shape, lambda j: (0, 0, 0)),
             pl.BlockSpec((block, 2 * hidden_width), lambda j: (j, 0)),
-        ],
-        out_specs=pl.BlockSpec((parts, slots // parts, block), lambda j: (0, 0, j)),
-        out_shape=jax.ShapeDtypeStruct((parts, slots // parts, width), jnp.bfloat16),
+            pl.BlockSpec(route.shape, lambda j: (0, 0)),
+        ],
+        out_specs=pl.BlockSpec(shape, lambda j: (0, 0, 0)),
+        out_shape=jax.ShapeDtypeStruct(shape, jnp.bfloat16),
         compiler_params=pltpu.CompilerParams(vmem_limit_bytes=VMEM),
         cost_estimate=pl.CostEstimate(
             flops=4 * slots * hidden_width * width,
@@ -398,7 +426,7 @@
             transcendentals=0,
         ),
         name="slot_rows",
-    )(grads, w_in)
+    )(grads, w_in, route)
 
 
 def displaced(rows, step):
@@ -466,7 +494,7 @@
         )
     )
 
-    *send_normed, send_scaled, select = pack(
+    *send_normed, send_scaled, select, choice = pack(
         place, ids_t, weights_t, norm_gain[None], residual, grad_out, experts, capacity
     )
     blocks = send_normed[:1] + [displaced(send_normed[k], k) for k in range(1, experts)]
@@ -487,7 +515,7 @@
     far, near = weight_messages(place, keep_normed, came_normed, mine, theirs)
     keep_scaled, _ = lax.optimization_barrier((keep_scaled, near[0]))
     far_down, near_down = weight_rows(
-        place, keep_scaled, came_scaled, hidden[None], their_hidden[None], 0, rings
+        place, keep_scaled, came_scaled, hidden[None], their_hidden[None]
     )
     came_down = lax.ppermute(far_down, "dp_0", SWAP)
     (far_in, near_in), far_both, near_both = ring_sum(far, near)
@@ -500,20 +528,13 @@
     grad_down = jnp.concatenate(halves_down, axis=0)[None]
 
     mine, route, _ = lax.optimization_barrier((mine, route, near_down))
-    slot_normed = slot_rows(mine, w_in, experts)
-    back_normed = exchange(slot_normed)
-    back_route = exchange(route[:, 0].reshape(experts, capacity))
+    slot_normed = slot_rows(mine, w_in, route, experts)
+    returned = exchange(slot_normed).reshape(slot_total, -1)
     resid = residual.astype(jnp.float32)
     inv_rms = lax.rsqrt(jnp.mean(resid * resid, axis=-1, keepdims=True) + eps)
     unit_rows = resid * inv_rms
-    grad_normed = contract(select, back_normed.reshape(slot_total, width), 0, 0)
-    token_route = jnp.sum(
-        select.reshape(experts, capacity, tok_rows).astype(jnp.float32)
-        * back_route.astype(jnp.float32)[:, :, None],
-        axis=1,
-    )
-    chosen = ids_t[:, None, :] == lax.broadcasted_iota(jnp.int32, (1, experts, tok_rows), 1)
-    route_t = jnp.sum(jnp.where(chosen, token_route[None], 0.0), axis=1)
+    grad_normed = contract(select, returned[:, :width], 0, 0)
+    route_t = contract(choice, returned[:, width:], 0, 0)[:, 0].reshape(topk, tok_rows)
     route_grad = (route_t / weights_t.astype(jnp.float32)).astype(jnp.bfloat16).T
     scaled_normed = grad_normed * norm_gain
     branch = inv_rms * (

time: 268 us -> 263 us (0.981)
  waiting for transfers between devices: 112 us -> 121 us
  starting transfers between devices: 58.9 us -> 51.6 us
  Pallas kernels: 74.6 us -> 69.4 us
    ppermute x2, waiting for transfers between devices: 0.01 us -> 16.2 us  [ring_sum(): low_side = lax.ppermute(low[3], 'ulysses', behind)]
    ppermute x2, waiting for transfers between devices: 15.5 us -> 0.01 us  [ring_sum(): low_last = lax.ppermute(low_both, 'ulysses', ahead)]
    all_to_all x3 -> x2, starting transfers between devices: 18.1 us -> 11.7 us  [exchange(): lax.all_to_all(rows, ('dp_0', 'expert'), split_axis=0, concat_axis=0, axi...]
    pallas_call x1, Pallas kernels: 16 us -> 11.1 us  [weight_messages(): pl.pallas_call(messages_kernel, grid_spec=pltpu.PrefetchScalarGridSpec(nu...]
    ppermute x1, waiting for transfers between devices: 11.1 us -> 14.2 us  [per_device(): came_down = lax.ppermute(far_down, 'dp_0', SWAP)]
  transfers between devices with their start and end apart: 28 -> 27, of which waited for: 10 -> 12; matrix products, arithmetic and copies ran while one was open for 5% -> 5% of each run, Pallas kernels for 25% -> 24%
where the time goes in v8:
time: 263 us; the launch traced here: 261 us
  waiting for transfers between devices  121 us (46%)
  Pallas kernels  69.4 us (26%)
  starting transfers between devices  51.6 us (20%)
  other arithmetic  14.2 us (5%)
    ppermute x7, waiting for transfers between devices, displaced(): return lax.ppermute(rows, ('dp_0', 'expert'), pairs)  68.3 us
    ppermute x7, starting transfers between devices, displaced(): return lax.ppermute(rows, ('dp_0', 'expert'), pairs)  21.2 us
    ppermute x2, waiting for transfers between devices, ring_sum(): low_side = lax.ppermute(low[3], 'ulysses', behind)  16.2 us
    ppermute x1, waiting for transfers between devices, per_device(): came_down = lax.ppermute(far_down, 'dp_0', SWAP)  14.2 us
    ppermute x2, waiting for transfers between devices, ring_sum(): high_side = lax.ppermute(high[1], 'ulysses', ahead)  12.9 us
    all_to_all x2, starting transfers between devices, exchange(): lax.all_to_all(rows, ('dp_0', 'expert'), split_axis=0, concat_axis=0, axi...  11.7 us
    pallas_call x1, Pallas kernels, weight_messages(): pl.pallas_call(messages_kernel, grid_spec=pltpu.PrefetchScalarGridSpec(nu...  11.1 us
    pallas_call x1, Pallas kernels, forward(): pl.pallas_call(forward_kernel, grid=(steps,), in_specs=[pl.BlockSpec(got....  10.5 us
  transfers between devices with their start and end apart: 27, of which 12 were waited for; matrix products, arithmetic and copies ran while one was open for 5% of the time, Pallas kernels for 24%

profile of v8, /device:TPU:0, one launch (start us, length us, event | category | flops | bytes accessed | tf_op | source)
XLA Modules:
  0.0 261.3 jit_solution(8379525792089120255)
XLA Ops:
  0.6 0.6 pad_add_fusion.place_ref._
  1.3 6.5 %pack.1 = (bf16[48,4096]{1,0:T(8,128)(2,1)}, bf16[48,4096]{1,0:T(8,128)(2,1)}, bf16[48,4096]{1,0:T(8,128)(2,1)}, bf16[48,4096]{1,0:T(8,128)(2,1)}, bf16[48,4096]...) custom-call(s32[4]{0:T(128)} %pad_add_fusion.place_ref._, ...), custom_call_target="tpu_custom_call" | custom-call | flops 805306368 | bytes 6291456 | tf_op jit(solution)/shard_map/pack/pallas_call | solution.py:90
  7.8 8.0 %all-to-all-start = ((bf16[8,48,4096]{2,1,0:T(8,128)(2,1)}), bf16[8,48,4096]{2,1,0:T(8,128)(2,1)}, u32[]{:S(2)}, u32[]{:S(2)}) async-start(bf16[8,48,4096]{2,1,0:T(8,128)(2,1)} %get-tuple-element.49), calls=%async_computation | async-start | bytes 6291456 | tf_op jit(solution)/shard_map/all_to_all | solution.py:465
  15.8 3.2 %collective-permute-start = (bf16[48,4096]{1,0:T(8,128)(2,1)}, bf16[48,4096]{1,0:T(8,128)(2,1)S(1)}, u32[]{:S(2)}, u32[]{:S(2)}) collective-permute-start(bf16[48,4096]{1,0:T(8,128)(2,1)} %get-tuple-element.51), channel_id=1, source_target_pairs={{0,65},{1,64},{2,67},{3,66},{4,69},{5,68},{6,71},{7,70},{64,1},{65... | collective-permute-start | bytes 1179656 | tf_op jit(solution)/shard_map/ppermute | solution.py:439
  19.1 1.5 collective-permute-start.1
  20.5 1.5 collective-permute-start.2
  22.0 1.2 collective-permute-start.3
  23.2 4.4 %collective-permute-start.4 = (bf16[48,4096]{1,0:T(8,128)(2,1)S(1)}, bf16[48,4096]{1,0:T(8,128)(2,1)S(1)}, u32[]{:S(2)}, u32[]{:S(2)}) collective-permute-start(bf16[48,4096]{1,0:T(8,128)(2,1)S(1)} %copy-done.21), channel_id=1, source_target_pairs={{0,69},{1,68},{2,71},{3,70},{4,65},{5,64},{6,67},{7,66},{64,5},{65... | collective-permute-start | bytes 1179656 | tf_op jit(solution)/shard_map/ppermute | solution.py:439
  27.6 33.9 %collective-permute-done.refs_1_ = bf16[48,4096]{1,0:T(8,128)(2,1)S(1)} collective-permute-done((bf16[48,4096]{1,0:T(8,128)(2,1)}, bf16[48,4096]{1,0:T(8,128)(2,1)S(1)}, u32[]{:S(2)}, u32[]{:S(2)}) %collective-permute-start) | collective-permute-done | bytes 393248 | tf_op jit(solution)/shard_map/ppermute | solution.py:439
  61.5 2.7 %collective-permute-start.5 = (bf16[48,4096]{1,0:T(8,128)(2,1)S(1)}, bf16[48,4096]{1,0:T(8,128)(2,1)}, u32[]{:S(2)}, u32[]{:S(2)}) collective-permute-start(bf16[48,4096]{1,0:T(8,128)(2,1)S(1)} %copy-done.20), channel_id=1, source_target_pairs={{0,6},{1,7},{2,0},{3,1},{4,2},{5,3},{6,4},{7,5},{64,70},{65,71},{6... | collective-permute-start | bytes 1179656 | tf_op jit(solution)/shard_map/ppermute | solution.py:439
  64.2 2.2 collective-permute-done.1.refs_2_
  66.4 6.7 %collective-permute-start.6 = (bf16[48,4096]{1,0:T(8,128)(2,1)S(1)}, bf16[48,4096]{1,0:T(8,128)(2,1)}, u32[]{:S(2)}, u32[]{:S(2)}) collective-permute-start(bf16[48,4096]{1,0:T(8,128)(2,1)S(1)} %copy-done.19), channel_id=1, source_target_pairs={{0,71},{1,70},{2,65},{3,64},{4,67},{5,66},{6,69},{7,68},{64,7},{65... | collective-permute-start | bytes 1179656 | tf_op jit(solution)/shard_map/ppermute | solution.py:439
  73.1 4.7 %collective-permute-done.2.refs_3_ = bf16[48,4096]{1,0:T(8,128)(2,1)S(1)} collective-permute-done((bf16[48,4096]{1,0:T(8,128)(2,1)}, bf16[48,4096]{1,0:T(8,128)(2,1)S(1)}, u32[]{:S(2)}, u32[]{:S(2)}) %collective-permute-start.2) | collective-permute-done | bytes 393248 | tf_op jit(solution)/shard_map/ppermute | solution.py:439
  77.8 17.2 %collective-permute-done.3.refs_4_ = bf16[48,4096]{1,0:T(8,128)(2,1)S(1)} collective-permute-done((bf16[48,4096]{1,0:T(8,128)(2,1)}, bf16[48,4096]{1,0:T(8,128)(2,1)S(1)}, u32[]{:S(2)}, u32[]{:S(2)}) %collective-permute-start.3) | collective-permute-done | bytes 393248 | tf_op jit(solution)/shard_map/ppermute | solution.py:439
  95.0 10.4 %collective-permute-done.4.refs_5_ = bf16[48,4096]{1,0:T(8,128)(2,1)S(1)} collective-permute-done((bf16[48,4096]{1,0:T(8,128)(2,1)S(1)}, bf16[48,4096]{1,0:T(8,128)(2,1)S(1)}, u32[]{:S(2)}, u32[]{:S(2)}) %collective-permute-start.4) | collective-permute-done | bytes 393248 | tf_op jit(solution)/shard_map/ppermute | solution.py:439
  105.4 0.7 copy-done.12
  106.2 5.1 %gather.1.got_ref.keep_ref.give_ref = bf16[8,48,4096]{2,1,0:T(8,128)(2,1)} custom-call(s32[4]{0:T(128)} %pad_add_fusion.place_ref._, bf16[48,4096]{1,0:T(8,128)(2,1)} %get-tuple-element.50.refs_0_, bf16[48,4096]{1,0:T(8,128)(2,1)} %copy-done.8, bf16[48,4096]{1,0:T(8,128)(2,1)} %copy-done.9, bf16[48,4096]{1,0:T(8,128)(2,1)} %copy-done.10, ...), custom_call_target="tpu_custom_call" | custom-call | flops 402653184 | bytes 6291456 | tf_op jit(solution)/shard_map/gather/pallas_call | solution.py:131
  111.2 5.1 %turn.2 = (bf16[2,4,256,384]{3,2,1,0:T(8,128)(2,1)}, bf16[2,4,256,384]{3,2,1,0:T(8,128)(2,1)}) custom-call(s32[4]{0:T(128)} %pad_add_fusion.place_ref._, bf16[8,48,4096]{2,1,0:T(8,128)(2,1)} %gather.1.got_ref.keep_ref.give_ref, bf16[8,48,4096]{2,1,0:T(8,128)(2,1)} %gather.1.got_ref.keep_ref.give_ref), custom_call_target="tpu_custom_call" | custom-call | flops 1610612736 | bytes 6291456 | tf_op jit(solution)/shard_map/turn/pallas_call | solution.py:262
  116.3 10.5 %forward.1 = (bf16[384,768]{1,0:T(8,128)(2,1)}, f32[384,768]{1,0:T(8,128)}, f32[384,768]{1,0:T(8,128)}) custom-call(bf16[8,48,4096]{2,1,0:T(8,128)(2,1)} %gather.1.got_ref.keep_ref.give_ref, bf16[4096,1536]{1,0:T(8,128)(2,1)} %bitcast.48, bf16[4096,1536]{1,0:T(8,128)(2,1)} %bitcast.49), custom_call_target="tpu_custom_call" | custom-call | flops 4831838208 | bytes 15728640 | tf_op jit(solution)/shard_map/forward/pallas_call | solution.py:168
  126.9 8.7 %back.1 = (bf16[2,384,768]{2,1,0:T(8,128)(2,1)}, bf16[384,128]{1,0:T(8,128)(2,1)}) custom-call(bf16[8,48,4096]{2,1,0:T(8,128)(2,1)} %all-to-all-done.got_ref.keep_ref.give_ref, bf16[768,4096]{1,0:T(8,128)(2,1)} %bitcast.53, bf16[384,768]{1,0:T(8,128)(2,1)} %get-tuple-element.58.hidden_ref, f32[384,768]{1,0:T(8,128)} %get-tuple-element.59.gate_ref, ...), custom_call_target="tpu_custom_call" | custom-call | flops 2415919104 | bytes 12386304 | tf_op jit(solution)/shard_map/back/pallas_call | solution.py:216
  136.0 5.2 %turn.3 = (bf16[2,4,256,384]{3,2,1,0:T(8,128)(2,1)}, bf16[2,4,256,384]{3,2,1,0:T(8,128)(2,1)}) custom-call(s32[4]{0:T(128)} %pad_add_fusion.place_ref._, bf16[8,48,4096]{2,1,0:T(8,128)(2,1)} %all-to-all-done.got_ref.keep_ref.give_ref, bf16[8,48,4096]{2,1,0:T(8,128)(2,1)} %all-to-all-done.got_ref.keep_ref.give_ref), custom_call_target="tpu_custom_call" | custom-call | flops 1610612736 | bytes 6291456 | tf_op jit(solution)/shard_map/turn/pallas_call | solution.py:262
  141.8 1.0 copy-done.17
  142.8 11.1 %grad_in.1 = (bf16[1,256,1536]{2,1,0:T(8,128)(2,1)}, bf16[1,256,1536]{2,1,0:T(8,128)(2,1)}, bf16[1,256,1536]{2,1,0:T(8,128)(2,1)}, bf16[1,256,1536]{2,1,0:T(8,12...) custom-call(s32[4]{0:T(128)} %pad_add_fusion.place_ref._, ...), custom_call_target="tpu_custom_call" | custom-call | flops 4831838208 | bytes 11796480 | tf_op jit(solution)/shard_map/grad_in/pallas_call | solution.py:367
  153.9 3.0 %collective-permute-start.11 = (bf16[1,256,1536]{2,1,0:T(8,128)(2,1)}, bf16[1,256,1536]{2,1,0:T(8,128)(2,1)}, u32[]{:S(2)}, u32[]{:S(2)}) collective-permute-start(bf16[1,256,1536]{2,1,0:T(8,128)(2,1)} %get-tuple-element.79), channel_id=1, source_target_pairs={{0,24},{8,0},{16,8},{24,16},{1,25},{9,1},{17,9},{25,17},{2,26},{10... | collective-permute-start | bytes 2359304 | tf_op jit(solution)/shard_map/ppermute | solution.py:451
  157.0 6.9 %shard_map.102 = (bf16[4,256,768]{2,1,0:T(8,128)(2,1)}, bf16[4,256,768]{2,1,0:T(8,128)(2,1)}) custom-call(s32[4]{0:T(128)} %pad_add_fusion.place_ref._, bf16[2,4,256,384]{3,2,1,0:T(8,128)(2,1)} %get-tuple-element.72.keep_ref, bf16[2,4,256,384]{3,2,1,0:T(8,128)(2,1)} %collective-permute-done.9.came_ref, bf16[1,384,768]{2,1,0:T(8,128)(2,1)} %bitcast.54, ...), custom_call_target="tpu_custom_call" | custom-call | flops 2415919104 | bytes 7471104 | tf_op jit(solution)/shard_map/pallas_call | solution.py:317
  163.9 10.2 %slot_rows.1 = bf16[8,48,4224]{2,1,0:T(8,128)(2,1)} custom-call(bf16[2,384,768]{2,1,0:T(8,128)(2,1)} %get-tuple-element.75.mine_ref.grads_ref, bf16[4096,1536]{1,0:T(8,128)(2,1)} %bitcast.50, bf16[384,128]{1,0:T(8,128)(2,1)} %get-tuple-element.76.route_ref), custom_call_target="tpu_custom_call" | custom-call | flops 4831838208 | bytes 15728640 | tf_op jit(solution)/shard_map/slot_rows/pallas_call | solution.py:412
  174.1 3.7 %all-to-all-start.1 = ((bf16[8,48,4224]{2,1,0:T(8,128)(2,1)}), bf16[8,48,4224]{2,1,0:T(8,128)(2,1)S(1)}, u32[]{:S(2)}, u32[]{:S(2)}) async-start(bf16[8,48,4224]{2,1,0:T(8,128)(2,1)} %slot_rows.1), calls=%async_computation.1 | async-start | bytes 6488064 | tf_op jit(solution)/shard_map/all_to_all | solution.py:465
  177.8 2.5 add_convert_fusion.3
  180.3 4.4 %collective-permute-done.14 = bf16[1,256,1536]{2,1,0:T(8,128)(2,1)} collective-permute-done((bf16[1,256,1536]{2,1,0:T(8,128)(2,1)}, bf16[1,256,1536]{2,1,0:T(8,128)(2,1)}, u32[]{:S(2)}, u32[]{:S(2)}) %collective-permute-start.14) | collective-permute-done | bytes 786464 | tf_op jit(solution)/shard_map/ppermute | solution.py:450
  184.7 1.3 add_convert_fusion.2
  186.0 14.2 %collective-permute-done.18 = bf16[4,256,768]{2,1,0:T(8,128)(2,1)} collective-permute-done((bf16[4,256,768]{2,1,0:T(8,128)(2,1)}, bf16[4,256,768]{2,1,0:T(8,128)(2,1)}, u32[]{:S(2)}, u32[]{:S(2)}) %collective-permute-start.18) | collective-permute-done | bytes 1572896 | tf_op jit(solution)/shard_map/ppermute | solution.py:520
  200.3 1.9 add_convert_fusion
  202.4 3.2 %collective-permute-start.16 = (bf16[1,256,1536]{2,1,0:T(8,128)(2,1)S(1)}, bf16[1,256,1536]{2,1,0:T(8,128)(2,1)S(1)}, u32[]{:S(2)}, u32[]{:S(2)}) collective-permute-start(bf16[1,256,1536]{2,1,0:T(8,128)(2,1)S(1)} %copy-done.18), channel_id=1, source_target_pairs={{0,24},{8,0},{16,8},{24,16},{1,25},{9,1},{17,9},{25,17},{2,26},{10... | collective-permute-start | bytes 2359304 | tf_op jit(solution)/shard_map/ppermute | solution.py:453
  205.9 3.3 %collective-permute-start.21 = (bf16[128,768]{1,0:T(8,128)(2,1)S(1)}, bf16[128,768]{1,0:T(8,128)(2,1)S(1)}, u32[]{:S(2)}, u32[]{:S(2)}) collective-permute-start(bf16[128,768]{1,0:T(8,128)(2,1)S(1)} %get-tuple-element.93), channel_id=1, source_target_pairs={{0,24},{8,0},{16,8},{24,16},{1,25},{9,1},{17,9},{25,17},{2,26},{10... | collective-permute-start | bytes 589832 | tf_op jit(solution)/shard_map/ppermute | solution.py:453
  209.2 1.6 collective-permute-done.19
  211.3 16.2 %collective-permute-done.21 = bf16[128,768]{1,0:T(8,128)(2,1)S(1)} collective-permute-done((bf16[128,768]{1,0:T(8,128)(2,1)S(1)}, bf16[128,768]{1,0:T(8,128)(2,1)S(1)}, u32[]{:S(2)}, u32[]{:S(2)}) %collective-permute-start.21) | collective-permute-done | bytes 196640 | tf_op jit(solution)/shard_map/ppermute | solution.py:453
  227.5 2.1 collective-permute-done.22
  229.6 3.7 %collective-permute-start.12 = (bf16[1,256,1536]{2,1,0:T(8,128)(2,1)}, bf16[1,256,1536]{2,1,0:T(8,128)(2,1)}, u32[]{:S(2)}, u32[]{:S(2)}) collective-permute-start(bf16[1,256,1536]{2,1,0:T(8,128)(2,1)} %add_convert_fusion.3), channel_id=1, source_target_pairs={{0,24},{8,0},{16,8},{24,16},{1,25},{9,1},{17,9},{25,17},{2,26},{10... | collective-permute-start | bytes 2359304 | tf_op jit(solution)/shard_map/ppermute | solution.py:457
  233.5 3.3 %collective-permute-start.23 = (bf16[128,768]{1,0:T(8,128)(2,1)S(1)}, bf16[128,768]{1,0:T(8,128)(2,1)S(1)}, u32[]{:S(2)}, u32[]{:S(2)}) collective-permute-start(bf16[128,768]{1,0:T(8,128)(2,1)S(1)} %get-tuple-element.89), channel_id=1, source_target_pairs={{0,24},{8,0},{16,8},{24,16},{1,25},{9,1},{17,9},{25,17},{2,26},{10... | collective-permute-start | bytes 589832 | tf_op jit(solution)/shard_map/ppermute | solution.py:457
  236.8 1.2 add_convert_fusion.1
  237.9 0.6 collective-permute-start.17
  238.5 12.9 %collective-permute-done.24 = bf16[128,768]{1,0:T(8,128)(2,1)S(1)} collective-permute-done((bf16[128,768]{1,0:T(8,128)(2,1)S(1)}, bf16[128,768]{1,0:T(8,128)(2,1)S(1)}, u32[]{:S(2)}, u32[]{:S(2)}) %collective-permute-start.24) | collective-permute-done | bytes 196640 | tf_op jit(solution)/shard_map/ppermute | solution.py:452
  251.4 1.1 collective-permute-done.23
  252.6 0.9 maximum_bitcast_fusion
  253.5 2.2 fusion.3
  255.8 1.6 fusion.7
  257.7 0.5 fusion.16
  258.2 3.1 %convert_add_fusion = f32[1,256,1536]{2,1,0:T(8,128)} fusion(bf16[1,256,1536]{2,1,0:T(8,128)(2,1)} %collective-permute-done.17, bf16[1,256,1536]{2,1,0:T(8,128)(2,1)} %collective-permute-done.13, bf16[1,256,1536]{2,1,0:T(8,128)(2,1)} %collective-permute-done.12, bf16[1,256,1536]{2,1,0:T(8,128)(2,1)S(1)} %copy-done.4), kind=kLoop, calls=%fused_computation.13 | loop fusion | flops 2752512 | bytes 4718592 | tf_op jit(solution)/shard_map/add | solution.py:545
  (77 shorter events, 2.6 us)
Async XLA Ops:
  7.8 15.4 %copy-start.21 = (bf16[48,4096]{1,0:T(8,128)(2,1)S(1)}, bf16[48,4096]{1,0:T(8,128)(2,1)}, u32[]{:S(2)}) copy-start(bf16[48,4096]{1,0:T(8,128)(2,1)} %get-tuple-element.55) | copy-start | bytes 1179652
  7.8 53.7 %copy-start.20 = (bf16[48,4096]{1,0:T(8,128)(2,1)S(1)}, bf16[48,4096]{1,0:T(8,128)(2,1)}, u32[]{:S(2)}) copy-start(bf16[48,4096]{1,0:T(8,128)(2,1)} %get-tuple-element.56) | copy-start | bytes 1179652
  7.8 58.6 %copy-start.19 = (bf16[48,4096]{1,0:T(8,128)(2,1)S(1)}, bf16[48,4096]{1,0:T(8,128)(2,1)}, u32[]{:S(2)}) copy-start(bf16[48,4096]{1,0:T(8,128)(2,1)} %get-tuple-element.57) | copy-start | bytes 1179652
  7.8 119.1 %all-to-all-start = ((bf16[8,48,4096]{2,1,0:T(8,128)(2,1)}), bf16[8,48,4096]{2,1,0:T(8,128)(2,1)}, u32[]{:S(2)}, u32[]{:S(2)}) async-start(bf16[8,48,4096]{2,1,0:T(8,128)(2,1)} %get-tuple-element.49), calls=%async_computation | async-start | bytes 6291456 | tf_op jit(solution)/shard_map/all_to_all | solution.py:465
  15.8 45.7 %collective-permute-start = (bf16[48,4096]{1,0:T(8,128)(2,1)}, bf16[48,4096]{1,0:T(8,128)(2,1)S(1)}, u32[]{:S(2)}, u32[]{:S(2)}) collective-permute-start(bf16[48,4096]{1,0:T(8,128)(2,1)} %get-tuple-element.51), channel_id=1, source_target_pairs={{0,65},{1,64},{2,67},{3,66},{4,69},{5,68},{6,71},{7,70},{64,1},{65... | collective-permute-start | bytes 1179656 | tf_op jit(solution)/shard_map/ppermute | solution.py:439
  19.1 47.3 %collective-permute-start.1 = (bf16[48,4096]{1,0:T(8,128)(2,1)}, bf16[48,4096]{1,0:T(8,128)(2,1)S(1)}, u32[]{:S(2)}, u32[]{:S(2)}) collective-permute-start(bf16[48,4096]{1,0:T(8,128)(2,1)} %get-tuple-element.52), channel_id=1, source_target_pairs={{0,2},{1,3},{2,4},{3,5},{4,6},{5,7},{6,0},{7,1},{64,66},{65,67},{6... | collective-permute-start | bytes 1179656 | tf_op jit(solution)/shard_map/ppermute | solution.py:439
  20.5 57.3 %collective-permute-start.2 = (bf16[48,4096]{1,0:T(8,128)(2,1)}, bf16[48,4096]{1,0:T(8,128)(2,1)S(1)}, u32[]{:S(2)}, u32[]{:S(2)}) collective-permute-start(bf16[48,4096]{1,0:T(8,128)(2,1)} %get-tuple-element.53), channel_id=1, source_target_pairs={{0,67},{1,66},{2,69},{3,68},{4,71},{5,70},{6,65},{7,64},{64,3},{65... | collective-permute-start | bytes 1179656 | tf_op jit(solution)/shard_map/ppermute | solution.py:439
  22.0 73.0 %collective-permute-start.3 = (bf16[48,4096]{1,0:T(8,128)(2,1)}, bf16[48,4096]{1,0:T(8,128)(2,1)S(1)}, u32[]{:S(2)}, u32[]{:S(2)}) collective-permute-start(bf16[48,4096]{1,0:T(8,128)(2,1)} %get-tuple-element.54), channel_id=1, source_target_pairs={{0,4},{1,5},{2,6},{3,7},{4,0},{5,1},{6,2},{7,3},{64,68},{65,69},{6... | collective-permute-start | bytes 1179656 | tf_op jit(solution)/shard_map/ppermute | solution.py:439
  23.2 82.1 %collective-permute-start.4 = (bf16[48,4096]{1,0:T(8,128)(2,1)S(1)}, bf16[48,4096]{1,0:T(8,128)(2,1)S(1)}, u32[]{:S(2)}, u32[]{:S(2)}) collective-permute-start(bf16[48,4096]{1,0:T(8,128)(2,1)S(1)} %copy-done.21), channel_id=1, source_target_pairs={{0,69},{1,68},{2,71},{3,70},{4,65},{5,64},{6,67},{7,66},{64,5},{65... | collective-permute-start | bytes 1179656 | tf_op jit(solution)/shard_map/ppermute | solution.py:439
  61.5 43.9 %copy-start.8 = (bf16[48,4096]{1,0:T(8,128)(2,1)}, bf16[48,4096]{1,0:T(8,128)(2,1)S(1)}, u32[]{:S(2)}) copy-start(bf16[48,4096]{1,0:T(8,128)(2,1)S(1)} %collective-permute-done.refs_1_) | copy-start | bytes 1179652
  61.5 43.8 %collective-permute-start.5 = (bf16[48,4096]{1,0:T(8,128)(2,1)S(1)}, bf16[48,4096]{1,0:T(8,128)(2,1)}, u32[]{:S(2)}, u32[]{:S(2)}) collective-permute-start(bf16[48,4096]{1,0:T(8,128)(2,1)S(1)} %copy-done.20), channel_id=1, source_target_pairs={{0,6},{1,7},{2,0},{3,1},{4,2},{5,3},{6,4},{7,5},{64,70},{65,71},{6... | collective-permute-start | bytes 1179656 | tf_op jit(solution)/shard_map/ppermute | solution.py:439
  66.4 39.0 %copy-start.9 = (bf16[48,4096]{1,0:T(8,128)(2,1)}, bf16[48,4096]{1,0:T(8,128)(2,1)S(1)}, u32[]{:S(2)}) copy-start(bf16[48,4096]{1,0:T(8,128)(2,1)S(1)} %collective-permute-done.1.refs_2_) | copy-start | bytes 1179652
  66.4 39.0 %collective-permute-start.6 = (bf16[48,4096]{1,0:T(8,128)(2,1)S(1)}, bf16[48,4096]{1,0:T(8,128)(2,1)}, u32[]{:S(2)}, u32[]{:S(2)}) collective-permute-start(bf16[48,4096]{1,0:T(8,128)(2,1)S(1)} %copy-done.19), channel_id=1, source_target_pairs={{0,71},{1,70},{2,65},{3,64},{4,67},{5,66},{6,69},{7,68},{64,7},{65... | collective-permute-start | bytes 1179656 | tf_op jit(solution)/shard_map/ppermute | solution.py:439
  77.8 27.6 %copy-start.10 = (bf16[48,4096]{1,0:T(8,128)(2,1)}, bf16[48,4096]{1,0:T(8,128)(2,1)S(1)}, u32[]{:S(2)}) copy-start(bf16[48,4096]{1,0:T(8,128)(2,1)S(1)} %collective-permute-done.2.refs_3_) | copy-start | bytes 1179652
  95.0 10.4 %copy-start.11 = (bf16[48,4096]{1,0:T(8,128)(2,1)}, bf16[48,4096]{1,0:T(8,128)(2,1)S(1)}, u32[]{:S(2)}) copy-start(bf16[48,4096]{1,0:T(8,128)(2,1)S(1)} %collective-permute-done.3.refs_4_) | copy-start | bytes 1179652
  116.3 25.5 %collective-permute-start.7 = (bf16[2,4,256,384]{3,2,1,0:T(8,128)(2,1)}, bf16[2,4,256,384]{3,2,1,0:T(8,128)(2,1)}, u32[]{:S(2)}, u32[]{:S(2)}) collective-permute-start(bf16[2,4,256,384]{3,2,1,0:T(8,128)(2,1)} %get-tuple-element.70), channel_id=1, source_target_pairs={{0,32},{32,0},{1,33},{33,1},{2,34},{34,2},{3,35},{35,3},{4,36},{36... | collective-permute-start | bytes 4718600 | tf_op jit(solution)/shard_map/ppermute | solution.py:506
  135.6 6.2 %collective-permute-start.8 = (bf16[2,384,768]{2,1,0:T(8,128)(2,1)}, bf16[2,384,768]{2,1,0:T(8,128)(2,1)S(1)}, u32[]{:S(2)}, u32[]{:S(2)}) collective-permute-start(bf16[2,384,768]{2,1,0:T(8,128)(2,1)} %get-tuple-element.75.mine_ref.grads_ref), channel_id=1, source_target_pairs={{0,32},{32,0},{1,33},{33,1},{2,34},{34,2},{3,35},{35,3},{4,36},{36... | collective-permute-start | bytes 3538952 | tf_op jit(solution)/shard_map/ppermute | solution.py:510
  136.0 5.3 %copy-start.7 = (bf16[384,768]{1,0:T(8,128)(2,1)S(1)}, bf16[384,768]{1,0:T(8,128)(2,1)}, u32[]{:S(2)}) copy-start(bf16[384,768]{1,0:T(8,128)(2,1)} %get-tuple-element.58.hidden_ref) | copy-start | bytes 1769476
  141.3 15.7 %collective-permute-start.9 = (bf16[2,4,256,384]{3,2,1,0:T(8,128)(2,1)}, bf16[2,4,256,384]{3,2,1,0:T(8,128)(2,1)}, u32[]{:S(2)}, u32[]{:S(2)}) collective-permute-start(bf16[2,4,256,384]{3,2,1,0:T(8,128)(2,1)} %get-tuple-element.73), channel_id=1, source_target_pairs={{0,32},{32,0},{1,33},{33,1},{2,34},{34,2},{3,35},{35,3},{4,36},{36... | collective-permute-start | bytes 4718600 | tf_op jit(solution)/shard_map/ppermute | solution.py:513
  141.3 15.6 %collective-permute-start.10 = (bf16[384,768]{1,0:T(8,128)(2,1)S(1)}, bf16[384,768]{1,0:T(8,128)(2,1)}, u32[]{:S(2)}, u32[]{:S(2)}) collective-permute-start(bf16[384,768]{1,0:T(8,128)(2,1)S(1)} %copy-done.7), channel_id=1, source_target_pairs={{0,32},{32,0},{1,33},{33,1},{2,34},{34,2},{3,35},{35,3},{4,36},{36... | collective-permute-start | bytes 1769480 | tf_op jit(solution)/shard_map/ppermute | solution.py:508
  141.8 1.0 copy-start.17
  153.9 23.9 %collective-permute-start.11 = (bf16[1,256,1536]{2,1,0:T(8,128)(2,1)}, bf16[1,256,1536]{2,1,0:T(8,128)(2,1)}, u32[]{:S(2)}, u32[]{:S(2)}) collective-permute-start(bf16[1,256,1536]{2,1,0:T(8,128)(2,1)} %get-tuple-element.79), channel_id=1, source_target_pairs={{0,24},{8,0},{16,8},{24,16},{1,25},{9,1},{17,9},{25,17},{2,26},{10... | collective-permute-start | bytes 2359304 | tf_op jit(solution)/shard_map/ppermute | solution.py:451
  163.9 36.4 %collective-permute-start.18 = (bf16[4,256,768]{2,1,0:T(8,128)(2,1)}, bf16[4,256,768]{2,1,0:T(8,128)(2,1)}, u32[]{:S(2)}, u32[]{:S(2)}) collective-permute-start(bf16[4,256,768]{2,1,0:T(8,128)(2,1)} %get-tuple-element.86), channel_id=1, source_target_pairs={{0,64},{64,0},{1,65},{65,1},{2,66},{66,2},{3,67},{67,3},{4,68},{68... | collective-permute-start | bytes 4718600 | tf_op jit(solution)/shard_map/ppermute | solution.py:520
  163.9 20.8 %collective-permute-start.14 = (bf16[1,256,1536]{2,1,0:T(8,128)(2,1)}, bf16[1,256,1536]{2,1,0:T(8,128)(2,1)}, u32[]{:S(2)}, u32[]{:S(2)}) collective-permute-start(bf16[1,256,1536]{2,1,0:T(8,128)(2,1)} %get-tuple-element.83), channel_id=1, source_target_pairs={{0,8},{8,16},{16,24},{24,0},{1,9},{9,17},{17,25},{25,1},{2,10},{10... | collective-permute-start | bytes 2359304 | tf_op jit(solution)/shard_map/ppermute | solution.py:450
  174.1 79.4 %all-to-all-start.1 = ((bf16[8,48,4224]{2,1,0:T(8,128)(2,1)}), bf16[8,48,4224]{2,1,0:T(8,128)(2,1)S(1)}, u32[]{:S(2)}, u32[]{:S(2)}) async-start(bf16[8,48,4224]{2,1,0:T(8,128)(2,1)} %slot_rows.1), calls=%async_computation.1 | async-start | bytes 6488064 | tf_op jit(solution)/shard_map/all_to_all | solution.py:465
  177.8 6.9 %copy-start.6 = (bf16[1,256,1536]{2,1,0:T(8,128)(2,1)S(1)}, bf16[1,256,1536]{2,1,0:T(8,128)(2,1)}, u32[]{:S(2)}) copy-start(bf16[1,256,1536]{2,1,0:T(8,128)(2,1)} %get-tuple-element.82) | copy-start | bytes 2359300
  180.3 19.9 %copy-start.2 = (bf16[4,256,768]{2,1,0:T(8,128)(2,1)S(1)}, bf16[4,256,768]{2,1,0:T(8,128)(2,1)}, u32[]{:S(2)}) copy-start(bf16[4,256,768]{2,1,0:T(8,128)(2,1)} %get-tuple-element.74) | copy-start | bytes 4718596
  200.3 2.1 copy-start.18
  202.2 3.4 %copy-start = (bf16[128,4096]{1,0:T(8,128)(2,1)S(1)}, bf16[128,4096]{1,0:T(8,128)(2,1)}, u32[]{:S(2)}) copy-start(bf16[128,4096]{1,0:T(8,128)(2,1)} %resid_ref) | copy-start | bytes 3145732
  202.3 8.6 %collective-permute-start.19 = (bf16[128,768]{1,0:T(8,128)(2,1)S(1)}, bf16[128,768]{1,0:T(8,128)(2,1)S(1)}, u32[]{:S(2)}, u32[]{:S(2)}) collective-permute-start(bf16[128,768]{1,0:T(8,128)(2,1)S(1)} %get-tuple-element.90), channel_id=1, source_target_pairs={{0,8},{8,16},{16,24},{24,0},{1,9},{9,17},{17,25},{25,1},{2,10},{10... | collective-permute-start | bytes 589832 | tf_op jit(solution)/shard_map/ppermute | solution.py:450
  202.3 34.4 %copy-start.5 = (bf16[1,256,1536]{2,1,0:T(8,128)(2,1)S(1)}, bf16[1,256,1536]{2,1,0:T(8,128)(2,1)}, u32[]{:S(2)}) copy-start(bf16[1,256,1536]{2,1,0:T(8,128)(2,1)} %get-tuple-element.81) | copy-start | bytes 2359300
  202.4 31.1 %collective-permute-start.16 = (bf16[1,256,1536]{2,1,0:T(8,128)(2,1)S(1)}, bf16[1,256,1536]{2,1,0:T(8,128)(2,1)S(1)}, u32[]{:S(2)}, u32[]{:S(2)}) collective-permute-start(bf16[1,256,1536]{2,1,0:T(8,128)(2,1)S(1)} %copy-done.18), channel_id=1, source_target_pairs={{0,24},{8,0},{16,8},{24,16},{1,25},{9,1},{17,9},{25,17},{2,26},{10... | collective-permute-start | bytes 2359304 | tf_op jit(solution)/shard_map/ppermute | solution.py:453
  205.6 31.2 %collective-permute-start.15 = (bf16[1,256,1536]{2,1,0:T(8,128)(2,1)S(1)}, bf16[1,256,1536]{2,1,0:T(8,128)(2,1)S(1)}, u32[]{:S(2)}, u32[]{:S(2)}) collective-permute-start(bf16[1,256,1536]{2,1,0:T(8,128)(2,1)S(1)} %add_convert_fusion.2), channel_id=1, source_target_pairs={{0,8},{8,16},{16,24},{24,0},{1,9},{9,17},{17,25},{25,1},{2,10},{10... | collective-permute-start | bytes 2359304 | tf_op jit(solution)/shard_map/ppermute | solution.py:456
  205.9 21.7 %collective-permute-start.21 = (bf16[128,768]{1,0:T(8,128)(2,1)S(1)}, bf16[128,768]{1,0:T(8,128)(2,1)S(1)}, u32[]{:S(2)}, u32[]{:S(2)}) collective-permute-start(bf16[128,768]{1,0:T(8,128)(2,1)S(1)} %get-tuple-element.93), channel_id=1, source_target_pairs={{0,24},{8,0},{16,8},{24,16},{1,25},{9,1},{17,9},{25,17},{2,26},{10... | collective-permute-start | bytes 589832 | tf_op jit(solution)/shard_map/ppermute | solution.py:453
  209.2 20.5 %collective-permute-start.22 = (bf16[128,768]{1,0:T(8,128)(2,1)S(1)}, bf16[128,768]{1,0:T(8,128)(2,1)S(1)}, u32[]{:S(2)}, u32[]{:S(2)}) collective-permute-start(bf16[128,768]{1,0:T(8,128)(2,1)S(1)} %get-tuple-element.92), channel_id=1, source_target_pairs={{0,24},{8,0},{16,8},{24,16},{1,25},{9,1},{17,9},{25,17},{2,26},{10... | collective-permute-start | bytes 589832 | tf_op jit(solution)/shard_map/ppermute | solution.py:451
  210.9 22.4 %collective-permute-start.20 = (bf16[128,768]{1,0:T(8,128)(2,1)S(1)}, bf16[128,768]{1,0:T(8,128)(2,1)S(1)}, u32[]{:S(2)}, u32[]{:S(2)}) collective-permute-start(bf16[128,768]{1,0:T(8,128)(2,1)S(1)} %fusion.11), channel_id=1, source_target_pairs={{0,8},{8,16},{16,24},{24,0},{1,9},{9,17},{17,25},{25,1},{2,10},{10... | collective-permute-start | bytes 589832 | tf_op jit(solution)/shard_map/ppermute | solution.py:456
  227.5 30.7 %collective-permute-start.13 = (bf16[1,256,1536]{2,1,0:T(8,128)(2,1)}, bf16[1,256,1536]{2,1,0:T(8,128)(2,1)}, u32[]{:S(2)}, u32[]{:S(2)}) collective-permute-start(bf16[1,256,1536]{2,1,0:T(8,128)(2,1)} %get-tuple-element.80), channel_id=1, source_target_pairs={{0,8},{8,16},{16,24},{24,0},{1,9},{9,17},{17,25},{25,1},{2,10},{10... | collective-permute-start | bytes 2359304 | tf_op jit(solution)/shard_map/ppermute | solution.py:452
  229.6 28.6 %collective-permute-start.12 = (bf16[1,256,1536]{2,1,0:T(8,128)(2,1)}, bf16[1,256,1536]{2,1,0:T(8,128)(2,1)}, u32[]{:S(2)}, u32[]{:S(2)}) collective-permute-start(bf16[1,256,1536]{2,1,0:T(8,128)(2,1)} %add_convert_fusion.3), channel_id=1, source_target_pairs={{0,24},{8,0},{16,8},{24,16},{1,25},{9,1},{17,9},{25,17},{2,26},{10... | collective-permute-start | bytes 2359304 | tf_op jit(solution)/shard_map/ppermute | solution.py:457
  233.3 18.1 %collective-permute-start.24 = (bf16[128,768]{1,0:T(8,128)(2,1)S(1)}, bf16[128,768]{1,0:T(8,128)(2,1)S(1)}, u32[]{:S(2)}, u32[]{:S(2)}) collective-permute-start(bf16[128,768]{1,0:T(8,128)(2,1)S(1)} %get-tuple-element.91), channel_id=1, source_target_pairs={{0,8},{8,16},{16,24},{24,0},{1,9},{9,17},{17,25},{25,1},{2,10},{10... | collective-permute-start | bytes 589832 | tf_op jit(solution)/shard_map/ppermute | solution.py:452
  233.5 19.1 %collective-permute-start.23 = (bf16[128,768]{1,0:T(8,128)(2,1)S(1)}, bf16[128,768]{1,0:T(8,128)(2,1)S(1)}, u32[]{:S(2)}, u32[]{:S(2)}) collective-permute-start(bf16[128,768]{1,0:T(8,128)(2,1)S(1)} %get-tuple-element.89), channel_id=1, source_target_pairs={{0,24},{8,0},{16,8},{24,16},{1,25},{9,1},{17,9},{25,17},{2,26},{10... | collective-permute-start | bytes 589832 | tf_op jit(solution)/shard_map/ppermute | solution.py:457
  237.9 15.6 %copy-start.14 = (bf16[384,128]{1,0:T(8,128)(2,1)S(1)}, bf16[384,128]{1,0:T(8,128)(2,1)}, u32[]{:S(2)}) copy-start(bf16[384,128]{1,0:T(8,128)(2,1)} %get-tuple-element.48) | copy-start | bytes 294916
  237.9 15.6 %copy-start.15 = (f32[4096]{0:T(1024)S(1)}, f32[4096]{0:T(1024)}, u32[]{:S(2)}) copy-start(f32[4096]{0:T(1024)} %param.8) | copy-start | bytes 49156
  237.9 19.5 %collective-permute-start.17 = (bf16[1,256,1536]{2,1,0:T(8,128)(2,1)}, bf16[1,256,1536]{2,1,0:T(8,128)(2,1)}, u32[]{:S(2)}, u32[]{:S(2)}) collective-permute-start(bf16[1,256,1536]{2,1,0:T(8,128)(2,1)} %add_convert_fusion.1), channel_id=1, source_target_pairs={{0,64},{64,0},{1,65},{65,1},{2,66},{66,2},{3,67},{67,3},{4,68},{68... | collective-permute-start | bytes 2359304 | tf_op jit(solution)/shard_map/ppermute | solution.py:522
  253.5 2.3 copy-start.1
  253.5 2.3 copy-start.3
  255.8 1.7 copy-start.13
  255.8 1.8 copy-start.16
  255.8 2.4 copy-start.4
  (1 other events, 0.8 us)

commit v9 on v8

--- a/solution.py
+++ b/solution.py
@@ -14,7 +14,7 @@
 
 eps = 1e-06
 
-VMEM = 62 * 2**20
+VMEM = 66_000_000
 
 
 def contract(left, right, over_left, over_right):
@@ -208,7 +208,7 @@
         route_ref[...] = jnp.broadcast_to(acc_ref[...], route_ref.shape).astype(jnp.bfloat16)
 
 
-def back(got, w_down, hidden, gate, up, block=256):
+def back(got, w_down, hidden, gate, up, block=384):
     parts, capacity, width = got.shape
     slots = parts * capacity
     hidden_width = w_down.shape[0]
@@ -388,12 +388,16 @@
     return far, near
 
 
-def slot_kernel(grads_ref, w_ref, route_ref, out_ref):
+def slot_kernel(grads_ref, w_ref, route_ref, out_ref, both_ref):
     width = grads_ref.shape[2]
     block = w_ref.shape[0]
-    rows = contract(grads_ref[0], w_ref[:, :width], 1, 1) + contract(
-        grads_ref[1], w_ref[:, width:], 1, 1
-    )
+
+    @pl.when(pl.program_id(0) == 0)
+    def _():
+        both_ref[:, :width] = grads_ref[0]
+        both_ref[:, width:] = grads_ref[1]
+
+    rows = contract(both_ref[...], w_ref[...], 1, 1)
     at = pl.ds(pl.multiple_of(pl.program_id(0) * block, block), block)
     out_ref[:, :, at] = rows.astype(jnp.bfloat16).reshape(out_ref.shape[:2] + (block,))
 
@@ -405,7 +409,7 @@
         )
 
 
-def slot_rows(grads, w_in, route, parts, block=1024):
+def slot_rows(grads, w_in, route, parts, block=512):
     _, slots, hidden_width = grads.shape
     width = w_in.shape[0]
     shape = (parts, slots // parts, width + route.shape[1])
@@ -419,6 +423,7 @@
         ],
         out_specs=pl.BlockSpec(shape, lambda j: (0, 0, 0)),
         out_shape=jax.ShapeDtypeStruct(shape, jnp.bfloat16),
+        scratch_shapes=[pltpu.VMEM((slots, 2 * hidden_width), jnp.bfloat16)],
         compiler_params=pltpu.CompilerParams(vmem_limit_bytes=VMEM),
         cost_estimate=pl.CostEstimate(
             flops=4 * slots * hidden_width * width,
@@ -541,6 +546,7 @@
         scaled_normed - unit_rows * jnp.mean(scaled_normed * unit_rows, axis=-1, keepdims=True)
     )
     grad_residual = (grad_out.astype(jnp.float32) + branch).astype(jnp.bfloat16)
+    near_in = lax.optimization_barrier(near_in)
     came_in, _ = lax.optimization_barrier((came_in, grad_residual))
     grad_in = near_in + came_in.astype(jnp.float32)
     return (grad_residual, route_grad, grad_in, grad_down)

time: 263 us -> 246 us (0.935)
  waiting for transfers between devices: 121 us -> 103 us
    ppermute x2, waiting for transfers between devices: 12.9 us -> 2.01 us  [ring_sum(): high_side = lax.ppermute(high[1], 'ulysses', ahead)]
    ppermute x2, starting transfers between devices: 6.51 us -> 1.85 us  [ring_sum(): low_side = lax.ppermute(low[3], 'ulysses', behind)]
    ppermute x2, waiting for transfers between devices: 16.2 us -> 12.8 us  [ring_sum(): low_side = lax.ppermute(low[3], 'ulysses', behind)]
    ppermute x2, starting transfers between devices: 0.15 us -> 3.26 us  [ring_sum(): low_two = lax.ppermute(low[2], 'ulysses', ahead)]
    ppermute x2, starting transfers between devices: 6.99 us -> 4.01 us  [ring_sum(): high_last = lax.ppermute(high_both, 'ulysses', behind)]
  transfers between devices with their start and end apart: 27 -> 27, of which waited for: 12 -> 12; matrix products, arithmetic and copies ran while one was open for 5% -> 6% of each run, Pallas kernels for 24% -> 27%
where the time goes in v9:
time: 246 us; the launch traced here: 245 us
  waiting for transfers between devices  103 us (42%)
  Pallas kernels  71.8 us (29%)
  starting transfers between devices  50.2 us (20%)
  other arithmetic  16.6 us (7%)
    ppermute x7, waiting for transfers between devices, displaced(): return lax.ppermute(rows, ('dp_0', 'expert'), pairs)  68.4 us
    ppermute x7, starting transfers between devices, displaced(): return lax.ppermute(rows, ('dp_0', 'expert'), pairs)  21.2 us
    ppermute x2, waiting for transfers between devices, ring_sum(): low_side = lax.ppermute(low[3], 'ulysses', behind)  12.8 us
    ppermute x1, waiting for transfers between devices, per_device(): came_down = lax.ppermute(far_down, 'dp_0', SWAP)  12.2 us
    pallas_call x1, Pallas kernels, slot_rows(): pl.pallas_call(slot_kernel, grid=(width // block,), in_specs=[pl.BlockSpe...  12.1 us
    all_to_all x2, starting transfers between devices, exchange(): lax.all_to_all(rows, ('dp_0', 'expert'), split_axis=0, concat_axis=0, axi...  11.7 us
    pallas_call x1, Pallas kernels, weight_messages(): pl.pallas_call(messages_kernel, grid_spec=pltpu.PrefetchScalarGridSpec(nu...  11.1 us
    pallas_call x1, Pallas kernels, forward(): pl.pallas_call(forward_kernel, grid=(steps,), in_specs=[pl.BlockSpec(got....  10.5 us
  transfers between devices with their start and end apart: 27, of which 12 were waited for; matrix products, arithmetic and copies ran while one was open for 6% of the time, Pallas kernels for 27%

profile of v9, /device:TPU:0, one launch (start us, length us, event | category | flops | bytes accessed | tf_op | source)
XLA Modules:
  0.0 245.0 jit_solution(8247684344810005520)
XLA Ops:
  1.2 6.5 %pack.1 = (bf16[48,4096]{1,0:T(8,128)(2,1)}, bf16[48,4096]{1,0:T(8,128)(2,1)}, bf16[48,4096]{1,0:T(8,128)(2,1)}, bf16[48,4096]{1,0:T(8,128)(2,1)}, bf16[48,4096]...) custom-call(s32[4]{0:T(128)} %pad_add_fusion.place_ref._, ...), custom_call_target="tpu_custom_call" | custom-call | flops 805306368 | bytes 6291456 | tf_op jit(solution)/shard_map/pack/pallas_call | solution.py:90
  7.8 8.0 %all-to-all-start = ((bf16[8,48,4096]{2,1,0:T(8,128)(2,1)}), bf16[8,48,4096]{2,1,0:T(8,128)(2,1)}, u32[]{:S(2)}, u32[]{:S(2)}) async-start(bf16[8,48,4096]{2,1,0:T(8,128)(2,1)} %get-tuple-element.49), calls=%async_computation | async-start | bytes 6291456 | tf_op jit(solution)/shard_map/all_to_all | solution.py:470
  15.8 3.2 %collective-permute-start = (bf16[48,4096]{1,0:T(8,128)(2,1)}, bf16[48,4096]{1,0:T(8,128)(2,1)S(1)}, u32[]{:S(2)}, u32[]{:S(2)}) collective-permute-start(bf16[48,4096]{1,0:T(8,128)(2,1)} %get-tuple-element.51), channel_id=1, source_target_pairs={{0,65},{1,64},{2,67},{3,66},{4,69},{5,68},{6,71},{7,70},{64,1},{65... | collective-permute-start | bytes 1179656 | tf_op jit(solution)/shard_map/ppermute | solution.py:444
  19.1 1.5 collective-permute-start.1
  20.5 1.5 collective-permute-start.2
  22.0 1.3 collective-permute-start.3
  23.3 4.3 %collective-permute-start.4 = (bf16[48,4096]{1,0:T(8,128)(2,1)S(1)}, bf16[48,4096]{1,0:T(8,128)(2,1)}, u32[]{:S(2)}, u32[]{:S(2)}) collective-permute-start(bf16[48,4096]{1,0:T(8,128)(2,1)S(1)} %copy-done.17), channel_id=1, source_target_pairs={{0,69},{1,68},{2,71},{3,70},{4,65},{5,64},{6,67},{7,66},{64,5},{65... | collective-permute-start | bytes 1179656 | tf_op jit(solution)/shard_map/ppermute | solution.py:444
  27.7 33.9 %collective-permute-done.refs_1_ = bf16[48,4096]{1,0:T(8,128)(2,1)S(1)} collective-permute-done((bf16[48,4096]{1,0:T(8,128)(2,1)}, bf16[48,4096]{1,0:T(8,128)(2,1)S(1)}, u32[]{:S(2)}, u32[]{:S(2)}) %collective-permute-start) | collective-permute-done | bytes 393248 | tf_op jit(solution)/shard_map/ppermute | solution.py:444
  61.5 2.7 %collective-permute-start.5 = (bf16[48,4096]{1,0:T(8,128)(2,1)S(1)}, bf16[48,4096]{1,0:T(8,128)(2,1)}, u32[]{:S(2)}, u32[]{:S(2)}) collective-permute-start(bf16[48,4096]{1,0:T(8,128)(2,1)S(1)} %copy-done.16), channel_id=1, source_target_pairs={{0,6},{1,7},{2,0},{3,1},{4,2},{5,3},{6,4},{7,5},{64,70},{65,71},{6... | collective-permute-start | bytes 1179656 | tf_op jit(solution)/shard_map/ppermute | solution.py:444
  64.2 2.2 collective-permute-done.1.refs_2_
  66.4 6.7 %collective-permute-start.6 = (bf16[48,4096]{1,0:T(8,128)(2,1)S(1)}, bf16[48,4096]{1,0:T(8,128)(2,1)}, u32[]{:S(2)}, u32[]{:S(2)}) collective-permute-start(bf16[48,4096]{1,0:T(8,128)(2,1)S(1)} %copy-done.15), channel_id=1, source_target_pairs={{0,71},{1,70},{2,65},{3,64},{4,67},{5,66},{6,69},{7,68},{64,7},{65... | collective-permute-start | bytes 1179656 | tf_op jit(solution)/shard_map/ppermute | solution.py:444
  73.1 4.6 %collective-permute-done.2.refs_3_ = bf16[48,4096]{1,0:T(8,128)(2,1)} collective-permute-done((bf16[48,4096]{1,0:T(8,128)(2,1)S(1)}, bf16[48,4096]{1,0:T(8,128)(2,1)}, u32[]{:S(2)}, u32[]{:S(2)}) %collective-permute-start.2) | collective-permute-done | bytes 393248 | tf_op jit(solution)/shard_map/ppermute | solution.py:444
  77.7 17.4 %collective-permute-done.3.refs_4_ = bf16[48,4096]{1,0:T(8,128)(2,1)} collective-permute-done((bf16[48,4096]{1,0:T(8,128)(2,1)S(1)}, bf16[48,4096]{1,0:T(8,128)(2,1)}, u32[]{:S(2)}, u32[]{:S(2)}) %collective-permute-start.3) | collective-permute-done | bytes 393248 | tf_op jit(solution)/shard_map/ppermute | solution.py:444
  95.1 10.3 %collective-permute-done.4.refs_5_ = bf16[48,4096]{1,0:T(8,128)(2,1)} collective-permute-done((bf16[48,4096]{1,0:T(8,128)(2,1)S(1)}, bf16[48,4096]{1,0:T(8,128)(2,1)}, u32[]{:S(2)}, u32[]{:S(2)}) %collective-permute-start.4) | collective-permute-done | bytes 393248 | tf_op jit(solution)/shard_map/ppermute | solution.py:444
  105.5 5.2 %gather.1.got_ref.keep_ref.give_ref = bf16[8,48,4096]{2,1,0:T(8,128)(2,1)} custom-call(s32[4]{0:T(128)} %pad_add_fusion.place_ref._, bf16[48,4096]{1,0:T(8,128)(2,1)} %get-tuple-element.50.refs_0_, bf16[48,4096]{1,0:T(8,128)(2,1)} %copy-done.8, bf16[48,4096]{1,0:T(8,128)(2,1)} %copy-done.9, bf16[48,4096]{1,0:T(8,128)(2,1)} %collective-permute-done.2.refs_3_, ...), custom_call_target="tpu_custom_call" | custom-call | flops 402653184 | bytes 6291456 | tf_op jit(solution)/shard_map/gather/pallas_call | solution.py:131
  110.6 5.1 %turn.2 = (bf16[2,4,256,384]{3,2,1,0:T(8,128)(2,1)}, bf16[2,4,256,384]{3,2,1,0:T(8,128)(2,1)}) custom-call(s32[4]{0:T(128)} %pad_add_fusion.place_ref._, bf16[8,48,4096]{2,1,0:T(8,128)(2,1)} %gather.1.got_ref.keep_ref.give_ref, bf16[8,48,4096]{2,1,0:T(8,128)(2,1)} %gather.1.got_ref.keep_ref.give_ref), custom_call_target="tpu_custom_call" | custom-call | flops 1610612736 | bytes 6291456 | tf_op jit(solution)/shard_map/turn/pallas_call | solution.py:262
  115.7 10.5 %forward.1 = (bf16[384,768]{1,0:T(8,128)(2,1)}, f32[384,768]{1,0:T(8,128)}, f32[384,768]{1,0:T(8,128)}) custom-call(bf16[8,48,4096]{2,1,0:T(8,128)(2,1)} %gather.1.got_ref.keep_ref.give_ref, bf16[4096,1536]{1,0:T(8,128)(2,1)} %bitcast.48, bf16[4096,1536]{1,0:T(8,128)(2,1)} %bitcast.49), custom_call_target="tpu_custom_call" | custom-call | flops 4831838208 | bytes 15728640 | tf_op jit(solution)/shard_map/forward/pallas_call | solution.py:168
  126.2 9.2 %back.1 = (bf16[2,384,768]{2,1,0:T(8,128)(2,1)}, bf16[384,128]{1,0:T(8,128)(2,1)}) custom-call(bf16[8,48,4096]{2,1,0:T(8,128)(2,1)} %all-to-all-done.got_ref.keep_ref.give_ref, bf16[768,4096]{1,0:T(8,128)(2,1)} %bitcast.53, bf16[384,768]{1,0:T(8,128)(2,1)} %get-tuple-element.58.hidden_ref, f32[384,768]{1,0:T(8,128)} %get-tuple-element.59.gate_ref, ...), custom_call_target="tpu_custom_call" | custom-call | flops 2415919104 | bytes 12386304 | tf_op jit(solution)/shard_map/back/pallas_call | solution.py:216
  135.9 5.2 %turn.3 = (bf16[2,4,256,384]{3,2,1,0:T(8,128)(2,1)}, bf16[2,4,256,384]{3,2,1,0:T(8,128)(2,1)}) custom-call(s32[4]{0:T(128)} %pad_add_fusion.place_ref._, bf16[8,48,4096]{2,1,0:T(8,128)(2,1)} %all-to-all-done.got_ref.keep_ref.give_ref, bf16[8,48,4096]{2,1,0:T(8,128)(2,1)} %all-to-all-done.got_ref.keep_ref.give_ref), custom_call_target="tpu_custom_call" | custom-call | flops 1610612736 | bytes 6291456 | tf_op jit(solution)/shard_map/turn/pallas_call | solution.py:262
  141.6 11.1 %grad_in.1 = (bf16[1,256,1536]{2,1,0:T(8,128)(2,1)}, bf16[1,256,1536]{2,1,0:T(8,128)(2,1)}, bf16[1,256,1536]{2,1,0:T(8,128)(2,1)}, bf16[1,256,1536]{2,1,0:T(8,12...) custom-call(s32[4]{0:T(128)} %pad_add_fusion.place_ref._, ...), custom_call_target="tpu_custom_call" | custom-call | flops 4831838208 | bytes 11796480 | tf_op jit(solution)/shard_map/grad_in/pallas_call | solution.py:367
  152.7 1.6 collective-permute-start.14
  154.3 6.9 %shard_map.102 = (bf16[4,256,768]{2,1,0:T(8,128)(2,1)}, bf16[4,256,768]{2,1,0:T(8,128)(2,1)}) custom-call(s32[4]{0:T(128)} %pad_add_fusion.place_ref._, bf16[2,4,256,384]{3,2,1,0:T(8,128)(2,1)} %get-tuple-element.72.keep_ref, bf16[2,4,256,384]{3,2,1,0:T(8,128)(2,1)} %collective-permute-done.9.came_ref, bf16[1,384,768]{2,1,0:T(8,128)(2,1)} %bitcast.54, ...), custom_call_target="tpu_custom_call" | custom-call | flops 2415919104 | bytes 7471104 | tf_op jit(solution)/shard_map/pallas_call | solution.py:317
  161.2 1.5 fusion.8
  162.7 1.7 collective-permute-start.11
  164.4 1.8 collective-permute-start.16
  166.3 12.1 %slot_rows.1 = bf16[8,48,4224]{2,1,0:T(8,128)(2,1)} custom-call(bf16[2,384,768]{2,1,0:T(8,128)(2,1)} %get-tuple-element.75.mine_ref.grads_ref, bf16[4096,1536]{1,0:T(8,128)(2,1)} %bitcast.50, bf16[384,128]{1,0:T(8,128)(2,1)} %get-tuple-element.76.route_ref), custom_call_target="tpu_custom_call" | custom-call | flops 4831838208 | bytes 15728640 | tf_op jit(solution)/shard_map/slot_rows/pallas_call | solution.py:416
  178.4 3.7 %all-to-all-start.1 = ((bf16[8,48,4224]{2,1,0:T(8,128)(2,1)}), bf16[8,48,4224]{2,1,0:T(8,128)(2,1)S(1)}, u32[]{:S(2)}, u32[]{:S(2)}) async-start(bf16[8,48,4224]{2,1,0:T(8,128)(2,1)} %slot_rows.1), calls=%async_computation.1 | async-start | bytes 6488064 | tf_op jit(solution)/shard_map/all_to_all | solution.py:470
  182.1 1.6 add_convert_fusion.2
  184.0 1.5 add_convert_fusion.3
  185.4 12.2 %collective-permute-done.18 = bf16[4,256,768]{2,1,0:T(8,128)(2,1)} collective-permute-done((bf16[4,256,768]{2,1,0:T(8,128)(2,1)}, bf16[4,256,768]{2,1,0:T(8,128)(2,1)}, u32[]{:S(2)}, u32[]{:S(2)}) %collective-permute-start.18) | collective-permute-done | bytes 1572896 | tf_op jit(solution)/shard_map/ppermute | solution.py:525
  197.6 1.8 add_convert_fusion
  199.5 1.6 collective-permute-start.19
  201.2 1.3 collective-permute-start.13
  202.5 2.0 collective-permute-start.12
  204.4 4.8 %collective-permute-done.19 = bf16[128,768]{1,0:T(8,128)(2,1)S(1)} collective-permute-done((bf16[128,768]{1,0:T(8,128)(2,1)S(1)}, bf16[128,768]{1,0:T(8,128)(2,1)S(1)}, u32[]{:S(2)}, u32[]{:S(2)}) %collective-permute-start.19) | collective-permute-done | bytes 196640 | tf_op jit(solution)/shard_map/ppermute | solution.py:455
  209.3 1.7 collective-permute-start.22
  211.5 2.3 add_convert_fusion.1
  213.8 12.8 %collective-permute-done.21 = bf16[128,768]{1,0:T(8,128)(2,1)S(1)} collective-permute-done((bf16[128,768]{1,0:T(8,128)(2,1)S(1)}, bf16[128,768]{1,0:T(8,128)(2,1)S(1)}, u32[]{:S(2)}, u32[]{:S(2)}) %collective-permute-start.21) | collective-permute-done | bytes 196640 | tf_op jit(solution)/shard_map/ppermute | solution.py:458
  227.2 1.5 collective-permute-done.22
  228.7 1.3 collective-permute-start.24
  230.1 2.1 collective-permute-start.23
  232.2 1.4 convert_add_fusion.1
  233.6 2.0 collective-permute-done.24
  235.9 0.9 maximum_bitcast_fusion
  236.9 2.2 fusion.3
  239.2 1.6 fusion.7
  240.8 1.0 collective-permute-done.17
  242.5 2.5 %convert_add_fusion = f32[1,256,1536]{2,1,0:T(8,128)} fusion(f32[1,256,1536]{2,1,0:T(8,128)S(1)} %copy-done.1, bf16[1,256,1536]{2,1,0:T(8,128)(2,1)} %collective-permute-done.17), kind=kLoop, calls=%fused_computation.13 | loop fusion | flops 786432 | bytes 3932160 | tf_op jit(solution)/shard_map/add | solution.py:551
  (76 shorter events, 4.3 us)
Async XLA Ops:
  7.8 11.3 %copy-start.20 = (bf16[48,4096]{1,0:T(8,128)(2,1)S(1)}, bf16[48,4096]{1,0:T(8,128)(2,1)}, u32[]{:S(2)}) copy-start(bf16[48,4096]{1,0:T(8,128)(2,1)} %get-tuple-element.52) | copy-start | bytes 1179652
  7.8 12.8 %copy-start.19 = (bf16[48,4096]{1,0:T(8,128)(2,1)S(1)}, bf16[48,4096]{1,0:T(8,128)(2,1)}, u32[]{:S(2)}) copy-start(bf16[48,4096]{1,0:T(8,128)(2,1)} %get-tuple-element.53) | copy-start | bytes 1179652
  7.8 14.2 %copy-start.18 = (bf16[48,4096]{1,0:T(8,128)(2,1)S(1)}, bf16[48,4096]{1,0:T(8,128)(2,1)}, u32[]{:S(2)}) copy-start(bf16[48,4096]{1,0:T(8,128)(2,1)} %get-tuple-element.54) | copy-start | bytes 1179652
  7.8 15.5 %copy-start.17 = (bf16[48,4096]{1,0:T(8,128)(2,1)S(1)}, bf16[48,4096]{1,0:T(8,128)(2,1)}, u32[]{:S(2)}) copy-start(bf16[48,4096]{1,0:T(8,128)(2,1)} %get-tuple-element.55) | copy-start | bytes 1179652
  7.8 53.7 %copy-start.16 = (bf16[48,4096]{1,0:T(8,128)(2,1)S(1)}, bf16[48,4096]{1,0:T(8,128)(2,1)}, u32[]{:S(2)}) copy-start(bf16[48,4096]{1,0:T(8,128)(2,1)} %get-tuple-element.56) | copy-start | bytes 1179652
  7.8 58.6 %copy-start.15 = (bf16[48,4096]{1,0:T(8,128)(2,1)S(1)}, bf16[48,4096]{1,0:T(8,128)(2,1)}, u32[]{:S(2)}) copy-start(bf16[48,4096]{1,0:T(8,128)(2,1)} %get-tuple-element.57) | copy-start | bytes 1179652
  7.8 118.4 %all-to-all-start = ((bf16[8,48,4096]{2,1,0:T(8,128)(2,1)}), bf16[8,48,4096]{2,1,0:T(8,128)(2,1)}, u32[]{:S(2)}, u32[]{:S(2)}) async-start(bf16[8,48,4096]{2,1,0:T(8,128)(2,1)} %get-tuple-element.49), calls=%async_computation | async-start | bytes 6291456 | tf_op jit(solution)/shard_map/all_to_all | solution.py:470
  15.8 45.7 %collective-permute-start = (bf16[48,4096]{1,0:T(8,128)(2,1)}, bf16[48,4096]{1,0:T(8,128)(2,1)S(1)}, u32[]{:S(2)}, u32[]{:S(2)}) collective-permute-start(bf16[48,4096]{1,0:T(8,128)(2,1)} %get-tuple-element.51), channel_id=1, source_target_pairs={{0,65},{1,64},{2,67},{3,66},{4,69},{5,68},{6,71},{7,70},{64,1},{65... | collective-permute-start | bytes 1179656 | tf_op jit(solution)/shard_map/ppermute | solution.py:444
  19.1 47.3 %collective-permute-start.1 = (bf16[48,4096]{1,0:T(8,128)(2,1)S(1)}, bf16[48,4096]{1,0:T(8,128)(2,1)S(1)}, u32[]{:S(2)}, u32[]{:S(2)}) collective-permute-start(bf16[48,4096]{1,0:T(8,128)(2,1)S(1)} %copy-done.20), channel_id=1, source_target_pairs={{0,2},{1,3},{2,4},{3,5},{4,6},{5,7},{6,0},{7,1},{64,66},{65,67},{6... | collective-permute-start | bytes 1179656 | tf_op jit(solution)/shard_map/ppermute | solution.py:444
  20.5 57.1 %collective-permute-start.2 = (bf16[48,4096]{1,0:T(8,128)(2,1)S(1)}, bf16[48,4096]{1,0:T(8,128)(2,1)}, u32[]{:S(2)}, u32[]{:S(2)}) collective-permute-start(bf16[48,4096]{1,0:T(8,128)(2,1)S(1)} %copy-done.19), channel_id=1, source_target_pairs={{0,67},{1,66},{2,69},{3,68},{4,71},{5,70},{6,65},{7,64},{64,3},{65... | collective-permute-start | bytes 1179656 | tf_op jit(solution)/shard_map/ppermute | solution.py:444
  22.0 73.1 %collective-permute-start.3 = (bf16[48,4096]{1,0:T(8,128)(2,1)S(1)}, bf16[48,4096]{1,0:T(8,128)(2,1)}, u32[]{:S(2)}, u32[]{:S(2)}) collective-permute-start(bf16[48,4096]{1,0:T(8,128)(2,1)S(1)} %copy-done.18), channel_id=1, source_target_pairs={{0,4},{1,5},{2,6},{3,7},{4,0},{5,1},{6,2},{7,3},{64,68},{65,69},{6... | collective-permute-start | bytes 1179656 | tf_op jit(solution)/shard_map/ppermute | solution.py:444
  23.3 82.1 %collective-permute-start.4 = (bf16[48,4096]{1,0:T(8,128)(2,1)S(1)}, bf16[48,4096]{1,0:T(8,128)(2,1)}, u32[]{:S(2)}, u32[]{:S(2)}) collective-permute-start(bf16[48,4096]{1,0:T(8,128)(2,1)S(1)} %copy-done.17), channel_id=1, source_target_pairs={{0,69},{1,68},{2,71},{3,70},{4,65},{5,64},{6,67},{7,66},{64,5},{65... | collective-permute-start | bytes 1179656 | tf_op jit(solution)/shard_map/ppermute | solution.py:444
  61.5 43.9 %copy-start.8 = (bf16[48,4096]{1,0:T(8,128)(2,1)}, bf16[48,4096]{1,0:T(8,128)(2,1)S(1)}, u32[]{:S(2)}) copy-start(bf16[48,4096]{1,0:T(8,128)(2,1)S(1)} %collective-permute-done.refs_1_) | copy-start | bytes 1179652
  61.5 43.9 %collective-permute-start.5 = (bf16[48,4096]{1,0:T(8,128)(2,1)S(1)}, bf16[48,4096]{1,0:T(8,128)(2,1)}, u32[]{:S(2)}, u32[]{:S(2)}) collective-permute-start(bf16[48,4096]{1,0:T(8,128)(2,1)S(1)} %copy-done.16), channel_id=1, source_target_pairs={{0,6},{1,7},{2,0},{3,1},{4,2},{5,3},{6,4},{7,5},{64,70},{65,71},{6... | collective-permute-start | bytes 1179656 | tf_op jit(solution)/shard_map/ppermute | solution.py:444
  66.4 39.1 %copy-start.9 = (bf16[48,4096]{1,0:T(8,128)(2,1)}, bf16[48,4096]{1,0:T(8,128)(2,1)S(1)}, u32[]{:S(2)}) copy-start(bf16[48,4096]{1,0:T(8,128)(2,1)S(1)} %collective-permute-done.1.refs_2_) | copy-start | bytes 1179652
  66.4 39.1 %collective-permute-start.6 = (bf16[48,4096]{1,0:T(8,128)(2,1)S(1)}, bf16[48,4096]{1,0:T(8,128)(2,1)}, u32[]{:S(2)}, u32[]{:S(2)}) collective-permute-start(bf16[48,4096]{1,0:T(8,128)(2,1)S(1)} %copy-done.15), channel_id=1, source_target_pairs={{0,71},{1,70},{2,65},{3,64},{4,67},{5,66},{6,69},{7,68},{64,7},{65... | collective-permute-start | bytes 1179656 | tf_op jit(solution)/shard_map/ppermute | solution.py:444
  115.7 25.9 %collective-permute-start.7 = (bf16[2,4,256,384]{3,2,1,0:T(8,128)(2,1)}, bf16[2,4,256,384]{3,2,1,0:T(8,128)(2,1)}, u32[]{:S(2)}, u32[]{:S(2)}) collective-permute-start(bf16[2,4,256,384]{3,2,1,0:T(8,128)(2,1)} %get-tuple-element.70), channel_id=1, source_target_pairs={{0,32},{32,0},{1,33},{33,1},{2,34},{34,2},{3,35},{35,3},{4,36},{36... | collective-permute-start | bytes 4718600 | tf_op jit(solution)/shard_map/ppermute | solution.py:511
  135.4 6.2 %collective-permute-start.8 = (bf16[2,384,768]{2,1,0:T(8,128)(2,1)}, bf16[2,384,768]{2,1,0:T(8,128)(2,1)}, u32[]{:S(2)}, u32[]{:S(2)}) collective-permute-start(bf16[2,384,768]{2,1,0:T(8,128)(2,1)} %get-tuple-element.75.mine_ref.grads_ref), channel_id=1, source_target_pairs={{0,32},{32,0},{1,33},{33,1},{2,34},{34,2},{3,35},{35,3},{4,36},{36... | collective-permute-start | bytes 3538952 | tf_op jit(solution)/shard_map/ppermute | solution.py:515
  135.9 5.2 %copy-start.7 = (bf16[384,768]{1,0:T(8,128)(2,1)S(1)}, bf16[384,768]{1,0:T(8,128)(2,1)}, u32[]{:S(2)}) copy-start(bf16[384,768]{1,0:T(8,128)(2,1)} %get-tuple-element.58.hidden_ref) | copy-start | bytes 1769476
  141.1 13.2 %collective-permute-start.9 = (bf16[2,4,256,384]{3,2,1,0:T(8,128)(2,1)}, bf16[2,4,256,384]{3,2,1,0:T(8,128)(2,1)}, u32[]{:S(2)}, u32[]{:S(2)}) collective-permute-start(bf16[2,4,256,384]{3,2,1,0:T(8,128)(2,1)} %get-tuple-element.73), channel_id=1, source_target_pairs={{0,32},{32,0},{1,33},{33,1},{2,34},{34,2},{3,35},{35,3},{4,36},{36... | collective-permute-start | bytes 4718600 | tf_op jit(solution)/shard_map/ppermute | solution.py:518
  141.1 13.2 %collective-permute-start.10 = (bf16[384,768]{1,0:T(8,128)(2,1)S(1)}, bf16[384,768]{1,0:T(8,128)(2,1)}, u32[]{:S(2)}, u32[]{:S(2)}) collective-permute-start(bf16[384,768]{1,0:T(8,128)(2,1)S(1)} %copy-done.7), channel_id=1, source_target_pairs={{0,32},{32,0},{1,33},{33,1},{2,34},{34,2},{3,35},{35,3},{4,36},{36... | collective-permute-start | bytes 1769480 | tf_op jit(solution)/shard_map/ppermute | solution.py:513
  152.7 29.4 %collective-permute-start.14 = (bf16[1,256,1536]{2,1,0:T(8,128)(2,1)}, bf16[1,256,1536]{2,1,0:T(8,128)(2,1)}, u32[]{:S(2)}, u32[]{:S(2)}) collective-permute-start(bf16[1,256,1536]{2,1,0:T(8,128)(2,1)} %get-tuple-element.83), channel_id=1, source_target_pairs={{0,8},{8,16},{16,24},{24,0},{1,9},{9,17},{17,25},{25,1},{2,10},{10... | collective-permute-start | bytes 2359304 | tf_op jit(solution)/shard_map/ppermute | solution.py:455
  161.2 36.4 %collective-permute-start.18 = (bf16[4,256,768]{2,1,0:T(8,128)(2,1)}, bf16[4,256,768]{2,1,0:T(8,128)(2,1)}, u32[]{:S(2)}, u32[]{:S(2)}) collective-permute-start(bf16[4,256,768]{2,1,0:T(8,128)(2,1)} %get-tuple-element.86), channel_id=1, source_target_pairs={{0,64},{64,0},{1,65},{65,1},{2,66},{66,2},{3,67},{67,3},{4,68},{68... | collective-permute-start | bytes 4718600 | tf_op jit(solution)/shard_map/ppermute | solution.py:525
  162.7 21.2 %collective-permute-start.11 = (bf16[1,256,1536]{2,1,0:T(8,128)(2,1)}, bf16[1,256,1536]{2,1,0:T(8,128)(2,1)}, u32[]{:S(2)}, u32[]{:S(2)}) collective-permute-start(bf16[1,256,1536]{2,1,0:T(8,128)(2,1)} %get-tuple-element.79), channel_id=1, source_target_pairs={{0,24},{8,0},{16,8},{24,16},{1,25},{9,1},{17,9},{25,17},{2,26},{10... | collective-permute-start | bytes 2359304 | tf_op jit(solution)/shard_map/ppermute | solution.py:456
  164.4 44.9 %collective-permute-start.16 = (bf16[1,256,1536]{2,1,0:T(8,128)(2,1)}, bf16[1,256,1536]{2,1,0:T(8,128)(2,1)}, u32[]{:S(2)}, u32[]{:S(2)}) collective-permute-start(bf16[1,256,1536]{2,1,0:T(8,128)(2,1)} %get-tuple-element.84), channel_id=1, source_target_pairs={{0,24},{8,0},{16,8},{24,16},{1,25},{9,1},{17,9},{25,17},{2,26},{10... | collective-permute-start | bytes 2359304 | tf_op jit(solution)/shard_map/ppermute | solution.py:458
  178.4 58.5 %all-to-all-start.1 = ((bf16[8,48,4224]{2,1,0:T(8,128)(2,1)}), bf16[8,48,4224]{2,1,0:T(8,128)(2,1)S(1)}, u32[]{:S(2)}, u32[]{:S(2)}) async-start(bf16[8,48,4224]{2,1,0:T(8,128)(2,1)} %slot_rows.1), calls=%async_computation.1 | async-start | bytes 6488064 | tf_op jit(solution)/shard_map/all_to_all | solution.py:470
  182.1 1.9 copy-start.5
  183.7 13.9 %copy-start.2 = (bf16[4,256,768]{2,1,0:T(8,128)(2,1)S(1)}, bf16[4,256,768]{2,1,0:T(8,128)(2,1)}, u32[]{:S(2)}) copy-start(bf16[4,256,768]{2,1,0:T(8,128)(2,1)} %get-tuple-element.74) | copy-start | bytes 4718596
  183.7 27.3 %collective-permute-start.15 = (bf16[1,256,1536]{2,1,0:T(8,128)(2,1)S(1)}, bf16[1,256,1536]{2,1,0:T(8,128)(2,1)S(1)}, u32[]{:S(2)}, u32[]{:S(2)}) collective-permute-start(bf16[1,256,1536]{2,1,0:T(8,128)(2,1)S(1)} %add_convert_fusion.2), channel_id=1, source_target_pairs={{0,8},{8,16},{16,24},{24,0},{1,9},{9,17},{17,25},{25,1},{2,10},{10... | collective-permute-start | bytes 2359304 | tf_op jit(solution)/shard_map/ppermute | solution.py:461
  199.5 1.7 copy-start.14
  199.5 12.0 %copy-start.4 = (bf16[1,256,1536]{2,1,0:T(8,128)(2,1)S(1)}, bf16[1,256,1536]{2,1,0:T(8,128)(2,1)}, u32[]{:S(2)}) copy-start(bf16[1,256,1536]{2,1,0:T(8,128)(2,1)} %get-tuple-element.81) | copy-start | bytes 2359300
  199.5 9.7 %collective-permute-start.19 = (bf16[128,768]{1,0:T(8,128)(2,1)S(1)}, bf16[128,768]{1,0:T(8,128)(2,1)S(1)}, u32[]{:S(2)}, u32[]{:S(2)}) collective-permute-start(bf16[128,768]{1,0:T(8,128)(2,1)S(1)} %get-tuple-element.90), channel_id=1, source_target_pairs={{0,8},{8,16},{16,24},{24,0},{1,9},{9,17},{17,25},{25,1},{2,10},{10... | collective-permute-start | bytes 589832 | tf_op jit(solution)/shard_map/ppermute | solution.py:455
  201.2 31.0 %collective-permute-start.13 = (bf16[1,256,1536]{2,1,0:T(8,128)(2,1)S(1)}, bf16[1,256,1536]{2,1,0:T(8,128)(2,1)S(1)}, u32[]{:S(2)}, u32[]{:S(2)}) collective-permute-start(bf16[1,256,1536]{2,1,0:T(8,128)(2,1)S(1)} %copy-done.14), channel_id=1, source_target_pairs={{0,8},{8,16},{16,24},{24,0},{1,9},{9,17},{17,25},{25,1},{2,10},{10... | collective-permute-start | bytes 2359304 | tf_op jit(solution)/shard_map/ppermute | solution.py:457
  202.5 29.7 %collective-permute-start.12 = (bf16[1,256,1536]{2,1,0:T(8,128)(2,1)S(1)}, bf16[1,256,1536]{2,1,0:T(8,128)(2,1)S(1)}, u32[]{:S(2)}, u32[]{:S(2)}) collective-permute-start(bf16[1,256,1536]{2,1,0:T(8,128)(2,1)S(1)} %add_convert_fusion.3), channel_id=1, source_target_pairs={{0,24},{8,0},{16,8},{24,16},{1,25},{9,1},{17,9},{25,17},{2,26},{10... | collective-permute-start | bytes 2359304 | tf_op jit(solution)/shard_map/ppermute | solution.py:462
  209.2 17.4 %collective-permute-start.21 = (bf16[128,768]{1,0:T(8,128)(2,1)S(1)}, bf16[128,768]{1,0:T(8,128)(2,1)S(1)}, u32[]{:S(2)}, u32[]{:S(2)}) collective-permute-start(bf16[128,768]{1,0:T(8,128)(2,1)S(1)} %get-tuple-element.93), channel_id=1, source_target_pairs={{0,24},{8,0},{16,8},{24,16},{1,25},{9,1},{17,9},{25,17},{2,26},{10... | collective-permute-start | bytes 589832 | tf_op jit(solution)/shard_map/ppermute | solution.py:458
  209.3 19.4 %collective-permute-start.22 = (bf16[128,768]{1,0:T(8,128)(2,1)S(1)}, bf16[128,768]{1,0:T(8,128)(2,1)S(1)}, u32[]{:S(2)}, u32[]{:S(2)}) collective-permute-start(bf16[128,768]{1,0:T(8,128)(2,1)S(1)} %get-tuple-element.92), channel_id=1, source_target_pairs={{0,24},{8,0},{16,8},{24,16},{1,25},{9,1},{17,9},{25,17},{2,26},{10... | collective-permute-start | bytes 589832 | tf_op jit(solution)/shard_map/ppermute | solution.py:456
  211.0 19.0 %collective-permute-start.20 = (bf16[128,768]{1,0:T(8,128)(2,1)S(1)}, bf16[128,768]{1,0:T(8,128)(2,1)S(1)}, u32[]{:S(2)}, u32[]{:S(2)}) collective-permute-start(bf16[128,768]{1,0:T(8,128)(2,1)S(1)} %fusion.11), channel_id=1, source_target_pairs={{0,8},{8,16},{16,24},{24,0},{1,9},{9,17},{17,25},{25,1},{2,10},{10... | collective-permute-start | bytes 589832 | tf_op jit(solution)/shard_map/ppermute | solution.py:461
  213.8 18.4 %copy-start.6 = (bf16[1,256,1536]{2,1,0:T(8,128)(2,1)S(1)}, bf16[1,256,1536]{2,1,0:T(8,128)(2,1)}, u32[]{:S(2)}) copy-start(bf16[1,256,1536]{2,1,0:T(8,128)(2,1)} %get-tuple-element.71) | copy-start | bytes 2359300
  226.6 15.2 %collective-permute-start.17 = (bf16[1,256,1536]{2,1,0:T(8,128)(2,1)}, bf16[1,256,1536]{2,1,0:T(8,128)(2,1)}, u32[]{:S(2)}, u32[]{:S(2)}) collective-permute-start(bf16[1,256,1536]{2,1,0:T(8,128)(2,1)} %add_convert_fusion.1), channel_id=1, source_target_pairs={{0,64},{64,0},{1,65},{65,1},{2,66},{66,2},{3,67},{67,3},{4,68},{68... | collective-permute-start | bytes 2359304 | tf_op jit(solution)/shard_map/ppermute | solution.py:527
  228.7 6.9 %collective-permute-start.24 = (bf16[128,768]{1,0:T(8,128)(2,1)S(1)}, bf16[128,768]{1,0:T(8,128)(2,1)S(1)}, u32[]{:S(2)}, u32[]{:S(2)}) collective-permute-start(bf16[128,768]{1,0:T(8,128)(2,1)S(1)} %get-tuple-element.91), channel_id=1, source_target_pairs={{0,8},{8,16},{16,24},{24,0},{1,9},{9,17},{17,25},{25,1},{2,10},{10... | collective-permute-start | bytes 589832 | tf_op jit(solution)/shard_map/ppermute | solution.py:457
  230.1 5.7 %collective-permute-start.23 = (bf16[128,768]{1,0:T(8,128)(2,1)S(1)}, bf16[128,768]{1,0:T(8,128)(2,1)S(1)}, u32[]{:S(2)}, u32[]{:S(2)}) collective-permute-start(bf16[128,768]{1,0:T(8,128)(2,1)S(1)} %get-tuple-element.89), channel_id=1, source_target_pairs={{0,24},{8,0},{16,8},{24,16},{1,25},{9,1},{17,9},{25,17},{2,26},{10... | collective-permute-start | bytes 589832 | tf_op jit(solution)/shard_map/ppermute | solution.py:462
  233.6 3.3 %copy-start.11 = (bf16[384,128]{1,0:T(8,128)(2,1)S(1)}, bf16[384,128]{1,0:T(8,128)(2,1)}, u32[]{:S(2)}) copy-start(bf16[384,128]{1,0:T(8,128)(2,1)} %get-tuple-element.48) | copy-start | bytes 294916
  233.6 3.3 %copy-start.12 = (f32[4096]{0:T(1024)S(1)}, f32[4096]{0:T(1024)}, u32[]{:S(2)}) copy-start(f32[4096]{0:T(1024)} %param.8) | copy-start | bytes 49156
  236.9 2.3 copy-start
  236.9 2.3 copy-start.3
  239.2 2.6 %copy-start.10 = (bf16[384,256]{1,0:T(8,128)(2,1)S(1)}, bf16[384,256]{1,0:T(8,128)(2,1)}, u32[]{:S(2)}) copy-start(bf16[384,256]{1,0:T(8,128)(2,1)} %get-tuple-element.77) | copy-start | bytes 589828
  239.2 2.8 %copy-start.13 = (bf16[128,2]{0,1:T(2,128)(2,1)S(1)}, bf16[128,2]{0,1:T(2,128)(2,1)}, u32[]{:S(2)}) copy-start(bf16[128,2]{0,1:T(2,128)(2,1)} %param.11) | copy-start | bytes 1540
  239.2 3.3 %copy-start.1 = (f32[1,256,1536]{2,1,0:T(8,128)S(1)}, f32[1,256,1536]{2,1,0:T(8,128)}, u32[]{:S(2)}) copy-start(f32[1,256,1536]{2,1,0:T(8,128)} %convert_add_fusion.1) | copy-start | bytes 4718596
